TPU v7x, 8 devices: a whole 2x2x1 slice. The times are simulated.
8 devices in a mesh: data: 2 (over z, y), model: 4 (over x, core).
Axes of the slice: x: 2, y: 2, z: 1, core: 2. Of those that a mesh axis runs over, the one named last changes fastest.
Arguments:
- x_saved: bfloat16 [2, 32, 2048, 768], P(None, 'data', 'model')
- h_saved: bfloat16 [2, 32, 2048, 3072], P(None, 'data', None, 'model')
- w_up: bfloat16 [2, 768, 3072], P(None, None, 'model')
- w_down: bfloat16 [2, 3072, 768], P(None, 'model')
- grad_out: bfloat16 [32, 2048, 768], P('data', 'model')
Outputs:
- output 1: bfloat16 [32, 2048, 768], P('data', 'model')
- output 2: float32 [2, 768, 3072], P(None, None, 'model')
- output 3: float32 [2, 3072, 768], P(None, 'model')
All inputs are finite; a program needn't handle non-finite values.
Results may differ from a plain program's by a relative error of at most 0.0126265.
Values are sent between devices in bfloat16 or wider.
A program may use at most 1 GiB of HBM per device.

v0:
```python
import jax
import jax.numpy as jnp
from jax import lax
from jax.sharding import PartitionSpec as P


def gelu_parts(pre_act):
    inner = 0.7978845608028654 * (pre_act + 0.044715 * pre_act * pre_act * pre_act)
    tanh_val = jnp.tanh(inner)
    gelu_out = 0.5 * pre_act * (1.0 + tanh_val)
    gelu_slope = 0.5 * (1.0 + tanh_val) + 0.5 * pre_act * (1.0 - tanh_val * tanh_val) * 0.7978845608028654 * (1.0 + 0.134145 * pre_act * pre_act)
    return gelu_out, gelu_slope


def solution(mesh):
    def device_step(x_saved, h_saved, w_up, w_down, grad_out):
        layers = w_up.shape[0]
        grad_next = grad_out
        up_list = []
        down_list = []
        for layer in reversed(range(layers)):
            grad_full = lax.all_gather(grad_next, "model", axis=1, tiled=True)
            d_act = jnp.einsum("bsd,fd->bsf", grad_full, w_down[layer], preferred_element_type=jnp.float32)
            gelu_out, gelu_slope = gelu_parts(h_saved[layer].astype(jnp.float32))
            d_pre = (d_act * gelu_slope).astype(jnp.bfloat16)
            part_sum = jnp.einsum("bsf,df->bsd", d_pre, w_up[layer], preferred_element_type=jnp.float32).astype(jnp.bfloat16)
            branch = lax.psum_scatter(part_sum, "model", scatter_dimension=1, tiled=True)
            new_grad = (grad_next.astype(jnp.float32) + branch.astype(jnp.float32)).astype(jnp.bfloat16)
            x_full = lax.all_gather(x_saved[layer], "model", axis=1, tiled=True)
            grad_down = jnp.einsum("bsf,bsd->fd", gelu_out.astype(jnp.bfloat16), grad_full, preferred_element_type=jnp.float32)
            grad_up = jnp.einsum("bsd,bsf->df", x_full, d_pre, preferred_element_type=jnp.float32)
            up_list.append(grad_up)
            down_list.append(grad_down)
            grad_next = new_grad
        up_total = lax.psum(jnp.stack(up_list[::-1]), "data")
        down_total = lax.psum(jnp.stack(down_list[::-1]), "data")
        return grad_next, up_total, down_total

    return jax.shard_map(
        device_step,
        mesh=mesh,
        in_specs=(P(None, "data", "model", None), P(None, "data", None, "model"), P(None, None, "model"), P(None, "model", None), P("data", "model", None)),
        out_specs=(P("data", "model", None), P(None, None, "model"), P(None, "model", None)),
        check_vma=False,
    )
```

profile of v0, /device:TPU:0, one launch (start us, length us, event | category | flops | bytes accessed | tf_op | source)
XLA Modules:
  0.0 2393.3 jit_solution(17893749053225339955)
XLA Ops:
  7.2 0.0 all-gather.7.cloned.1.call-start
  7.2 0.7 all-gather.7.cloned.1.call-update
  7.9 0.0 reduce-scatter.3.cloned.1.call-start
  7.9 1.4 fusion.89
  9.3 299.2 %all-gather.7.cloned.1.call-done = bf16[16,2048,768]{2,1,0:T(8,128)(2,1)} async-done(((bf16[16,512,768]{2,1,0:T(8,128)(2,1)}), bf16[16,2048,768]{2,1,0:T(8,128)(2,1)}) %all-gather.7.cloned.1.call-update) | async-done | bytes 50331664 | tf_op jit(solution)/shard_map/all_gather | solution.py:22
  308.5 0.0 copy-start.4
  308.5 99.4 %fusion.14 = bf16[16,2048,768]{2,1,0:T(8,128)(2,1)} fusion(bf16[2,16,2048,768]{3,2,1,0:T(8,128)(2,1)} %param.6, bf16[16,2048,768]{2,1,0:T(8,128)(2,1)} %all-gather.7.cloned.1.call-done, bf16[768,768,1]{1,0,2:T(8,128)(2,1)S(1)} %fusion.89), kind=kOutput, calls=%fused_computation.28 | convolution fusion | flops 39158022144 | bytes 152174592 | tf_op jit(solution)/shard_map/bsd,fd->bsf/dot_general | solution.py:23
  407.9 0.0 copy-done.4
  407.9 47.9 %convolution_convert_fusion.1 = bf16[16,2048,768]{2,1,0:T(8,128)(2,1)} fusion(bf16[16,2048,768]{2,1,0:T(8,128)(2,1)} %fusion.14, bf16[2,768,768]{2,1,0:T(8,128)(2,1)S(1)} %copy-done.4), kind=kOutput, calls=%fused_computation.45 | convolution fusion | flops 38679871488 | bytes 101842944 | tf_op jit(solution)/shard_map/bsf,df->bsd/dot_general | solution.py:26
  455.8 0.0 reduce-scatter.3.cloned.1.call-update
  455.8 0.0 all-gather.13.cloned.1.call-start
  455.9 23.3 fusion.60
  479.1 0.0 copy-start
  479.1 0.0 all-gather.13.cloned.1.call-update
  479.2 0.0 all-gather.9.cloned.1.call-start
  479.2 317.7 %reduce-scatter.3.cloned.1.call-done = bf16[16,512,768]{2,1,0:T(8,128)(2,1)} async-done(((bf16[16,2048,768]{2,1,0:T(8,128)(2,1)}), bf16[16,512,768]{2,1,0:T(8,128)(2,1)}) %reduce-scatter.3.cloned.1.call-update) | async-done | bytes 12582928 | tf_op jit(solution)/shard_map/reduce_scatter | solution.py:27
  796.9 19.1 add_convert_fusion.1
  816.0 0.0 all-gather.9.cloned.1.call-update
  816.0 0.0 all-gather.11.cloned.1.call-start
  816.1 0.5 all-gather.11.cloned.1.call-update
  816.6 0.0 all-reduce.3.cloned.1.call-start
  816.7 0.0 copy-done
  816.7 1.2 fusion.87
  817.9 276.8 %all-gather.13.cloned.1.call-done = bf16[1,16,2048,768]{3,2,1,0:T(8,128)(2,1)} async-done(((bf16[1,16,512,768]{3,2,1,0:T(8,128)(2,1)}), bf16[1,16,2048,768]{3,2,1,0:T(8,128)(2,1)}) %all-gather.13.cloned.1.call-update) | async-done | bytes 50331664 | tf_op jit(solution)/shard_map/all_gather | solution.py:29
  1094.7 59.7 %fusion.41 = f32[1,768,768]{1,2,0:T(8,128)} fusion(bf16[16,2048,768]{2,1,0:T(8,128)(2,1)} %fusion.14, bf16[1,16,2048,768]{3,2,1,0:T(8,128)(2,1)} %all-gather.13.cloned.1.call-done), kind=kOutput, calls=%fused_computation.53 | convolution fusion | flops 38654705664 | bytes 103022592 | tf_op jit(solution)/shard_map/bsd,bsf->df/dot_general | solution.py:31
  1154.4 0.0 copy-start.3
  1154.4 62.6 %fusion.35 = f32[1,768,768]{2,1,0:T(8,128)} fusion(bf16[16,2048,768]{2,1,0:T(8,128)(2,1)} %all-gather.7.cloned.1.call-done, bf16[2,16,2048,768]{3,2,1,0:T(8,128)(2,1)} %param.6), kind=kOutput, calls=%fused_computation.51 | convolution fusion | flops 38906363904 | bytes 103022592 | tf_op jit(solution)/shard_map/bsf,bsd->fd/dot_general | solution.py:30
  1217.0 175.8 %all-gather.9.cloned.1.call-done = bf16[16,2048,768]{2,1,0:T(8,128)(2,1)} async-done(((bf16[16,512,768]{2,1,0:T(8,128)(2,1)}), bf16[16,2048,768]{2,1,0:T(8,128)(2,1)}) %all-gather.9.cloned.1.call-update) | async-done | bytes 50331664 | tf_op jit(solution)/shard_map/all_gather | solution.py:22
  1392.8 0.0 copy-done.3
  1392.8 99.7 %fusion.8 = bf16[16,2048,768]{2,1,0:T(8,128)(2,1)} fusion(bf16[2,16,2048,768]{3,2,1,0:T(8,128)(2,1)} %param.6, bf16[16,2048,768]{2,1,0:T(8,128)(2,1)} %all-gather.9.cloned.1.call-done, bf16[768,768,1]{1,0,2:T(8,128)(2,1)S(1)} %copy-done.3), kind=kOutput, calls=%fused_computation.22 | convolution fusion | flops 39158022144 | bytes 152174592 | tf_op jit(solution)/shard_map/bsd,fd->bsf/dot_general | solution.py:23
  1492.5 0.0 copy-start.2
  1492.5 197.9 %all-gather.11.cloned.1.call-done = bf16[1,16,2048,768]{3,2,1,0:T(8,128)(2,1)} async-done(((bf16[1,16,512,768]{3,2,1,0:T(8,128)(2,1)}), bf16[1,16,2048,768]{3,2,1,0:T(8,128)(2,1)}) %all-gather.11.cloned.1.call-update) | async-done | bytes 50331664 | tf_op jit(solution)/shard_map/all_gather | solution.py:29
  1690.4 51.4 %fusion.38 = f32[1,768,768]{1,2,0:T(8,128)S(1)} fusion(bf16[16,2048,768]{2,1,0:T(8,128)(2,1)} %fusion.8, bf16[1,16,2048,768]{3,2,1,0:T(8,128)(2,1)} %all-gather.11.cloned.1.call-done), kind=kOutput, calls=%fused_computation.52 | convolution fusion | flops 38654705664 | bytes 103022592 | tf_op jit(solution)/shard_map/bsd,bsf->df/dot_general | solution.py:31
  1741.7 0.0 copy-done.2
  1741.8 2.5 pad_maximum_fusion
  1744.2 0.0 copy-start.1
  1744.2 0.0 copy-start.5
  1744.2 61.6 %fusion.32 = f32[1,768,768]{2,1,0:T(8,128)S(1)} fusion(bf16[16,2048,768]{2,1,0:T(8,128)(2,1)} %all-gather.9.cloned.1.call-done, bf16[2,16,2048,768]{3,2,1,0:T(8,128)(2,1)} %param.6), kind=kOutput, calls=%fused_computation.50 | convolution fusion | flops 38906363904 | bytes 103022592 | tf_op jit(solution)/shard_map/bsf,bsd->fd/dot_general | solution.py:30
  1805.9 0.0 copy-done.1
  1805.9 2.5 pad_maximum_fusion.1
  1808.4 0.0 all-reduce.3.cloned.1.call-update
  1808.4 0.0 reduce-scatter.5.cloned.1.call-start
  1808.4 0.0 copy-done.5
  1808.4 49.0 %convolution_convert_fusion = bf16[16,2048,768]{2,1,0:T(8,128)(2,1)} fusion(bf16[16,2048,768]{2,1,0:T(8,128)(2,1)} %fusion.8, bf16[2,768,768]{2,1,0:T(8,128)(2,1)S(1)} %copy-done.5), kind=kOutput, calls=%fused_computation.44 | convolution fusion | flops 38679871488 | bytes 101842944 | tf_op jit(solution)/shard_map/bsf,df->bsd/dot_general | solution.py:26
  1857.4 0.0 reduce-scatter.5.cloned.1.call-update
  1857.4 166.2 %all-reduce.3.cloned.1.call-done = (f32[2,768,768]{1,2,0:T(8,128)}, f32[2,768,768]{2,1,0:T(8,128)}) async-done(((f32[2,768,768]{1,2,0:T(8,128)}, f32[2,768,768]{2,1,0:T(8,128)}), (f32[2,768,768]{1,2,0:T(8,128)}, f32[2,768,768]{2,1,0:T(8,128)})) %all-reduce.3.cloned.1.call-update) | async-done | bytes 9437200 | tf_op jit(solution)/shard_map/psum | solution.py:35
  2023.7 6.0 copy.12
  2029.7 337.5 %reduce-scatter.5.cloned.1.call-done = bf16[16,512,768]{2,1,0:T(8,128)(2,1)} async-done(((bf16[16,2048,768]{2,1,0:T(8,128)(2,1)}), bf16[16,512,768]{2,1,0:T(8,128)(2,1)}) %reduce-scatter.5.cloned.1.call-update) | async-done | bytes 12582928 | tf_op jit(solution)/shard_map/reduce_scatter | solution.py:27
  2367.2 14.0 add_convert_fusion
  2381.2 4.8 copy.19
Async XLA Ops:
  7.2 301.3 %all-gather.7.cloned.1.call-start = ((), (), s32[]{:S(2)}) async-start(), calls=%async_computation.2 | async-start | bytes 62914560 | tf_op jit(solution)/shard_map/all_gather | solution.py:22
  7.9 789.1 %reduce-scatter.3.cloned.1.call-start = ((), (), s32[]{:S(2)}) async-start(), calls=%async_computation.3 | async-start | bytes 62914560 | tf_op jit(solution)/shard_map/reduce_scatter | solution.py:27
  308.5 99.4 %copy-start.4 = (bf16[2,768,768]{2,1,0:T(8,128)(2,1)S(1)}, bf16[2,768,768]{2,1,0:T(8,128)(2,1)}, u32[]{:S(2)}) copy-start(bf16[2,768,768]{2,1,0:T(8,128)(2,1)} %param.7) | copy-start | bytes 7077892
  455.8 638.8 %all-gather.13.cloned.1.call-start = ((), (), s32[]{:S(2)}) async-start(), calls=%async_computation.7 | async-start | bytes 62914560 | tf_op jit(solution)/shard_map/all_gather | solution.py:29
  479.1 337.5 %copy-start = (bf16[2,768,768]{2,1,0:T(8,128)(2,1)S(1)}, bf16[2,768,768]{2,1,0:T(8,128)(2,1)}, u32[]{:S(2)}) copy-start(bf16[2,768,768]{2,1,0:T(8,128)(2,1)} %param.8) | copy-start | bytes 7077892
  479.2 913.6 %all-gather.9.cloned.1.call-start = ((), (), s32[]{:S(2)}) async-start(), calls=%async_computation.4 | async-start | bytes 62914560 | tf_op jit(solution)/shard_map/all_gather | solution.py:22
  816.0 874.3 %all-gather.11.cloned.1.call-start = ((), (), s32[]{:S(2)}) async-start(), calls=%async_computation.6 | async-start | bytes 62914560 | tf_op jit(solution)/shard_map/all_gather | solution.py:29
  816.6 1207.0 %all-reduce.3.cloned.1.call-start = ((), (), s32[]{:S(2)}) async-start(), calls=%async_computation.8 | async-start | bytes 18874368 | tf_op jit(solution)/shard_map/psum | solution.py:35
  1154.4 238.4 %copy-start.3 = (bf16[768,768,1]{1,0,2:T(8,128)(2,1)S(1)}, bf16[768,768,1]{1,0,2:T(8,128)(2,1)}, u32[]{:S(2)}) copy-start(bf16[768,768,1]{1,0,2:T(8,128)(2,1)} %fusion.87) | copy-start | bytes 3538948
  1492.5 249.2 %copy-start.2 = (f32[1,768,768]{1,2,0:T(8,128)S(1)}, f32[1,768,768]{1,2,0:T(8,128)}, u32[]{:S(2)}) copy-start(f32[1,768,768]{1,2,0:T(8,128)} %fusion.41) | copy-start | bytes 7077892
  1744.2 61.6 %copy-start.1 = (f32[1,768,768]{2,1,0:T(8,128)S(1)}, f32[1,768,768]{2,1,0:T(8,128)}, u32[]{:S(2)}) copy-start(f32[1,768,768]{2,1,0:T(8,128)} %fusion.35) | copy-start | bytes 7077892
  1744.2 64.2 %copy-start.5 = (bf16[2,768,768]{2,1,0:T(8,128)(2,1)S(1)}, bf16[2,768,768]{2,1,0:T(8,128)(2,1)}, u32[]{:S(2)}) copy-start(bf16[2,768,768]{2,1,0:T(8,128)(2,1)} %param.7) | copy-start | bytes 7077892
  1808.4 558.8 %reduce-scatter.5.cloned.1.call-start = ((), (), s32[]{:S(2)}) async-start(), calls=%async_computation.5 | async-start | bytes 62914560 | tf_op jit(solution)/shard_map/reduce_scatter | solution.py:27
Sparse Core Ops, SparseCore 0:
  9.5 298.9 all-gather.6
  455.9 340.9 reduce-scatter.2
  798.5 296.1 all-gather.12
  1096.6 296.1 all-gather.8
  1394.2 296.1 all-gather.10
  1808.5 215.1 all-reduce.2
  2026.2 340.9 reduce-scatter.4
where the time goes:
time: 2400 us; the launch traced here: 2390 us
  waiting for transfers between devices  1770 us (74%)
  matrix products  531 us (22%)
  other arithmetic  38 us (2%)
  local copies, waits for them, and re-layouts  36.7 us (2%)
    reduce_scatter x2, waiting for transfers between devices, device_step(): lax.psum_scatter(part_sum, 'model', scatter_dimension=1, tiled=True)  655 us
    all_gather x2, waiting for transfers between devices, device_step(): grad_full = lax.all_gather(grad_next, 'model', axis=1, tiled=True)  475 us
    all_gather x2, waiting for transfers between devices, device_step(): x_full = lax.all_gather(x_saved[layer], 'model', axis=1, tiled=True)  475 us
    dot_general x2, matrix products, device_step(): jnp.einsum('bsd,fd->bsf', grad_full, w_down[layer], preferred_element_typ...  199 us
    psum x1, waiting for transfers between devices, device_step(): up_total = lax.psum(jnp.stack(up_list[::-1]), 'data')  166 us
    dot_general x2, matrix products, device_step(): jnp.einsum('bsf,bsd->fd', gelu_out.astype(jnp.bfloat16), grad_full, prefe...  124 us
    dot_general x2, matrix products, device_step(): jnp.einsum('bsd,bsf->df', x_full, d_pre, preferred_element_type=jnp.float32)  111 us
    dot_general x2, matrix products, device_step(): jnp.einsum('bsf,df->bsd', d_pre, w_up[layer], preferred_element_type=jnp....  96.9 us
  transfers between devices with their start and end apart: 7, of which 7 were waited for; matrix products, arithmetic and copies ran while one was open for 13% of the time, Pallas kernels for 0%

commit v1 on v0

v1 whole, which is shorter than its diff:
```python
import functools

import jax
import jax.numpy as jnp
from jax import lax
from jax.experimental import pallas as pl
from jax.experimental.pallas import tpu as pltpu
from jax.sharding import PartitionSpec as P


BF16 = jnp.bfloat16
F32 = jnp.float32
BLOCKS = (384, 256)
LANES = 128
SMALL = 64


def gelu_parts(pre_act):
    root = 0.7978845608028654
    cubic = (0.134145 * pre_act) * pre_act
    gate = 0.5 + 0.5 * jnp.tanh(pre_act * (root + (root / 3) * cubic))
    gelu_out = pre_act * gate
    gelu_slope = gate + gelu_out * (1.0 - gate) * (2 * root + (2 * root) * cubic)
    return gelu_out, gelu_slope


def dot(lhs, rhs, lhs_dim, rhs_dim):
    return lax.dot_general(lhs, rhs, (((lhs_dim,), (rhs_dim,)), ((), ())), preferred_element_type=F32)


def unit_grads(grad, h, down):
    d_act = dot(grad, down, 1, 1)
    gelu_out, gelu_slope = gelu_parts(h.astype(F32))
    return (d_act * gelu_slope).astype(BF16), gelu_out.astype(BF16)


def block_body(has_carry, final, rows, start, _, *refs):
    refs = list(refs)
    grad_ref, x_ref, h_a, h_b, up_a, up_b, down_a, down_b = (refs.pop(0) for _ in range(8))
    carry_ref = refs.pop(0) if has_carry else None
    out_ref, dw_a, dw_b, h_ref, pre_ref, act_ref, sum_ref, dw_ref, up_ref, down_ref, sem = refs
    row, source = pl.program_id(0), pl.program_id(1)
    width = pre_ref.shape[1]

    @pl.when((row == 0) & (source == 0))
    def _():
        dw_ref[...] = jnp.zeros_like(dw_ref)
        for s, (up, down) in enumerate(((up_a, down_a), (up_b, down_b))):
            up_ref[s] = up[(0,) * (len(up.shape) - 2) + (slice(None), slice(start, start + width))]
            down_ref[s] = down[(0,) * (len(down.shape) - 2) + (slice(start, start + width),)]

    for s, ref in enumerate((h_a, h_b)):
        @pl.when(source == s)
        def _():
            h_ref[...] = ref[(0,) * (len(ref.shape) - 2)]

    grad = grad_ref[0]
    x = x_ref[0, 0]
    for low in range(0, width, 256):
        cols = slice(low, min(low + 256, width))
        pre_ref[:, cols], act_ref[:, cols] = unit_grads(grad, h_ref[:, cols], down_ref[source, cols, :])
    pre, act = pre_ref[...], act_ref[...]
    dw_ref[source, 0] += dot(pre, x, 0, 0)
    dw_ref[source, 1] += dot(act, grad, 0, 0)
    part = dot(pre, up_ref[source], 1, 1)

    @pl.when(source == 0)
    def _():
        sum_ref[...] = part + carry_ref[0] if has_carry else part

    @pl.when(source == 1)
    def _():
        total = sum_ref[...] + part
        out_ref[0] = (grad.astype(F32) + total).astype(BF16) if final else total

    copies = [pltpu.make_async_copy(dw_ref.at[s], dw, sem.at[s]) for s, dw in enumerate((dw_a, dw_b))]
    for s in range(2):
        @pl.when((row == rows - 1) & (source == s))
        def _():
            copies[s].start()

    @pl.when((row == rows - 1) & (source == 1))
    def _():
        copies[0].wait()
        copies[1].wait()


def block_call(quarter, layer, grad, x_saved, h_pair, ups, downs, start, width, carry, final):
    rows, seq, hidden = grad.shape

    def h_spec(h):
        if h.ndim == 4:
            return pl.BlockSpec((1, 1, seq, width), lambda b, s, ids: (layer, b, ids[0], 0))
        return pl.BlockSpec((1, seq, width), lambda b, s, ids: (b, 0, 0))

    def w_spec(w):
        shape = (1,) * (w.ndim - 2) + w.shape[-2:]
        return pl.BlockSpec(shape, lambda b, s, ids: (layer,) * (w.ndim - 2) + (0, 0), pipeline_mode=pl.Buffered(1))

    row_spec = pl.BlockSpec((1, seq, hidden), lambda b, s, ids: (b, 0, 0))
    any_spec = pl.BlockSpec(memory_space=pl.ANY)
    in_specs = [row_spec, pl.BlockSpec((1, 1, seq, hidden), lambda b, s, ids: (layer, b, 0, 0))]
    in_specs += [h_spec(h) for h in h_pair]
    in_specs += [w_spec(w) for w in (*ups, *downs)]
    operands = [grad, x_saved, *h_pair, *ups, *downs]
    if carry is not None:
        in_specs.append(row_spec)
        operands.append(carry)
    dw_shape = (2, width, hidden)
    return pl.pallas_call(
        functools.partial(block_body, carry is not None, final, rows, start),
        out_shape=[jax.ShapeDtypeStruct(grad.shape, BF16 if final else F32)] + [jax.ShapeDtypeStruct(dw_shape, F32)] * 2,
        grid_spec=pltpu.PrefetchScalarGridSpec(
            num_scalar_prefetch=1,
            grid=(rows, 2),
            in_specs=in_specs,
            out_specs=[row_spec, any_spec, any_spec],
            scratch_shapes=[pltpu.VMEM((seq, width), BF16)] * 3
            + [pltpu.VMEM((seq, hidden), F32), pltpu.VMEM((2,) + dw_shape, F32)]
            + [pltpu.VMEM((2, hidden, width), BF16), pltpu.VMEM((2, width, hidden), BF16), pltpu.SemaphoreType.DMA((2,))],
        ),
        compiler_params=pltpu.CompilerParams(dimension_semantics=("arbitrary", "arbitrary"), vmem_limit_bytes=56 * 2**20),
        cost_estimate=pl.CostEstimate(
            flops=16 * rows * seq * hidden * width, bytes_accessed=8 * rows * seq * hidden, transcendentals=2 * rows * seq * width),
    )(quarter, *operands)


def swap_lanes(a, b):
    left = lax.broadcasted_iota(jnp.int32, a.shape, 1) < SMALL
    return jnp.where(left, a, pltpu.roll(b, SMALL, 1)), jnp.where(left, pltpu.roll(a, SMALL, 1), b)


def pack_body(_, lo_ref, hi_ref, left_ref, right_ref):
    left, right = swap_lanes(lo_ref[0, 0].astype(F32), hi_ref[0, 0].astype(F32))
    left_ref[0], right_ref[0] = left.astype(BF16), right.astype(BF16)


def pack_call(target, h_saved, layer, start, seq):
    pairs = h_saved.shape[1] // 2
    specs = [pl.BlockSpec((1, 1, seq, LANES), lambda b, ids, r=r: (layer, b + r * pairs, ids[0], start // LANES)) for r in range(2)]
    return pl.pallas_call(
        pack_body,
        out_shape=[jax.ShapeDtypeStruct((pairs, seq, LANES), BF16)] * 2,
        grid_spec=pltpu.PrefetchScalarGridSpec(
            num_scalar_prefetch=1,
            grid=(pairs,),
            in_specs=specs,
            out_specs=[pl.BlockSpec((1, seq, LANES), lambda b, ids: (b, 0, 0))] * 2,
        ),
        compiler_params=pltpu.CompilerParams(dimension_semantics=("arbitrary",)),
        cost_estimate=pl.CostEstimate(flops=pairs * seq * LANES, bytes_accessed=8 * pairs * seq * LANES, transcendentals=0),
    )(target, h_saved, h_saved)


def small_body(grad_lo, grad_hi, x_lo, x_hi, h_a, h_b, down_a, down_b, dw_ref, pre_ref):
    @pl.when(pl.program_id(0) == 0)
    def _():
        dw_ref[...] = jnp.zeros_like(dw_ref)

    h_pair = swap_lanes(h_a[0].astype(F32), h_b[0].astype(F32))
    down = jnp.concatenate([down_a[...], down_b[...]])
    for r, (h, grad_ref, x_ref) in enumerate(zip(h_pair, (grad_lo, grad_hi), (x_lo, x_hi))):
        grad, x = grad_ref[0], x_ref[0, 0]
        pre, act = unit_grads(grad, h, down)
        pre_ref[r, 0] = pre
        dw_ref[0] += dot(pre, x, 0, 0)
        dw_ref[1] += dot(act, grad, 0, 0)


def small_call(layer, grad, x_saved, h_pair, down_pair, start):
    rows, seq, hidden = grad.shape
    pairs = rows // 2

    def row_specs(lead, index):
        return [pl.BlockSpec(lead + (1, seq, hidden), lambda b, r=r: index + (b + r * pairs, 0, 0)) for r in range(2)]

    h_spec = pl.BlockSpec((1, seq, LANES), lambda b: (b, 0, 0))
    down_spec = pl.BlockSpec((SMALL, hidden), lambda b: (start // SMALL, 0))
    dw_shape = (2, LANES, hidden)
    return pl.pallas_call(
        small_body,
        out_shape=[jax.ShapeDtypeStruct(dw_shape, F32), jax.ShapeDtypeStruct((2, pairs, seq, LANES), BF16)],
        grid=(pairs,),
        in_specs=row_specs((), ()) + row_specs((1,), (layer,)) + [h_spec, h_spec, down_spec, down_spec],
        out_specs=[pl.BlockSpec(dw_shape, lambda b: (0, 0, 0)), pl.BlockSpec((2, 1, seq, LANES), lambda b: (0, b, 0, 0))],
        compiler_params=pltpu.CompilerParams(dimension_semantics=("arbitrary",), vmem_limit_bytes=40 * 2**20),
        cost_estimate=pl.CostEstimate(
            flops=12 * rows * seq * hidden * SMALL, bytes_accessed=4 * rows * seq * hidden, transcendentals=2 * rows * seq * SMALL),
    )(grad, grad, x_saved, x_saved, *h_pair, *down_pair)


def finish_body(grad_ref, carry_ref, pre_a, pre_b, up_a, up_b, *refs):
    out_ref, up_ref = refs[-2:]

    @pl.when(pl.program_id(0) == 0)
    def _():
        first, second = swap_lanes(up_a[...].astype(F32), up_b[...].astype(F32))
        up_ref[:, :LANES], up_ref[:, LANES:] = first.astype(BF16), second.astype(BF16)

    total = carry_ref[0] + dot(jnp.concatenate([pre_a[0, 0], pre_b[0, 0]], axis=1), up_ref[...], 1, 1)
    out_ref[0] = (grad_ref[0].astype(F32) + total).astype(BF16)


def finish_call(grad, carry, pre_pair, up_pair, start, half, out):
    rows, seq, hidden = grad.shape
    pairs = rows // 2
    row_spec = pl.BlockSpec((1, seq, hidden), lambda b: (b + half * pairs, 0, 0))
    pre_spec = pl.BlockSpec((1, 1, seq, LANES), lambda b: (half, b, 0, 0))
    up_spec = pl.BlockSpec((hidden, LANES), lambda b: (0, start // LANES))
    return pl.pallas_call(
        finish_body,
        out_shape=jax.ShapeDtypeStruct(grad.shape, BF16),
        grid=(pairs,),
        in_specs=[row_spec, row_spec, pre_spec, pre_spec, up_spec, up_spec]
        + ([pl.BlockSpec(memory_space=pl.ANY)] if out is not None else []),
        out_specs=row_spec,
        scratch_shapes=[pltpu.VMEM((hidden, 2 * LANES), BF16)],
        input_output_aliases={6: 0} if out is not None else {},
        compiler_params=pltpu.CompilerParams(dimension_semantics=("arbitrary",), vmem_limit_bytes=40 * 2**20),
        cost_estimate=pl.CostEstimate(flops=4 * rows * seq * hidden * SMALL, bytes_accessed=4 * rows * seq * hidden, transcendentals=0),
    )(grad, carry, *pre_pair, *up_pair, *(() if out is None else (out,)))


def place_body(pieces, first_ref, *refs):
    up_ref, down_ref = refs[-2:]
    first = first_ref[0] == 1
    kept = jnp.concatenate([r[...] for r in refs[:pieces]])
    other = jnp.concatenate([r[...] for r in refs[pieces : 2 * pieces]])
    up_ref[0] = jnp.where(first, kept, other).T
    down_ref[0] = jnp.where(first, other, kept)


def place_call(first, kept, other, layer, start, layers, width, bufs):
    size, hidden = kept[0].shape
    step = min(size, LANES)
    row_spec = pl.BlockSpec((step, hidden), lambda i, first: (i, 0))
    out_shape = [jax.ShapeDtypeStruct((layers, hidden, width), F32), jax.ShapeDtypeStruct((layers, width, hidden), F32)]
    any_spec = pl.BlockSpec(memory_space=pl.ANY)
    count = 2 * len(kept)
    return pl.pallas_call(
        functools.partial(place_body, len(kept)),
        out_shape=out_shape,
        grid_spec=pltpu.PrefetchScalarGridSpec(
            num_scalar_prefetch=1,
            grid=(size // step,),
            in_specs=[row_spec] * count + ([any_spec, any_spec] if bufs is not None else []),
            out_specs=[
                pl.BlockSpec((1, hidden, LANES), lambda i, first: (layer, 0, start // LANES + i)),
                pl.BlockSpec((1, LANES, hidden), lambda i, first: (layer, start // LANES + i, 0)),
            ],
        ),
        input_output_aliases={1 + count: 0, 2 + count: 1} if bufs is not None else {},
        compiler_params=pltpu.CompilerParams(dimension_semantics=("arbitrary",)),
        cost_estimate=pl.CostEstimate(flops=4 * size * hidden, bytes_accessed=16 * size * hidden, transcendentals=0),
    )(first, *kept, *other, *(bufs or ()))


def solution(mesh):
    n_model = mesh.shape["model"]

    def to_model(value, flip):
        return lax.ppermute(value, "model", [(i, i ^ flip) for i in range(n_model)])

    def to_data(value):
        return lax.ppermute(value, "data", [(0, 1), (1, 0)])

    def all_blocks(x_saved, h_saved, w_up, w_down, grad_out):
        me = lax.axis_index("model")
        first = lax.axis_index("data") == 0
        first_flag = jnp.reshape(first, (1,)).astype(jnp.int32)
        quarter = jnp.reshape(me, (1,)).astype(jnp.int32)
        layers = w_up.shape[0]
        rows, seq = grad_out.shape[:2]
        width = h_saved.shape[-1]

        held = [h_saved, None]

        def h_from(layer, flip, start=0, size=width):
            held[0], held[1] = lax.optimization_barrier((held[0], held[1]))
            begin = (me ^ flip) * seq
            held[1] = lax.dynamic_slice(held[0], (layer, 0, begin, start), (1, rows, seq, size))[0]
            return to_model(held[1], flip)

        held[1] = jnp.where(first, w_up[1], w_down[1])
        far_w = [None, to_model(held[1], 2)]
        h_one = [h_from(1, 2), h_from(1, 3)]
        h_near = [None, h_from(1, 1)]
        w_pair = lax.optimization_barrier((w_up, w_down, held[1]))
        far_w[0] = jnp.where(first, w_pair[0][0], w_pair[1][0])
        far_w[0] = to_model(far_w[0], 2)
        h_near[0] = h_from(0, 1)
        h_zero = []
        for j, size in enumerate(BLOCKS):
            start = sum(BLOCKS[:j])
            h_zero.append([h_from(0, 2, start, size), h_from(0, 3, start, size)])
        small_start = width - LANES
        packed = []
        for flip in (2, 3):
            packed.append(pack_call(jnp.reshape(me ^ flip, (1,)).astype(jnp.int32), h_saved, 0, small_start, seq))
        h_small = [[to_model(packed[0][j], 2), to_model(packed[1][j], 3)] for j in range(2)]

        up, down = [{0: w_up} for _ in range(layers)], [{0: w_down} for _ in range(layers)]
        near_up, near_down = to_model(w_up, 1), to_model(w_down, 1)
        for layer in range(layers):
            other = to_data(far_w[layer])
            up[layer][1], down[layer][1] = near_up, near_down
            up[layer][2], down[layer][2] = jnp.where(first, far_w[layer], other), jnp.where(first, other, far_w[layer])
            up[layer][3] = to_model(up[layer][2], 1)
            down[layer][3] = to_model(down[layer][2], 1)

        def call(layer, grad, hs, flips, carry, final, start=0, size=width):
            ups, downs = [up[layer][f] for f in flips], [down[layer][f] for f in flips]
            return block_call(quarter, layer, grad, x_saved, hs, ups, downs, start, size, carry, final)

        def partial_sum(keep, give):
            value = keep + to_model(give, 1)
            away = jnp.where(first, value[1], value[0])
            stay = jnp.where(first, value[0], value[1])
            return stay + to_data(away)

        def place(pieces, layer, start, bufs):
            kept, other = zip(*pieces)
            return place_call(first_flag, kept, other, layer, start, layers, width, bufs)

        carry, dw_0, dw_1 = call(1, grad_out, [h_saved, h_near[1]], (0, 1), None, False)
        near = partial_sum(dw_0, dw_1)
        grad_mid, dw_2, dw_3 = call(1, grad_out, h_one, (2, 3), carry, True)
        far = partial_sum(dw_2, dw_3)
        kept = near + to_model(far, 2)
        bufs = place([(kept, to_data(kept))], 1, 0, None)

        carry, dw_0, dw_1 = call(0, grad_mid, [h_saved, h_near[0]], (0, 1), None, False)
        near = partial_sum(dw_0, dw_1)
        units = [(0, 0, 384), (1, 384, 128), (1, 512, 128), (2, small_start, SMALL), (3, small_start + SMALL, SMALL)]
        near_part = lax.optimization_barrier(tuple(near[start : start + size] for _, start, size in units))
        pres, pieces = [], []
        for j in range(4):
            base = sum(BLOCKS[:j]) if j < 2 else small_start + (j - 2) * SMALL
            if j < 2:
                flips = (2, 3)
                carry, dw_2, dw_3 = call(0, grad_mid, h_zero[j], flips, carry, False, base, BLOCKS[j])
            else:
                dw, pre = small_call(0, grad_mid, x_saved, h_small[j - 2], [down[0][f] for f in (2, 3)], base)
                dw_2, dw_3 = dw[:, :SMALL], dw[:, SMALL:]
                pres.append(pre)
            far = partial_sum(dw_2, dw_3)
            for u, (block, start, size) in enumerate(units):
                if block == j:
                    kept = near_part[u] + to_model(far[start - base : start - base + size], 2)
                    pieces.append((kept, to_data(kept)))
        for u in range(3):
            bufs = place([pieces[u]], 0, units[u][1], bufs)
        grad_x = None
        for half in range(2):
            grad_x = finish_call(grad_mid, carry, pres, [up[0][f] for f in (2, 3)], small_start, half, grad_x)
        bufs = place(pieces[3:], 0, small_start, bufs)
        return grad_x, bufs[0], bufs[1]

    return jax.shard_map(
        all_blocks,
        mesh=mesh,
        in_specs=(P(None, "data", "model", None), P(None, "data", None, "model"), P(None, None, "model"), P(None, "model", None), P("data", "model", None)),
        out_specs=(P("data", "model", None), P(None, None, "model"), P(None, "model", None)),
        check_vma=False,
    )
```

time: 2400 us -> 1660 us (0.69)
  waiting for transfers between devices: 1770 us -> 914 us
  Pallas kernels: 0 us -> 590 us
  matrix products: 531 us -> 0 us
  starting transfers between devices: 0.28 us -> 39.4 us
  local copies, waits for them, and re-layouts: 36.7 us -> 75 us
    all_gather x4 -> x0, waiting for transfers between devices: 950 us -> none  [the longest x2 475 us: device_step(): grad_full = lax.all_gather(grad_next, 'model', axis=1, tiled=True)]
    ppermute x0 -> x48, waiting for transfers between devices: none -> 914 us  [the longest x33 772 us: to_model(): return lax.ppermute(value, 'model', [(i, i ^ flip) for i in range(n_model)])]
    reduce_scatter x2 -> x0, waiting for transfers between devices: 655 us -> none  [device_step(): lax.psum_scatter(part_sum, 'model', scatter_dimension=1, tiled=True)]
    pallas_call x0 -> x16, Pallas kernels: none -> 590 us  [the longest x5 507 us: block_call(): pl.pallas_call(functools.partial(block_body, carry is not None, final, ro...]
    dot_general x8 -> x0, matrix products: 531 us -> none  [the longest x2 199 us: device_step(): jnp.einsum('bsd,fd->bsf', grad_full, w_down[layer], preferred_element_typ...]
    psum x1 -> x0, waiting for transfers between devices: 166 us -> none  [device_step(): up_total = lax.psum(jnp.stack(up_list[::-1]), 'data')]
    squeeze x0 -> x8, local copies, waits for them, and re-layouts: none -> 65 us  [h_from(): lax.dynamic_slice(held[0], (layer, 0, begin, start), (1, rows, seq, size))]
    ppermute x0 -> x48, starting transfers between devices: none -> 39.4 us  [the longest x33 22.4 us: to_model(): return lax.ppermute(value, 'model', [(i, i ^ flip) for i in range(n_model)])]
  transfers between devices with their start and end apart: 7 -> 48, of which waited for: 7 -> 19; matrix products, arithmetic and copies ran while one was open for 13% -> 4% of each run, Pallas kernels for 0% -> 35%
where the time goes in v1:
time: 1660 us
  waiting for transfers between devices  914 us (55%)
  Pallas kernels  590 us (36%)
  local copies, waits for them, and re-layouts  75 us (5%)
  starting transfers between devices  39.4 us (2%)
  other arithmetic  36.6 us (2%)
    ppermute x33, waiting for transfers between devices, to_model(): return lax.ppermute(value, 'model', [(i, i ^ flip) for i in range(n_model)])  772 us
    pallas_call x5, Pallas kernels, block_call(): pl.pallas_call(functools.partial(block_body, carry is not None, final, ro...  507 us
    ppermute x15, waiting for transfers between devices, to_data(): return lax.ppermute(value, 'data', [(0, 1), (1, 0)])  142 us
    squeeze x8, local copies, waits for them, and re-layouts, h_from(): lax.dynamic_slice(held[0], (layer, 0, begin, start), (1, rows, seq, size))  65 us
  transfers between devices with their start and end apart: 48, of which 19 were waited for; matrix products, arithmetic and copies ran while one was open for 4% of the time, Pallas kernels for 35%

profile of v1, /device:TPU:0, one launch (start us, length us, event | category | flops | bytes accessed | tf_op | source)
XLA Modules:
  0.0 1656.0 jit_solution(12920566946205291684)
XLA Ops:
  0.7 2.8 select_bitcast_fusion.5
  3.4 10.6 dynamic-slice_bitcast_fusion.3
  14.0 10.6 dynamic-slice_bitcast_fusion.2
  24.6 11.3 dynamic-slice_bitcast_fusion.1
  36.7 2.6 collective-permute-start.1
  39.3 2.0 collective-permute-start.2
  41.3 1.4 select_bitcast_fusion.4
  42.8 562.7 %collective-permute-done.2 = bf16[768,768]{1,0:T(8,128)(2,1)S(1)} collective-permute-done((bf16[768,768]{1,0:T(8,128)(2,1)S(1)}, bf16[768,768]{1,0:T(8,128)(2,1)S(1)}, u32[]{:S(2)}, u32[]{:S(2)}) %collective-permute-start.2) | collective-permute-done | bytes 1179680 | tf_op jit(solution)/shard_map/ppermute | solution.py:262
  605.5 2.2 collective-permute-start.3
  607.7 22.9 %collective-permute-done.11 = bf16[768,768]{1,0:T(8,128)(2,1)S(1)} collective-permute-done((bf16[768,768]{1,0:T(8,128)(2,1)S(1)}, bf16[768,768]{1,0:T(8,128)(2,1)S(1)}, u32[]{:S(2)}, u32[]{:S(2)}) %collective-permute-start.11) | collective-permute-done | bytes 1179680 | tf_op jit(solution)/shard_map/ppermute | solution.py:262
  630.6 1.7 collective-permute-start.12
  633.1 25.3 %collective-permute-done.12 = bf16[768,768]{1,0:T(8,128)(2,1)S(1)} collective-permute-done((bf16[768,768]{1,0:T(8,128)(2,1)S(1)}, bf16[768,768]{1,0:T(8,128)(2,1)S(1)}, u32[]{:S(2)}, u32[]{:S(2)}) %collective-permute-start.12) | collective-permute-done | bytes 1179680 | tf_op jit(solution)/shard_map/ppermute | solution.py:265
  659.4 10.6 dynamic-slice_bitcast_fusion
  670.1 6.3 dynamic-slice_bitcast_fusion.5
  676.3 6.3 dynamic-slice_bitcast_fusion.4
  682.6 4.6 dynamic-slice_bitcast_fusion.7
  687.2 6.1 shard_map.81
  693.4 6.1 shard_map.82
  699.5 4.7 dynamic-slice_bitcast_fusion.6
  707.8 119.6 %shard_map.76 = (f32[16,512,768]{2,1,0:T(8,128)}, f32[2,768,768]{2,1,0:T(8,128)}, f32[2,768,768]{2,1,0:T(8,128)}) custom-call(s32[1]{0:T(128)} %bitcast._, bf16[16,512,768]{2,1,0:T(8,128)(2,1)} %refs_0_.3, bf16[2,16,512,768]{3,2,1,0:T(8,128)(2,1)} %x_hi.3, bf16[2,16,2048,768]{3,2,1,0:T(8,128)(2,1)} %hi_ref.3, ...), custom_call_target="tpu_custom_call" | custom-call | flops 77309411328 | bytes 50331648 | tf_op jit(solution)/shard_map/pallas_call | solution.py:110
  829.8 121.4 %shard_map.77 = (bf16[16,512,768]{2,1,0:T(8,128)(2,1)}, f32[2,768,768]{2,1,0:T(8,128)}, f32[2,768,768]{2,1,0:T(8,128)}) custom-call(s32[1]{0:T(128)} %bitcast._, bf16[16,512,768]{2,1,0:T(8,128)(2,1)} %refs_0_.3, bf16[2,16,512,768]{3,2,1,0:T(8,128)(2,1)} %x_hi.3, bf16[16,512,768]{2,1,0:T(8,128)(2,1)} %collective-permute-done.refs_2_, ...), custom_call_target="tpu_custom_call" | custom-call | flops 77309411328 | bytes 50331648 | tf_op jit(solution)/shard_map/pallas_call | solution.py:110
  953.3 119.4 %shard_map.78 = (f32[16,512,768]{2,1,0:T(8,128)}, f32[2,768,768]{2,1,0:T(8,128)}, f32[2,768,768]{2,1,0:T(8,128)}) custom-call(s32[1]{0:T(128)} %bitcast._, bf16[16,512,768]{2,1,0:T(8,128)(2,1)} %get-tuple-element.55.refs_0_.grad_lo.grad_hi.grad_ref, bf16[2,16,512,768]{3,2,1,0:T(8,128)(2,1)} %x_hi.3, bf16[2,16,2048,768]{3,2,1,0:T(8,128)(2,1)} %hi_ref.3, ...), custom_call_target="tpu_custom_call" | custom-call | flops 77309411328 | bytes 50331648 | tf_op jit(solution)/shard_map/pallas_call | solution.py:110
  1072.9 27.9 %collective-permute-done.15.refs_2_ = bf16[16,512,384]{2,1,0:T(8,128)(2,1)} collective-permute-done((bf16[16,512,384]{2,1,0:T(8,128)(2,1)}, bf16[16,512,384]{2,1,0:T(8,128)(2,1)}, u32[]{:S(2)}, u32[]{:S(2)}) %collective-permute-start.15) | collective-permute-done | bytes 6291488 | tf_op jit(solution)/shard_map/ppermute | solution.py:262
  1100.7 78.3 %shard_map.79 = (f32[16,512,768]{2,1,0:T(8,128)}, f32[2,384,768]{2,1,0:T(8,128)}, f32[2,384,768]{2,1,0:T(8,128)}) custom-call(s32[1]{0:T(128)} %bitcast._, bf16[16,512,768]{2,1,0:T(8,128)(2,1)} %get-tuple-element.55.refs_0_.grad_lo.grad_hi.grad_ref, bf16[2,16,512,768]{3,2,1,0:T(8,128)(2,1)} %x_hi.3, bf16[16,512,384]{2,1,0:T(8,128)(2,1)} %collective-permute-done.15.refs_2_, ...), custom_call_target="tpu_custom_call" | custom-call | flops 38654705664 | bytes 50331648 | tf_op jit(solution)/shard_map/pallas_call | solution.py:110
  1180.2 2.9 add.94
  1183.2 1.7 select_bitcast_fusion
  1186.1 93.7 %collective-permute-done.10.refs_3_ = bf16[16,512,256]{2,1,0:T(8,128)(2,1)} collective-permute-done((bf16[16,512,256]{2,1,0:T(8,128)(2,1)}, bf16[16,512,256]{2,1,0:T(8,128)(2,1)}, u32[]{:S(2)}, u32[]{:S(2)}) %collective-permute-start.10) | collective-permute-done | bytes 4194336 | tf_op jit(solution)/shard_map/ppermute | solution.py:262
  1279.8 1.2 collective-permute-start.21
  1281.1 1.5 collective-permute-start.45
  1282.6 68.1 %shard_map.80 = (f32[16,512,768]{2,1,0:T(8,128)}, f32[2,256,768]{2,1,0:T(8,128)}, f32[2,256,768]{2,1,0:T(8,128)}) custom-call(s32[1]{0:T(128)} %bitcast._, bf16[16,512,768]{2,1,0:T(8,128)(2,1)} %get-tuple-element.55.refs_0_.grad_lo.grad_hi.grad_ref, bf16[2,16,512,768]{3,2,1,0:T(8,128)(2,1)} %x_hi.3, bf16[16,512,256]{2,1,0:T(8,128)(2,1)} %collective-permute-done.9.refs_2_, ...), custom_call_target="tpu_custom_call" | custom-call | flops 25769803776 | bytes 50331648 | tf_op jit(solution)/shard_map/pallas_call | solution.py:110
  1352.9 15.5 shard_map.84
  1368.5 3.1 add.92
  1372.2 3.6 bitcast_add_fusion
  1375.8 1.2 collective-permute-done.18.h_a
  1377.0 19.9 %collective-permute-done.19.h_b = bf16[8,512,128]{2,1,0:T(8,128)(2,1)S(1)} collective-permute-done((bf16[8,512,128]{2,1,0:T(8,128)(2,1)}, bf16[8,512,128]{2,1,0:T(8,128)(2,1)S(1)}, u32[]{:S(2)}, u32[]{:S(2)}) %collective-permute-start.19) | collective-permute-done | bytes 1048608 | tf_op jit(solution)/shard_map/ppermute | solution.py:262
  1399.1 15.5 shard_map.83
  1415.2 3.1 add.77
  1418.6 1.5 collective-permute-start.23
  1421.3 2.0 add.89
  1424.7 1.7 add.85
  1427.4 23.7 %collective-permute-done.43 = f32[768,768]{1,0:T(8,128)} collective-permute-done((f32[768,768]{1,0:T(8,128)S(1)}, f32[768,768]{1,0:T(8,128)}, u32[]{:S(2)}, u32[]{:S(2)}) %collective-permute-start.43) | collective-permute-done | bytes 2359328 | tf_op jit(solution)/shard_map/ppermute | solution.py:265
  1452.4 1.5 collective-permute-start.25
  1454.0 4.4 fusion.refs_0_
  1458.3 68.4 %collective-permute-done.39 = f32[384,768]{1,0:T(8,128)S(1)} collective-permute-done((f32[384,768]{1,0:T(8,128)S(1)}, f32[384,768]{1,0:T(8,128)S(1)}, u32[]{:S(2)}, u32[]{:S(2)}) %collective-permute-start.39) | collective-permute-done | bytes 1179680 | tf_op jit(solution)/shard_map/ppermute | solution.py:265
  1527.5 16.1 collective-permute-done.33
  1546.1 25.7 %collective-permute-done.40 = f32[384,768]{1,0:T(8,128)S(1)} collective-permute-done((f32[384,768]{1,0:T(8,128)S(1)}, f32[384,768]{1,0:T(8,128)S(1)}, u32[]{:S(2)}, u32[]{:S(2)}) %collective-permute-start.40) | collective-permute-done | bytes 1179680 | tf_op jit(solution)/shard_map/ppermute | solution.py:262
  1577.4 8.2 collective-permute-done.36
  1587.3 6.7 collective-permute-done.34
  1594.0 1.5 collective-permute-start.37
  1596.3 2.0 collective-permute-done.29
  1598.3 1.5 collective-permute-start.35
  1599.9 1.7 add.84.refs_1_
  1602.4 1.6 add.81.refs_0_
  1605.3 1.6 copy-done.5
  1606.8 1.3 copy-done.7
  1608.1 11.9 shard_map.85.refs_0_
  1620.0 11.9 shard_map.86
  1631.9 5.9 shard_map.87
  1637.8 3.8 shard_map.88
  1641.6 2.0 shard_map.89
  1644.8 2.0 shard_map.90
  1646.9 2.2 collective-permute-done.31.refs_3_
  1649.0 4.1 collective-permute-done.30.refs_2_
  1653.8 2.1 shard_map.91
  (172 shorter events, 39.0 us)
Async XLA Ops:
  24.6 16.7 %copy-start.12 = (bf16[2,768,768]{2,1,0:T(8,128)(2,1)S(1)}, bf16[2,768,768]{2,1,0:T(8,128)(2,1)}, u32[]{:S(2)}) copy-start(bf16[2,768,768]{2,1,0:T(8,128)(2,1)} %refs_6_.3) | copy-start | bytes 7077892
  35.9 671.6 %collective-permute-start.6 = (bf16[16,512,768]{2,1,0:T(8,128)(2,1)}, bf16[16,512,768]{2,1,0:T(8,128)(2,1)}, u32[]{:S(2)}, u32[]{:S(2)}) collective-permute-start(bf16[16,512,768]{2,1,0:T(8,128)(2,1)} %dynamic-slice_bitcast_fusion.1), channel_id=1, source_target_pairs={{0,1},{1,0},{2,3},{3,2},{4,5},{5,4},{6,7},{7,6}} | collective-permute-start | bytes 37748744 | tf_op jit(solution)/shard_map/ppermute | solution.py:262
  36.7 792.5 %collective-permute-start.1 = (bf16[16,512,768]{2,1,0:T(8,128)(2,1)}, bf16[16,512,768]{2,1,0:T(8,128)(2,1)}, u32[]{:S(2)}, u32[]{:S(2)}) collective-permute-start(bf16[16,512,768]{2,1,0:T(8,128)(2,1)} %dynamic-slice_bitcast_fusion.2), channel_id=1, source_target_pairs={{0,3},{1,2},{2,1},{3,0},{4,7},{5,6},{6,5},{7,4}} | collective-permute-start | bytes 37748744 | tf_op jit(solution)/shard_map/ppermute | solution.py:262
  39.3 790.0 %collective-permute-start = (bf16[16,512,768]{2,1,0:T(8,128)(2,1)}, bf16[16,512,768]{2,1,0:T(8,128)(2,1)}, u32[]{:S(2)}, u32[]{:S(2)}) collective-permute-start(bf16[16,512,768]{2,1,0:T(8,128)(2,1)} %dynamic-slice_bitcast_fusion.3), channel_id=1, source_target_pairs={{0,2},{1,3},{2,0},{3,1},{4,6},{5,7},{6,4},{7,5}} | collective-permute-start | bytes 37748744 | tf_op jit(solution)/shard_map/ppermute | solution.py:262
  39.3 566.2 %collective-permute-start.2 = (bf16[768,768]{1,0:T(8,128)(2,1)S(1)}, bf16[768,768]{1,0:T(8,128)(2,1)S(1)}, u32[]{:S(2)}, u32[]{:S(2)}) collective-permute-start(bf16[768,768]{1,0:T(8,128)(2,1)S(1)} %copy-done.22), channel_id=1, source_target_pairs={{0,2},{1,3},{2,0},{3,1},{4,6},{5,7},{6,4},{7,5}} | collective-permute-start | bytes 3538952 | tf_op jit(solution)/shard_map/ppermute | solution.py:262
  42.7 587.9 %collective-permute-start.11 = (bf16[768,768]{1,0:T(8,128)(2,1)S(1)}, bf16[768,768]{1,0:T(8,128)(2,1)S(1)}, u32[]{:S(2)}, u32[]{:S(2)}) collective-permute-start(bf16[768,768]{1,0:T(8,128)(2,1)S(1)} %select_bitcast_fusion.4), channel_id=1, source_target_pairs={{0,2},{1,3},{2,0},{3,1},{4,6},{5,7},{6,4},{7,5}} | collective-permute-start | bytes 3538952 | tf_op jit(solution)/shard_map/ppermute | solution.py:262
  605.5 27.6 %collective-permute-start.3 = (bf16[768,768]{1,0:T(8,128)(2,1)S(1)}, bf16[768,768]{1,0:T(8,128)(2,1)S(1)}, u32[]{:S(2)}, u32[]{:S(2)}) collective-permute-start(bf16[768,768]{1,0:T(8,128)(2,1)S(1)} %collective-permute-done.2), channel_id=1, source_target_pairs={{0,4},{4,0},{1,5},{5,1},{2,6},{6,2},{3,7},{7,3}} | collective-permute-start | bytes 3538952 | tf_op jit(solution)/shard_map/ppermute | solution.py:265
  630.6 27.8 %collective-permute-start.12 = (bf16[768,768]{1,0:T(8,128)(2,1)S(1)}, bf16[768,768]{1,0:T(8,128)(2,1)S(1)}, u32[]{:S(2)}, u32[]{:S(2)}) collective-permute-start(bf16[768,768]{1,0:T(8,128)(2,1)S(1)} %collective-permute-done.11), channel_id=1, source_target_pairs={{0,4},{4,0},{1,5},{5,1},{2,6},{6,2},{3,7},{7,3}} | collective-permute-start | bytes 3538952 | tf_op jit(solution)/shard_map/ppermute | solution.py:265
  633.1 25.3 %copy-start.18 = (bf16[768,768]{1,0:T(8,128)(2,1)}, bf16[768,768]{1,0:T(8,128)(2,1)S(1)}, u32[]{:S(2)}) copy-start(bf16[768,768]{1,0:T(8,128)(2,1)S(1)} %collective-permute-done.3) | copy-start | bytes 3538948
  633.1 72.9 %collective-permute-start.7 = (bf16[2,768,768]{2,1,0:T(8,128)(2,1)}, bf16[2,768,768]{2,1,0:T(8,128)(2,1)}, u32[]{:S(2)}, u32[]{:S(2)}) collective-permute-start(bf16[2,768,768]{2,1,0:T(8,128)(2,1)} %refs_4_.3), channel_id=1, source_target_pairs={{0,1},{1,0},{2,3},{3,2},{4,5},{5,4},{6,7},{7,6}} | collective-permute-start | bytes 7077896 | tf_op jit(solution)/shard_map/ppermute | solution.py:262
  659.4 47.2 %collective-permute-start.8 = (bf16[2,768,768]{2,1,0:T(8,128)(2,1)S(1)}, bf16[2,768,768]{2,1,0:T(8,128)(2,1)}, u32[]{:S(2)}, u32[]{:S(2)}) collective-permute-start(bf16[2,768,768]{2,1,0:T(8,128)(2,1)S(1)} %copy-done.12), channel_id=1, source_target_pairs={{0,1},{1,0},{2,3},{3,2},{4,5},{5,4},{6,7},{7,6}} | collective-permute-start | bytes 7077896 | tf_op jit(solution)/shard_map/ppermute | solution.py:262
  706.0 123.2 %copy-start = (bf16[768,768]{1,0:T(8,128)(2,1)}, bf16[768,768]{1,0:T(8,128)(2,1)S(1)}, u32[]{:S(2)}) copy-start(bf16[768,768]{1,0:T(8,128)(2,1)S(1)} %get-tuple-element.104.refs_4_.up_a) | copy-start | bytes 3538948
  706.0 123.3 %copy-start.2 = (bf16[768,768]{1,0:T(8,128)(2,1)}, bf16[768,768]{1,0:T(8,128)(2,1)S(1)}, u32[]{:S(2)}) copy-start(bf16[768,768]{1,0:T(8,128)(2,1)S(1)} %get-tuple-element.103.refs_6_.down_a) | copy-start | bytes 3538948
  706.1 246.6 %collective-permute-start.17 = (bf16[16,512,768]{2,1,0:T(8,128)(2,1)}, bf16[16,512,768]{2,1,0:T(8,128)(2,1)}, u32[]{:S(2)}, u32[]{:S(2)}) collective-permute-start(bf16[16,512,768]{2,1,0:T(8,128)(2,1)} %dynamic-slice_bitcast_fusion), channel_id=1, source_target_pairs={{0,1},{1,0},{2,3},{3,2},{4,5},{5,4},{6,7},{7,6}} | collective-permute-start | bytes 37748744 | tf_op jit(solution)/shard_map/ppermute | solution.py:262
  706.9 120.5 %collective-permute-start.4 = (bf16[768,768]{1,0:T(8,128)(2,1)S(1)}, bf16[768,768]{1,0:T(8,128)(2,1)S(1)}, u32[]{:S(2)}, u32[]{:S(2)}) collective-permute-start(bf16[768,768]{1,0:T(8,128)(2,1)S(1)} %get-tuple-element.106.refs_4_), channel_id=1, source_target_pairs={{0,1},{1,0},{2,3},{3,2},{4,5},{5,4},{6,7},{7,6}} | collective-permute-start | bytes 3538952 | tf_op jit(solution)/shard_map/ppermute | solution.py:262
  707.4 120.9 %collective-permute-start.5 = (bf16[768,768]{1,0:T(8,128)(2,1)S(1)}, bf16[768,768]{1,0:T(8,128)(2,1)S(1)}, u32[]{:S(2)}, u32[]{:S(2)}) collective-permute-start(bf16[768,768]{1,0:T(8,128)(2,1)S(1)} %get-tuple-element.105.refs_6_), channel_id=1, source_target_pairs={{0,1},{1,0},{2,3},{3,2},{4,5},{5,4},{6,7},{7,6}} | collective-permute-start | bytes 3538952 | tf_op jit(solution)/shard_map/ppermute | solution.py:262
  827.4 245.4 %collective-permute-start.16 = (bf16[16,512,384]{2,1,0:T(8,128)(2,1)}, bf16[16,512,384]{2,1,0:T(8,128)(2,1)}, u32[]{:S(2)}, u32[]{:S(2)}) collective-permute-start(bf16[16,512,384]{2,1,0:T(8,128)(2,1)} %dynamic-slice_bitcast_fusion.4), channel_id=1, source_target_pairs={{0,3},{1,2},{2,1},{3,0},{4,7},{5,6},{6,5},{7,4}} | collective-permute-start | bytes 18874376 | tf_op jit(solution)/shard_map/ppermute | solution.py:262
  828.3 272.4 %collective-permute-start.15 = (bf16[16,512,384]{2,1,0:T(8,128)(2,1)}, bf16[16,512,384]{2,1,0:T(8,128)(2,1)}, u32[]{:S(2)}, u32[]{:S(2)}) collective-permute-start(bf16[16,512,384]{2,1,0:T(8,128)(2,1)} %dynamic-slice_bitcast_fusion.5), channel_id=1, source_target_pairs={{0,2},{1,3},{2,0},{3,1},{4,6},{5,7},{6,4},{7,5}} | collective-permute-start | bytes 18874376 | tf_op jit(solution)/shard_map/ppermute | solution.py:262
  829.2 121.9 %collective-permute-start.13 = (bf16[768,768]{1,0:T(8,128)(2,1)S(1)}, bf16[768,768]{1,0:T(8,128)(2,1)S(1)}, u32[]{:S(2)}, u32[]{:S(2)}) collective-permute-start(bf16[768,768]{1,0:T(8,128)(2,1)S(1)} %get-tuple-element.104.refs_4_.up_a), channel_id=1, source_target_pairs={{0,1},{1,0},{2,3},{3,2},{4,5},{5,4},{6,7},{7,6}} | collective-permute-start | bytes 3538952 | tf_op jit(solution)/shard_map/ppermute | solution.py:262
  829.3 123.0 %collective-permute-start.14 = (bf16[768,768]{1,0:T(8,128)(2,1)S(1)}, bf16[768,768]{1,0:T(8,128)(2,1)S(1)}, u32[]{:S(2)}, u32[]{:S(2)}) collective-permute-start(bf16[768,768]{1,0:T(8,128)(2,1)S(1)} %get-tuple-element.103.refs_6_.down_a), channel_id=1, source_target_pairs={{0,1},{1,0},{2,3},{3,2},{4,5},{5,4},{6,7},{7,6}} | collective-permute-start | bytes 3538952 | tf_op jit(solution)/shard_map/ppermute | solution.py:262
  951.1 121.6 %copy-start.6 = (bf16[768,768]{1,0:T(8,128)(2,1)}, bf16[768,768]{1,0:T(8,128)(2,1)S(1)}, u32[]{:S(2)}) copy-start(bf16[768,768]{1,0:T(8,128)(2,1)S(1)} %collective-permute-done.13.refs_5_.up_b) | copy-start | bytes 3538948
  951.2 329.9 %collective-permute-start.9 = (bf16[16,512,256]{2,1,0:T(8,128)(2,1)}, bf16[16,512,256]{2,1,0:T(8,128)(2,1)}, u32[]{:S(2)}, u32[]{:S(2)}) collective-permute-start(bf16[16,512,256]{2,1,0:T(8,128)(2,1)} %dynamic-slice_bitcast_fusion.7), channel_id=1, source_target_pairs={{0,2},{1,3},{2,0},{3,1},{4,6},{5,7},{6,4},{7,5}} | collective-permute-start | bytes 12582920 | tf_op jit(solution)/shard_map/ppermute | solution.py:262
  952.3 120.5 %copy-start.8 = (bf16[768,768]{1,0:T(8,128)(2,1)}, bf16[768,768]{1,0:T(8,128)(2,1)S(1)}, u32[]{:S(2)}) copy-start(bf16[768,768]{1,0:T(8,128)(2,1)S(1)} %collective-permute-done.14.refs_7_.down_b) | copy-start | bytes 3538948
  952.3 327.5 %collective-permute-start.10 = (bf16[16,512,256]{2,1,0:T(8,128)(2,1)}, bf16[16,512,256]{2,1,0:T(8,128)(2,1)}, u32[]{:S(2)}, u32[]{:S(2)}) collective-permute-start(bf16[16,512,256]{2,1,0:T(8,128)(2,1)} %dynamic-slice_bitcast_fusion.6), channel_id=1, source_target_pairs={{0,3},{1,2},{2,1},{3,0},{4,7},{5,6},{6,5},{7,4}} | collective-permute-start | bytes 12582920 | tf_op jit(solution)/shard_map/ppermute | solution.py:262
  952.6 226.4 %collective-permute-start.44 = (f32[2,768,768]{2,1,0:T(8,128)}, f32[2,768,768]{2,1,0:T(8,128)}, u32[]{:S(2)}, u32[]{:S(2)}) collective-permute-start(f32[2,768,768]{2,1,0:T(8,128)} %get-tuple-element.88), channel_id=1, source_target_pairs={{0,1},{1,0},{2,3},{3,2},{4,5},{5,4},{6,7},{7,6}} | collective-permute-start | bytes 14155784 | tf_op jit(solution)/shard_map/ppermute | solution.py:262
  1072.8 279.0 %collective-permute-start.42 = (f32[2,768,768]{2,1,0:T(8,128)}, f32[2,768,768]{2,1,0:T(8,128)}, u32[]{:S(2)}, u32[]{:S(2)}) collective-permute-start(f32[2,768,768]{2,1,0:T(8,128)} %get-tuple-element.86), channel_id=1, source_target_pairs={{0,1},{1,0},{2,3},{3,2},{4,5},{5,4},{6,7},{7,6}} | collective-permute-start | bytes 14155784 | tf_op jit(solution)/shard_map/ppermute | solution.py:262
  1100.7 313.9 %collective-permute-start.22 = (f32[2,768,768]{2,1,0:T(8,128)}, f32[2,768,768]{2,1,0:T(8,128)}, u32[]{:S(2)}, u32[]{:S(2)}) collective-permute-start(f32[2,768,768]{2,1,0:T(8,128)} %get-tuple-element.73), channel_id=1, source_target_pairs={{0,1},{1,0},{2,3},{3,2},{4,5},{5,4},{6,7},{7,6}} | collective-permute-start | bytes 14155784 | tf_op jit(solution)/shard_map/ppermute | solution.py:262
  1100.7 79.5 %slice-start.6 = ((s8[4718592]{0:T(1024)(128)(4,1)}), s8[4194304]{0:T(1024)(128)(4,1)S(1)}, s32[]{:S(2)}) async-start(s8[4718592]{0:T(1024)(128)(4,1)} %bitcast.60), calls=%async_computation.6 | async-start | bytes 8388608
  1100.7 78.3 %copy-start.29 = (bf16[8,512,128]{2,1,0:T(8,128)(2,1)S(1)}, bf16[8,512,128]{2,1,0:T(8,128)(2,1)}, u32[]{:S(2)}) copy-start(bf16[8,512,128]{2,1,0:T(8,128)(2,1)} %get-tuple-element.69) | copy-start | bytes 3145732
  1100.7 79.5 %slice-start.7 = ((s8[4718592]{0:T(1024)(128)(4,1)}), s8[524288]{0:T(1024)(128)(4,1)S(1)}, s32[]{:S(2)}) async-start(s8[4718592]{0:T(1024)(128)(4,1)} %bitcast.60), calls=%async_computation.7 | async-start | bytes 1048576
  1179.1 171.6 %collective-permute-start.20 = (bf16[8,512,128]{2,1,0:T(8,128)(2,1)S(1)}, bf16[8,512,128]{2,1,0:T(8,128)(2,1)S(1)}, u32[]{:S(2)}, u32[]{:S(2)}) collective-permute-start(bf16[8,512,128]{2,1,0:T(8,128)(2,1)S(1)} %copy-done.29), channel_id=1, source_target_pairs={{0,2},{1,3},{2,0},{3,1},{4,6},{5,7},{6,4},{7,5}} | collective-permute-start | bytes 3145736 | tf_op jit(solution)/shard_map/ppermute | solution.py:262
  1183.2 96.6 %copy-start.28 = (bf16[8,512,128]{2,1,0:T(8,128)(2,1)S(1)}, bf16[8,512,128]{2,1,0:T(8,128)(2,1)}, u32[]{:S(2)}) copy-start(bf16[8,512,128]{2,1,0:T(8,128)(2,1)} %get-tuple-element.70) | copy-start | bytes 3145732
  1279.8 71.4 %collective-permute-start.21 = (bf16[8,512,128]{2,1,0:T(8,128)(2,1)S(1)}, bf16[8,512,128]{2,1,0:T(8,128)(2,1)S(1)}, u32[]{:S(2)}, u32[]{:S(2)}) collective-permute-start(bf16[8,512,128]{2,1,0:T(8,128)(2,1)S(1)} %copy-done.28), channel_id=1, source_target_pairs={{0,3},{1,2},{2,1},{3,0},{4,7},{5,6},{6,5},{7,4}} | collective-permute-start | bytes 3145736 | tf_op jit(solution)/shard_map/ppermute | solution.py:262
  1281.1 90.9 %collective-permute-start.45 = (f32[768,768]{1,0:T(8,128)}, f32[768,768]{1,0:T(8,128)}, u32[]{:S(2)}, u32[]{:S(2)}) collective-permute-start(f32[768,768]{1,0:T(8,128)} %select_bitcast_fusion), channel_id=1, source_target_pairs={{0,4},{4,0},{1,5},{5,1},{2,6},{6,2},{3,7},{7,3}} | collective-permute-start | bytes 7077896 | tf_op jit(solution)/shard_map/ppermute | solution.py:265
  1282.6 70.3 %copy-start.3 = (bf16[768,768]{1,0:T(8,128)(2,1)S(1)}, bf16[768,768]{1,0:T(8,128)(2,1)}, u32[]{:S(2)}) copy-start(bf16[768,768]{1,0:T(8,128)(2,1)} %copy-done.2) | copy-start | bytes 3538948
  1282.6 70.3 %copy-start.9 = (bf16[768,768]{1,0:T(8,128)(2,1)S(1)}, bf16[768,768]{1,0:T(8,128)(2,1)}, u32[]{:S(2)}) copy-start(bf16[768,768]{1,0:T(8,128)(2,1)} %copy-done.8) | copy-start | bytes 3538948
  1350.7 26.3 %collective-permute-start.18 = (bf16[8,512,128]{2,1,0:T(8,128)(2,1)}, bf16[8,512,128]{2,1,0:T(8,128)(2,1)S(1)}, u32[]{:S(2)}, u32[]{:S(2)}) collective-permute-start(bf16[8,512,128]{2,1,0:T(8,128)(2,1)} %get-tuple-element.66), channel_id=1, source_target_pairs={{0,2},{1,3},{2,0},{3,1},{4,6},{5,7},{6,4},{7,5}} | collective-permute-start | bytes 3145736 | tf_op jit(solution)/shard_map/ppermute | solution.py:262
  1351.3 45.7 %collective-permute-start.19 = (bf16[8,512,128]{2,1,0:T(8,128)(2,1)}, bf16[8,512,128]{2,1,0:T(8,128)(2,1)S(1)}, u32[]{:S(2)}, u32[]{:S(2)}) collective-permute-start(bf16[8,512,128]{2,1,0:T(8,128)(2,1)} %get-tuple-element.67), channel_id=1, source_target_pairs={{0,3},{1,2},{2,1},{3,0},{4,7},{5,6},{6,5},{7,4}} | collective-permute-start | bytes 3145736 | tf_op jit(solution)/shard_map/ppermute | solution.py:262
  1351.8 16.7 %slice-start.3 = ((s8[4718592]{0:T(1024)(128)(4,1)}), s8[524288]{0:T(1024)(128)(4,1)S(1)}, s32[]{:S(2)}) async-start(s8[4718592]{0:T(1024)(128)(4,1)} %bitcast.56), calls=%async_computation.3 | async-start | bytes 1048576
  1351.8 69.5 %collective-permute-start.38 = (f32[2,384,768]{2,1,0:T(8,128)}, f32[2,384,768]{2,1,0:T(8,128)}, u32[]{:S(2)}, u32[]{:S(2)}) collective-permute-start(f32[2,384,768]{2,1,0:T(8,128)} %get-tuple-element.84), channel_id=1, source_target_pairs={{0,1},{1,0},{2,3},{3,2},{4,5},{5,4},{6,7},{7,6}} | collective-permute-start | bytes 7077896 | tf_op jit(solution)/shard_map/ppermute | solution.py:262
  1372.0 25.5 %collective-permute-start.27 = (f32[2,64,768]{2,1,0:T(8,128)S(1)}, f32[2,64,768]{2,1,0:T(8,128)S(1)}, u32[]{:S(2)}, u32[]{:S(2)}) collective-permute-start(f32[2,64,768]{2,1,0:T(8,128)S(1)} %slice.117), channel_id=1, source_target_pairs={{0,1},{1,0},{2,3},{3,2},{4,5},{5,4},{6,7},{7,6}} | collective-permute-start | bytes 1179656 | tf_op jit(solution)/shard_map/ppermute | solution.py:262
  1372.2 43.0 %slice-start.4 = ((s8[4718592]{0:T(1024)(128)(4,1)}), s8[524288]{0:T(1024)(128)(4,1)S(1)}, s32[]{:S(2)}) async-start(s8[4718592]{0:T(1024)(128)(4,1)} %bitcast.58), calls=%async_computation.4 | async-start | bytes 1048576
  1377.0 38.2 %slice-start.5 = ((s8[4718592]{0:T(1024)(128)(4,1)}), s8[4194304]{0:T(1024)(128)(4,1)S(1)}, s32[]{:S(2)}) async-start(s8[4718592]{0:T(1024)(128)(4,1)} %bitcast.58), calls=%async_computation.5 | async-start | bytes 8388608
  1377.0 47.1 %collective-permute-start.32 = (f32[2,256,768]{2,1,0:T(8,128)}, f32[2,256,768]{2,1,0:T(8,128)}, u32[]{:S(2)}, u32[]{:S(2)}) collective-permute-start(f32[2,256,768]{2,1,0:T(8,128)} %get-tuple-element.80), channel_id=1, source_target_pairs={{0,1},{1,0},{2,3},{3,2},{4,5},{5,4},{6,7},{7,6}} | collective-permute-start | bytes 4718600 | tf_op jit(solution)/shard_map/ppermute | solution.py:262
  1396.9 54.1 %collective-permute-start.43 = (f32[768,768]{1,0:T(8,128)S(1)}, f32[768,768]{1,0:T(8,128)}, u32[]{:S(2)}, u32[]{:S(2)}) collective-permute-start(f32[768,768]{1,0:T(8,128)S(1)} %select_bitcast_fusion.1), channel_id=1, source_target_pairs={{0,4},{4,0},{1,5},{5,1},{2,6},{6,2},{3,7},{7,3}} | collective-permute-start | bytes 7077896 | tf_op jit(solution)/shard_map/ppermute | solution.py:265
  1398.2 54.3 %collective-permute-start.46 = (f32[768,768]{1,0:T(8,128)}, f32[768,768]{1,0:T(8,128)}, u32[]{:S(2)}, u32[]{:S(2)}) collective-permute-start(f32[768,768]{1,0:T(8,128)} %bitcast_add_fusion), channel_id=1, source_target_pairs={{0,2},{1,3},{2,0},{3,1},{4,6},{5,7},{6,4},{7,5}} | collective-permute-start | bytes 7077896 | tf_op jit(solution)/shard_map/ppermute | solution.py:262
  1414.7 3.9 collective-permute-start.24
  1418.6 126.2 %collective-permute-start.23 = (f32[768,768]{1,0:T(8,128)S(1)}, f32[768,768]{1,0:T(8,128)S(1)}, u32[]{:S(2)}, u32[]{:S(2)}) collective-permute-start(f32[768,768]{1,0:T(8,128)S(1)} %select_bitcast_fusion.2), channel_id=1, source_target_pairs={{0,4},{4,0},{1,5},{5,1},{2,6},{6,2},{3,7},{7,3}} | collective-permute-start | bytes 7077896 | tf_op jit(solution)/shard_map/ppermute | solution.py:265
  1423.4 103.3 %collective-permute-start.39 = (f32[384,768]{1,0:T(8,128)S(1)}, f32[384,768]{1,0:T(8,128)S(1)}, u32[]{:S(2)}, u32[]{:S(2)}) collective-permute-start(f32[384,768]{1,0:T(8,128)S(1)} %select_bitcast_fusion.3), channel_id=1, source_target_pairs={{0,4},{4,0},{1,5},{5,1},{2,6},{6,2},{3,7},{7,3}} | collective-permute-start | bytes 3538952 | tf_op jit(solution)/shard_map/ppermute | solution.py:265
  1426.5 117.1 %collective-permute-start.33 = (f32[256,768]{1,0:T(8,128)S(1)}, f32[256,768]{1,0:T(8,128)S(1)}, u32[]{:S(2)}, u32[]{:S(2)}) collective-permute-start(f32[256,768]{1,0:T(8,128)S(1)} %select_bitcast_fusion.6), channel_id=1, source_target_pairs={{0,4},{4,0},{1,5},{5,1},{2,6},{6,2},{3,7},{7,3}} | collective-permute-start | bytes 2359304 | tf_op jit(solution)/shard_map/ppermute | solution.py:265
  1451.0 123.5 %collective-permute-start.28 = (f32[64,768]{1,0:T(8,128)S(1)}, f32[64,768]{1,0:T(8,128)S(1)}, u32[]{:S(2)}, u32[]{:S(2)}) collective-permute-start(f32[64,768]{1,0:T(8,128)S(1)} %select_bitcast_fusion.7), channel_id=1, source_target_pairs={{0,4},{4,0},{1,5},{5,1},{2,6},{6,2},{3,7},{7,3}} | collective-permute-start | bytes 589832 | tf_op jit(solution)/shard_map/ppermute | solution.py:265
  1452.4 123.2 %collective-permute-start.25 = (f32[64,768]{1,0:T(8,128)S(1)}, f32[64,768]{1,0:T(8,128)S(1)}, u32[]{:S(2)}, u32[]{:S(2)}) collective-permute-start(f32[64,768]{1,0:T(8,128)S(1)} %select_bitcast_fusion.8), channel_id=1, source_target_pairs={{0,4},{4,0},{1,5},{5,1},{2,6},{6,2},{3,7},{7,3}} | collective-permute-start | bytes 589832 | tf_op jit(solution)/shard_map/ppermute | solution.py:265
  1526.8 77.3 %collective-permute-start.47 = (f32[768,768]{1,0:T(8,128)}, f32[768,768]{1,0:T(8,128)}, u32[]{:S(2)}, u32[]{:S(2)}) collective-permute-start(f32[768,768]{1,0:T(8,128)} %fusion.refs_0_), channel_id=1, source_target_pairs={{0,4},{4,0},{1,5},{5,1},{2,6},{6,2},{3,7},{7,3}} | collective-permute-start | bytes 7077896 | tf_op jit(solution)/shard_map/ppermute | solution.py:265
  1543.6 28.2 %collective-permute-start.40 = (f32[384,768]{1,0:T(8,128)S(1)}, f32[384,768]{1,0:T(8,128)S(1)}, u32[]{:S(2)}, u32[]{:S(2)}) collective-permute-start(f32[384,768]{1,0:T(8,128)S(1)} %bitcast_add_fusion.3), channel_id=1, source_target_pairs={{0,2},{1,3},{2,0},{3,1},{4,6},{5,7},{6,4},{7,5}} | collective-permute-start | bytes 3538952 | tf_op jit(solution)/shard_map/ppermute | solution.py:262
  1573.0 64.8 %collective-permute-start.41 = (f32[384,768]{1,0:T(8,128)}, f32[384,768]{1,0:T(8,128)}, u32[]{:S(2)}, u32[]{:S(2)}) collective-permute-start(f32[384,768]{1,0:T(8,128)} %add.91.refs_0_), channel_id=1, source_target_pairs={{0,4},{4,0},{1,5},{5,1},{2,6},{6,2},{3,7},{7,3}} | collective-permute-start | bytes 3538952 | tf_op jit(solution)/shard_map/ppermute | solution.py:265
  1573.6 12.0 collective-permute-start.36
  1574.5 19.5 %collective-permute-start.34 = (f32[128,768]{1,0:T(8,128)S(1)}, f32[128,768]{1,0:T(8,128)S(1)}, u32[]{:S(2)}, u32[]{:S(2)}) collective-permute-start(f32[128,768]{1,0:T(8,128)S(1)} %get-tuple-element.108), channel_id=1, source_target_pairs={{0,2},{1,3},{2,0},{3,1},{4,6},{5,7},{6,4},{7,5}} | collective-permute-start | bytes 1179656 | tf_op jit(solution)/shard_map/ppermute | solution.py:262
  1575.7 29.6 %copy-start.1 = (bf16[768,768]{1,0:T(8,128)(2,1)S(1)}, bf16[768,768]{1,0:T(8,128)(2,1)}, u32[]{:S(2)}) copy-start(bf16[768,768]{1,0:T(8,128)(2,1)} %copy-done) | copy-start | bytes 3538948
  1575.7 22.6 %collective-permute-start.29 = (f32[64,768]{1,0:T(8,128)S(1)}, f32[64,768]{1,0:T(8,128)}, u32[]{:S(2)}, u32[]{:S(2)}) collective-permute-start(f32[64,768]{1,0:T(8,128)S(1)} %bitcast_add_fusion.5), channel_id=1, source_target_pairs={{0,2},{1,3},{2,0},{3,1},{4,6},{5,7},{6,4},{7,5}} | collective-permute-start | bytes 589832 | tf_op jit(solution)/shard_map/ppermute | solution.py:262
  1585.6 16.0 collective-permute-start.26
  1594.0 47.6 %collective-permute-start.37 = (f32[128,768]{1,0:T(8,128)}, f32[128,768]{1,0:T(8,128)}, u32[]{:S(2)}, u32[]{:S(2)}) collective-permute-start(f32[128,768]{1,0:T(8,128)} %add.88.refs_0_), channel_id=1, source_target_pairs={{0,4},{4,0},{1,5},{5,1},{2,6},{6,2},{3,7},{7,3}} | collective-permute-start | bytes 1179656 | tf_op jit(solution)/shard_map/ppermute | solution.py:265
  1598.3 46.5 %collective-permute-start.35 = (f32[128,768]{1,0:T(8,128)}, f32[128,768]{1,0:T(8,128)}, u32[]{:S(2)}, u32[]{:S(2)}) collective-permute-start(f32[128,768]{1,0:T(8,128)} %add.87.refs_0_), channel_id=1, source_target_pairs={{0,4},{4,0},{1,5},{5,1},{2,6},{6,2},{3,7},{7,3}} | collective-permute-start | bytes 1179656 | tf_op jit(solution)/shard_map/ppermute | solution.py:265
  1601.6 47.5 %collective-permute-start.31 = (f32[64,768]{1,0:T(8,128)}, f32[64,768]{1,0:T(8,128)}, u32[]{:S(2)}, u32[]{:S(2)}) collective-permute-start(f32[64,768]{1,0:T(8,128)} %add.84.refs_1_), channel_id=1, source_target_pairs={{0,4},{4,0},{1,5},{5,1},{2,6},{6,2},{3,7},{7,3}} | collective-permute-start | bytes 589832 | tf_op jit(solution)/shard_map/ppermute | solution.py:265
  1604.1 49.1 %collective-permute-start.30 = (f32[64,768]{1,0:T(8,128)}, f32[64,768]{1,0:T(8,128)S(1)}, u32[]{:S(2)}, u32[]{:S(2)}) collective-permute-start(f32[64,768]{1,0:T(8,128)} %add.81.refs_0_), channel_id=1, source_target_pairs={{0,4},{4,0},{1,5},{5,1},{2,6},{6,2},{3,7},{7,3}} | collective-permute-start | bytes 589832 | tf_op jit(solution)/shard_map/ppermute | solution.py:265
  (22 other events, 73.1 us)

commit v2 on v1

--- a/solution.py
+++ b/solution.py
@@ -13,6 +13,7 @@
 BLOCKS = (384, 256)
 LANES = 128
 SMALL = 64
+ALL_VMEM = 66_000_000
 
 
 def gelu_parts(pre_act):
@@ -119,7 +120,7 @@
             + [pltpu.VMEM((seq, hidden), F32), pltpu.VMEM((2,) + dw_shape, F32)]
             + [pltpu.VMEM((2, hidden, width), BF16), pltpu.VMEM((2, width, hidden), BF16), pltpu.SemaphoreType.DMA((2,))],
         ),
-        compiler_params=pltpu.CompilerParams(dimension_semantics=("arbitrary", "arbitrary"), vmem_limit_bytes=56 * 2**20),
+        compiler_params=pltpu.CompilerParams(dimension_semantics=("arbitrary", "arbitrary"), vmem_limit_bytes=ALL_VMEM),
         cost_estimate=pl.CostEstimate(
             flops=16 * rows * seq * hidden * width, bytes_accessed=8 * rows * seq * hidden, transcendentals=2 * rows * seq * width),
     )(quarter, *operands)
@@ -130,95 +131,179 @@
     return jnp.where(left, a, pltpu.roll(b, SMALL, 1)), jnp.where(left, pltpu.roll(a, SMALL, 1), b)
 
 
-def pack_body(_, lo_ref, hi_ref, left_ref, right_ref):
+def pack_body(chunk, _, lo_ref, hi_ref, left_ref, right_a, right_b):
     left, right = swap_lanes(lo_ref[0, 0].astype(F32), hi_ref[0, 0].astype(F32))
-    left_ref[0], right_ref[0] = left.astype(BF16), right.astype(BF16)
+    left_ref[0] = left.astype(BF16)
+
+    @pl.when(pl.program_id(0) < chunk)
+    def _():
+        right_a[0] = right.astype(BF16)
+
+    @pl.when(pl.program_id(0) >= chunk)
+    def _():
+        right_b[0] = right.astype(BF16)
 
 
 def pack_call(target, h_saved, layer, start, seq):
     pairs = h_saved.shape[1] // 2
+    chunk = pairs // 2
     specs = [pl.BlockSpec((1, 1, seq, LANES), lambda b, ids, r=r: (layer, b + r * pairs, ids[0], start // LANES)) for r in range(2)]
-    return pl.pallas_call(
-        pack_body,
-        out_shape=[jax.ShapeDtypeStruct((pairs, seq, LANES), BF16)] * 2,
+    block = (1, seq, LANES)
+    return pl.pallas_call(
+        functools.partial(pack_body, chunk),
+        out_shape=[jax.ShapeDtypeStruct((n, seq, LANES), BF16) for n in (pairs, chunk, chunk)],
         grid_spec=pltpu.PrefetchScalarGridSpec(
             num_scalar_prefetch=1,
             grid=(pairs,),
             in_specs=specs,
-            out_specs=[pl.BlockSpec((1, seq, LANES), lambda b, ids: (b, 0, 0))] * 2,
+            out_specs=[
+                pl.BlockSpec(block, lambda b, ids: (b, 0, 0)),
+                pl.BlockSpec(block, lambda b, ids: (jnp.minimum(b, chunk - 1), 0, 0)),
+                pl.BlockSpec(block, lambda b, ids: (jnp.maximum(b - chunk, 0), 0, 0)),
+            ],
         ),
-        compiler_params=pltpu.CompilerParams(dimension_semantics=("arbitrary",)),
+        compiler_params=pltpu.CompilerParams(dimension_semantics=("arbitrary",), vmem_limit_bytes=ALL_VMEM),
         cost_estimate=pl.CostEstimate(flops=pairs * seq * LANES, bytes_accessed=8 * pairs * seq * LANES, transcendentals=0),
     )(target, h_saved, h_saved)
 
 
-def small_body(grad_lo, grad_hi, x_lo, x_hi, h_a, h_b, down_a, down_b, dw_ref, pre_ref):
+def wide_body(start, grad_ref, x_ref, h_a, h_b, up_a, up_b, down_a, down_b, carry_ref, out_ref, dw_a, dw_b):
     @pl.when(pl.program_id(0) == 0)
     def _():
-        dw_ref[...] = jnp.zeros_like(dw_ref)
-
-    h_pair = swap_lanes(h_a[0].astype(F32), h_b[0].astype(F32))
+        dw_a[...] = jnp.zeros_like(dw_a)
+        dw_b[...] = jnp.zeros_like(dw_b)
+
+    grad, x = grad_ref[0], x_ref[0, 0]
+    cols = slice(start, start + h_a.shape[2])
+    total = grad.astype(F32) + carry_ref[0]
+    for h, up, down, dw in ((h_a, up_a, down_a, dw_a), (h_b, up_b, down_b, dw_b)):
+        pre, act = unit_grads(grad, h[0], down[cols, :])
+        dw[0] += dot(pre, x, 0, 0)
+        dw[1] += dot(act, grad, 0, 0)
+        total += dot(pre, up[:, cols], 1, 1)
+    out_ref[0] = total
+
+
+def wide_call(layer, grad, x_saved, h_pair, ups, downs, start, carry):
+    rows, seq, hidden = grad.shape
+    width = h_pair[0].shape[2]
+    row_spec = pl.BlockSpec((1, seq, hidden), lambda b: (b, 0, 0))
+    h_spec = pl.BlockSpec((1, seq, width), lambda b: (b, 0, 0))
+    w_spec = pl.BlockSpec(ups[0].shape, lambda b: (0, 0), pipeline_mode=pl.Buffered(1))
+    dw_shape = (2, width, hidden)
+    return pl.pallas_call(
+        functools.partial(wide_body, start),
+        out_shape=[jax.ShapeDtypeStruct(grad.shape, F32)] + [jax.ShapeDtypeStruct(dw_shape, F32)] * 2,
+        grid=(rows,),
+        in_specs=[row_spec, pl.BlockSpec((1, 1, seq, hidden), lambda b: (layer, b, 0, 0)), h_spec, h_spec]
+        + [w_spec] * 4 + [row_spec],
+        out_specs=[row_spec] + [pl.BlockSpec(dw_shape, lambda b: (0, 0, 0), pipeline_mode=pl.Buffered(1))] * 2,
+        compiler_params=pltpu.CompilerParams(dimension_semantics=("arbitrary",), vmem_limit_bytes=ALL_VMEM),
+        cost_estimate=pl.CostEstimate(
+            flops=16 * rows * seq * hidden * width, bytes_accessed=12 * rows * seq * hidden, transcendentals=2 * rows * seq * width),
+    )(grad, x_saved, *h_pair, *ups, *downs, carry)
+
+
+def small_body(has_init, grad_ref, x_ref, h_a, h_b, down_a, down_b, *refs):
+    dw_pair, pre_ref, h_ref = refs[-4:-2], refs[-2], refs[-1]
+
+    @pl.when(pl.program_id(0) == 0)
+    def _():
+        for i, dw in enumerate(dw_pair):
+            dw[...] = refs[i][...] if has_init else jnp.zeros_like(dw)
+
+    h_ref[0], h_ref[1] = swap_lanes(h_a[0].astype(F32), h_b[0].astype(F32))
     down = jnp.concatenate([down_a[...], down_b[...]])
-    for r, (h, grad_ref, x_ref) in enumerate(zip(h_pair, (grad_lo, grad_hi), (x_lo, x_hi))):
-        grad, x = grad_ref[0], x_ref[0, 0]
-        pre, act = unit_grads(grad, h, down)
+
+    @pl.loop(0, 2)
+    def _(r):
+        grad, x = grad_ref[r, 0], x_ref[0, r, 0]
+        pre, act = unit_grads(grad, h_ref[r], down)
         pre_ref[r, 0] = pre
-        dw_ref[0] += dot(pre, x, 0, 0)
-        dw_ref[1] += dot(act, grad, 0, 0)
-
-
-def small_call(layer, grad, x_saved, h_pair, down_pair, start):
+        for kind, part in enumerate((dot(pre, x, 0, 0), dot(act, grad, 0, 0))):
+            dw_pair[0][kind] += part[:SMALL]
+            dw_pair[1][kind] += part[SMALL:]
+
+
+def small_call(layer, grad, x_saved, h_pair, down_pair, start, first_pair, init):
     rows, seq, hidden = grad.shape
-    pairs = rows // 2
-
-    def row_specs(lead, index):
-        return [pl.BlockSpec(lead + (1, seq, hidden), lambda b, r=r: index + (b + r * pairs, 0, 0)) for r in range(2)]
-
+    pairs = h_pair[0].shape[0]
+    grad = grad.reshape(2, rows // 2, seq, hidden)
+    x_saved = x_saved.reshape(-1, 2, rows // 2, seq, hidden)
     h_spec = pl.BlockSpec((1, seq, LANES), lambda b: (b, 0, 0))
     down_spec = pl.BlockSpec((SMALL, hidden), lambda b: (start // SMALL, 0))
-    dw_shape = (2, LANES, hidden)
-    return pl.pallas_call(
-        small_body,
-        out_shape=[jax.ShapeDtypeStruct(dw_shape, F32), jax.ShapeDtypeStruct((2, pairs, seq, LANES), BF16)],
+    dw_shape = (2, SMALL, hidden)
+    dw_spec = pl.BlockSpec(dw_shape, lambda b: (0, 0, 0))
+    return pl.pallas_call(
+        functools.partial(small_body, init is not None),
+        out_shape=[jax.ShapeDtypeStruct(dw_shape, F32)] * 2 + [jax.ShapeDtypeStruct((2, pairs, seq, LANES), BF16)],
         grid=(pairs,),
-        in_specs=row_specs((), ()) + row_specs((1,), (layer,)) + [h_spec, h_spec, down_spec, down_spec],
-        out_specs=[pl.BlockSpec(dw_shape, lambda b: (0, 0, 0)), pl.BlockSpec((2, 1, seq, LANES), lambda b: (0, b, 0, 0))],
-        compiler_params=pltpu.CompilerParams(dimension_semantics=("arbitrary",), vmem_limit_bytes=40 * 2**20),
+        in_specs=[
+            pl.BlockSpec((2, 1, seq, hidden), lambda b: (0, b + first_pair, 0, 0)),
+            pl.BlockSpec((1, 2, 1, seq, hidden), lambda b: (layer, 0, b + first_pair, 0, 0)),
+            h_spec, h_spec, down_spec, down_spec,
+        ]
+        + ([dw_spec] * 2 if init is not None else []),
+        out_specs=[dw_spec, dw_spec, pl.BlockSpec((2, 1, seq, LANES), lambda b: (0, b, 0, 0))],
+        scratch_shapes=[pltpu.VMEM((2, seq, LANES), F32)],
+        compiler_params=pltpu.CompilerParams(dimension_semantics=("arbitrary",), vmem_limit_bytes=ALL_VMEM),
         cost_estimate=pl.CostEstimate(
-            flops=12 * rows * seq * hidden * SMALL, bytes_accessed=4 * rows * seq * hidden, transcendentals=2 * rows * seq * SMALL),
-    )(grad, grad, x_saved, x_saved, *h_pair, *down_pair)
-
-
-def finish_body(grad_ref, carry_ref, pre_a, pre_b, up_a, up_b, *refs):
+            flops=24 * pairs * seq * hidden * SMALL, bytes_accessed=8 * pairs * seq * hidden, transcendentals=4 * pairs * seq * SMALL),
+    )(grad, x_saved, *h_pair, *down_pair, *(init or ()))
+
+
+def finish_body(carry_ref, pre_a, pre_b, up_a, up_b, *refs):
     out_ref, up_ref = refs[-2:]
 
-    @pl.when(pl.program_id(0) == 0)
+    @pl.when((pl.program_id(0) == 0) & (pl.program_id(1) == 0))
     def _():
         first, second = swap_lanes(up_a[...].astype(F32), up_b[...].astype(F32))
         up_ref[:, :LANES], up_ref[:, LANES:] = first.astype(BF16), second.astype(BF16)
 
     total = carry_ref[0] + dot(jnp.concatenate([pre_a[0, 0], pre_b[0, 0]], axis=1), up_ref[...], 1, 1)
-    out_ref[0] = (grad_ref[0].astype(F32) + total).astype(BF16)
-
-
-def finish_call(grad, carry, pre_pair, up_pair, start, half, out):
-    rows, seq, hidden = grad.shape
-    pairs = rows // 2
-    row_spec = pl.BlockSpec((1, seq, hidden), lambda b: (b + half * pairs, 0, 0))
-    pre_spec = pl.BlockSpec((1, 1, seq, LANES), lambda b: (half, b, 0, 0))
-    up_spec = pl.BlockSpec((hidden, LANES), lambda b: (0, start // LANES))
+    out_ref[0] = total.astype(BF16)
+
+
+def finish_call(carry, pre_pair, up_pair, start, pairs, offset, out):
+    rows, seq, hidden = carry.shape
+    row_spec = pl.BlockSpec((1, seq, hidden), lambda r, b: (b + pairs[0] + r * rows // 2, 0, 0))
+    pre_specs = [pl.BlockSpec((1, 1, seq, LANES), lambda r, b, first=first: (r, b + first, 0, 0)) for first in (pairs[0], pairs[0] - offset)]
+    up_spec = pl.BlockSpec((hidden, LANES), lambda r, b: (0, start // LANES))
+    count = 2 * (pairs[1] - pairs[0])
     return pl.pallas_call(
         finish_body,
-        out_shape=jax.ShapeDtypeStruct(grad.shape, BF16),
-        grid=(pairs,),
-        in_specs=[row_spec, row_spec, pre_spec, pre_spec, up_spec, up_spec]
-        + ([pl.BlockSpec(memory_space=pl.ANY)] if out is not None else []),
+        out_shape=jax.ShapeDtypeStruct(carry.shape, BF16),
+        grid=(2, pairs[1] - pairs[0]),
+        in_specs=[row_spec, *pre_specs, up_spec, up_spec] + ([pl.BlockSpec(memory_space=pl.ANY)] if out is not None else []),
         out_specs=row_spec,
         scratch_shapes=[pltpu.VMEM((hidden, 2 * LANES), BF16)],
-        input_output_aliases={6: 0} if out is not None else {},
-        compiler_params=pltpu.CompilerParams(dimension_semantics=("arbitrary",), vmem_limit_bytes=40 * 2**20),
-        cost_estimate=pl.CostEstimate(flops=4 * rows * seq * hidden * SMALL, bytes_accessed=4 * rows * seq * hidden, transcendentals=0),
-    )(grad, carry, *pre_pair, *up_pair, *(() if out is None else (out,)))
+        input_output_aliases={5: 0} if out is not None else {},
+        compiler_params=pltpu.CompilerParams(dimension_semantics=("arbitrary", "arbitrary"), vmem_limit_bytes=ALL_VMEM),
+        cost_estimate=pl.CostEstimate(flops=4 * count * seq * hidden * LANES, bytes_accessed=7 * count * seq * hidden, transcendentals=0),
+    )(carry, *pre_pair, *up_pair, *(() if out is None else (out,)))
+
+
+def pair_body(first_ref, mine_ref, theirs_ref, stay_ref, away_ref):
+    first = first_ref[0] == 1
+    up, down = mine_ref[0] + theirs_ref[0], mine_ref[1] + theirs_ref[1]
+    stay_ref[...] = jnp.where(first, up, down)
+    away_ref[...] = jnp.where(first, down, up)
+
+
+def pair_call(first, mine, theirs):
+    shape = mine.shape[1:]
+    return pl.pallas_call(
+        pair_body,
+        out_shape=[jax.ShapeDtypeStruct(shape, F32)] * 2,
+        grid_spec=pltpu.PrefetchScalarGridSpec(
+            num_scalar_prefetch=1,
+            grid=(1,),
+            in_specs=[pl.BlockSpec(mine.shape, lambda i, first: (0, 0, 0))] * 2,
+            out_specs=[pl.BlockSpec(shape, lambda i, first: (0, 0))] * 2,
+        ),
+        compiler_params=pltpu.CompilerParams(dimension_semantics=("arbitrary",), vmem_limit_bytes=ALL_VMEM),
+        cost_estimate=pl.CostEstimate(flops=4 * mine.size, bytes_accessed=12 * mine.size, transcendentals=0),
+    )(first, mine, theirs)
 
 
 def place_body(pieces, first_ref, *refs):
@@ -250,7 +335,7 @@
             ],
         ),
         input_output_aliases={1 + count: 0, 2 + count: 1} if bufs is not None else {},
-        compiler_params=pltpu.CompilerParams(dimension_semantics=("arbitrary",)),
+        compiler_params=pltpu.CompilerParams(dimension_semantics=("arbitrary",), vmem_limit_bytes=ALL_VMEM),
         cost_estimate=pl.CostEstimate(flops=4 * size * hidden, bytes_accessed=16 * size * hidden, transcendentals=0),
     )(first, *kept, *other, *(bufs or ()))
 
@@ -297,7 +382,7 @@
         packed = []
         for flip in (2, 3):
             packed.append(pack_call(jnp.reshape(me ^ flip, (1,)).astype(jnp.int32), h_saved, 0, small_start, seq))
-        h_small = [[to_model(packed[0][j], 2), to_model(packed[1][j], 3)] for j in range(2)]
+        h_small = [[to_model(packed[0][j], 2), to_model(packed[1][j], 3)] for j in range(3)]
 
         up, down = [{0: w_up} for _ in range(layers)], [{0: w_down} for _ in range(layers)]
         near_up, near_down = to_model(w_up, 1), to_model(w_down, 1)
@@ -312,10 +397,14 @@
             ups, downs = [up[layer][f] for f in flips], [down[layer][f] for f in flips]
             return block_call(quarter, layer, grad, x_saved, hs, ups, downs, start, size, carry, final)
 
-        def partial_sum(keep, give):
-            value = keep + to_model(give, 1)
-            away = jnp.where(first, value[1], value[0])
-            stay = jnp.where(first, value[0], value[1])
+        def partial_sum(keep, give, fused=False):
+            theirs = to_model(give, 1)
+            if fused:
+                stay, away = pair_call(first_flag, keep, theirs)
+            else:
+                value = keep + theirs
+                away = jnp.where(first, value[1], value[0])
+                stay = jnp.where(first, value[0], value[1])
             return stay + to_data(away)
 
         def place(pieces, layer, start, bufs):
@@ -333,26 +422,32 @@
         near = partial_sum(dw_0, dw_1)
         units = [(0, 0, 384), (1, 384, 128), (1, 512, 128), (2, small_start, SMALL), (3, small_start + SMALL, SMALL)]
         near_part = lax.optimization_barrier(tuple(near[start : start + size] for _, start, size in units))
-        pres, pieces = [], []
+        down_pair, up_pair = [down[0][f] for f in (2, 3)], [up[0][f] for f in (2, 3)]
+        chunk = rows // 4
+        pieces = []
         for j in range(4):
             base = sum(BLOCKS[:j]) if j < 2 else small_start + (j - 2) * SMALL
-            if j < 2:
-                flips = (2, 3)
-                carry, dw_2, dw_3 = call(0, grad_mid, h_zero[j], flips, carry, False, base, BLOCKS[j])
+            if j == 0:
+                carry, dw_2, dw_3 = call(0, grad_mid, h_zero[j], (2, 3), carry, False, base, BLOCKS[j])
+            elif j == 1:
+                carry, dw_2, dw_3 = wide_call(0, grad_mid, x_saved, h_zero[j], up_pair, down_pair, base, carry)
+            elif j == 2:
+                dw_2, dw_3, pre_1 = small_call(0, grad_mid, x_saved, h_small[0], down_pair, base, 0, None)
             else:
-                dw, pre = small_call(0, grad_mid, x_saved, h_small[j - 2], [down[0][f] for f in (2, 3)], base)
-                dw_2, dw_3 = dw[:, :SMALL], dw[:, SMALL:]
-                pres.append(pre)
-            far = partial_sum(dw_2, dw_3)
+                dw_2, dw_3, pre_2 = small_call(0, grad_mid, x_saved, h_small[1], down_pair, base, 0, None)
+                grad_x = finish_call(carry, (pre_1, pre_2), up_pair, small_start, (0, chunk), 0, None)
+                dw_2, dw_3, pre_2 = small_call(0, grad_mid, x_saved, h_small[2], down_pair, base, chunk, (dw_2, dw_3))
+            far = partial_sum(dw_2, dw_3, j >= 2)
             for u, (block, start, size) in enumerate(units):
                 if block == j:
-                    kept = near_part[u] + to_model(far[start - base : start - base + size], 2)
+                    part = to_model(far[start - base : start - base + size], 2)
+                    kept = near_part[u] + part
                     pieces.append((kept, to_data(kept)))
         for u in range(3):
             bufs = place([pieces[u]], 0, units[u][1], bufs)
-        grad_x = None
         for half in range(2):
-            grad_x = finish_call(grad_mid, carry, pres, [up[0][f] for f in (2, 3)], small_start, half, grad_x)
+            low = chunk + half * chunk // 2
+            grad_x = finish_call(carry, (pre_1, pre_2), up_pair, small_start, (low, low + chunk // 2), chunk, grad_x)
         bufs = place(pieces[3:], 0, small_start, bufs)
         return grad_x, bufs[0], bufs[1]
 

time: 1660 us -> 1660 us (level)
  waiting for transfers between devices: 914 us -> 891 us
  other arithmetic: 36.6 us -> 54.1 us
    pallas_call x6 -> x11, Pallas kernels: 67.1 us -> 141 us  [the longest x1 54.4 us: wide_call(): pl.pallas_call(functools.partial(wide_body, start), out_shape=[jax.ShapeD...]
    pallas_call x5 -> x4, Pallas kernels: 507 us -> 438 us  [block_call(): pl.pallas_call(functools.partial(block_body, carry is not None, final, ro...]
    ppermute x33 -> x35, waiting for transfers between devices: 772 us -> 765 us  [to_model(): return lax.ppermute(value, 'model', [(i, i ^ flip) for i in range(n_model)])]
  transfers between devices with their start and end apart: 48 -> 50, of which waited for: 19 -> 14; matrix products, arithmetic and copies ran while one was open for 4% -> 5% of each run, Pallas kernels for 35% -> 36%
where the time goes in v2:
time: 1660 us; the launch traced here: 1650 us
  waiting for transfers between devices  891 us (54%)
  Pallas kernels  596 us (36%)
  local copies, waits for them, and re-layouts  70 us (4%)
  other arithmetic  54.1 us (3%)
  starting transfers between devices  41.9 us (3%)
    ppermute x35, waiting for transfers between devices, to_model(): return lax.ppermute(value, 'model', [(i, i ^ flip) for i in range(n_model)])  765 us
    pallas_call x4, Pallas kernels, block_call(): pl.pallas_call(functools.partial(block_body, carry is not None, final, ro...  438 us
    ppermute x15, waiting for transfers between devices, to_data(): return lax.ppermute(value, 'data', [(0, 1), (1, 0)])  126 us
    squeeze x8, local copies, waits for them, and re-layouts, h_from(): lax.dynamic_slice(held[0], (layer, 0, begin, start), (1, rows, seq, size))  61.4 us
    pallas_call x1, Pallas kernels, wide_call(): pl.pallas_call(functools.partial(wide_body, start), out_shape=[jax.ShapeD...  54.4 us
    pallas_call x3, Pallas kernels, small_call(): pl.pallas_call(functools.partial(small_body, init is not None), out_shape...  47 us
  transfers between devices with their start and end apart: 50, of which 14 were waited for; matrix products, arithmetic and copies ran while one was open for 5% of the time, Pallas kernels for 36%

profile of v2, /device:TPU:0, one launch (start us, length us, event | category | flops | bytes accessed | tf_op | source)
XLA Modules:
  0.0 1653.6 jit_solution(2963760334386132188)
XLA Ops:
  0.6 2.8 select_bitcast_fusion.5
  3.4 10.6 dynamic-slice_bitcast_fusion.3
  14.0 10.6 dynamic-slice_bitcast_fusion.2
  24.6 7.5 dynamic-slice_bitcast_fusion.1
  33.0 2.6 collective-permute-start.1
  35.5 2.0 collective-permute-start.2
  37.8 564.0 %collective-permute-done.2 = bf16[768,768]{1,0:T(8,128)(2,1)S(1)} collective-permute-done((bf16[768,768]{1,0:T(8,128)(2,1)S(1)}, bf16[768,768]{1,0:T(8,128)(2,1)S(1)}, u32[]{:S(2)}, u32[]{:S(2)}) %collective-permute-start.2) | collective-permute-done | bytes 1179680 | tf_op jit(solution)/shard_map/ppermute | solution.py:347
  601.8 2.1 collective-permute-start.3
  603.9 22.9 %collective-permute-done.11 = bf16[768,768]{1,0:T(8,128)(2,1)S(1)} collective-permute-done((bf16[768,768]{1,0:T(8,128)(2,1)S(1)}, bf16[768,768]{1,0:T(8,128)(2,1)S(1)}, u32[]{:S(2)}, u32[]{:S(2)}) %collective-permute-start.11) | collective-permute-done | bytes 1179680 | tf_op jit(solution)/shard_map/ppermute | solution.py:347
  626.9 1.7 collective-permute-start.12
  629.4 25.3 %collective-permute-done.12 = bf16[768,768]{1,0:T(8,128)(2,1)S(1)} collective-permute-done((bf16[768,768]{1,0:T(8,128)(2,1)S(1)}, bf16[768,768]{1,0:T(8,128)(2,1)S(1)}, u32[]{:S(2)}, u32[]{:S(2)}) %collective-permute-start.12) | collective-permute-done | bytes 1179680 | tf_op jit(solution)/shard_map/ppermute | solution.py:350
  655.6 10.6 dynamic-slice_bitcast_fusion
  666.3 6.3 dynamic-slice_bitcast_fusion.5
  672.6 6.3 dynamic-slice_bitcast_fusion.4
  678.9 3.0 broadcast_select_fusion.2
  681.9 1.6 broadcast_select_fusion
  684.5 119.6 %shard_map.76 = (f32[16,512,768]{2,1,0:T(8,128)}, f32[2,768,768]{2,1,0:T(8,128)}, f32[2,768,768]{2,1,0:T(8,128)}) custom-call(s32[1]{0:T(128)} %bitcast._, bf16[16,512,768]{2,1,0:T(8,128)(2,1)} %refs_0_.3, bf16[2,16,512,768]{3,2,1,0:T(8,128)(2,1)} %x_ref.1, bf16[2,16,2048,768]{3,2,1,0:T(8,128)(2,1)} %hi_ref.3, ...), custom_call_target="tpu_custom_call" | custom-call | flops 77309411328 | bytes 50331648 | tf_op jit(solution)/shard_map/pallas_call | solution.py:111
  806.3 121.2 %shard_map.77 = (bf16[16,512,768]{2,1,0:T(8,128)(2,1)}, f32[2,768,768]{2,1,0:T(8,128)}, f32[2,768,768]{2,1,0:T(8,128)}) custom-call(s32[1]{0:T(128)} %bitcast._, bf16[16,512,768]{2,1,0:T(8,128)(2,1)} %refs_0_.3, bf16[2,16,512,768]{3,2,1,0:T(8,128)(2,1)} %x_ref.1, bf16[16,512,768]{2,1,0:T(8,128)(2,1)} %collective-permute-done.refs_2_, ...), custom_call_target="tpu_custom_call" | custom-call | flops 77309411328 | bytes 50331648 | tf_op jit(solution)/shard_map/pallas_call | solution.py:111
  928.1 119.4 %shard_map.78 = (f32[16,512,768]{2,1,0:T(8,128)}, f32[2,768,768]{2,1,0:T(8,128)}, f32[2,768,768]{2,1,0:T(8,128)}) custom-call(s32[1]{0:T(128)} %bitcast._, bf16[16,512,768]{2,1,0:T(8,128)(2,1)} %get-tuple-element.66.refs_0_.grad_ref, bf16[2,16,512,768]{3,2,1,0:T(8,128)(2,1)} %x_ref.1, bf16[2,16,2048,768]{3,2,1,0:T(8,128)(2,1)} %hi_ref.3, ...), custom_call_target="tpu_custom_call" | custom-call | flops 77309411328 | bytes 50331648 | tf_op jit(solution)/shard_map/pallas_call | solution.py:111
  1048.0 27.8 %collective-permute-done.16.refs_3_ = bf16[16,512,384]{2,1,0:T(8,128)(2,1)} collective-permute-done((bf16[16,512,384]{2,1,0:T(8,128)(2,1)}, bf16[16,512,384]{2,1,0:T(8,128)(2,1)}, u32[]{:S(2)}, u32[]{:S(2)}) %collective-permute-start.16) | collective-permute-done | bytes 6291488 | tf_op jit(solution)/shard_map/ppermute | solution.py:347
  1075.8 78.1 %shard_map.79 = (f32[16,512,768]{2,1,0:T(8,128)}, f32[2,384,768]{2,1,0:T(8,128)}, f32[2,384,768]{2,1,0:T(8,128)}) custom-call(s32[1]{0:T(128)} %bitcast._, bf16[16,512,768]{2,1,0:T(8,128)(2,1)} %get-tuple-element.66.refs_0_.grad_ref, bf16[2,16,512,768]{3,2,1,0:T(8,128)(2,1)} %x_ref.1, bf16[16,512,384]{2,1,0:T(8,128)(2,1)} %collective-permute-done.15.refs_2_, ...), custom_call_target="tpu_custom_call" | custom-call | flops 38654705664 | bytes 50331648 | tf_op jit(solution)/shard_map/pallas_call | solution.py:111
  1154.8 4.8 dynamic-slice_bitcast_fusion.7
  1159.5 4.7 dynamic-slice_bitcast_fusion.6
  1165.9 2.9 add.86
  1168.9 1.9 select_bitcast_fusion
  1171.8 1.4 copy-done.4
  1174.4 6.3 shard_map.81
  1180.7 6.3 shard_map.82
  1187.0 2.8 add.81
  1191.3 1.5 collective-permute-start.22
  1192.8 3.1 add.84
  1196.7 3.9 add.71
  1200.7 1.8 select_bitcast_fusion.1
  1202.4 24.4 %collective-permute-done.47 = f32[768,768]{1,0:T(8,128)} collective-permute-done((f32[768,768]{1,0:T(8,128)}, f32[768,768]{1,0:T(8,128)}, u32[]{:S(2)}, u32[]{:S(2)}) %collective-permute-start.47) | collective-permute-done | bytes 2359328 | tf_op jit(solution)/shard_map/ppermute | solution.py:350
  1228.1 1.7 select_bitcast_fusion.2
  1229.8 3.5 bitcast_add_fusion
  1233.4 125.3 %collective-permute-done.22.h_a = bf16[4,512,128]{2,1,0:T(8,128)(2,1)S(1)} collective-permute-done((bf16[4,512,128]{2,1,0:T(8,128)(2,1)S(1)}, bf16[4,512,128]{2,1,0:T(8,128)(2,1)S(1)}, u32[]{:S(2)}, u32[]{:S(2)}) %collective-permute-start.22) | collective-permute-done | bytes 524320 | tf_op jit(solution)/shard_map/ppermute | solution.py:347
  1359.2 10.4 collective-permute-done.23.h_b
  1370.8 10.4 collective-permute-done.20.h_a
  1384.5 54.4 %shard_map.80 = (f32[16,512,768]{2,1,0:T(8,128)}, f32[2,256,768]{2,1,0:T(8,128)}, f32[2,256,768]{2,1,0:T(8,128)}) custom-call(bf16[16,512,768]{2,1,0:T(8,128)(2,1)} %get-tuple-element.66.refs_0_.grad_ref, bf16[2,16,512,768]{3,2,1,0:T(8,128)(2,1)} %x_ref.1, bf16[16,512,256]{2,1,0:T(8,128)(2,1)} %collective-permute-done.9.h_a, ...), custom_call_target="tpu_custom_call" | custom-call | flops 25769803776 | bytes 75497472 | tf_op jit(solution)/shard_map/pallas_call | solution.py:194
  1439.8 9.5 collective-permute-done.45
  1449.3 12.4 shard_map.84
  1461.7 12.8 shard_map.85
  1474.5 3.2 bitcast_add_fusion.3
  1478.2 5.7 fusion.refs_0_
  1485.2 2.4 collective-permute-done.19.h_b
  1488.7 21.8 %shard_map.83 = (f32[2,64,768]{2,1,0:T(8,128)}, f32[2,64,768]{2,1,0:T(8,128)}, bf16[2,8,512,128]{3,2,1,0:T(8,128)(2,1)}) custom-call(bf16[2,8,512,768]{3,2,1,0:T(8,128)(2,1)} %bitcast.53, bf16[2,2,8,512,768]{4,3,2,1,0:T(8,128)(2,1)} %bitcast.50, bf16[8,512,128]{2,1,0:T(8,128)(2,1)} %collective-permute-done.18.h_a, ...), custom_call_target="tpu_custom_call" | custom-call | flops 4831838208 | bytes 25165824 | tf_op jit(solution)/shard_map/pallas_call | solution.py:237
  1511.3 1.9 shard_map.90
  1514.1 2.1 add.77
  1517.4 3.5 bitcast_add_fusion.2
  1522.6 2.5 add.83.refs_0_
  1525.9 45.5 %collective-permute-done.35 = f32[256,768]{1,0:T(8,128)S(1)} collective-permute-done((f32[256,768]{1,0:T(8,128)S(1)}, f32[256,768]{1,0:T(8,128)S(1)}, u32[]{:S(2)}, u32[]{:S(2)}) %collective-permute-start.35) | collective-permute-done | bytes 786464 | tf_op jit(solution)/shard_map/ppermute | solution.py:350
  1574.5 1.9 shard_map.89
  1579.5 20.7 %collective-permute-done.27 = f32[64,768]{1,0:T(8,128)S(1)} collective-permute-done((f32[64,768]{1,0:T(8,128)}, f32[64,768]{1,0:T(8,128)S(1)}, u32[]{:S(2)}, u32[]{:S(2)}) %collective-permute-start.27) | collective-permute-done | bytes 196640 | tf_op jit(solution)/shard_map/ppermute | solution.py:350
  1606.5 1.4 collective-permute-done.31
  1609.2 1.6 add.76.refs_1_
  1613.5 11.1 shard_map.86.refs_0_
  1624.6 6.2 shard_map.87.refs_0_
  1630.8 6.2 shard_map.88
  1637.0 5.9 shard_map.91
  1642.9 3.8 shard_map.92
  1646.7 2.0 shard_map.93
  1648.7 2.0 shard_map.94
  1651.5 2.1 shard_map.95
  (160 shorter events, 46.4 us)
Async XLA Ops:
  24.6 11.0 copy-start.14
  24.6 13.0 copy-start.5
  24.6 13.0 copy-start.6
  32.1 651.9 %collective-permute-start.6 = (bf16[16,512,768]{2,1,0:T(8,128)(2,1)S(1)}, bf16[16,512,768]{2,1,0:T(8,128)(2,1)}, u32[]{:S(2)}, u32[]{:S(2)}) collective-permute-start(bf16[16,512,768]{2,1,0:T(8,128)(2,1)S(1)} %dynamic-slice_bitcast_fusion.1), channel_id=1, source_target_pairs={{0,1},{1,0},{2,3},{3,2},{4,5},{5,4},{6,7},{7,6}} | collective-permute-start | bytes 37748744 | tf_op jit(solution)/shard_map/ppermute | solution.py:347
  33.0 772.6 %collective-permute-start.1 = (bf16[16,512,768]{2,1,0:T(8,128)(2,1)}, bf16[16,512,768]{2,1,0:T(8,128)(2,1)}, u32[]{:S(2)}, u32[]{:S(2)}) collective-permute-start(bf16[16,512,768]{2,1,0:T(8,128)(2,1)} %dynamic-slice_bitcast_fusion.2), channel_id=1, source_target_pairs={{0,3},{1,2},{2,1},{3,0},{4,7},{5,6},{6,5},{7,4}} | collective-permute-start | bytes 37748744 | tf_op jit(solution)/shard_map/ppermute | solution.py:347
  35.5 770.8 %collective-permute-start = (bf16[16,512,768]{2,1,0:T(8,128)(2,1)}, bf16[16,512,768]{2,1,0:T(8,128)(2,1)}, u32[]{:S(2)}, u32[]{:S(2)}) collective-permute-start(bf16[16,512,768]{2,1,0:T(8,128)(2,1)} %dynamic-slice_bitcast_fusion.3), channel_id=1, source_target_pairs={{0,2},{1,3},{2,0},{3,1},{4,6},{5,7},{6,4},{7,5}} | collective-permute-start | bytes 37748744 | tf_op jit(solution)/shard_map/ppermute | solution.py:347
  35.5 566.2 %collective-permute-start.2 = (bf16[768,768]{1,0:T(8,128)(2,1)S(1)}, bf16[768,768]{1,0:T(8,128)(2,1)S(1)}, u32[]{:S(2)}, u32[]{:S(2)}) collective-permute-start(bf16[768,768]{1,0:T(8,128)(2,1)S(1)} %copy-done.14), channel_id=1, source_target_pairs={{0,2},{1,3},{2,0},{3,1},{4,6},{5,7},{6,4},{7,5}} | collective-permute-start | bytes 3538952 | tf_op jit(solution)/shard_map/ppermute | solution.py:347
  37.7 589.2 %collective-permute-start.11 = (bf16[768,768]{1,0:T(8,128)(2,1)S(1)}, bf16[768,768]{1,0:T(8,128)(2,1)S(1)}, u32[]{:S(2)}, u32[]{:S(2)}) collective-permute-start(bf16[768,768]{1,0:T(8,128)(2,1)S(1)} %select_bitcast_fusion.4), channel_id=1, source_target_pairs={{0,2},{1,3},{2,0},{3,1},{4,6},{5,7},{6,4},{7,5}} | collective-permute-start | bytes 3538952 | tf_op jit(solution)/shard_map/ppermute | solution.py:347
  601.8 27.5 %collective-permute-start.3 = (bf16[768,768]{1,0:T(8,128)(2,1)S(1)}, bf16[768,768]{1,0:T(8,128)(2,1)S(1)}, u32[]{:S(2)}, u32[]{:S(2)}) collective-permute-start(bf16[768,768]{1,0:T(8,128)(2,1)S(1)} %collective-permute-done.2), channel_id=1, source_target_pairs={{0,4},{4,0},{1,5},{5,1},{2,6},{6,2},{3,7},{7,3}} | collective-permute-start | bytes 3538952 | tf_op jit(solution)/shard_map/ppermute | solution.py:350
  626.9 27.8 %collective-permute-start.12 = (bf16[768,768]{1,0:T(8,128)(2,1)S(1)}, bf16[768,768]{1,0:T(8,128)(2,1)S(1)}, u32[]{:S(2)}, u32[]{:S(2)}) collective-permute-start(bf16[768,768]{1,0:T(8,128)(2,1)S(1)} %collective-permute-done.11), channel_id=1, source_target_pairs={{0,4},{4,0},{1,5},{5,1},{2,6},{6,2},{3,7},{7,3}} | collective-permute-start | bytes 3538952 | tf_op jit(solution)/shard_map/ppermute | solution.py:350
  629.3 25.3 %copy-start.11 = (bf16[768,768]{1,0:T(8,128)(2,1)}, bf16[768,768]{1,0:T(8,128)(2,1)S(1)}, u32[]{:S(2)}) copy-start(bf16[768,768]{1,0:T(8,128)(2,1)S(1)} %collective-permute-done.3) | copy-start | bytes 3538948
  629.3 54.1 %collective-permute-start.7 = (bf16[2,768,768]{2,1,0:T(8,128)(2,1)S(1)}, bf16[2,768,768]{2,1,0:T(8,128)(2,1)}, u32[]{:S(2)}, u32[]{:S(2)}) collective-permute-start(bf16[2,768,768]{2,1,0:T(8,128)(2,1)S(1)} %copy-done.6), channel_id=1, source_target_pairs={{0,1},{1,0},{2,3},{3,2},{4,5},{5,4},{6,7},{7,6}} | collective-permute-start | bytes 7077896 | tf_op jit(solution)/shard_map/ppermute | solution.py:347
  655.6 28.3 %collective-permute-start.8 = (bf16[2,768,768]{2,1,0:T(8,128)(2,1)S(1)}, bf16[2,768,768]{2,1,0:T(8,128)(2,1)}, u32[]{:S(2)}, u32[]{:S(2)}) collective-permute-start(bf16[2,768,768]{2,1,0:T(8,128)(2,1)S(1)} %copy-done.5), channel_id=1, source_target_pairs={{0,1},{1,0},{2,3},{3,2},{4,5},{5,4},{6,7},{7,6}} | collective-permute-start | bytes 7077896 | tf_op jit(solution)/shard_map/ppermute | solution.py:347
  683.5 244.1 %collective-permute-start.17 = (bf16[16,512,768]{2,1,0:T(8,128)(2,1)}, bf16[16,512,768]{2,1,0:T(8,128)(2,1)}, u32[]{:S(2)}, u32[]{:S(2)}) collective-permute-start(bf16[16,512,768]{2,1,0:T(8,128)(2,1)} %dynamic-slice_bitcast_fusion), channel_id=1, source_target_pairs={{0,1},{1,0},{2,3},{3,2},{4,5},{5,4},{6,7},{7,6}} | collective-permute-start | bytes 37748744 | tf_op jit(solution)/shard_map/ppermute | solution.py:347
  684.0 120.1 %collective-permute-start.4 = (bf16[768,768]{1,0:T(8,128)(2,1)}, bf16[768,768]{1,0:T(8,128)(2,1)}, u32[]{:S(2)}, u32[]{:S(2)}) collective-permute-start(bf16[768,768]{1,0:T(8,128)(2,1)} %get-tuple-element.128.refs_4_), channel_id=1, source_target_pairs={{0,1},{1,0},{2,3},{3,2},{4,5},{5,4},{6,7},{7,6}} | collective-permute-start | bytes 3538952 | tf_op jit(solution)/shard_map/ppermute | solution.py:347
  684.0 121.4 %collective-permute-start.5 = (bf16[768,768]{1,0:T(8,128)(2,1)}, bf16[768,768]{1,0:T(8,128)(2,1)}, u32[]{:S(2)}, u32[]{:S(2)}) collective-permute-start(bf16[768,768]{1,0:T(8,128)(2,1)} %get-tuple-element.127.refs_6_), channel_id=1, source_target_pairs={{0,1},{1,0},{2,3},{3,2},{4,5},{5,4},{6,7},{7,6}} | collective-permute-start | bytes 3538952 | tf_op jit(solution)/shard_map/ppermute | solution.py:347
  804.1 271.7 %collective-permute-start.15 = (bf16[16,512,384]{2,1,0:T(8,128)(2,1)}, bf16[16,512,384]{2,1,0:T(8,128)(2,1)}, u32[]{:S(2)}, u32[]{:S(2)}) collective-permute-start(bf16[16,512,384]{2,1,0:T(8,128)(2,1)} %dynamic-slice_bitcast_fusion.5), channel_id=1, source_target_pairs={{0,2},{1,3},{2,0},{3,1},{4,6},{5,7},{6,4},{7,5}} | collective-permute-start | bytes 18874376 | tf_op jit(solution)/shard_map/ppermute | solution.py:347
  805.4 270.4 %collective-permute-start.16 = (bf16[16,512,384]{2,1,0:T(8,128)(2,1)}, bf16[16,512,384]{2,1,0:T(8,128)(2,1)}, u32[]{:S(2)}, u32[]{:S(2)}) collective-permute-start(bf16[16,512,384]{2,1,0:T(8,128)(2,1)} %dynamic-slice_bitcast_fusion.4), channel_id=1, source_target_pairs={{0,3},{1,2},{2,1},{3,0},{4,7},{5,6},{6,5},{7,4}} | collective-permute-start | bytes 18874376 | tf_op jit(solution)/shard_map/ppermute | solution.py:347
  805.6 241.9 %collective-permute-start.13 = (bf16[768,768]{1,0:T(8,128)(2,1)}, bf16[768,768]{1,0:T(8,128)(2,1)}, u32[]{:S(2)}, u32[]{:S(2)}) collective-permute-start(bf16[768,768]{1,0:T(8,128)(2,1)} %get-tuple-element.126.refs_4_.up_a), channel_id=1, source_target_pairs={{0,1},{1,0},{2,3},{3,2},{4,5},{5,4},{6,7},{7,6}} | collective-permute-start | bytes 3538952 | tf_op jit(solution)/shard_map/ppermute | solution.py:347
  806.3 241.4 %collective-permute-start.14 = (bf16[768,768]{1,0:T(8,128)(2,1)}, bf16[768,768]{1,0:T(8,128)(2,1)}, u32[]{:S(2)}, u32[]{:S(2)}) collective-permute-start(bf16[768,768]{1,0:T(8,128)(2,1)} %get-tuple-element.125.refs_6_.down_a), channel_id=1, source_target_pairs={{0,1},{1,0},{2,3},{3,2},{4,5},{5,4},{6,7},{7,6}} | collective-permute-start | bytes 3538952 | tf_op jit(solution)/shard_map/ppermute | solution.py:347
  927.6 237.5 %collective-permute-start.46 = (f32[2,768,768]{2,1,0:T(8,128)}, f32[2,768,768]{2,1,0:T(8,128)}, u32[]{:S(2)}, u32[]{:S(2)}) collective-permute-start(f32[2,768,768]{2,1,0:T(8,128)} %get-tuple-element.110), channel_id=1, source_target_pairs={{0,1},{1,0},{2,3},{3,2},{4,5},{5,4},{6,7},{7,6}} | collective-permute-start | bytes 14155784 | tf_op jit(solution)/shard_map/ppermute | solution.py:347
  1047.5 143.5 %collective-permute-start.44 = (f32[2,768,768]{2,1,0:T(8,128)}, f32[2,768,768]{2,1,0:T(8,128)}, u32[]{:S(2)}, u32[]{:S(2)}) collective-permute-start(f32[2,768,768]{2,1,0:T(8,128)} %get-tuple-element.108), channel_id=1, source_target_pairs={{0,1},{1,0},{2,3},{3,2},{4,5},{5,4},{6,7},{7,6}} | collective-permute-start | bytes 14155784 | tf_op jit(solution)/shard_map/ppermute | solution.py:347
  1047.7 148.2 %collective-permute-start.24 = (f32[2,768,768]{2,1,0:T(8,128)}, f32[2,768,768]{2,1,0:T(8,128)}, u32[]{:S(2)}, u32[]{:S(2)}) collective-permute-start(f32[2,768,768]{2,1,0:T(8,128)} %get-tuple-element.89), channel_id=1, source_target_pairs={{0,1},{1,0},{2,3},{3,2},{4,5},{5,4},{6,7},{7,6}} | collective-permute-start | bytes 14155784 | tf_op jit(solution)/shard_map/ppermute | solution.py:347
  1154.0 17.8 %collective-permute-start.40 = (f32[2,384,768]{2,1,0:T(8,128)}, f32[2,384,768]{2,1,0:T(8,128)S(1)}, u32[]{:S(2)}, u32[]{:S(2)}) collective-permute-start(f32[2,384,768]{2,1,0:T(8,128)} %get-tuple-element.106), channel_id=1, source_target_pairs={{0,1},{1,0},{2,3},{3,2},{4,5},{5,4},{6,7},{7,6}} | collective-permute-start | bytes 7077896 | tf_op jit(solution)/shard_map/ppermute | solution.py:347
  1154.8 11.2 slice-start.6
  1159.5 6.4 slice-start.7
  1164.2 218.2 %collective-permute-start.10 = (bf16[16,512,256]{2,1,0:T(8,128)(2,1)}, bf16[16,512,256]{2,1,0:T(8,128)(2,1)}, u32[]{:S(2)}, u32[]{:S(2)}) collective-permute-start(bf16[16,512,256]{2,1,0:T(8,128)(2,1)} %dynamic-slice_bitcast_fusion.6), channel_id=1, source_target_pairs={{0,3},{1,2},{2,1},{3,0},{4,7},{5,6},{6,5},{7,4}} | collective-permute-start | bytes 12582920 | tf_op jit(solution)/shard_map/ppermute | solution.py:347
  1165.1 218.2 %collective-permute-start.9 = (bf16[16,512,256]{2,1,0:T(8,128)(2,1)}, bf16[16,512,256]{2,1,0:T(8,128)(2,1)}, u32[]{:S(2)}, u32[]{:S(2)}) collective-permute-start(bf16[16,512,256]{2,1,0:T(8,128)(2,1)} %dynamic-slice_bitcast_fusion.7), channel_id=1, source_target_pairs={{0,2},{1,3},{2,0},{3,1},{4,6},{5,7},{6,4},{7,5}} | collective-permute-start | bytes 12582920 | tf_op jit(solution)/shard_map/ppermute | solution.py:347
  1173.2 53.7 %collective-permute-start.47 = (f32[768,768]{1,0:T(8,128)}, f32[768,768]{1,0:T(8,128)}, u32[]{:S(2)}, u32[]{:S(2)}) collective-permute-start(f32[768,768]{1,0:T(8,128)} %select_bitcast_fusion), channel_id=1, source_target_pairs={{0,4},{4,0},{1,5},{5,1},{2,6},{6,2},{3,7},{7,3}} | collective-permute-start | bytes 7077896 | tf_op jit(solution)/shard_map/ppermute | solution.py:350
  1187.0 5.8 slice-start.3
  1191.3 167.4 %collective-permute-start.22 = (bf16[4,512,128]{2,1,0:T(8,128)(2,1)S(1)}, bf16[4,512,128]{2,1,0:T(8,128)(2,1)S(1)}, u32[]{:S(2)}, u32[]{:S(2)}) collective-permute-start(bf16[4,512,128]{2,1,0:T(8,128)(2,1)S(1)} %copy-done.21), channel_id=1, source_target_pairs={{0,2},{1,3},{2,0},{3,1},{4,6},{5,7},{6,4},{7,5}} | collective-permute-start | bytes 1572872 | tf_op jit(solution)/shard_map/ppermute | solution.py:347
  1196.0 173.6 %collective-permute-start.23 = (bf16[4,512,128]{2,1,0:T(8,128)(2,1)S(1)}, bf16[4,512,128]{2,1,0:T(8,128)(2,1)}, u32[]{:S(2)}, u32[]{:S(2)}) collective-permute-start(bf16[4,512,128]{2,1,0:T(8,128)(2,1)S(1)} %copy-done.20), channel_id=1, source_target_pairs={{0,3},{1,2},{2,1},{3,0},{4,7},{5,6},{6,5},{7,4}} | collective-permute-start | bytes 1572872 | tf_op jit(solution)/shard_map/ppermute | solution.py:347
  1196.7 33.1 %slice-start = ((s8[4718592]{0:T(1024)(128)(4,1)}), s8[4194304]{0:T(1024)(128)(4,1)S(1)}, s32[]{:S(2)}) async-start(s8[4718592]{0:T(1024)(128)(4,1)} %bitcast.54), calls=%async_computation | async-start | bytes 8388608
  1200.6 27.5 %copy-start = (f32[2,768,768]{2,1,0:T(8,128)}, f32[2,768,768]{2,1,0:T(8,128)S(1)}, u32[]{:S(2)}) copy-start(f32[2,768,768]{2,1,0:T(8,128)S(1)} %add.71) | copy-start | bytes 14155780
  1200.6 26.2 %copy-start.19 = (bf16[4,512,128]{2,1,0:T(8,128)(2,1)S(1)}, bf16[4,512,128]{2,1,0:T(8,128)(2,1)}, u32[]{:S(2)}) copy-start(bf16[4,512,128]{2,1,0:T(8,128)(2,1)} %get-tuple-element.80) | copy-start | bytes 1572868
  1200.7 29.2 %slice-start.1 = ((s8[4718592]{0:T(1024)(128)(4,1)}), s8[524288]{0:T(1024)(128)(4,1)S(1)}, s32[]{:S(2)}) async-start(s8[4718592]{0:T(1024)(128)(4,1)} %bitcast.54), calls=%async_computation.1 | async-start | bytes 1048576
  1226.9 154.4 %collective-permute-start.20 = (bf16[4,512,128]{2,1,0:T(8,128)(2,1)S(1)}, bf16[4,512,128]{2,1,0:T(8,128)(2,1)}, u32[]{:S(2)}, u32[]{:S(2)}) collective-permute-start(bf16[4,512,128]{2,1,0:T(8,128)(2,1)S(1)} %copy-done.19), channel_id=1, source_target_pairs={{0,2},{1,3},{2,0},{3,1},{4,6},{5,7},{6,4},{7,5}} | collective-permute-start | bytes 1572872 | tf_op jit(solution)/shard_map/ppermute | solution.py:347
  1358.7 80.3 %copy-start.15 = (bf16[4,512,128]{2,1,0:T(8,128)(2,1)}, bf16[4,512,128]{2,1,0:T(8,128)(2,1)S(1)}, u32[]{:S(2)}) copy-start(bf16[4,512,128]{2,1,0:T(8,128)(2,1)S(1)} %collective-permute-done.22.h_a) | copy-start | bytes 1572868
  1358.7 80.3 %collective-permute-start.21 = (bf16[4,512,128]{2,1,0:T(8,128)(2,1)}, bf16[4,512,128]{2,1,0:T(8,128)(2,1)}, u32[]{:S(2)}, u32[]{:S(2)}) collective-permute-start(bf16[4,512,128]{2,1,0:T(8,128)(2,1)} %get-tuple-element.81), channel_id=1, source_target_pairs={{0,3},{1,2},{2,1},{3,0},{4,7},{5,6},{6,5},{7,4}} | collective-permute-start | bytes 1572872 | tf_op jit(solution)/shard_map/ppermute | solution.py:347
  1369.6 70.2 %collective-permute-start.41 = (f32[384,768]{1,0:T(8,128)}, f32[384,768]{1,0:T(8,128)}, u32[]{:S(2)}, u32[]{:S(2)}) collective-permute-start(f32[384,768]{1,0:T(8,128)} %select_bitcast_fusion.3), channel_id=1, source_target_pairs={{0,4},{4,0},{1,5},{5,1},{2,6},{6,2},{3,7},{7,3}} | collective-permute-start | bytes 3538952 | tf_op jit(solution)/shard_map/ppermute | solution.py:350
  1381.2 68.1 %collective-permute-start.45 = (f32[768,768]{1,0:T(8,128)}, f32[768,768]{1,0:T(8,128)}, u32[]{:S(2)}, u32[]{:S(2)}) collective-permute-start(f32[768,768]{1,0:T(8,128)} %select_bitcast_fusion.1), channel_id=1, source_target_pairs={{0,4},{4,0},{1,5},{5,1},{2,6},{6,2},{3,7},{7,3}} | collective-permute-start | bytes 7077896 | tf_op jit(solution)/shard_map/ppermute | solution.py:350
  1382.5 133.8 %collective-permute-start.25 = (f32[768,768]{1,0:T(8,128)}, f32[768,768]{1,0:T(8,128)}, u32[]{:S(2)}, u32[]{:S(2)}) collective-permute-start(f32[768,768]{1,0:T(8,128)} %select_bitcast_fusion.2), channel_id=1, source_target_pairs={{0,4},{4,0},{1,5},{5,1},{2,6},{6,2},{3,7},{7,3}} | collective-permute-start | bytes 7077896 | tf_op jit(solution)/shard_map/ppermute | solution.py:350
  1383.3 94.5 %collective-permute-start.48 = (f32[768,768]{1,0:T(8,128)}, f32[768,768]{1,0:T(8,128)}, u32[]{:S(2)}, u32[]{:S(2)}) collective-permute-start(f32[768,768]{1,0:T(8,128)} %bitcast_add_fusion), channel_id=1, source_target_pairs={{0,2},{1,3},{2,0},{3,1},{4,6},{5,7},{6,4},{7,5}} | collective-permute-start | bytes 7077896 | tf_op jit(solution)/shard_map/ppermute | solution.py:347
  1438.9 45.0 %collective-permute-start.18 = (bf16[8,512,128]{2,1,0:T(8,128)(2,1)}, bf16[8,512,128]{2,1,0:T(8,128)(2,1)}, u32[]{:S(2)}, u32[]{:S(2)}) collective-permute-start(bf16[8,512,128]{2,1,0:T(8,128)(2,1)} %get-tuple-element.77), channel_id=1, source_target_pairs={{0,2},{1,3},{2,0},{3,1},{4,6},{5,7},{6,4},{7,5}} | collective-permute-start | bytes 3145736 | tf_op jit(solution)/shard_map/ppermute | solution.py:347
  1439.8 47.8 %collective-permute-start.19 = (bf16[8,512,128]{2,1,0:T(8,128)(2,1)}, bf16[8,512,128]{2,1,0:T(8,128)(2,1)}, u32[]{:S(2)}, u32[]{:S(2)}) collective-permute-start(bf16[8,512,128]{2,1,0:T(8,128)(2,1)} %get-tuple-element.78), channel_id=1, source_target_pairs={{0,3},{1,2},{2,1},{3,0},{4,7},{5,6},{6,5},{7,4}} | collective-permute-start | bytes 3145736 | tf_op jit(solution)/shard_map/ppermute | solution.py:347
  1449.3 63.9 %collective-permute-start.34 = (f32[2,256,768]{2,1,0:T(8,128)}, f32[2,256,768]{2,1,0:T(8,128)}, u32[]{:S(2)}, u32[]{:S(2)}) collective-permute-start(f32[2,256,768]{2,1,0:T(8,128)} %get-tuple-element.102), channel_id=1, source_target_pairs={{0,1},{1,0},{2,3},{3,2},{4,5},{5,4},{6,7},{7,6}} | collective-permute-start | bytes 4718600 | tf_op jit(solution)/shard_map/ppermute | solution.py:347
  1477.8 32.8 %collective-permute-start.29 = (f32[2,64,768]{2,1,0:T(8,128)S(1)}, f32[2,64,768]{2,1,0:T(8,128)S(1)}, u32[]{:S(2)}, u32[]{:S(2)}) collective-permute-start(f32[2,64,768]{2,1,0:T(8,128)S(1)} %copy-done.22), channel_id=1, source_target_pairs={{0,1},{1,0},{2,3},{3,2},{4,5},{5,4},{6,7},{7,6}} | collective-permute-start | bytes 1179656 | tf_op jit(solution)/shard_map/ppermute | solution.py:347
  1484.0 38.6 %collective-permute-start.42 = (f32[384,768]{1,0:T(8,128)}, f32[384,768]{1,0:T(8,128)}, u32[]{:S(2)}, u32[]{:S(2)}) collective-permute-start(f32[384,768]{1,0:T(8,128)} %bitcast_add_fusion.3), channel_id=1, source_target_pairs={{0,2},{1,3},{2,0},{3,1},{4,6},{5,7},{6,4},{7,5}} | collective-permute-start | bytes 3538952 | tf_op jit(solution)/shard_map/ppermute | solution.py:347
  1487.5 124.9 %collective-permute-start.49 = (f32[768,768]{1,0:T(8,128)}, f32[768,768]{1,0:T(8,128)}, u32[]{:S(2)}, u32[]{:S(2)}) collective-permute-start(f32[768,768]{1,0:T(8,128)} %fusion.refs_0_), channel_id=1, source_target_pairs={{0,4},{4,0},{1,5},{5,1},{2,6},{6,2},{3,7},{7,3}} | collective-permute-start | bytes 7077896 | tf_op jit(solution)/shard_map/ppermute | solution.py:350
  1510.6 63.2 %collective-permute-start.26 = (f32[2,64,768]{2,1,0:T(8,128)}, f32[2,64,768]{2,1,0:T(8,128)S(1)}, u32[]{:S(2)}, u32[]{:S(2)}) collective-permute-start(f32[2,64,768]{2,1,0:T(8,128)} %get-tuple-element.92), channel_id=1, source_target_pairs={{0,1},{1,0},{2,3},{3,2},{4,5},{5,4},{6,7},{7,6}} | collective-permute-start | bytes 1179656 | tf_op jit(solution)/shard_map/ppermute | solution.py:347
  1513.2 64.0 %collective-permute-start.30 = (f32[64,768]{1,0:T(8,128)}, f32[64,768]{1,0:T(8,128)}, u32[]{:S(2)}, u32[]{:S(2)}) collective-permute-start(f32[64,768]{1,0:T(8,128)} %get-tuple-element.99), channel_id=1, source_target_pairs={{0,4},{4,0},{1,5},{5,1},{2,6},{6,2},{3,7},{7,3}} | collective-permute-start | bytes 589832 | tf_op jit(solution)/shard_map/ppermute | solution.py:350
  1516.3 55.1 %collective-permute-start.35 = (f32[256,768]{1,0:T(8,128)S(1)}, f32[256,768]{1,0:T(8,128)S(1)}, u32[]{:S(2)}, u32[]{:S(2)}) collective-permute-start(f32[256,768]{1,0:T(8,128)S(1)} %select_bitcast_fusion.6), channel_id=1, source_target_pairs={{0,4},{4,0},{1,5},{5,1},{2,6},{6,2},{3,7},{7,3}} | collective-permute-start | bytes 2359304 | tf_op jit(solution)/shard_map/ppermute | solution.py:350
  1525.0 117.9 %collective-permute-start.43 = (f32[384,768]{1,0:T(8,128)}, f32[384,768]{1,0:T(8,128)}, u32[]{:S(2)}, u32[]{:S(2)}) collective-permute-start(f32[384,768]{1,0:T(8,128)} %add.83.refs_0_), channel_id=1, source_target_pairs={{0,4},{4,0},{1,5},{5,1},{2,6},{6,2},{3,7},{7,3}} | collective-permute-start | bytes 3538952 | tf_op jit(solution)/shard_map/ppermute | solution.py:350
  1572.5 29.8 %collective-permute-start.38 = (f32[128,768]{1,0:T(8,128)}, f32[128,768]{1,0:T(8,128)}, u32[]{:S(2)}, u32[]{:S(2)}) collective-permute-start(f32[128,768]{1,0:T(8,128)} %get-tuple-element.129), channel_id=1, source_target_pairs={{0,2},{1,3},{2,0},{3,1},{4,6},{5,7},{6,4},{7,5}} | collective-permute-start | bytes 1179656 | tf_op jit(solution)/shard_map/ppermute | solution.py:347
  1576.4 27.9 %collective-permute-start.36 = (f32[128,768]{1,0:T(8,128)}, f32[128,768]{1,0:T(8,128)S(1)}, u32[]{:S(2)}, u32[]{:S(2)}) collective-permute-start(f32[128,768]{1,0:T(8,128)} %get-tuple-element.130), channel_id=1, source_target_pairs={{0,2},{1,3},{2,0},{3,1},{4,6},{5,7},{6,4},{7,5}} | collective-permute-start | bytes 1179656 | tf_op jit(solution)/shard_map/ppermute | solution.py:347
  1577.2 23.0 %collective-permute-start.27 = (f32[64,768]{1,0:T(8,128)}, f32[64,768]{1,0:T(8,128)S(1)}, u32[]{:S(2)}, u32[]{:S(2)}) collective-permute-start(f32[64,768]{1,0:T(8,128)} %get-tuple-element.94), channel_id=1, source_target_pairs={{0,4},{4,0},{1,5},{5,1},{2,6},{6,2},{3,7},{7,3}} | collective-permute-start | bytes 589832 | tf_op jit(solution)/shard_map/ppermute | solution.py:350
  1600.1 7.8 collective-permute-start.31
  1602.3 8.5 collective-permute-start.28
  1604.2 20.4 %copy-start.7 = (f32[128,768]{1,0:T(8,128)}, f32[128,768]{1,0:T(8,128)S(1)}, u32[]{:S(2)}) copy-start(f32[128,768]{1,0:T(8,128)S(1)} %add.80.refs_0_) | copy-start | bytes 1179652
  1604.2 42.5 %collective-permute-start.39 = (f32[128,768]{1,0:T(8,128)S(1)}, f32[128,768]{1,0:T(8,128)}, u32[]{:S(2)}, u32[]{:S(2)}) collective-permute-start(f32[128,768]{1,0:T(8,128)S(1)} %add.80.refs_0_), channel_id=1, source_target_pairs={{0,4},{4,0},{1,5},{5,1},{2,6},{6,2},{3,7},{7,3}} | collective-permute-start | bytes 1179656 | tf_op jit(solution)/shard_map/ppermute | solution.py:350
  1606.5 18.1 %copy-start.8 = (f32[128,768]{1,0:T(8,128)}, f32[128,768]{1,0:T(8,128)S(1)}, u32[]{:S(2)}) copy-start(f32[128,768]{1,0:T(8,128)S(1)} %add.79.refs_0_) | copy-start | bytes 1179652
  1607.9 40.8 %collective-permute-start.37 = (f32[128,768]{1,0:T(8,128)S(1)}, f32[128,768]{1,0:T(8,128)}, u32[]{:S(2)}, u32[]{:S(2)}) collective-permute-start(f32[128,768]{1,0:T(8,128)S(1)} %add.79.refs_0_), channel_id=1, source_target_pairs={{0,4},{4,0},{1,5},{5,1},{2,6},{6,2},{3,7},{7,3}} | collective-permute-start | bytes 1179656 | tf_op jit(solution)/shard_map/ppermute | solution.py:350
  1610.8 40.0 %collective-permute-start.33 = (f32[64,768]{1,0:T(8,128)}, f32[64,768]{1,0:T(8,128)}, u32[]{:S(2)}, u32[]{:S(2)}) collective-permute-start(f32[64,768]{1,0:T(8,128)} %add.76.refs_1_), channel_id=1, source_target_pairs={{0,4},{4,0},{1,5},{5,1},{2,6},{6,2},{3,7},{7,3}} | collective-permute-start | bytes 589832 | tf_op jit(solution)/shard_map/ppermute | solution.py:350
  1612.5 38.3 %collective-permute-start.32 = (f32[64,768]{1,0:T(8,128)}, f32[64,768]{1,0:T(8,128)S(1)}, u32[]{:S(2)}, u32[]{:S(2)}) collective-permute-start(f32[64,768]{1,0:T(8,128)} %add.74.refs_0_), channel_id=1, source_target_pairs={{0,4},{4,0},{1,5},{5,1},{2,6},{6,2},{3,7},{7,3}} | collective-permute-start | bytes 589832 | tf_op jit(solution)/shard_map/ppermute | solution.py:350
  (17 other events, 44.8 us)

commit v3 on v2

--- a/solution.py
+++ b/solution.py
@@ -13,6 +13,7 @@
 BLOCKS = (384, 256)
 LANES = 128
 SMALL = 64
+EARLY = 5
 ALL_VMEM = 66_000_000
 
 
@@ -146,12 +147,12 @@
 
 def pack_call(target, h_saved, layer, start, seq):
     pairs = h_saved.shape[1] // 2
-    chunk = pairs // 2
+    chunk = EARLY
     specs = [pl.BlockSpec((1, 1, seq, LANES), lambda b, ids, r=r: (layer, b + r * pairs, ids[0], start // LANES)) for r in range(2)]
     block = (1, seq, LANES)
     return pl.pallas_call(
         functools.partial(pack_body, chunk),
-        out_shape=[jax.ShapeDtypeStruct((n, seq, LANES), BF16) for n in (pairs, chunk, chunk)],
+        out_shape=[jax.ShapeDtypeStruct((n, seq, LANES), BF16) for n in (pairs, chunk, pairs - chunk)],
         grid_spec=pltpu.PrefetchScalarGridSpec(
             num_scalar_prefetch=1,
             grid=(pairs,),
@@ -204,83 +205,97 @@
     )(grad, x_saved, *h_pair, *ups, *downs, carry)
 
 
-def small_body(has_init, grad_ref, x_ref, h_a, h_b, down_a, down_b, *refs):
-    dw_pair, pre_ref, h_ref = refs[-4:-2], refs[-2], refs[-1]
-
-    @pl.when(pl.program_id(0) == 0)
+def small_body(has_init, finish, grad_ref, x_ref, h_a, h_b, down_a, down_b, *refs):
+    refs = list(refs)
+    carry_ref, early_ref, up_ref = (refs.pop(0) for _ in range(3)) if finish else (None,) * 3
+    dw_pair, out_ref = refs[-3:-1], refs[-1]
+    second = pl.program_id(1)
+
+    @pl.when((pl.program_id(0) == 0) & (second == 0))
     def _():
         for i, dw in enumerate(dw_pair):
             dw[...] = refs[i][...] if has_init else jnp.zeros_like(dw)
 
-    h_ref[0], h_ref[1] = swap_lanes(h_a[0].astype(F32), h_b[0].astype(F32))
-    down = jnp.concatenate([down_a[...], down_b[...]])
-
-    @pl.loop(0, 2)
-    def _(r):
-        grad, x = grad_ref[r, 0], x_ref[0, r, 0]
-        pre, act = unit_grads(grad, h_ref[r], down)
-        pre_ref[r, 0] = pre
-        for kind, part in enumerate((dot(pre, x, 0, 0), dot(act, grad, 0, 0))):
-            dw_pair[0][kind] += part[:SMALL]
-            dw_pair[1][kind] += part[SMALL:]
-
-
-def small_call(layer, grad, x_saved, h_pair, down_pair, start, first_pair, init):
+    h_pair = swap_lanes(h_a[0].astype(F32), h_b[0].astype(F32))
+    grad, x = grad_ref[0], x_ref[0, 0]
+    pre, act = unit_grads(grad, jnp.where(second == 0, *h_pair), jnp.concatenate([down_a[...], down_b[...]]))
+    for kind, part in enumerate((dot(pre, x, 0, 0), dot(act, grad, 0, 0))):
+        dw_pair[0][kind] += part[:SMALL]
+        dw_pair[1][kind] += part[SMALL:]
+    if finish:
+        total = carry_ref[0] + dot(jnp.concatenate([early_ref[0, 0], pre], axis=1), up_ref[...], 1, 1)
+        out_ref[0] = total.astype(BF16)
+    else:
+        out_ref[0, 0] = pre
+
+
+def small_call(layer, grad, x_saved, h_pair, down_pair, start, first_pair, init, finish):
     rows, seq, hidden = grad.shape
     pairs = h_pair[0].shape[0]
-    grad = grad.reshape(2, rows // 2, seq, hidden)
-    x_saved = x_saved.reshape(-1, 2, rows // 2, seq, hidden)
-    h_spec = pl.BlockSpec((1, seq, LANES), lambda b: (b, 0, 0))
-    down_spec = pl.BlockSpec((SMALL, hidden), lambda b: (start // SMALL, 0))
+    half = rows // 2
+    row_spec = pl.BlockSpec((1, seq, hidden), lambda b, r: (b + first_pair + r * half, 0, 0))
+    pre_spec = pl.BlockSpec((1, 1, seq, LANES), lambda b, r: (r, b, 0, 0))
+    h_spec = pl.BlockSpec((1, seq, LANES), lambda b, r: (b, 0, 0))
+    down_spec = pl.BlockSpec((SMALL, hidden), lambda b, r: (start // SMALL, 0))
     dw_shape = (2, SMALL, hidden)
-    dw_spec = pl.BlockSpec(dw_shape, lambda b: (0, 0, 0))
-    return pl.pallas_call(
-        functools.partial(small_body, init is not None),
-        out_shape=[jax.ShapeDtypeStruct(dw_shape, F32)] * 2 + [jax.ShapeDtypeStruct((2, pairs, seq, LANES), BF16)],
-        grid=(pairs,),
-        in_specs=[
-            pl.BlockSpec((2, 1, seq, hidden), lambda b: (0, b + first_pair, 0, 0)),
-            pl.BlockSpec((1, 2, 1, seq, hidden), lambda b: (layer, 0, b + first_pair, 0, 0)),
-            h_spec, h_spec, down_spec, down_spec,
-        ]
-        + ([dw_spec] * 2 if init is not None else []),
-        out_specs=[dw_spec, dw_spec, pl.BlockSpec((2, 1, seq, LANES), lambda b: (0, b, 0, 0))],
-        scratch_shapes=[pltpu.VMEM((2, seq, LANES), F32)],
-        compiler_params=pltpu.CompilerParams(dimension_semantics=("arbitrary",), vmem_limit_bytes=ALL_VMEM),
+    dw_spec = pl.BlockSpec(dw_shape, lambda b, r: (0, 0, 0))
+    in_specs = [row_spec, pl.BlockSpec((1, 1, seq, hidden), lambda b, r: (layer, b + first_pair + r * half, 0, 0)), h_spec, h_spec, down_spec, down_spec]
+    if finish:
+        in_specs += [row_spec, pre_spec, pl.BlockSpec(finish[2].shape, lambda b, r: (0, 0))]
+    if init:
+        in_specs += [dw_spec] * 2
+    return pl.pallas_call(
+        functools.partial(small_body, init is not None, finish is not None),
+        out_shape=[jax.ShapeDtypeStruct(dw_shape, F32)] * 2
+        + [jax.ShapeDtypeStruct(grad.shape if finish else (2, pairs, seq, LANES), BF16)],
+        grid=(pairs, 2),
+        in_specs=in_specs,
+        out_specs=[dw_spec, dw_spec, row_spec if finish else pre_spec],
+        compiler_params=pltpu.CompilerParams(dimension_semantics=("arbitrary", "arbitrary"), vmem_limit_bytes=ALL_VMEM),
         cost_estimate=pl.CostEstimate(
             flops=24 * pairs * seq * hidden * SMALL, bytes_accessed=8 * pairs * seq * hidden, transcendentals=4 * pairs * seq * SMALL),
-    )(grad, x_saved, *h_pair, *down_pair, *(init or ()))
-
-
-def finish_body(carry_ref, pre_a, pre_b, up_a, up_b, *refs):
-    out_ref, up_ref = refs[-2:]
-
-    @pl.when((pl.program_id(0) == 0) & (pl.program_id(1) == 0))
-    def _():
-        first, second = swap_lanes(up_a[...].astype(F32), up_b[...].astype(F32))
-        up_ref[:, :LANES], up_ref[:, LANES:] = first.astype(BF16), second.astype(BF16)
-
+    )(grad, x_saved, *h_pair, *down_pair, *(finish or ()), *(init or ()))
+
+
+def join_body(up_a, up_b, out_ref):
+    first, second = swap_lanes(up_a[...].astype(F32), up_b[...].astype(F32))
+    out_ref[:, :LANES], out_ref[:, LANES:] = first.astype(BF16), second.astype(BF16)
+
+
+def join_call(up_pair, start):
+    hidden = up_pair[0].shape[0]
+    up_spec = pl.BlockSpec((hidden, LANES), lambda i: (0, start // LANES))
+    return pl.pallas_call(
+        join_body,
+        out_shape=jax.ShapeDtypeStruct((hidden, 2 * LANES), BF16),
+        grid=(1,),
+        in_specs=[up_spec, up_spec],
+        out_specs=pl.BlockSpec((hidden, 2 * LANES), lambda i: (0, 0)),
+        compiler_params=pltpu.CompilerParams(dimension_semantics=("arbitrary",), vmem_limit_bytes=ALL_VMEM),
+        cost_estimate=pl.CostEstimate(flops=hidden * LANES, bytes_accessed=8 * hidden * LANES, transcendentals=0),
+    )(*up_pair)
+
+
+def finish_body(carry_ref, pre_a, pre_b, up_ref, _, out_ref):
     total = carry_ref[0] + dot(jnp.concatenate([pre_a[0, 0], pre_b[0, 0]], axis=1), up_ref[...], 1, 1)
     out_ref[0] = total.astype(BF16)
 
 
-def finish_call(carry, pre_pair, up_pair, start, pairs, offset, out):
+def finish_call(carry, pre_pair, ups, half, out):
     rows, seq, hidden = carry.shape
-    row_spec = pl.BlockSpec((1, seq, hidden), lambda r, b: (b + pairs[0] + r * rows // 2, 0, 0))
-    pre_specs = [pl.BlockSpec((1, 1, seq, LANES), lambda r, b, first=first: (r, b + first, 0, 0)) for first in (pairs[0], pairs[0] - offset)]
-    up_spec = pl.BlockSpec((hidden, LANES), lambda r, b: (0, start // LANES))
-    count = 2 * (pairs[1] - pairs[0])
+    count = rows // 2 - EARLY
+    row_spec = pl.BlockSpec((1, seq, hidden), lambda b: (b + EARLY + half * rows // 2, 0, 0))
+    pre_specs = [pl.BlockSpec((1, 1, seq, LANES), lambda b, first=first: (half, b + first, 0, 0)) for first in (EARLY, 0)]
     return pl.pallas_call(
         finish_body,
         out_shape=jax.ShapeDtypeStruct(carry.shape, BF16),
-        grid=(2, pairs[1] - pairs[0]),
-        in_specs=[row_spec, *pre_specs, up_spec, up_spec] + ([pl.BlockSpec(memory_space=pl.ANY)] if out is not None else []),
+        grid=(count,),
+        in_specs=[row_spec, *pre_specs, pl.BlockSpec(ups.shape, lambda b: (0, 0)), pl.BlockSpec(memory_space=pl.ANY)],
         out_specs=row_spec,
-        scratch_shapes=[pltpu.VMEM((hidden, 2 * LANES), BF16)],
-        input_output_aliases={5: 0} if out is not None else {},
-        compiler_params=pltpu.CompilerParams(dimension_semantics=("arbitrary", "arbitrary"), vmem_limit_bytes=ALL_VMEM),
+        input_output_aliases={4: 0},
+        compiler_params=pltpu.CompilerParams(dimension_semantics=("arbitrary",), vmem_limit_bytes=ALL_VMEM),
         cost_estimate=pl.CostEstimate(flops=4 * count * seq * hidden * LANES, bytes_accessed=7 * count * seq * hidden, transcendentals=0),
-    )(carry, *pre_pair, *up_pair, *(() if out is None else (out,)))
+    )(carry, *pre_pair, ups, out)
 
 
 def pair_body(first_ref, mine_ref, theirs_ref, stay_ref, away_ref):
@@ -291,16 +306,15 @@
 
 
 def pair_call(first, mine, theirs):
-    shape = mine.shape[1:]
+    _, size, hidden = mine.shape
+    step = min(size, LANES)
+    both_spec = pl.BlockSpec((2, step, hidden), lambda i, first: (0, i, 0))
+    one_spec = pl.BlockSpec((step, hidden), lambda i, first: (i, 0))
     return pl.pallas_call(
         pair_body,
-        out_shape=[jax.ShapeDtypeStruct(shape, F32)] * 2,
+        out_shape=[jax.ShapeDtypeStruct((size, hidden), F32)] * 2,
         grid_spec=pltpu.PrefetchScalarGridSpec(
-            num_scalar_prefetch=1,
-            grid=(1,),
-            in_specs=[pl.BlockSpec(mine.shape, lambda i, first: (0, 0, 0))] * 2,
-            out_specs=[pl.BlockSpec(shape, lambda i, first: (0, 0))] * 2,
-        ),
+            num_scalar_prefetch=1, grid=(size // step,), in_specs=[both_spec] * 2, out_specs=[one_spec] * 2),
         compiler_params=pltpu.CompilerParams(dimension_semantics=("arbitrary",), vmem_limit_bytes=ALL_VMEM),
         cost_estimate=pl.CostEstimate(flops=4 * mine.size, bytes_accessed=12 * mine.size, transcendentals=0),
     )(first, mine, theirs)
@@ -397,14 +411,9 @@
             ups, downs = [up[layer][f] for f in flips], [down[layer][f] for f in flips]
             return block_call(quarter, layer, grad, x_saved, hs, ups, downs, start, size, carry, final)
 
-        def partial_sum(keep, give, fused=False):
+        def partial_sum(keep, give):
             theirs = to_model(give, 1)
-            if fused:
-                stay, away = pair_call(first_flag, keep, theirs)
-            else:
-                value = keep + theirs
-                away = jnp.where(first, value[1], value[0])
-                stay = jnp.where(first, value[0], value[1])
+            stay, away = pair_call(first_flag, keep, theirs)
             return stay + to_data(away)
 
         def place(pieces, layer, start, bufs):
@@ -423,7 +432,7 @@
         units = [(0, 0, 384), (1, 384, 128), (1, 512, 128), (2, small_start, SMALL), (3, small_start + SMALL, SMALL)]
         near_part = lax.optimization_barrier(tuple(near[start : start + size] for _, start, size in units))
         down_pair, up_pair = [down[0][f] for f in (2, 3)], [up[0][f] for f in (2, 3)]
-        chunk = rows // 4
+        small_up = join_call(up_pair, small_start)
         pieces = []
         for j in range(4):
             base = sum(BLOCKS[:j]) if j < 2 else small_start + (j - 2) * SMALL
@@ -432,12 +441,12 @@
             elif j == 1:
                 carry, dw_2, dw_3 = wide_call(0, grad_mid, x_saved, h_zero[j], up_pair, down_pair, base, carry)
             elif j == 2:
-                dw_2, dw_3, pre_1 = small_call(0, grad_mid, x_saved, h_small[0], down_pair, base, 0, None)
+                dw_2, dw_3, pre_1 = small_call(0, grad_mid, x_saved, h_small[0], down_pair, base, 0, None, None)
             else:
-                dw_2, dw_3, pre_2 = small_call(0, grad_mid, x_saved, h_small[1], down_pair, base, 0, None)
-                grad_x = finish_call(carry, (pre_1, pre_2), up_pair, small_start, (0, chunk), 0, None)
-                dw_2, dw_3, pre_2 = small_call(0, grad_mid, x_saved, h_small[2], down_pair, base, chunk, (dw_2, dw_3))
-            far = partial_sum(dw_2, dw_3, j >= 2)
+                dw_2, dw_3, grad_x = small_call(
+                    0, grad_mid, x_saved, h_small[1], down_pair, base, 0, None, (carry, pre_1, small_up))
+                dw_2, dw_3, pre_2 = small_call(0, grad_mid, x_saved, h_small[2], down_pair, base, EARLY, (dw_2, dw_3), None)
+            far = partial_sum(dw_2, dw_3)
             for u, (block, start, size) in enumerate(units):
                 if block == j:
                     part = to_model(far[start - base : start - base + size], 2)
@@ -446,8 +455,7 @@
         for u in range(3):
             bufs = place([pieces[u]], 0, units[u][1], bufs)
         for half in range(2):
-            low = chunk + half * chunk // 2
-            grad_x = finish_call(carry, (pre_1, pre_2), up_pair, small_start, (low, low + chunk // 2), chunk, grad_x)
+            grad_x = finish_call(carry, (pre_1, pre_2), small_up, half, grad_x)
         bufs = place(pieces[3:], 0, small_start, bufs)
         return grad_x, bufs[0], bufs[1]
 

time: 1660 us -> 1630 us (0.982)
  Pallas kernels: 596 us -> 620 us
  waiting for transfers between devices: 891 us -> 867 us
  other arithmetic: 54.1 us -> 31.7 us
    ppermute x15, waiting for transfers between devices: 126 us -> 86.7 us  [to_data(): return lax.ppermute(value, 'data', [(0, 1), (1, 0)])]
    pallas_call x5 -> x11, Pallas kernels: 50.9 us -> 87.8 us  [the longest x3 53.4 us: small_call(): pl.pallas_call(functools.partial(small_body, init is not None, finish is...]
  transfers between devices with their start and end apart: 50 -> 50, of which waited for: 14 -> 13; matrix products, arithmetic and copies ran while one was open for 5% -> 4% of each run, Pallas kernels for 36% -> 38%
where the time goes in v3:
time: 1630 us
  waiting for transfers between devices  867 us (53%)
  Pallas kernels  620 us (38%)
  local copies, waits for them, and re-layouts  66.8 us (4%)
  starting transfers between devices  41.4 us (3%)
  other arithmetic  31.7 us (2%)
    ppermute x35, waiting for transfers between devices, to_model(): return lax.ppermute(value, 'model', [(i, i ^ flip) for i in range(n_model)])  780 us
    pallas_call x4, Pallas kernels, block_call(): pl.pallas_call(functools.partial(block_body, carry is not None, final, ro...  439 us
    ppermute x15, waiting for transfers between devices, to_data(): return lax.ppermute(value, 'data', [(0, 1), (1, 0)])  86.7 us
    squeeze x8, local copies, waits for them, and re-layouts, h_from(): lax.dynamic_slice(held[0], (layer, 0, begin, start), (1, rows, seq, size))  61.1 us
    pallas_call x1, Pallas kernels, wide_call(): pl.pallas_call(functools.partial(wide_body, start), out_shape=[jax.ShapeD...  54.5 us
    pallas_call x3, Pallas kernels, small_call(): pl.pallas_call(functools.partial(small_body, init is not None, finish is...  53.4 us
  transfers between devices with their start and end apart: 50, of which 13 were waited for; matrix products, arithmetic and copies ran while one was open for 4% of the time, Pallas kernels for 38%

profile of v3, /device:TPU:0, one launch (start us, length us, event | category | flops | bytes accessed | tf_op | source)
XLA Modules:
  0.0 1627.7 jit_solution(17677287836286730497)
XLA Ops:
  0.6 2.8 select_bitcast_fusion.1
  3.4 10.6 dynamic-slice_bitcast_fusion.3
  14.0 10.6 dynamic-slice_bitcast_fusion.2
  24.6 7.5 dynamic-slice_bitcast_fusion.1
  33.0 2.6 collective-permute-start.1
  35.6 2.0 collective-permute-start.2
  37.8 564.0 %collective-permute-done.2 = bf16[768,768]{1,0:T(8,128)(2,1)S(1)} collective-permute-done((bf16[768,768]{1,0:T(8,128)(2,1)S(1)}, bf16[768,768]{1,0:T(8,128)(2,1)S(1)}, u32[]{:S(2)}, u32[]{:S(2)}) %collective-permute-start.2) | collective-permute-done | bytes 1179680 | tf_op jit(solution)/shard_map/ppermute | solution.py:361
  601.8 2.1 collective-permute-start.3
  603.9 22.9 %collective-permute-done.11 = bf16[768,768]{1,0:T(8,128)(2,1)S(1)} collective-permute-done((bf16[768,768]{1,0:T(8,128)(2,1)S(1)}, bf16[768,768]{1,0:T(8,128)(2,1)S(1)}, u32[]{:S(2)}, u32[]{:S(2)}) %collective-permute-start.11) | collective-permute-done | bytes 1179680 | tf_op jit(solution)/shard_map/ppermute | solution.py:361
  626.9 1.7 collective-permute-start.12
  629.4 25.3 %collective-permute-done.12 = bf16[768,768]{1,0:T(8,128)(2,1)S(1)} collective-permute-done((bf16[768,768]{1,0:T(8,128)(2,1)S(1)}, bf16[768,768]{1,0:T(8,128)(2,1)S(1)}, u32[]{:S(2)}, u32[]{:S(2)}) %collective-permute-start.12) | collective-permute-done | bytes 1179680 | tf_op jit(solution)/shard_map/ppermute | solution.py:364
  655.7 10.7 dynamic-slice_bitcast_fusion
  666.3 6.2 dynamic-slice_bitcast_fusion.5
  672.5 6.3 dynamic-slice_bitcast_fusion.4
  678.8 3.0 broadcast_select_fusion.2
  681.9 1.6 broadcast_select_fusion
  684.5 119.7 %shard_map.76 = (f32[16,512,768]{2,1,0:T(8,128)}, f32[2,768,768]{2,1,0:T(8,128)}, f32[2,768,768]{2,1,0:T(8,128)}) custom-call(s32[1]{0:T(128)} %bitcast._, bf16[16,512,768]{2,1,0:T(8,128)(2,1)} %refs_0_.3, bf16[2,16,512,768]{3,2,1,0:T(8,128)(2,1)} %x_ref.7, bf16[2,16,2048,768]{3,2,1,0:T(8,128)(2,1)} %hi_ref.3, ...), custom_call_target="tpu_custom_call" | custom-call | flops 77309411328 | bytes 50331648 | tf_op jit(solution)/shard_map/pallas_call | solution.py:112
  806.5 121.2 %shard_map.77 = (bf16[16,512,768]{2,1,0:T(8,128)(2,1)}, f32[2,768,768]{2,1,0:T(8,128)}, f32[2,768,768]{2,1,0:T(8,128)}) custom-call(s32[1]{0:T(128)} %bitcast._, bf16[16,512,768]{2,1,0:T(8,128)(2,1)} %refs_0_.3, bf16[2,16,512,768]{3,2,1,0:T(8,128)(2,1)} %x_ref.7, bf16[16,512,768]{2,1,0:T(8,128)(2,1)} %collective-permute-done.refs_2_, ...), custom_call_target="tpu_custom_call" | custom-call | flops 77309411328 | bytes 50331648 | tf_op jit(solution)/shard_map/pallas_call | solution.py:112
  928.1 119.5 %shard_map.78 = (f32[16,512,768]{2,1,0:T(8,128)}, f32[2,768,768]{2,1,0:T(8,128)}, f32[2,768,768]{2,1,0:T(8,128)}) custom-call(s32[1]{0:T(128)} %bitcast._, bf16[16,512,768]{2,1,0:T(8,128)(2,1)} %get-tuple-element.76.refs_0_.grad_ref, bf16[2,16,512,768]{3,2,1,0:T(8,128)(2,1)} %x_ref.7, bf16[2,16,2048,768]{3,2,1,0:T(8,128)(2,1)} %hi_ref.3, ...), custom_call_target="tpu_custom_call" | custom-call | flops 77309411328 | bytes 50331648 | tf_op jit(solution)/shard_map/pallas_call | solution.py:112
  1047.9 27.9 %collective-permute-done.16.refs_3_ = bf16[16,512,384]{2,1,0:T(8,128)(2,1)} collective-permute-done((bf16[16,512,384]{2,1,0:T(8,128)(2,1)}, bf16[16,512,384]{2,1,0:T(8,128)(2,1)}, u32[]{:S(2)}, u32[]{:S(2)}) %collective-permute-start.16) | collective-permute-done | bytes 6291488 | tf_op jit(solution)/shard_map/ppermute | solution.py:361
  1075.8 78.2 %shard_map.79 = (f32[16,512,768]{2,1,0:T(8,128)}, f32[2,384,768]{2,1,0:T(8,128)}, f32[2,384,768]{2,1,0:T(8,128)}) custom-call(s32[1]{0:T(128)} %bitcast._, bf16[16,512,768]{2,1,0:T(8,128)(2,1)} %get-tuple-element.76.refs_0_.grad_ref, bf16[2,16,512,768]{3,2,1,0:T(8,128)(2,1)} %x_ref.7, bf16[16,512,384]{2,1,0:T(8,128)(2,1)} %collective-permute-done.15.refs_2_, ...), custom_call_target="tpu_custom_call" | custom-call | flops 38654705664 | bytes 50331648 | tf_op jit(solution)/shard_map/pallas_call | solution.py:112
  1154.9 4.6 dynamic-slice_bitcast_fusion.7
  1159.4 4.6 dynamic-slice_bitcast_fusion.6
  1165.7 7.1 shard_map.95
  1172.8 1.3 collective-permute-start.47
  1174.1 6.3 shard_map.81
  1180.4 4.5 shard_map.93
  1184.9 1.5 collective-permute-start.22
  1186.4 7.0 shard_map.94
  1193.4 33.1 %collective-permute-done.47 = f32[768,768]{1,0:T(8,128)} collective-permute-done((f32[768,768]{1,0:T(8,128)}, f32[768,768]{1,0:T(8,128)}, u32[]{:S(2)}, u32[]{:S(2)}) %collective-permute-start.47) | collective-permute-done | bytes 2359328 | tf_op jit(solution)/shard_map/ppermute | solution.py:364
  1227.7 4.1 add.67
  1231.8 25.2 %collective-permute-done.10.h_b = bf16[16,512,256]{2,1,0:T(8,128)(2,1)} collective-permute-done((bf16[16,512,256]{2,1,0:T(8,128)(2,1)}, bf16[16,512,256]{2,1,0:T(8,128)(2,1)}, u32[]{:S(2)}, u32[]{:S(2)}) %collective-permute-start.10) | collective-permute-done | bytes 4194336 | tf_op jit(solution)/shard_map/ppermute | solution.py:361
  1258.3 89.0 %collective-permute-done.9.h_a = bf16[16,512,256]{2,1,0:T(8,128)(2,1)} collective-permute-done((bf16[16,512,256]{2,1,0:T(8,128)(2,1)}, bf16[16,512,256]{2,1,0:T(8,128)(2,1)}, u32[]{:S(2)}, u32[]{:S(2)}) %collective-permute-start.9) | collective-permute-done | bytes 4194336 | tf_op jit(solution)/shard_map/ppermute | solution.py:361
  1348.6 54.5 %shard_map.80 = (f32[16,512,768]{2,1,0:T(8,128)}, f32[2,256,768]{2,1,0:T(8,128)}, f32[2,256,768]{2,1,0:T(8,128)}) custom-call(bf16[16,512,768]{2,1,0:T(8,128)(2,1)} %get-tuple-element.76.refs_0_.grad_ref, bf16[2,16,512,768]{3,2,1,0:T(8,128)(2,1)} %x_ref.7, bf16[16,512,256]{2,1,0:T(8,128)(2,1)} %collective-permute-done.9.h_a, ...), custom_call_target="tpu_custom_call" | custom-call | flops 25769803776 | bytes 75497472 | tf_op jit(solution)/shard_map/pallas_call | solution.py:195
  1403.1 7.1 shard_map.89
  1410.2 1.5 collective-permute-start.25
  1411.7 6.3 shard_map.82
  1420.3 2.0 shard_map.84.refs_2_.up_ref
  1422.3 2.9 add.64
  1425.2 4.2 add_add_fusion.refs_0_
  1429.4 49.8 %collective-permute-done.23.h_b = bf16[5,512,128]{2,1,0:T(8,128)(2,1)S(1)} collective-permute-done((bf16[5,512,128]{2,1,0:T(8,128)(2,1)}, bf16[5,512,128]{2,1,0:T(8,128)(2,1)S(1)}, u32[]{:S(2)}, u32[]{:S(2)}) %collective-permute-start.23) | collective-permute-done | bytes 655392 | tf_op jit(solution)/shard_map/ppermute | solution.py:361
  1479.8 1.4 collective-permute-start.21
  1482.5 22.7 %shard_map.83 = (f32[2,64,768]{2,1,0:T(8,128)}, f32[2,64,768]{2,1,0:T(8,128)}, bf16[2,8,512,128]{3,2,1,0:T(8,128)(2,1)}) custom-call(bf16[16,512,768]{2,1,0:T(8,128)(2,1)} %get-tuple-element.76.refs_0_.grad_ref, bf16[2,16,512,768]{3,2,1,0:T(8,128)(2,1)} %x_ref.7, bf16[8,512,128]{2,1,0:T(8,128)(2,1)} %collective-permute-done.18.h_a, ...), custom_call_target="tpu_custom_call" | custom-call | flops 4831838208 | bytes 25165824 | tf_op jit(solution)/shard_map/pallas_call | solution.py:247
  1505.2 20.4 %shard_map.85 = (f32[2,64,768]{2,1,0:T(8,128)}, f32[2,64,768]{2,1,0:T(8,128)}, bf16[16,512,768]{2,1,0:T(8,128)(2,1)}) custom-call(bf16[16,512,768]{2,1,0:T(8,128)(2,1)} %get-tuple-element.76.refs_0_.grad_ref, bf16[2,16,512,768]{3,2,1,0:T(8,128)(2,1)} %x_ref.7, bf16[5,512,128]{2,1,0:T(8,128)(2,1)} %copy-done.11, bf16[5,512,128]{2,1,0:T(8,128)(2,1)} %copy-done.12, ...), custom_call_target="tpu_custom_call" | custom-call | flops 3019898880 | bytes 15728640 | tf_op jit(solution)/shard_map/pallas_call | solution.py:247
  1525.6 2.9 shard_map.92
  1528.5 1.3 collective-permute-start.35
  1529.8 10.3 shard_map.86
  1540.2 2.7 add.56
  1544.4 2.5 add.65.refs_0_
  1548.6 1.9 shard_map.91
  1553.0 1.5 add.61
  1555.4 1.5 collective-permute-start.38
  1556.9 1.9 shard_map.90
  1559.4 22.1 %collective-permute-done.30 = f32[64,768]{1,0:T(8,128)} collective-permute-done((f32[64,768]{1,0:T(8,128)}, f32[64,768]{1,0:T(8,128)}, u32[]{:S(2)}, u32[]{:S(2)}) %collective-permute-start.30) | collective-permute-done | bytes 196640 | tf_op jit(solution)/shard_map/ppermute | solution.py:364
  1583.3 4.3 collective-permute-done.27
  1587.5 1.5 collective-permute-start.31
  1596.0 1.6 add.60.refs_1_
  1600.3 5.4 shard_map.87._
  1605.7 5.4 shard_map.88
  1611.1 5.9 shard_map.96
  1617.0 3.8 shard_map.97
  1620.8 2.0 shard_map.98
  1622.8 2.0 shard_map.99
  1625.6 2.1 shard_map.100
  (121 shorter events, 36.7 us)
Async XLA Ops:
  24.6 11.0 copy-start.10
  24.6 13.0 copy-start
  24.6 13.0 copy-start.1
  32.1 651.9 %collective-permute-start.6 = (bf16[16,512,768]{2,1,0:T(8,128)(2,1)S(1)}, bf16[16,512,768]{2,1,0:T(8,128)(2,1)}, u32[]{:S(2)}, u32[]{:S(2)}) collective-permute-start(bf16[16,512,768]{2,1,0:T(8,128)(2,1)S(1)} %dynamic-slice_bitcast_fusion.1), channel_id=1, source_target_pairs={{0,1},{1,0},{2,3},{3,2},{4,5},{5,4},{6,7},{7,6}} | collective-permute-start | bytes 37748744 | tf_op jit(solution)/shard_map/ppermute | solution.py:361
  33.0 772.6 %collective-permute-start.1 = (bf16[16,512,768]{2,1,0:T(8,128)(2,1)}, bf16[16,512,768]{2,1,0:T(8,128)(2,1)}, u32[]{:S(2)}, u32[]{:S(2)}) collective-permute-start(bf16[16,512,768]{2,1,0:T(8,128)(2,1)} %dynamic-slice_bitcast_fusion.2), channel_id=1, source_target_pairs={{0,3},{1,2},{2,1},{3,0},{4,7},{5,6},{6,5},{7,4}} | collective-permute-start | bytes 37748744 | tf_op jit(solution)/shard_map/ppermute | solution.py:361
  35.6 770.9 %collective-permute-start = (bf16[16,512,768]{2,1,0:T(8,128)(2,1)}, bf16[16,512,768]{2,1,0:T(8,128)(2,1)}, u32[]{:S(2)}, u32[]{:S(2)}) collective-permute-start(bf16[16,512,768]{2,1,0:T(8,128)(2,1)} %dynamic-slice_bitcast_fusion.3), channel_id=1, source_target_pairs={{0,2},{1,3},{2,0},{3,1},{4,6},{5,7},{6,4},{7,5}} | collective-permute-start | bytes 37748744 | tf_op jit(solution)/shard_map/ppermute | solution.py:361
  35.6 566.2 %collective-permute-start.2 = (bf16[768,768]{1,0:T(8,128)(2,1)S(1)}, bf16[768,768]{1,0:T(8,128)(2,1)S(1)}, u32[]{:S(2)}, u32[]{:S(2)}) collective-permute-start(bf16[768,768]{1,0:T(8,128)(2,1)S(1)} %copy-done.10), channel_id=1, source_target_pairs={{0,2},{1,3},{2,0},{3,1},{4,6},{5,7},{6,4},{7,5}} | collective-permute-start | bytes 3538952 | tf_op jit(solution)/shard_map/ppermute | solution.py:361
  37.7 589.2 %collective-permute-start.11 = (bf16[768,768]{1,0:T(8,128)(2,1)S(1)}, bf16[768,768]{1,0:T(8,128)(2,1)S(1)}, u32[]{:S(2)}, u32[]{:S(2)}) collective-permute-start(bf16[768,768]{1,0:T(8,128)(2,1)S(1)} %select_bitcast_fusion), channel_id=1, source_target_pairs={{0,2},{1,3},{2,0},{3,1},{4,6},{5,7},{6,4},{7,5}} | collective-permute-start | bytes 3538952 | tf_op jit(solution)/shard_map/ppermute | solution.py:361
  601.8 27.5 %collective-permute-start.3 = (bf16[768,768]{1,0:T(8,128)(2,1)S(1)}, bf16[768,768]{1,0:T(8,128)(2,1)S(1)}, u32[]{:S(2)}, u32[]{:S(2)}) collective-permute-start(bf16[768,768]{1,0:T(8,128)(2,1)S(1)} %collective-permute-done.2), channel_id=1, source_target_pairs={{0,4},{4,0},{1,5},{5,1},{2,6},{6,2},{3,7},{7,3}} | collective-permute-start | bytes 3538952 | tf_op jit(solution)/shard_map/ppermute | solution.py:364
  626.9 2.5 copy-start.5
  626.9 27.8 %collective-permute-start.12 = (bf16[768,768]{1,0:T(8,128)(2,1)S(1)}, bf16[768,768]{1,0:T(8,128)(2,1)S(1)}, u32[]{:S(2)}, u32[]{:S(2)}) collective-permute-start(bf16[768,768]{1,0:T(8,128)(2,1)S(1)} %collective-permute-done.11), channel_id=1, source_target_pairs={{0,4},{4,0},{1,5},{5,1},{2,6},{6,2},{3,7},{7,3}} | collective-permute-start | bytes 3538952 | tf_op jit(solution)/shard_map/ppermute | solution.py:364
  629.4 25.3 %copy-start.7 = (bf16[768,768]{1,0:T(8,128)(2,1)}, bf16[768,768]{1,0:T(8,128)(2,1)S(1)}, u32[]{:S(2)}) copy-start(bf16[768,768]{1,0:T(8,128)(2,1)S(1)} %collective-permute-done.3) | copy-start | bytes 3538948
  629.4 54.1 %collective-permute-start.7 = (bf16[2,768,768]{2,1,0:T(8,128)(2,1)S(1)}, bf16[2,768,768]{2,1,0:T(8,128)(2,1)}, u32[]{:S(2)}, u32[]{:S(2)}) collective-permute-start(bf16[2,768,768]{2,1,0:T(8,128)(2,1)S(1)} %copy-done.1), channel_id=1, source_target_pairs={{0,1},{1,0},{2,3},{3,2},{4,5},{5,4},{6,7},{7,6}} | collective-permute-start | bytes 7077896 | tf_op jit(solution)/shard_map/ppermute | solution.py:361
  654.6 1.0 copy-start.8
  655.7 28.3 %collective-permute-start.8 = (bf16[2,768,768]{2,1,0:T(8,128)(2,1)S(1)}, bf16[2,768,768]{2,1,0:T(8,128)(2,1)}, u32[]{:S(2)}, u32[]{:S(2)}) collective-permute-start(bf16[2,768,768]{2,1,0:T(8,128)(2,1)S(1)} %copy-done), channel_id=1, source_target_pairs={{0,1},{1,0},{2,3},{3,2},{4,5},{5,4},{6,7},{7,6}} | collective-permute-start | bytes 7077896 | tf_op jit(solution)/shard_map/ppermute | solution.py:361
  678.8 3.0 copy-start.6
  678.8 3.0 copy-start.9
  683.5 244.2 %collective-permute-start.17 = (bf16[16,512,768]{2,1,0:T(8,128)(2,1)}, bf16[16,512,768]{2,1,0:T(8,128)(2,1)}, u32[]{:S(2)}, u32[]{:S(2)}) collective-permute-start(bf16[16,512,768]{2,1,0:T(8,128)(2,1)} %dynamic-slice_bitcast_fusion), channel_id=1, source_target_pairs={{0,1},{1,0},{2,3},{3,2},{4,5},{5,4},{6,7},{7,6}} | collective-permute-start | bytes 37748744 | tf_op jit(solution)/shard_map/ppermute | solution.py:361
  684.0 120.3 %collective-permute-start.4 = (bf16[768,768]{1,0:T(8,128)(2,1)}, bf16[768,768]{1,0:T(8,128)(2,1)}, u32[]{:S(2)}, u32[]{:S(2)}) collective-permute-start(bf16[768,768]{1,0:T(8,128)(2,1)} %get-tuple-element.148.refs_4_), channel_id=1, source_target_pairs={{0,1},{1,0},{2,3},{3,2},{4,5},{5,4},{6,7},{7,6}} | collective-permute-start | bytes 3538952 | tf_op jit(solution)/shard_map/ppermute | solution.py:361
  684.0 121.4 %collective-permute-start.5 = (bf16[768,768]{1,0:T(8,128)(2,1)}, bf16[768,768]{1,0:T(8,128)(2,1)}, u32[]{:S(2)}, u32[]{:S(2)}) collective-permute-start(bf16[768,768]{1,0:T(8,128)(2,1)} %get-tuple-element.147.refs_6_), channel_id=1, source_target_pairs={{0,1},{1,0},{2,3},{3,2},{4,5},{5,4},{6,7},{7,6}} | collective-permute-start | bytes 3538952 | tf_op jit(solution)/shard_map/ppermute | solution.py:361
  804.2 271.5 %collective-permute-start.15 = (bf16[16,512,384]{2,1,0:T(8,128)(2,1)}, bf16[16,512,384]{2,1,0:T(8,128)(2,1)}, u32[]{:S(2)}, u32[]{:S(2)}) collective-permute-start(bf16[16,512,384]{2,1,0:T(8,128)(2,1)} %dynamic-slice_bitcast_fusion.5), channel_id=1, source_target_pairs={{0,2},{1,3},{2,0},{3,1},{4,6},{5,7},{6,4},{7,5}} | collective-permute-start | bytes 18874376 | tf_op jit(solution)/shard_map/ppermute | solution.py:361
  805.4 270.3 %collective-permute-start.16 = (bf16[16,512,384]{2,1,0:T(8,128)(2,1)}, bf16[16,512,384]{2,1,0:T(8,128)(2,1)}, u32[]{:S(2)}, u32[]{:S(2)}) collective-permute-start(bf16[16,512,384]{2,1,0:T(8,128)(2,1)} %dynamic-slice_bitcast_fusion.4), channel_id=1, source_target_pairs={{0,3},{1,2},{2,1},{3,0},{4,7},{5,6},{6,5},{7,4}} | collective-permute-start | bytes 18874376 | tf_op jit(solution)/shard_map/ppermute | solution.py:361
  805.6 242.0 %collective-permute-start.13 = (bf16[768,768]{1,0:T(8,128)(2,1)}, bf16[768,768]{1,0:T(8,128)(2,1)}, u32[]{:S(2)}, u32[]{:S(2)}) collective-permute-start(bf16[768,768]{1,0:T(8,128)(2,1)} %get-tuple-element.146.refs_4_.up_a), channel_id=1, source_target_pairs={{0,1},{1,0},{2,3},{3,2},{4,5},{5,4},{6,7},{7,6}} | collective-permute-start | bytes 3538952 | tf_op jit(solution)/shard_map/ppermute | solution.py:361
  806.4 241.5 %collective-permute-start.14 = (bf16[768,768]{1,0:T(8,128)(2,1)}, bf16[768,768]{1,0:T(8,128)(2,1)}, u32[]{:S(2)}, u32[]{:S(2)}) collective-permute-start(bf16[768,768]{1,0:T(8,128)(2,1)} %get-tuple-element.145.refs_6_.down_a), channel_id=1, source_target_pairs={{0,1},{1,0},{2,3},{3,2},{4,5},{5,4},{6,7},{7,6}} | collective-permute-start | bytes 3538952 | tf_op jit(solution)/shard_map/ppermute | solution.py:361
  927.6 238.1 %collective-permute-start.46 = (f32[2,768,768]{2,1,0:T(8,128)}, f32[2,768,768]{2,1,0:T(8,128)}, u32[]{:S(2)}, u32[]{:S(2)}) collective-permute-start(f32[2,768,768]{2,1,0:T(8,128)} %get-tuple-element.128), channel_id=1, source_target_pairs={{0,1},{1,0},{2,3},{3,2},{4,5},{5,4},{6,7},{7,6}} | collective-permute-start | bytes 14155784 | tf_op jit(solution)/shard_map/ppermute | solution.py:361
  1047.6 137.3 %collective-permute-start.44 = (f32[2,768,768]{2,1,0:T(8,128)}, f32[2,768,768]{2,1,0:T(8,128)}, u32[]{:S(2)}, u32[]{:S(2)}) collective-permute-start(f32[2,768,768]{2,1,0:T(8,128)} %get-tuple-element.124), channel_id=1, source_target_pairs={{0,1},{1,0},{2,3},{3,2},{4,5},{5,4},{6,7},{7,6}} | collective-permute-start | bytes 14155784 | tf_op jit(solution)/shard_map/ppermute | solution.py:361
  1154.0 20.1 %collective-permute-start.40 = (f32[2,384,768]{2,1,0:T(8,128)}, f32[2,384,768]{2,1,0:T(8,128)}, u32[]{:S(2)}, u32[]{:S(2)}) collective-permute-start(f32[2,384,768]{2,1,0:T(8,128)} %get-tuple-element.120), channel_id=1, source_target_pairs={{0,1},{1,0},{2,3},{3,2},{4,5},{5,4},{6,7},{7,6}} | collective-permute-start | bytes 7077896 | tf_op jit(solution)/shard_map/ppermute | solution.py:361
  1164.1 93.0 %collective-permute-start.10 = (bf16[16,512,256]{2,1,0:T(8,128)(2,1)}, bf16[16,512,256]{2,1,0:T(8,128)(2,1)}, u32[]{:S(2)}, u32[]{:S(2)}) collective-permute-start(bf16[16,512,256]{2,1,0:T(8,128)(2,1)} %dynamic-slice_bitcast_fusion.6), channel_id=1, source_target_pairs={{0,3},{1,2},{2,1},{3,0},{4,7},{5,6},{6,5},{7,4}} | collective-permute-start | bytes 12582920 | tf_op jit(solution)/shard_map/ppermute | solution.py:361
  1164.9 182.4 %collective-permute-start.9 = (bf16[16,512,256]{2,1,0:T(8,128)(2,1)}, bf16[16,512,256]{2,1,0:T(8,128)(2,1)}, u32[]{:S(2)}, u32[]{:S(2)}) collective-permute-start(bf16[16,512,256]{2,1,0:T(8,128)(2,1)} %dynamic-slice_bitcast_fusion.7), channel_id=1, source_target_pairs={{0,2},{1,3},{2,0},{3,1},{4,6},{5,7},{6,4},{7,5}} | collective-permute-start | bytes 12582920 | tf_op jit(solution)/shard_map/ppermute | solution.py:361
  1172.8 53.7 %collective-permute-start.47 = (f32[768,768]{1,0:T(8,128)}, f32[768,768]{1,0:T(8,128)}, u32[]{:S(2)}, u32[]{:S(2)}) collective-permute-start(f32[768,768]{1,0:T(8,128)} %get-tuple-element.130), channel_id=1, source_target_pairs={{0,4},{4,0},{1,5},{5,1},{2,6},{6,2},{3,7},{7,3}} | collective-permute-start | bytes 7077896 | tf_op jit(solution)/shard_map/ppermute | solution.py:364
  1174.1 229.0 %collective-permute-start.24 = (f32[2,768,768]{2,1,0:T(8,128)}, f32[2,768,768]{2,1,0:T(8,128)}, u32[]{:S(2)}, u32[]{:S(2)}) collective-permute-start(f32[2,768,768]{2,1,0:T(8,128)} %get-tuple-element.99), channel_id=1, source_target_pairs={{0,1},{1,0},{2,3},{3,2},{4,5},{5,4},{6,7},{7,6}} | collective-permute-start | bytes 14155784 | tf_op jit(solution)/shard_map/ppermute | solution.py:361
  1184.9 225.3 %collective-permute-start.22 = (bf16[5,512,128]{2,1,0:T(8,128)(2,1)}, bf16[5,512,128]{2,1,0:T(8,128)(2,1)S(1)}, u32[]{:S(2)}, u32[]{:S(2)}) collective-permute-start(bf16[5,512,128]{2,1,0:T(8,128)(2,1)} %get-tuple-element.92), channel_id=1, source_target_pairs={{0,2},{1,3},{2,0},{3,1},{4,6},{5,7},{6,4},{7,5}} | collective-permute-start | bytes 1966088 | tf_op jit(solution)/shard_map/ppermute | solution.py:361
  1226.5 191.5 %collective-permute-start.41 = (f32[384,768]{1,0:T(8,128)}, f32[384,768]{1,0:T(8,128)}, u32[]{:S(2)}, u32[]{:S(2)}) collective-permute-start(f32[384,768]{1,0:T(8,128)} %get-tuple-element.122), channel_id=1, source_target_pairs={{0,4},{4,0},{1,5},{5,1},{2,6},{6,2},{3,7},{7,3}} | collective-permute-start | bytes 3538952 | tf_op jit(solution)/shard_map/ppermute | solution.py:364
  1257.0 161.5 %collective-permute-start.45 = (f32[768,768]{1,0:T(8,128)}, f32[768,768]{1,0:T(8,128)}, u32[]{:S(2)}, u32[]{:S(2)}) collective-permute-start(f32[768,768]{1,0:T(8,128)} %get-tuple-element.126), channel_id=1, source_target_pairs={{0,4},{4,0},{1,5},{5,1},{2,6},{6,2},{3,7},{7,3}} | collective-permute-start | bytes 7077896 | tf_op jit(solution)/shard_map/ppermute | solution.py:364
  1347.3 72.2 %collective-permute-start.48 = (f32[768,768]{1,0:T(8,128)}, f32[768,768]{1,0:T(8,128)}, u32[]{:S(2)}, u32[]{:S(2)}) collective-permute-start(f32[768,768]{1,0:T(8,128)} %add.67), channel_id=1, source_target_pairs={{0,2},{1,3},{2,0},{3,1},{4,6},{5,7},{6,4},{7,5}} | collective-permute-start | bytes 7077896 | tf_op jit(solution)/shard_map/ppermute | solution.py:361
  1403.1 78.7 %collective-permute-start.34 = (f32[2,256,768]{2,1,0:T(8,128)}, f32[2,256,768]{2,1,0:T(8,128)}, u32[]{:S(2)}, u32[]{:S(2)}) collective-permute-start(f32[2,256,768]{2,1,0:T(8,128)} %get-tuple-element.114), channel_id=1, source_target_pairs={{0,1},{1,0},{2,3},{3,2},{4,5},{5,4},{6,7},{7,6}} | collective-permute-start | bytes 4718600 | tf_op jit(solution)/shard_map/ppermute | solution.py:361
  1410.2 7.8 copy-start.11
  1410.2 130.0 %collective-permute-start.25 = (f32[768,768]{1,0:T(8,128)}, f32[768,768]{1,0:T(8,128)}, u32[]{:S(2)}, u32[]{:S(2)}) collective-permute-start(f32[768,768]{1,0:T(8,128)} %get-tuple-element.101), channel_id=1, source_target_pairs={{0,4},{4,0},{1,5},{5,1},{2,6},{6,2},{3,7},{7,3}} | collective-permute-start | bytes 7077896 | tf_op jit(solution)/shard_map/ppermute | solution.py:364
  1418.0 61.8 %collective-permute-start.18 = (bf16[8,512,128]{2,1,0:T(8,128)(2,1)}, bf16[8,512,128]{2,1,0:T(8,128)(2,1)}, u32[]{:S(2)}, u32[]{:S(2)}) collective-permute-start(bf16[8,512,128]{2,1,0:T(8,128)(2,1)} %get-tuple-element.87), channel_id=1, source_target_pairs={{0,2},{1,3},{2,0},{3,1},{4,6},{5,7},{6,4},{7,5}} | collective-permute-start | bytes 3145736 | tf_op jit(solution)/shard_map/ppermute | solution.py:361
  1418.6 62.6 %collective-permute-start.19 = (bf16[8,512,128]{2,1,0:T(8,128)(2,1)}, bf16[8,512,128]{2,1,0:T(8,128)(2,1)}, u32[]{:S(2)}, u32[]{:S(2)}) collective-permute-start(bf16[8,512,128]{2,1,0:T(8,128)(2,1)} %get-tuple-element.88), channel_id=1, source_target_pairs={{0,3},{1,2},{2,1},{3,0},{4,7},{5,6},{6,5},{7,4}} | collective-permute-start | bytes 3145736 | tf_op jit(solution)/shard_map/ppermute | solution.py:361
  1419.6 59.7 %collective-permute-start.23 = (bf16[5,512,128]{2,1,0:T(8,128)(2,1)}, bf16[5,512,128]{2,1,0:T(8,128)(2,1)S(1)}, u32[]{:S(2)}, u32[]{:S(2)}) collective-permute-start(bf16[5,512,128]{2,1,0:T(8,128)(2,1)} %get-tuple-element.93), channel_id=1, source_target_pairs={{0,3},{1,2},{2,1},{3,0},{4,7},{5,6},{6,5},{7,4}} | collective-permute-start | bytes 1966088 | tf_op jit(solution)/shard_map/ppermute | solution.py:361
  1422.3 2.9 copy-start.2
  1479.2 26.0 %copy-start.12 = (bf16[5,512,128]{2,1,0:T(8,128)(2,1)}, bf16[5,512,128]{2,1,0:T(8,128)(2,1)S(1)}, u32[]{:S(2)}) copy-start(bf16[5,512,128]{2,1,0:T(8,128)(2,1)S(1)} %collective-permute-done.23.h_b) | copy-start | bytes 1966084
  1479.2 49.3 %collective-permute-start.20 = (bf16[3,512,128]{2,1,0:T(8,128)(2,1)}, bf16[3,512,128]{2,1,0:T(8,128)(2,1)}, u32[]{:S(2)}, u32[]{:S(2)}) collective-permute-start(bf16[3,512,128]{2,1,0:T(8,128)(2,1)} %get-tuple-element.90), channel_id=1, source_target_pairs={{0,2},{1,3},{2,0},{3,1},{4,6},{5,7},{6,4},{7,5}} | collective-permute-start | bytes 1179656 | tf_op jit(solution)/shard_map/ppermute | solution.py:361
  1479.8 50.0 %collective-permute-start.21 = (bf16[3,512,128]{2,1,0:T(8,128)(2,1)}, bf16[3,512,128]{2,1,0:T(8,128)(2,1)}, u32[]{:S(2)}, u32[]{:S(2)}) collective-permute-start(bf16[3,512,128]{2,1,0:T(8,128)(2,1)} %get-tuple-element.91), channel_id=1, source_target_pairs={{0,3},{1,2},{2,1},{3,0},{4,7},{5,6},{6,5},{7,4}} | collective-permute-start | bytes 1179656 | tf_op jit(solution)/shard_map/ppermute | solution.py:361
  1481.2 63.2 %collective-permute-start.42 = (f32[384,768]{1,0:T(8,128)}, f32[384,768]{1,0:T(8,128)}, u32[]{:S(2)}, u32[]{:S(2)}) collective-permute-start(f32[384,768]{1,0:T(8,128)} %add.64), channel_id=1, source_target_pairs={{0,2},{1,3},{2,0},{3,1},{4,6},{5,7},{6,4},{7,5}} | collective-permute-start | bytes 3538952 | tf_op jit(solution)/shard_map/ppermute | solution.py:361
  1481.7 117.8 %collective-permute-start.49 = (f32[768,768]{1,0:T(8,128)}, f32[768,768]{1,0:T(8,128)}, u32[]{:S(2)}, u32[]{:S(2)}) collective-permute-start(f32[768,768]{1,0:T(8,128)} %add_add_fusion.refs_0_), channel_id=1, source_target_pairs={{0,4},{4,0},{1,5},{5,1},{2,6},{6,2},{3,7},{7,3}} | collective-permute-start | bytes 7077896 | tf_op jit(solution)/shard_map/ppermute | solution.py:364
  1528.5 24.5 %collective-permute-start.35 = (f32[256,768]{1,0:T(8,128)}, f32[256,768]{1,0:T(8,128)}, u32[]{:S(2)}, u32[]{:S(2)}) collective-permute-start(f32[256,768]{1,0:T(8,128)} %get-tuple-element.116), channel_id=1, source_target_pairs={{0,4},{4,0},{1,5},{5,1},{2,6},{6,2},{3,7},{7,3}} | collective-permute-start | bytes 2359304 | tf_op jit(solution)/shard_map/ppermute | solution.py:364
  1540.1 7.7 collective-permute-start.29
  1546.9 70.1 %collective-permute-start.43 = (f32[384,768]{1,0:T(8,128)}, f32[384,768]{1,0:T(8,128)}, u32[]{:S(2)}, u32[]{:S(2)}) collective-permute-start(f32[384,768]{1,0:T(8,128)} %add.65.refs_0_), channel_id=1, source_target_pairs={{0,4},{4,0},{1,5},{5,1},{2,6},{6,2},{3,7},{7,3}} | collective-permute-start | bytes 3538952 | tf_op jit(solution)/shard_map/ppermute | solution.py:364
  1547.6 9.3 collective-permute-start.26
  1550.5 30.9 %collective-permute-start.30 = (f32[64,768]{1,0:T(8,128)}, f32[64,768]{1,0:T(8,128)}, u32[]{:S(2)}, u32[]{:S(2)}) collective-permute-start(f32[64,768]{1,0:T(8,128)} %get-tuple-element.111), channel_id=1, source_target_pairs={{0,4},{4,0},{1,5},{5,1},{2,6},{6,2},{3,7},{7,3}} | collective-permute-start | bytes 589832 | tf_op jit(solution)/shard_map/ppermute | solution.py:364
  1555.4 34.6 %collective-permute-start.38 = (f32[128,768]{1,0:T(8,128)}, f32[128,768]{1,0:T(8,128)S(1)}, u32[]{:S(2)}, u32[]{:S(2)}) collective-permute-start(f32[128,768]{1,0:T(8,128)} %get-tuple-element.149), channel_id=1, source_target_pairs={{0,2},{1,3},{2,0},{3,1},{4,6},{5,7},{6,4},{7,5}} | collective-permute-start | bytes 1179656 | tf_op jit(solution)/shard_map/ppermute | solution.py:361
  1558.8 33.5 %collective-permute-start.36 = (f32[128,768]{1,0:T(8,128)}, f32[128,768]{1,0:T(8,128)S(1)}, u32[]{:S(2)}, u32[]{:S(2)}) collective-permute-start(f32[128,768]{1,0:T(8,128)} %get-tuple-element.150), channel_id=1, source_target_pairs={{0,2},{1,3},{2,0},{3,1},{4,6},{5,7},{6,4},{7,5}} | collective-permute-start | bytes 1179656 | tf_op jit(solution)/shard_map/ppermute | solution.py:361
  1581.5 6.1 collective-permute-start.27
  1587.5 7.6 collective-permute-start.31
  1590.0 0.7 copy-start.13
  1590.7 6.8 collective-permute-start.28
  1592.3 13.4 copy-start.3
  1592.3 28.5 %collective-permute-start.39 = (f32[128,768]{1,0:T(8,128)S(1)}, f32[128,768]{1,0:T(8,128)}, u32[]{:S(2)}, u32[]{:S(2)}) collective-permute-start(f32[128,768]{1,0:T(8,128)S(1)} %add.63.refs_0_), channel_id=1, source_target_pairs={{0,4},{4,0},{1,5},{5,1},{2,6},{6,2},{3,7},{7,3}} | collective-permute-start | bytes 1179656 | tf_op jit(solution)/shard_map/ppermute | solution.py:364
  1594.2 11.5 copy-start.4
  1595.1 27.7 %collective-permute-start.37 = (f32[128,768]{1,0:T(8,128)S(1)}, f32[128,768]{1,0:T(8,128)}, u32[]{:S(2)}, u32[]{:S(2)}) collective-permute-start(f32[128,768]{1,0:T(8,128)S(1)} %add.62.refs_0_), channel_id=1, source_target_pairs={{0,4},{4,0},{1,5},{5,1},{2,6},{6,2},{3,7},{7,3}} | collective-permute-start | bytes 1179656 | tf_op jit(solution)/shard_map/ppermute | solution.py:364
  1597.6 27.3 %collective-permute-start.33 = (f32[64,768]{1,0:T(8,128)}, f32[64,768]{1,0:T(8,128)}, u32[]{:S(2)}, u32[]{:S(2)}) collective-permute-start(f32[64,768]{1,0:T(8,128)} %add.60.refs_1_), channel_id=1, source_target_pairs={{0,4},{4,0},{1,5},{5,1},{2,6},{6,2},{3,7},{7,3}} | collective-permute-start | bytes 589832 | tf_op jit(solution)/shard_map/ppermute | solution.py:364
  1599.5 25.4 %collective-permute-start.32 = (f32[64,768]{1,0:T(8,128)}, f32[64,768]{1,0:T(8,128)S(1)}, u32[]{:S(2)}, u32[]{:S(2)}) collective-permute-start(f32[64,768]{1,0:T(8,128)} %add.58.refs_0_), channel_id=1, source_target_pairs={{0,4},{4,0},{1,5},{5,1},{2,6},{6,2},{3,7},{7,3}} | collective-permute-start | bytes 589832 | tf_op jit(solution)/shard_map/ppermute | solution.py:364
  (2 other events, 1.4 us)

commit v4 on v3

--- a/solution.py
+++ b/solution.py
@@ -209,49 +209,54 @@
     refs = list(refs)
     carry_ref, early_ref, up_ref = (refs.pop(0) for _ in range(3)) if finish else (None,) * 3
     dw_pair, out_ref = refs[-3:-1], refs[-1]
-    second = pl.program_id(1)
-
-    @pl.when((pl.program_id(0) == 0) & (second == 0))
+
+    @pl.when(pl.program_id(0) == 0)
     def _():
         for i, dw in enumerate(dw_pair):
             dw[...] = refs[i][...] if has_init else jnp.zeros_like(dw)
 
     h_pair = swap_lanes(h_a[0].astype(F32), h_b[0].astype(F32))
-    grad, x = grad_ref[0], x_ref[0, 0]
-    pre, act = unit_grads(grad, jnp.where(second == 0, *h_pair), jnp.concatenate([down_a[...], down_b[...]]))
-    for kind, part in enumerate((dot(pre, x, 0, 0), dot(act, grad, 0, 0))):
-        dw_pair[0][kind] += part[:SMALL]
-        dw_pair[1][kind] += part[SMALL:]
+    down = jnp.concatenate([down_a[...], down_b[...]])
+    for r, h in enumerate(h_pair):
+        grad, x = grad_ref[r, 0], x_ref[0, r, 0]
+        pre, act = unit_grads(grad, h, down)
+        for kind, part in enumerate((dot(pre, x, 0, 0), dot(act, grad, 0, 0))):
+            dw_pair[0][kind] += part[:SMALL]
+            dw_pair[1][kind] += part[SMALL:]
+        if finish:
+            total = carry_ref[r, 0] + dot(jnp.concatenate([early_ref[r, 0], pre], axis=1), up_ref[...], 1, 1)
+            out_ref[r, 0] = total.astype(BF16)
+        else:
+            out_ref[r, 0] = pre
+
+
+def paired(value, axis=0):
+    shape = value.shape
+    return value.reshape(shape[:axis] + (2, shape[axis] // 2) + shape[axis + 1 :])
+
+
+def small_call(layer, grad, x_saved, h_pair, down_pair, start, first_pair, init, finish):
+    _, _, seq, hidden = grad.shape
+    pairs = h_pair[0].shape[0]
+    row_spec = pl.BlockSpec((2, 1, seq, hidden), lambda b: (0, b + first_pair, 0, 0))
+    pre_spec = pl.BlockSpec((2, 1, seq, LANES), lambda b: (0, b, 0, 0))
+    h_spec = pl.BlockSpec((1, seq, LANES), lambda b: (b, 0, 0))
+    down_spec = pl.BlockSpec((SMALL, hidden), lambda b: (start // SMALL, 0))
+    dw_shape = (2, SMALL, hidden)
+    dw_spec = pl.BlockSpec(dw_shape, lambda b: (0, 0, 0))
+    in_specs = [row_spec, pl.BlockSpec((1, 2, 1, seq, hidden), lambda b: (layer, 0, b + first_pair, 0, 0)), h_spec, h_spec, down_spec, down_spec]
     if finish:
-        total = carry_ref[0] + dot(jnp.concatenate([early_ref[0, 0], pre], axis=1), up_ref[...], 1, 1)
-        out_ref[0] = total.astype(BF16)
-    else:
-        out_ref[0, 0] = pre
-
-
-def small_call(layer, grad, x_saved, h_pair, down_pair, start, first_pair, init, finish):
-    rows, seq, hidden = grad.shape
-    pairs = h_pair[0].shape[0]
-    half = rows // 2
-    row_spec = pl.BlockSpec((1, seq, hidden), lambda b, r: (b + first_pair + r * half, 0, 0))
-    pre_spec = pl.BlockSpec((1, 1, seq, LANES), lambda b, r: (r, b, 0, 0))
-    h_spec = pl.BlockSpec((1, seq, LANES), lambda b, r: (b, 0, 0))
-    down_spec = pl.BlockSpec((SMALL, hidden), lambda b, r: (start // SMALL, 0))
-    dw_shape = (2, SMALL, hidden)
-    dw_spec = pl.BlockSpec(dw_shape, lambda b, r: (0, 0, 0))
-    in_specs = [row_spec, pl.BlockSpec((1, 1, seq, hidden), lambda b, r: (layer, b + first_pair + r * half, 0, 0)), h_spec, h_spec, down_spec, down_spec]
-    if finish:
-        in_specs += [row_spec, pre_spec, pl.BlockSpec(finish[2].shape, lambda b, r: (0, 0))]
+        in_specs += [row_spec, pre_spec, pl.BlockSpec(finish[2].shape, lambda b: (0, 0))]
     if init:
         in_specs += [dw_spec] * 2
     return pl.pallas_call(
         functools.partial(small_body, init is not None, finish is not None),
         out_shape=[jax.ShapeDtypeStruct(dw_shape, F32)] * 2
         + [jax.ShapeDtypeStruct(grad.shape if finish else (2, pairs, seq, LANES), BF16)],
-        grid=(pairs, 2),
+        grid=(pairs,),
         in_specs=in_specs,
         out_specs=[dw_spec, dw_spec, row_spec if finish else pre_spec],
-        compiler_params=pltpu.CompilerParams(dimension_semantics=("arbitrary", "arbitrary"), vmem_limit_bytes=ALL_VMEM),
+        compiler_params=pltpu.CompilerParams(dimension_semantics=("arbitrary",), vmem_limit_bytes=ALL_VMEM),
         cost_estimate=pl.CostEstimate(
             flops=24 * pairs * seq * hidden * SMALL, bytes_accessed=8 * pairs * seq * hidden, transcendentals=4 * pairs * seq * SMALL),
     )(grad, x_saved, *h_pair, *down_pair, *(finish or ()), *(init or ()))
@@ -277,14 +282,14 @@
 
 
 def finish_body(carry_ref, pre_a, pre_b, up_ref, _, out_ref):
-    total = carry_ref[0] + dot(jnp.concatenate([pre_a[0, 0], pre_b[0, 0]], axis=1), up_ref[...], 1, 1)
-    out_ref[0] = total.astype(BF16)
+    total = carry_ref[0, 0] + dot(jnp.concatenate([pre_a[0, 0], pre_b[0, 0]], axis=1), up_ref[...], 1, 1)
+    out_ref[0, 0] = total.astype(BF16)
 
 
 def finish_call(carry, pre_pair, ups, half, out):
-    rows, seq, hidden = carry.shape
-    count = rows // 2 - EARLY
-    row_spec = pl.BlockSpec((1, seq, hidden), lambda b: (b + EARLY + half * rows // 2, 0, 0))
+    _, pairs, seq, hidden = carry.shape
+    count = pairs - EARLY
+    row_spec = pl.BlockSpec((1, 1, seq, hidden), lambda b: (half, b + EARLY, 0, 0))
     pre_specs = [pl.BlockSpec((1, 1, seq, LANES), lambda b, first=first: (half, b + first, 0, 0)) for first in (EARLY, 0)]
     return pl.pallas_call(
         finish_body,
@@ -330,22 +335,23 @@
 
 
 def place_call(first, kept, other, layer, start, layers, width, bufs):
-    size, hidden = kept[0].shape
-    step = min(size, LANES)
-    row_spec = pl.BlockSpec((step, hidden), lambda i, first: (i, 0))
+    hidden = kept[0].shape[1]
+    size = sum(k.shape[0] for k in kept)
+    step = LANES if len(kept) == 1 else size
     out_shape = [jax.ShapeDtypeStruct((layers, hidden, width), F32), jax.ShapeDtypeStruct((layers, width, hidden), F32)]
     any_spec = pl.BlockSpec(memory_space=pl.ANY)
     count = 2 * len(kept)
+    piece_specs = [pl.BlockSpec((min(k.shape[0], step) if len(kept) == 1 else k.shape[0], hidden), lambda i, first: (i, 0)) for k in kept]
     return pl.pallas_call(
         functools.partial(place_body, len(kept)),
         out_shape=out_shape,
         grid_spec=pltpu.PrefetchScalarGridSpec(
             num_scalar_prefetch=1,
             grid=(size // step,),
-            in_specs=[row_spec] * count + ([any_spec, any_spec] if bufs is not None else []),
+            in_specs=piece_specs * 2 + ([any_spec, any_spec] if bufs is not None else []),
             out_specs=[
-                pl.BlockSpec((1, hidden, LANES), lambda i, first: (layer, 0, start // LANES + i)),
-                pl.BlockSpec((1, LANES, hidden), lambda i, first: (layer, start // LANES + i, 0)),
+                pl.BlockSpec((1, hidden, step), lambda i, first: (layer, 0, start // step + i)),
+                pl.BlockSpec((1, step, hidden), lambda i, first: (layer, start // step + i, 0)),
             ],
         ),
         input_output_aliases={1 + count: 0, 2 + count: 1} if bufs is not None else {},
@@ -429,34 +435,36 @@
 
         carry, dw_0, dw_1 = call(0, grad_mid, [h_saved, h_near[0]], (0, 1), None, False)
         near = partial_sum(dw_0, dw_1)
-        units = [(0, 0, 384), (1, 384, 128), (1, 512, 128), (2, small_start, SMALL), (3, small_start + SMALL, SMALL)]
-        near_part = lax.optimization_barrier(tuple(near[start : start + size] for _, start, size in units))
+        bounds = [0, 384, 512, width - SMALL, width]
+        near_part = lax.optimization_barrier(tuple(near[a:b] for a, b in zip(bounds, bounds[1:])))
+        pieces = []
+
+        def exchange(unit, far):
+            part = to_model(far, 2)
+            kept = near_part[unit] + part
+            pieces.append((kept, to_data(kept)))
+
         down_pair, up_pair = [down[0][f] for f in (2, 3)], [up[0][f] for f in (2, 3)]
         small_up = join_call(up_pair, small_start)
-        pieces = []
-        for j in range(4):
-            base = sum(BLOCKS[:j]) if j < 2 else small_start + (j - 2) * SMALL
-            if j == 0:
-                carry, dw_2, dw_3 = call(0, grad_mid, h_zero[j], (2, 3), carry, False, base, BLOCKS[j])
-            elif j == 1:
-                carry, dw_2, dw_3 = wide_call(0, grad_mid, x_saved, h_zero[j], up_pair, down_pair, base, carry)
-            elif j == 2:
-                dw_2, dw_3, pre_1 = small_call(0, grad_mid, x_saved, h_small[0], down_pair, base, 0, None, None)
-            else:
-                dw_2, dw_3, grad_x = small_call(
-                    0, grad_mid, x_saved, h_small[1], down_pair, base, 0, None, (carry, pre_1, small_up))
-                dw_2, dw_3, pre_2 = small_call(0, grad_mid, x_saved, h_small[2], down_pair, base, EARLY, (dw_2, dw_3), None)
-            far = partial_sum(dw_2, dw_3)
-            for u, (block, start, size) in enumerate(units):
-                if block == j:
-                    part = to_model(far[start - base : start - base + size], 2)
-                    kept = near_part[u] + part
-                    pieces.append((kept, to_data(kept)))
-        for u in range(3):
-            bufs = place([pieces[u]], 0, units[u][1], bufs)
+        carry, dw_2, dw_3 = call(0, grad_mid, h_zero[0], (2, 3), carry, False, 0, BLOCKS[0])
+        exchange(0, partial_sum(dw_2, dw_3))
+        carry, dw_2, dw_3 = wide_call(0, grad_mid, x_saved, h_zero[1], up_pair, down_pair, BLOCKS[0], carry)
+        far = partial_sum(dw_2, dw_3)
+        exchange(1, far[: bounds[2] - bounds[1]])
+        carry, grad_mid, x_saved = paired(carry), paired(grad_mid), paired(x_saved, 1)
+        dw_2, dw_3, pre_1 = small_call(0, grad_mid, x_saved, h_small[0], down_pair, small_start, 0, None, None)
+        exchange(2, jnp.concatenate([far[bounds[2] - bounds[1] :], partial_sum(dw_2, dw_3)]))
+        dw_2, dw_3, grad_x = small_call(
+            0, grad_mid, x_saved, h_small[1], down_pair, small_start + SMALL, 0, None, (carry, pre_1, small_up))
+        dw_2, dw_3, pre_2 = small_call(
+            0, grad_mid, x_saved, h_small[2], down_pair, small_start + SMALL, EARLY, (dw_2, dw_3), None)
+        exchange(3, partial_sum(dw_2, dw_3))
         for half in range(2):
             grad_x = finish_call(carry, (pre_1, pre_2), small_up, half, grad_x)
-        bufs = place(pieces[3:], 0, small_start, bufs)
+        for unit in range(2):
+            bufs = place([pieces[unit]], 0, bounds[unit], bufs)
+        bufs = place(pieces[2:], 0, bounds[2], bufs)
+        grad_x = grad_x.reshape(grad_out.shape)
         return grad_x, bufs[0], bufs[1]
 
     return jax.shard_map(

time: 1630 us -> 1650 us (1.012)
  waiting for transfers between devices: 867 us -> 897 us
    ppermute x15 -> x14, waiting for transfers between devices: 86.7 us -> 120 us  [to_data(): return lax.ppermute(value, 'data', [(0, 1), (1, 0)])]
    ppermute x35 -> x34, waiting for transfers between devices: 780 us -> 777 us  [to_model(): return lax.ppermute(value, 'model', [(i, i ^ flip) for i in range(n_model)])]
  transfers between devices with their start and end apart: 50 -> 48, of which waited for: 13 -> 12; matrix products, arithmetic and copies ran while one was open for 4% -> 4% of each run, Pallas kernels for 38% -> 37%
where the time goes in v4:
time: 1650 us
  waiting for transfers between devices  897 us (54%)
  Pallas kernels  609 us (37%)
  local copies, waits for them, and re-layouts  69.9 us (4%)
  starting transfers between devices  40.2 us (2%)
  other arithmetic  30.1 us (2%)
    ppermute x34, waiting for transfers between devices, to_model(): return lax.ppermute(value, 'model', [(i, i ^ flip) for i in range(n_model)])  777 us
    pallas_call x4, Pallas kernels, block_call(): pl.pallas_call(functools.partial(block_body, carry is not None, final, ro...  438 us
    ppermute x14, waiting for transfers between devices, to_data(): return lax.ppermute(value, 'data', [(0, 1), (1, 0)])  120 us
    squeeze x8, local copies, waits for them, and re-layouts, h_from(): lax.dynamic_slice(held[0], (layer, 0, begin, start), (1, rows, seq, size))  64.3 us
    pallas_call x1, Pallas kernels, wide_call(): pl.pallas_call(functools.partial(wide_body, start), out_shape=[jax.ShapeD...  54.4 us
    pallas_call x3, Pallas kernels, small_call(): pl.pallas_call(functools.partial(small_body, init is not None, finish is...  43.9 us
  transfers between devices with their start and end apart: 48, of which 12 were waited for; matrix products, arithmetic and copies ran while one was open for 4% of the time, Pallas kernels for 37%

profile of v4, /device:TPU:0, one launch (start us, length us, event | category | flops | bytes accessed | tf_op | source)
XLA Modules:
  0.0 1647.0 jit_solution(11970103823291481172)
XLA Ops:
  0.6 1.8 select_bitcast_fusion.1
  2.4 10.6 dynamic-slice_bitcast_fusion.3
  13.0 10.6 dynamic-slice_bitcast_fusion.2
  23.6 10.6 dynamic-slice_bitcast_fusion.1
  35.0 2.6 collective-permute-start.1
  37.6 2.0 collective-permute-start.2
  39.7 1.7 select_bitcast_fusion
  41.5 562.4 %collective-permute-done.2 = bf16[768,768]{1,0:T(8,128)(2,1)S(1)} collective-permute-done((bf16[768,768]{1,0:T(8,128)(2,1)S(1)}, bf16[768,768]{1,0:T(8,128)(2,1)S(1)}, u32[]{:S(2)}, u32[]{:S(2)}) %collective-permute-start.2) | collective-permute-done | bytes 1179680 | tf_op jit(solution)/shard_map/ppermute | solution.py:367
  603.9 2.2 collective-permute-start.3
  606.0 22.9 %collective-permute-done.11 = bf16[768,768]{1,0:T(8,128)(2,1)S(1)} collective-permute-done((bf16[768,768]{1,0:T(8,128)(2,1)S(1)}, bf16[768,768]{1,0:T(8,128)(2,1)S(1)}, u32[]{:S(2)}, u32[]{:S(2)}) %collective-permute-start.11) | collective-permute-done | bytes 1179680 | tf_op jit(solution)/shard_map/ppermute | solution.py:367
  630.0 1.7 collective-permute-start.12
  631.7 26.1 %collective-permute-done.12 = bf16[768,768]{1,0:T(8,128)(2,1)S(1)} collective-permute-done((bf16[768,768]{1,0:T(8,128)(2,1)S(1)}, bf16[768,768]{1,0:T(8,128)(2,1)S(1)}, u32[]{:S(2)}, u32[]{:S(2)}) %collective-permute-start.12) | collective-permute-done | bytes 1179680 | tf_op jit(solution)/shard_map/ppermute | solution.py:370
  658.8 10.6 dynamic-slice_bitcast_fusion
  669.5 6.2 dynamic-slice_bitcast_fusion.5
  675.7 6.3 dynamic-slice_bitcast_fusion.4
  682.0 4.6 dynamic-slice_bitcast_fusion.7
  686.6 6.2 shard_map.81
  692.8 4.8 dynamic-slice_bitcast_fusion.6
  697.6 1.5 broadcast_select_fusion.2
  700.1 1.6 broadcast_select_fusion
  702.7 119.6 %shard_map.76 = (f32[16,512,768]{2,1,0:T(8,128)}, f32[2,768,768]{2,1,0:T(8,128)}, f32[2,768,768]{2,1,0:T(8,128)}) custom-call(s32[1]{0:T(128)} %bitcast._, bf16[16,512,768]{2,1,0:T(8,128)(2,1)} %refs_0_.3, bf16[2,16,512,768]{3,2,1,0:T(8,128)(2,1)} %x_ref.1, bf16[2,16,2048,768]{3,2,1,0:T(8,128)(2,1)} %hi_ref.3, ...), custom_call_target="tpu_custom_call" | custom-call | flops 77309411328 | bytes 50331648 | tf_op jit(solution)/shard_map/pallas_call | solution.py:112
  824.6 121.1 %shard_map.77 = (bf16[16,512,768]{2,1,0:T(8,128)(2,1)}, f32[2,768,768]{2,1,0:T(8,128)}, f32[2,768,768]{2,1,0:T(8,128)}) custom-call(s32[1]{0:T(128)} %bitcast._, bf16[16,512,768]{2,1,0:T(8,128)(2,1)} %refs_0_.3, bf16[2,16,512,768]{3,2,1,0:T(8,128)(2,1)} %x_ref.1, bf16[16,512,768]{2,1,0:T(8,128)(2,1)} %collective-permute-done.refs_2_, ...), custom_call_target="tpu_custom_call" | custom-call | flops 77309411328 | bytes 50331648 | tf_op jit(solution)/shard_map/pallas_call | solution.py:112
  947.9 119.5 %shard_map.78 = (f32[16,512,768]{2,1,0:T(8,128)}, f32[2,768,768]{2,1,0:T(8,128)}, f32[2,768,768]{2,1,0:T(8,128)}) custom-call(s32[1]{0:T(128)} %bitcast._, bf16[16,512,768]{2,1,0:T(8,128)(2,1)} %get-tuple-element.73.refs_0_.grad_ref, bf16[2,16,512,768]{3,2,1,0:T(8,128)(2,1)} %x_ref.1, bf16[2,16,2048,768]{3,2,1,0:T(8,128)(2,1)} %hi_ref.3, ...), custom_call_target="tpu_custom_call" | custom-call | flops 77309411328 | bytes 50331648 | tf_op jit(solution)/shard_map/pallas_call | solution.py:112
  1067.4 28.1 %collective-permute-done.15.refs_2_ = bf16[16,512,384]{2,1,0:T(8,128)(2,1)} collective-permute-done((bf16[16,512,384]{2,1,0:T(8,128)(2,1)}, bf16[16,512,384]{2,1,0:T(8,128)(2,1)}, u32[]{:S(2)}, u32[]{:S(2)}) %collective-permute-start.15) | collective-permute-done | bytes 6291488 | tf_op jit(solution)/shard_map/ppermute | solution.py:367
  1095.5 78.1 %shard_map.79 = (f32[16,512,768]{2,1,0:T(8,128)}, f32[2,384,768]{2,1,0:T(8,128)}, f32[2,384,768]{2,1,0:T(8,128)}) custom-call(s32[1]{0:T(128)} %bitcast._, bf16[16,512,768]{2,1,0:T(8,128)(2,1)} %get-tuple-element.73.refs_0_.grad_ref, bf16[2,16,512,768]{3,2,1,0:T(8,128)(2,1)} %x_ref.1, bf16[16,512,384]{2,1,0:T(8,128)(2,1)} %collective-permute-done.15.refs_2_, ...), custom_call_target="tpu_custom_call" | custom-call | flops 38654705664 | bytes 50331648 | tf_op jit(solution)/shard_map/pallas_call | solution.py:112
  1174.9 7.0 shard_map.95
  1181.9 93.0 %collective-permute-done.10.h_b = bf16[16,512,256]{2,1,0:T(8,128)(2,1)} collective-permute-done((bf16[16,512,256]{2,1,0:T(8,128)(2,1)}, bf16[16,512,256]{2,1,0:T(8,128)(2,1)}, u32[]{:S(2)}, u32[]{:S(2)}) %collective-permute-start.10) | collective-permute-done | bytes 4194336 | tf_op jit(solution)/shard_map/ppermute | solution.py:367
  1276.3 54.4 %shard_map.80 = (f32[16,512,768]{2,1,0:T(8,128)}, f32[2,256,768]{2,1,0:T(8,128)}, f32[2,256,768]{2,1,0:T(8,128)}) custom-call(bf16[16,512,768]{2,1,0:T(8,128)(2,1)} %get-tuple-element.73.refs_0_.grad_ref, bf16[2,16,512,768]{3,2,1,0:T(8,128)(2,1)} %x_ref.1, bf16[16,512,256]{2,1,0:T(8,128)(2,1)} %collective-permute-done.9.h_a, ...), custom_call_target="tpu_custom_call" | custom-call | flops 25769803776 | bytes 75497472 | tf_op jit(solution)/shard_map/pallas_call | solution.py:195
  1330.8 7.1 shard_map.94
  1338.7 4.1 add.63
  1342.8 1.2 collective-permute-start.46
  1344.0 6.3 shard_map.82
  1350.6 4.5 shard_map.93
  1356.2 7.0 shard_map.89
  1364.1 2.8 shard_map.90
  1367.0 51.2 %collective-permute-done.19.h_b = bf16[8,512,128]{2,1,0:T(8,128)(2,1)} collective-permute-done((bf16[8,512,128]{2,1,0:T(8,128)(2,1)}, bf16[8,512,128]{2,1,0:T(8,128)(2,1)}, u32[]{:S(2)}, u32[]{:S(2)}) %collective-permute-start.19) | collective-permute-done | bytes 1048608 | tf_op jit(solution)/shard_map/ppermute | solution.py:367
  1419.3 16.9 %shard_map.83 = (f32[2,64,768]{2,1,0:T(8,128)}, f32[2,64,768]{2,1,0:T(8,128)}, bf16[2,8,512,128]{3,2,1,0:T(8,128)(2,1)}) custom-call(bf16[2,8,512,768]{3,2,1,0:T(8,128)(2,1)} %bitcast.34, bf16[2,2,8,512,768]{4,3,2,1,0:T(8,128)(2,1)} %bitcast.28, bf16[8,512,128]{2,1,0:T(8,128)(2,1)} %collective-permute-done.18.h_a, ...), custom_call_target="tpu_custom_call" | custom-call | flops 4831838208 | bytes 25165824 | tf_op jit(solution)/shard_map/pallas_call | solution.py:252
  1436.8 2.8 add.60
  1439.6 1.5 collective-permute-start.40
  1441.1 4.2 add_add_fusion.refs_0_
  1445.8 1.9 shard_map.91
  1447.7 1.6 collective-permute-start.29
  1449.3 90.0 %collective-permute-done.29 = f32[64,768]{1,0:T(8,128)} collective-permute-done((f32[64,768]{1,0:T(8,128)}, f32[64,768]{1,0:T(8,128)}, u32[]{:S(2)}, u32[]{:S(2)}) %collective-permute-start.29) | collective-permute-done | bytes 196640 | tf_op jit(solution)/shard_map/ppermute | solution.py:370
  1539.3 1.5 collective-permute-start.22
  1540.7 1.9 shard_map.84.refs_2_.up_ref
  1543.7 1.4 add.54
  1548.8 2.0 add.53
  1550.8 3.2 add.61.refs_0_
  1554.1 3.1 collective-permute-done.22.h_a
  1557.2 1.5 collective-permute-start.30
  1558.7 11.6 collective-permute-done.23.h_b
  1570.7 18.7 %shard_map.85 = (f32[2,64,768]{2,1,0:T(8,128)}, f32[2,64,768]{2,1,0:T(8,128)}, bf16[2,8,512,768]{3,2,1,0:T(8,128)(2,1)}) custom-call(bf16[2,8,512,768]{3,2,1,0:T(8,128)(2,1)} %bitcast.35, bf16[2,2,8,512,768]{4,3,2,1,0:T(8,128)(2,1)} %bitcast.29, bf16[5,512,128]{2,1,0:T(8,128)(2,1)} %collective-permute-done.22.h_a, ...), custom_call_target="tpu_custom_call" | custom-call | flops 3019898880 | bytes 15728640 | tf_op jit(solution)/shard_map/pallas_call | solution.py:252
  1590.4 8.3 shard_map.86
  1601.3 1.9 shard_map.92
  1604.4 1.9 add.56.refs_0_
  1607.2 4.0 collective-permute-done.32
  1614.4 1.5 collective-permute-start.33
  1615.9 4.2 collective-permute-done.33
  1621.0 5.4 shard_map.87._
  1626.4 5.4 shard_map.88
  1631.8 5.9 shard_map.96
  1637.7 3.8 shard_map.97
  1642.2 2.0 shard_map.98
  1644.3 2.7 shard_map.99
  (124 shorter events, 33.1 us)
Async XLA Ops:
  34.2 668.0 %collective-permute-start.6 = (bf16[16,512,768]{2,1,0:T(8,128)(2,1)}, bf16[16,512,768]{2,1,0:T(8,128)(2,1)}, u32[]{:S(2)}, u32[]{:S(2)}) collective-permute-start(bf16[16,512,768]{2,1,0:T(8,128)(2,1)} %dynamic-slice_bitcast_fusion.1), channel_id=1, source_target_pairs={{0,1},{1,0},{2,3},{3,2},{4,5},{5,4},{6,7},{7,6}} | collective-permute-start | bytes 37748744 | tf_op jit(solution)/shard_map/ppermute | solution.py:367
  35.0 789.0 %collective-permute-start.1 = (bf16[16,512,768]{2,1,0:T(8,128)(2,1)}, bf16[16,512,768]{2,1,0:T(8,128)(2,1)}, u32[]{:S(2)}, u32[]{:S(2)}) collective-permute-start(bf16[16,512,768]{2,1,0:T(8,128)(2,1)} %dynamic-slice_bitcast_fusion.2), channel_id=1, source_target_pairs={{0,3},{1,2},{2,1},{3,0},{4,7},{5,6},{6,5},{7,4}} | collective-permute-start | bytes 37748744 | tf_op jit(solution)/shard_map/ppermute | solution.py:367
  37.6 786.6 %collective-permute-start = (bf16[16,512,768]{2,1,0:T(8,128)(2,1)}, bf16[16,512,768]{2,1,0:T(8,128)(2,1)}, u32[]{:S(2)}, u32[]{:S(2)}) collective-permute-start(bf16[16,512,768]{2,1,0:T(8,128)(2,1)} %dynamic-slice_bitcast_fusion.3), channel_id=1, source_target_pairs={{0,2},{1,3},{2,0},{3,1},{4,6},{5,7},{6,4},{7,5}} | collective-permute-start | bytes 37748744 | tf_op jit(solution)/shard_map/ppermute | solution.py:367
  37.6 566.2 %collective-permute-start.2 = (bf16[768,768]{1,0:T(8,128)(2,1)S(1)}, bf16[768,768]{1,0:T(8,128)(2,1)S(1)}, u32[]{:S(2)}, u32[]{:S(2)}) collective-permute-start(bf16[768,768]{1,0:T(8,128)(2,1)S(1)} %select_bitcast_fusion.1), channel_id=1, source_target_pairs={{0,2},{1,3},{2,0},{3,1},{4,6},{5,7},{6,4},{7,5}} | collective-permute-start | bytes 3538952 | tf_op jit(solution)/shard_map/ppermute | solution.py:367
  41.4 587.5 %collective-permute-start.11 = (bf16[768,768]{1,0:T(8,128)(2,1)S(1)}, bf16[768,768]{1,0:T(8,128)(2,1)S(1)}, u32[]{:S(2)}, u32[]{:S(2)}) collective-permute-start(bf16[768,768]{1,0:T(8,128)(2,1)S(1)} %select_bitcast_fusion), channel_id=1, source_target_pairs={{0,2},{1,3},{2,0},{3,1},{4,6},{5,7},{6,4},{7,5}} | collective-permute-start | bytes 3538952 | tf_op jit(solution)/shard_map/ppermute | solution.py:367
  603.9 53.9 %copy-start.6 = (bf16[768,768]{1,0:T(8,128)(2,1)}, bf16[768,768]{1,0:T(8,128)(2,1)S(1)}, u32[]{:S(2)}) copy-start(bf16[768,768]{1,0:T(8,128)(2,1)S(1)} %collective-permute-done.2) | copy-start | bytes 3538948
  603.9 27.8 %collective-permute-start.3 = (bf16[768,768]{1,0:T(8,128)(2,1)S(1)}, bf16[768,768]{1,0:T(8,128)(2,1)S(1)}, u32[]{:S(2)}, u32[]{:S(2)}) collective-permute-start(bf16[768,768]{1,0:T(8,128)(2,1)S(1)} %collective-permute-done.2), channel_id=1, source_target_pairs={{0,4},{4,0},{1,5},{5,1},{2,6},{6,2},{3,7},{7,3}} | collective-permute-start | bytes 3538952 | tf_op jit(solution)/shard_map/ppermute | solution.py:370
  630.0 27.8 %collective-permute-start.12 = (bf16[768,768]{1,0:T(8,128)(2,1)S(1)}, bf16[768,768]{1,0:T(8,128)(2,1)S(1)}, u32[]{:S(2)}, u32[]{:S(2)}) collective-permute-start(bf16[768,768]{1,0:T(8,128)(2,1)S(1)} %collective-permute-done.11), channel_id=1, source_target_pairs={{0,4},{4,0},{1,5},{5,1},{2,6},{6,2},{3,7},{7,3}} | collective-permute-start | bytes 3538952 | tf_op jit(solution)/shard_map/ppermute | solution.py:370
  631.7 26.1 %copy-start.8 = (bf16[768,768]{1,0:T(8,128)(2,1)}, bf16[768,768]{1,0:T(8,128)(2,1)S(1)}, u32[]{:S(2)}) copy-start(bf16[768,768]{1,0:T(8,128)(2,1)S(1)} %collective-permute-done.3) | copy-start | bytes 3538948
  631.7 70.0 %collective-permute-start.7 = (bf16[2,768,768]{2,1,0:T(8,128)(2,1)}, bf16[2,768,768]{2,1,0:T(8,128)(2,1)}, u32[]{:S(2)}, u32[]{:S(2)}) collective-permute-start(bf16[2,768,768]{2,1,0:T(8,128)(2,1)} %refs_4_.3), channel_id=1, source_target_pairs={{0,1},{1,0},{2,3},{3,2},{4,5},{5,4},{6,7},{7,6}} | collective-permute-start | bytes 7077896 | tf_op jit(solution)/shard_map/ppermute | solution.py:367
  658.8 43.4 %collective-permute-start.8 = (bf16[2,768,768]{2,1,0:T(8,128)(2,1)}, bf16[2,768,768]{2,1,0:T(8,128)(2,1)}, u32[]{:S(2)}, u32[]{:S(2)}) collective-permute-start(bf16[2,768,768]{2,1,0:T(8,128)(2,1)} %refs_6_.3), channel_id=1, source_target_pairs={{0,1},{1,0},{2,3},{3,2},{4,5},{5,4},{6,7},{7,6}} | collective-permute-start | bytes 7077896 | tf_op jit(solution)/shard_map/ppermute | solution.py:367
  692.8 4.8 copy-start.7
  692.8 4.8 copy-start.9
  697.6 1.7 copy-start.5
  697.6 2.5 copy-start.11
  701.7 245.6 %collective-permute-start.17 = (bf16[16,512,768]{2,1,0:T(8,128)(2,1)}, bf16[16,512,768]{2,1,0:T(8,128)(2,1)}, u32[]{:S(2)}, u32[]{:S(2)}) collective-permute-start(bf16[16,512,768]{2,1,0:T(8,128)(2,1)} %dynamic-slice_bitcast_fusion), channel_id=1, source_target_pairs={{0,1},{1,0},{2,3},{3,2},{4,5},{5,4},{6,7},{7,6}} | collective-permute-start | bytes 37748744 | tf_op jit(solution)/shard_map/ppermute | solution.py:367
  702.2 120.2 %collective-permute-start.4 = (bf16[768,768]{1,0:T(8,128)(2,1)}, bf16[768,768]{1,0:T(8,128)(2,1)}, u32[]{:S(2)}, u32[]{:S(2)}) collective-permute-start(bf16[768,768]{1,0:T(8,128)(2,1)} %get-tuple-element.138.refs_4_), channel_id=1, source_target_pairs={{0,1},{1,0},{2,3},{3,2},{4,5},{5,4},{6,7},{7,6}} | collective-permute-start | bytes 3538952 | tf_op jit(solution)/shard_map/ppermute | solution.py:367
  702.2 120.9 %collective-permute-start.5 = (bf16[768,768]{1,0:T(8,128)(2,1)}, bf16[768,768]{1,0:T(8,128)(2,1)}, u32[]{:S(2)}, u32[]{:S(2)}) collective-permute-start(bf16[768,768]{1,0:T(8,128)(2,1)} %get-tuple-element.137.refs_6_), channel_id=1, source_target_pairs={{0,1},{1,0},{2,3},{3,2},{4,5},{5,4},{6,7},{7,6}} | collective-permute-start | bytes 3538952 | tf_op jit(solution)/shard_map/ppermute | solution.py:367
  822.4 245.0 %collective-permute-start.16 = (bf16[16,512,384]{2,1,0:T(8,128)(2,1)}, bf16[16,512,384]{2,1,0:T(8,128)(2,1)}, u32[]{:S(2)}, u32[]{:S(2)}) collective-permute-start(bf16[16,512,384]{2,1,0:T(8,128)(2,1)} %dynamic-slice_bitcast_fusion.4), channel_id=1, source_target_pairs={{0,3},{1,2},{2,1},{3,0},{4,7},{5,6},{6,5},{7,4}} | collective-permute-start | bytes 18874376 | tf_op jit(solution)/shard_map/ppermute | solution.py:367
  823.2 272.4 %collective-permute-start.15 = (bf16[16,512,384]{2,1,0:T(8,128)(2,1)}, bf16[16,512,384]{2,1,0:T(8,128)(2,1)}, u32[]{:S(2)}, u32[]{:S(2)}) collective-permute-start(bf16[16,512,384]{2,1,0:T(8,128)(2,1)} %dynamic-slice_bitcast_fusion.5), channel_id=1, source_target_pairs={{0,2},{1,3},{2,0},{3,1},{4,6},{5,7},{6,4},{7,5}} | collective-permute-start | bytes 18874376 | tf_op jit(solution)/shard_map/ppermute | solution.py:367
  824.0 121.7 %collective-permute-start.13 = (bf16[768,768]{1,0:T(8,128)(2,1)}, bf16[768,768]{1,0:T(8,128)(2,1)}, u32[]{:S(2)}, u32[]{:S(2)}) collective-permute-start(bf16[768,768]{1,0:T(8,128)(2,1)} %get-tuple-element.136.refs_4_.up_a), channel_id=1, source_target_pairs={{0,1},{1,0},{2,3},{3,2},{4,5},{5,4},{6,7},{7,6}} | collective-permute-start | bytes 3538952 | tf_op jit(solution)/shard_map/ppermute | solution.py:367
  824.3 122.6 %collective-permute-start.14 = (bf16[768,768]{1,0:T(8,128)(2,1)}, bf16[768,768]{1,0:T(8,128)(2,1)}, u32[]{:S(2)}, u32[]{:S(2)}) collective-permute-start(bf16[768,768]{1,0:T(8,128)(2,1)} %get-tuple-element.135.refs_6_.down_a), channel_id=1, source_target_pairs={{0,1},{1,0},{2,3},{3,2},{4,5},{5,4},{6,7},{7,6}} | collective-permute-start | bytes 3538952 | tf_op jit(solution)/shard_map/ppermute | solution.py:367
  945.7 329.4 %collective-permute-start.9 = (bf16[16,512,256]{2,1,0:T(8,128)(2,1)}, bf16[16,512,256]{2,1,0:T(8,128)(2,1)}, u32[]{:S(2)}, u32[]{:S(2)}) collective-permute-start(bf16[16,512,256]{2,1,0:T(8,128)(2,1)} %dynamic-slice_bitcast_fusion.7), channel_id=1, source_target_pairs={{0,2},{1,3},{2,0},{3,1},{4,6},{5,7},{6,4},{7,5}} | collective-permute-start | bytes 12582920 | tf_op jit(solution)/shard_map/ppermute | solution.py:367
  946.9 328.0 %collective-permute-start.10 = (bf16[16,512,256]{2,1,0:T(8,128)(2,1)}, bf16[16,512,256]{2,1,0:T(8,128)(2,1)}, u32[]{:S(2)}, u32[]{:S(2)}) collective-permute-start(bf16[16,512,256]{2,1,0:T(8,128)(2,1)} %dynamic-slice_bitcast_fusion.6), channel_id=1, source_target_pairs={{0,3},{1,2},{2,1},{3,0},{4,7},{5,6},{6,5},{7,4}} | collective-permute-start | bytes 12582920 | tf_op jit(solution)/shard_map/ppermute | solution.py:367
  947.3 226.4 %collective-permute-start.44 = (f32[2,768,768]{2,1,0:T(8,128)}, f32[2,768,768]{2,1,0:T(8,128)}, u32[]{:S(2)}, u32[]{:S(2)}) collective-permute-start(f32[2,768,768]{2,1,0:T(8,128)} %get-tuple-element.124), channel_id=1, source_target_pairs={{0,1},{1,0},{2,3},{3,2},{4,5},{5,4},{6,7},{7,6}} | collective-permute-start | bytes 14155784 | tf_op jit(solution)/shard_map/ppermute | solution.py:367
  1067.4 263.4 %collective-permute-start.42 = (f32[2,768,768]{2,1,0:T(8,128)}, f32[2,768,768]{2,1,0:T(8,128)}, u32[]{:S(2)}, u32[]{:S(2)}) collective-permute-start(f32[2,768,768]{2,1,0:T(8,128)} %get-tuple-element.120), channel_id=1, source_target_pairs={{0,1},{1,0},{2,3},{3,2},{4,5},{5,4},{6,7},{7,6}} | collective-permute-start | bytes 14155784 | tf_op jit(solution)/shard_map/ppermute | solution.py:367
  1095.5 259.5 %collective-permute-start.24 = (f32[2,768,768]{2,1,0:T(8,128)}, f32[2,768,768]{2,1,0:T(8,128)}, u32[]{:S(2)}, u32[]{:S(2)}) collective-permute-start(f32[2,768,768]{2,1,0:T(8,128)} %get-tuple-element.96), channel_id=1, source_target_pairs={{0,1},{1,0},{2,3},{3,2},{4,5},{5,4},{6,7},{7,6}} | collective-permute-start | bytes 14155784 | tf_op jit(solution)/shard_map/ppermute | solution.py:367
  1173.7 169.1 %collective-permute-start.18 = (bf16[8,512,128]{2,1,0:T(8,128)(2,1)}, bf16[8,512,128]{2,1,0:T(8,128)(2,1)}, u32[]{:S(2)}, u32[]{:S(2)}) collective-permute-start(bf16[8,512,128]{2,1,0:T(8,128)(2,1)} %get-tuple-element.84), channel_id=1, source_target_pairs={{0,2},{1,3},{2,0},{3,1},{4,6},{5,7},{6,4},{7,5}} | collective-permute-start | bytes 3145736 | tf_op jit(solution)/shard_map/ppermute | solution.py:367
  1274.9 75.3 %collective-permute-start.38 = (f32[2,384,768]{2,1,0:T(8,128)}, f32[2,384,768]{2,1,0:T(8,128)}, u32[]{:S(2)}, u32[]{:S(2)}) collective-permute-start(f32[2,384,768]{2,1,0:T(8,128)} %get-tuple-element.116), channel_id=1, source_target_pairs={{0,1},{1,0},{2,3},{3,2},{4,5},{5,4},{6,7},{7,6}} | collective-permute-start | bytes 7077896 | tf_op jit(solution)/shard_map/ppermute | solution.py:367
  1275.1 62.7 %collective-permute-start.45 = (f32[768,768]{1,0:T(8,128)}, f32[768,768]{1,0:T(8,128)}, u32[]{:S(2)}, u32[]{:S(2)}) collective-permute-start(f32[768,768]{1,0:T(8,128)} %get-tuple-element.126), channel_id=1, source_target_pairs={{0,4},{4,0},{1,5},{5,1},{2,6},{6,2},{3,7},{7,3}} | collective-permute-start | bytes 7077896 | tf_op jit(solution)/shard_map/ppermute | solution.py:370
  1330.7 32.5 %collective-permute-start.26 = (f32[2,256,768]{2,1,0:T(8,128)}, f32[2,256,768]{2,1,0:T(8,128)}, u32[]{:S(2)}, u32[]{:S(2)}) collective-permute-start(f32[2,256,768]{2,1,0:T(8,128)} %get-tuple-element.101), channel_id=1, source_target_pairs={{0,1},{1,0},{2,3},{3,2},{4,5},{5,4},{6,7},{7,6}} | collective-permute-start | bytes 4718600 | tf_op jit(solution)/shard_map/ppermute | solution.py:367
  1337.8 101.8 %collective-permute-start.43 = (f32[768,768]{1,0:T(8,128)}, f32[768,768]{1,0:T(8,128)}, u32[]{:S(2)}, u32[]{:S(2)}) collective-permute-start(f32[768,768]{1,0:T(8,128)} %get-tuple-element.122), channel_id=1, source_target_pairs={{0,4},{4,0},{1,5},{5,1},{2,6},{6,2},{3,7},{7,3}} | collective-permute-start | bytes 7077896 | tf_op jit(solution)/shard_map/ppermute | solution.py:370
  1342.8 98.4 %collective-permute-start.46 = (f32[768,768]{1,0:T(8,128)}, f32[768,768]{1,0:T(8,128)}, u32[]{:S(2)}, u32[]{:S(2)}) collective-permute-start(f32[768,768]{1,0:T(8,128)} %add.63), channel_id=1, source_target_pairs={{0,2},{1,3},{2,0},{3,1},{4,6},{5,7},{6,4},{7,5}} | collective-permute-start | bytes 7077896 | tf_op jit(solution)/shard_map/ppermute | solution.py:367
  1350.2 67.9 %collective-permute-start.19 = (bf16[8,512,128]{2,1,0:T(8,128)(2,1)}, bf16[8,512,128]{2,1,0:T(8,128)(2,1)}, u32[]{:S(2)}, u32[]{:S(2)}) collective-permute-start(bf16[8,512,128]{2,1,0:T(8,128)(2,1)} %get-tuple-element.85), channel_id=1, source_target_pairs={{0,3},{1,2},{2,1},{3,0},{4,7},{5,6},{6,5},{7,4}} | collective-permute-start | bytes 3145736 | tf_op jit(solution)/shard_map/ppermute | solution.py:367
  1355.1 81.1 %collective-permute-start.39 = (f32[384,768]{1,0:T(8,128)}, f32[384,768]{1,0:T(8,128)}, u32[]{:S(2)}, u32[]{:S(2)}) collective-permute-start(f32[384,768]{1,0:T(8,128)} %get-tuple-element.118), channel_id=1, source_target_pairs={{0,4},{4,0},{1,5},{5,1},{2,6},{6,2},{3,7},{7,3}} | collective-permute-start | bytes 3538952 | tf_op jit(solution)/shard_map/ppermute | solution.py:370
  1363.3 183.6 %collective-permute-start.25 = (f32[768,768]{1,0:T(8,128)}, f32[768,768]{1,0:T(8,128)}, u32[]{:S(2)}, u32[]{:S(2)}) collective-permute-start(f32[768,768]{1,0:T(8,128)} %get-tuple-element.98), channel_id=1, source_target_pairs={{0,4},{4,0},{1,5},{5,1},{2,6},{6,2},{3,7},{7,3}} | collective-permute-start | bytes 7077896 | tf_op jit(solution)/shard_map/ppermute | solution.py:370
  1418.1 122.6 %collective-permute-start.27 = (f32[256,768]{1,0:T(8,128)}, f32[256,768]{1,0:T(8,128)}, u32[]{:S(2)}, u32[]{:S(2)}) collective-permute-start(f32[256,768]{1,0:T(8,128)} %get-tuple-element.103), channel_id=1, source_target_pairs={{0,4},{4,0},{1,5},{5,1},{2,6},{6,2},{3,7},{7,3}} | collective-permute-start | bytes 2359304 | tf_op jit(solution)/shard_map/ppermute | solution.py:370
  1436.2 5.0 copy-start.2
  1436.2 9.6 collective-permute-start.28
  1439.6 106.3 %collective-permute-start.40 = (f32[384,768]{1,0:T(8,128)}, f32[384,768]{1,0:T(8,128)}, u32[]{:S(2)}, u32[]{:S(2)}) collective-permute-start(f32[384,768]{1,0:T(8,128)} %add.60), channel_id=1, source_target_pairs={{0,2},{1,3},{2,0},{3,1},{4,6},{5,7},{6,4},{7,5}} | collective-permute-start | bytes 3538952 | tf_op jit(solution)/shard_map/ppermute | solution.py:367
  1445.3 98.3 %copy-start.12 = (f32[256,768]{1,0:T(8,128)S(1)}, f32[256,768]{1,0:T(8,128)}, u32[]{:S(2)}) copy-start(f32[256,768]{1,0:T(8,128)} %get-tuple-element.102) | copy-start | bytes 2359300
  1445.3 186.5 %collective-permute-start.47 = (f32[768,768]{1,0:T(8,128)}, f32[768,768]{1,0:T(8,128)}, u32[]{:S(2)}, u32[]{:S(2)}) collective-permute-start(f32[768,768]{1,0:T(8,128)} %add_add_fusion.refs_0_), channel_id=1, source_target_pairs={{0,4},{4,0},{1,5},{5,1},{2,6},{6,2},{3,7},{7,3}} | collective-permute-start | bytes 7077896 | tf_op jit(solution)/shard_map/ppermute | solution.py:370
  1447.7 95.0 %copy-start.17 = (f32[64,768]{1,0:T(8,128)S(1)}, f32[64,768]{1,0:T(8,128)}, u32[]{:S(2)}) copy-start(f32[64,768]{1,0:T(8,128)} %get-tuple-element.106) | copy-start | bytes 589828
  1447.7 91.5 %collective-permute-start.29 = (f32[64,768]{1,0:T(8,128)}, f32[64,768]{1,0:T(8,128)}, u32[]{:S(2)}, u32[]{:S(2)}) collective-permute-start(f32[64,768]{1,0:T(8,128)} %get-tuple-element.107), channel_id=1, source_target_pairs={{0,4},{4,0},{1,5},{5,1},{2,6},{6,2},{3,7},{7,3}} | collective-permute-start | bytes 589832 | tf_op jit(solution)/shard_map/ppermute | solution.py:370
  1539.3 17.9 %collective-permute-start.22 = (bf16[5,512,128]{2,1,0:T(8,128)(2,1)}, bf16[5,512,128]{2,1,0:T(8,128)(2,1)}, u32[]{:S(2)}, u32[]{:S(2)}) collective-permute-start(bf16[5,512,128]{2,1,0:T(8,128)(2,1)} %get-tuple-element.89), channel_id=1, source_target_pairs={{0,2},{1,3},{2,0},{3,1},{4,6},{5,7},{6,4},{7,5}} | collective-permute-start | bytes 1966088 | tf_op jit(solution)/shard_map/ppermute | solution.py:367
  1540.7 29.5 %collective-permute-start.23 = (bf16[5,512,128]{2,1,0:T(8,128)(2,1)}, bf16[5,512,128]{2,1,0:T(8,128)(2,1)}, u32[]{:S(2)}, u32[]{:S(2)}) collective-permute-start(bf16[5,512,128]{2,1,0:T(8,128)(2,1)} %get-tuple-element.90), channel_id=1, source_target_pairs={{0,3},{1,2},{2,1},{3,0},{4,7},{5,6},{6,5},{7,4}} | collective-permute-start | bytes 1966088 | tf_op jit(solution)/shard_map/ppermute | solution.py:367
  1543.7 5.1 copy-start.1
  1545.9 43.6 %collective-permute-start.20 = (bf16[3,512,128]{2,1,0:T(8,128)(2,1)}, bf16[3,512,128]{2,1,0:T(8,128)(2,1)S(1)}, u32[]{:S(2)}, u32[]{:S(2)}) collective-permute-start(bf16[3,512,128]{2,1,0:T(8,128)(2,1)} %get-tuple-element.87), channel_id=1, source_target_pairs={{0,2},{1,3},{2,0},{3,1},{4,6},{5,7},{6,4},{7,5}} | collective-permute-start | bytes 1179656 | tf_op jit(solution)/shard_map/ppermute | solution.py:367
  1546.9 42.6 %collective-permute-start.21 = (bf16[3,512,128]{2,1,0:T(8,128)(2,1)}, bf16[3,512,128]{2,1,0:T(8,128)(2,1)S(1)}, u32[]{:S(2)}, u32[]{:S(2)}) collective-permute-start(bf16[3,512,128]{2,1,0:T(8,128)(2,1)} %get-tuple-element.88), channel_id=1, source_target_pairs={{0,3},{1,2},{2,1},{3,0},{4,7},{5,6},{6,5},{7,4}} | collective-permute-start | bytes 1179656 | tf_op jit(solution)/shard_map/ppermute | solution.py:367
  1550.7 3.3 copy-start
  1557.2 47.2 %collective-permute-start.30 = (f32[192,768]{1,0:T(8,128)}, f32[192,768]{1,0:T(8,128)}, u32[]{:S(2)}, u32[]{:S(2)}) collective-permute-start(f32[192,768]{1,0:T(8,128)} %pad_maximum_fusion), channel_id=1, source_target_pairs={{0,2},{1,3},{2,0},{3,1},{4,6},{5,7},{6,4},{7,5}} | collective-permute-start | bytes 1769480 | tf_op jit(solution)/shard_map/ppermute | solution.py:367
  1570.2 67.5 %collective-permute-start.41 = (f32[384,768]{1,0:T(8,128)}, f32[384,768]{1,0:T(8,128)}, u32[]{:S(2)}, u32[]{:S(2)}) collective-permute-start(f32[384,768]{1,0:T(8,128)} %add.61.refs_0_), channel_id=1, source_target_pairs={{0,4},{4,0},{1,5},{5,1},{2,6},{6,2},{3,7},{7,3}} | collective-permute-start | bytes 3538952 | tf_op jit(solution)/shard_map/ppermute | solution.py:370
  1590.4 14.0 slice-start
  1598.7 13.5 slice-start.1
  1598.7 2.6 collective-permute-start.31
  1599.6 12.6 collective-permute-start.36
  1603.2 16.9 %slice-start.2 = ((f32[768,768]{1,0:T(8,128)}), f32[64,768]{1,0:T(8,128)S(1)}, s32[]{:S(2)}) async-start(f32[768,768]{1,0:T(8,128)} %copy-done), calls=%async_computation.2 | async-start | bytes 393216 | tf_op jit(solution)/shard_map/slice | solution.py:439
  1603.2 8.0 collective-permute-start.32
  1606.3 38.0 %collective-permute-start.34 = (f32[192,768]{1,0:T(8,128)}, f32[192,768]{1,0:T(8,128)}, u32[]{:S(2)}, u32[]{:S(2)}) collective-permute-start(f32[192,768]{1,0:T(8,128)} %add.56.refs_0_), channel_id=1, source_target_pairs={{0,4},{4,0},{1,5},{5,1},{2,6},{6,2},{3,7},{7,3}} | collective-permute-start | bytes 1769480 | tf_op jit(solution)/shard_map/ppermute | solution.py:370
  1613.2 13.2 copy-start.3
  1613.2 28.3 %collective-permute-start.37 = (f32[128,768]{1,0:T(8,128)S(1)}, f32[128,768]{1,0:T(8,128)S(1)}, u32[]{:S(2)}, u32[]{:S(2)}) collective-permute-start(f32[128,768]{1,0:T(8,128)S(1)} %add.59.refs_0_), channel_id=1, source_target_pairs={{0,4},{4,0},{1,5},{5,1},{2,6},{6,2},{3,7},{7,3}} | collective-permute-start | bytes 1179656 | tf_op jit(solution)/shard_map/ppermute | solution.py:370
  1614.4 5.7 collective-permute-start.33
  1620.1 6.3 copy-start.13
  1620.1 24.2 %collective-permute-start.35 = (f32[64,768]{1,0:T(8,128)S(1)}, f32[64,768]{1,0:T(8,128)}, u32[]{:S(2)}, u32[]{:S(2)}) collective-permute-start(f32[64,768]{1,0:T(8,128)S(1)} %add.58.refs_1_), channel_id=1, source_target_pairs={{0,4},{4,0},{1,5},{5,1},{2,6},{6,2},{3,7},{7,3}} | collective-permute-start | bytes 589832 | tf_op jit(solution)/shard_map/ppermute | solution.py:370
  (5 other events, 4.5 us)

commit v5 on v4

--- a/solution.py
+++ b/solution.py
@@ -13,7 +13,8 @@
 BLOCKS = (384, 256)
 LANES = 128
 SMALL = 64
-EARLY = 5
+CHUNKS = (3, 3, 2)
+FIRST = 192
 ALL_VMEM = 66_000_000
 
 
@@ -132,36 +133,31 @@
     return jnp.where(left, a, pltpu.roll(b, SMALL, 1)), jnp.where(left, pltpu.roll(a, SMALL, 1), b)
 
 
-def pack_body(chunk, _, lo_ref, hi_ref, left_ref, right_a, right_b):
+def pack_body(_, lo_ref, hi_ref, left_ref, *right_refs):
     left, right = swap_lanes(lo_ref[0, 0].astype(F32), hi_ref[0, 0].astype(F32))
     left_ref[0] = left.astype(BF16)
-
-    @pl.when(pl.program_id(0) < chunk)
-    def _():
-        right_a[0] = right.astype(BF16)
-
-    @pl.when(pl.program_id(0) >= chunk)
-    def _():
-        right_b[0] = right.astype(BF16)
+    for j, ref in enumerate(right_refs):
+        low = sum(CHUNKS[:j])
+
+        @pl.when((pl.program_id(0) >= low) & (pl.program_id(0) < low + CHUNKS[j]))
+        def _():
+            ref[0] = right.astype(BF16)
 
 
 def pack_call(target, h_saved, layer, start, seq):
     pairs = h_saved.shape[1] // 2
-    chunk = EARLY
     specs = [pl.BlockSpec((1, 1, seq, LANES), lambda b, ids, r=r: (layer, b + r * pairs, ids[0], start // LANES)) for r in range(2)]
     block = (1, seq, LANES)
-    return pl.pallas_call(
-        functools.partial(pack_body, chunk),
-        out_shape=[jax.ShapeDtypeStruct((n, seq, LANES), BF16) for n in (pairs, chunk, pairs - chunk)],
+    chunk_specs = [
+        pl.BlockSpec(block, lambda b, ids, low=sum(CHUNKS[:j]), n=n: (jnp.clip(b - low, 0, n - 1), 0, 0)) for j, n in enumerate(CHUNKS)]
+    return pl.pallas_call(
+        pack_body,
+        out_shape=[jax.ShapeDtypeStruct((n, seq, LANES), BF16) for n in (pairs, *CHUNKS)],
         grid_spec=pltpu.PrefetchScalarGridSpec(
             num_scalar_prefetch=1,
             grid=(pairs,),
             in_specs=specs,
-            out_specs=[
-                pl.BlockSpec(block, lambda b, ids: (b, 0, 0)),
-                pl.BlockSpec(block, lambda b, ids: (jnp.minimum(b, chunk - 1), 0, 0)),
-                pl.BlockSpec(block, lambda b, ids: (jnp.maximum(b - chunk, 0), 0, 0)),
-            ],
+            out_specs=[pl.BlockSpec(block, lambda b, ids: (b, 0, 0)), *chunk_specs],
         ),
         compiler_params=pltpu.CompilerParams(dimension_semantics=("arbitrary",), vmem_limit_bytes=ALL_VMEM),
         cost_estimate=pl.CostEstimate(flops=pairs * seq * LANES, bytes_accessed=8 * pairs * seq * LANES, transcendentals=0),
@@ -286,20 +282,21 @@
     out_ref[0, 0] = total.astype(BF16)
 
 
-def finish_call(carry, pre_pair, ups, half, out):
-    _, pairs, seq, hidden = carry.shape
-    count = pairs - EARLY
-    row_spec = pl.BlockSpec((1, 1, seq, hidden), lambda b: (half, b + EARLY, 0, 0))
-    pre_specs = [pl.BlockSpec((1, 1, seq, LANES), lambda b, first=first: (half, b + first, 0, 0)) for first in (EARLY, 0)]
+def finish_call(carry, pre_pair, ups, first_pair, first_half, halves, out):
+    _, _, seq, hidden = carry.shape
+    count = pre_pair[1].shape[1]
+    row_spec = pl.BlockSpec((1, 1, seq, hidden), lambda r, b: (r + first_half, b + first_pair, 0, 0))
+    pre_specs = [pl.BlockSpec((1, 1, seq, LANES), lambda r, b, first=first: (r + first_half, b + first, 0, 0)) for first in (first_pair, 0)]
+    rows = halves * count
     return pl.pallas_call(
         finish_body,
         out_shape=jax.ShapeDtypeStruct(carry.shape, BF16),
-        grid=(count,),
-        in_specs=[row_spec, *pre_specs, pl.BlockSpec(ups.shape, lambda b: (0, 0)), pl.BlockSpec(memory_space=pl.ANY)],
+        grid=(halves, count),
+        in_specs=[row_spec, *pre_specs, pl.BlockSpec(ups.shape, lambda r, b: (0, 0)), pl.BlockSpec(memory_space=pl.ANY)],
         out_specs=row_spec,
         input_output_aliases={4: 0},
-        compiler_params=pltpu.CompilerParams(dimension_semantics=("arbitrary",), vmem_limit_bytes=ALL_VMEM),
-        cost_estimate=pl.CostEstimate(flops=4 * count * seq * hidden * LANES, bytes_accessed=7 * count * seq * hidden, transcendentals=0),
+        compiler_params=pltpu.CompilerParams(dimension_semantics=("arbitrary", "arbitrary"), vmem_limit_bytes=ALL_VMEM),
+        cost_estimate=pl.CostEstimate(flops=4 * rows * seq * hidden * LANES, bytes_accessed=7 * rows * seq * hidden, transcendentals=0),
     )(carry, *pre_pair, ups, out)
 
 
@@ -325,39 +322,73 @@
     )(first, mine, theirs)
 
 
-def place_body(pieces, first_ref, *refs):
+def place_body(first_ref, kept_ref, other_ref, *refs):
     up_ref, down_ref = refs[-2:]
     first = first_ref[0] == 1
-    kept = jnp.concatenate([r[...] for r in refs[:pieces]])
-    other = jnp.concatenate([r[...] for r in refs[pieces : 2 * pieces]])
+    kept, other = kept_ref[...], other_ref[...]
     up_ref[0] = jnp.where(first, kept, other).T
     down_ref[0] = jnp.where(first, other, kept)
 
 
 def place_call(first, kept, other, layer, start, layers, width, bufs):
-    hidden = kept[0].shape[1]
-    size = sum(k.shape[0] for k in kept)
-    step = LANES if len(kept) == 1 else size
+    size, hidden = kept.shape
+    row_spec = pl.BlockSpec((LANES, hidden), lambda i, first: (i, 0))
     out_shape = [jax.ShapeDtypeStruct((layers, hidden, width), F32), jax.ShapeDtypeStruct((layers, width, hidden), F32)]
     any_spec = pl.BlockSpec(memory_space=pl.ANY)
-    count = 2 * len(kept)
-    piece_specs = [pl.BlockSpec((min(k.shape[0], step) if len(kept) == 1 else k.shape[0], hidden), lambda i, first: (i, 0)) for k in kept]
-    return pl.pallas_call(
-        functools.partial(place_body, len(kept)),
+    return pl.pallas_call(
+        place_body,
         out_shape=out_shape,
         grid_spec=pltpu.PrefetchScalarGridSpec(
             num_scalar_prefetch=1,
-            grid=(size // step,),
-            in_specs=piece_specs * 2 + ([any_spec, any_spec] if bufs is not None else []),
+            grid=(size // LANES,),
+            in_specs=[row_spec, row_spec] + ([any_spec, any_spec] if bufs is not None else []),
             out_specs=[
-                pl.BlockSpec((1, hidden, step), lambda i, first: (layer, 0, start // step + i)),
-                pl.BlockSpec((1, step, hidden), lambda i, first: (layer, start // step + i, 0)),
+                pl.BlockSpec((1, hidden, LANES), lambda i, first: (layer, 0, start // LANES + i)),
+                pl.BlockSpec((1, LANES, hidden), lambda i, first: (layer, start // LANES + i, 0)),
             ],
         ),
-        input_output_aliases={1 + count: 0, 2 + count: 1} if bufs is not None else {},
+        input_output_aliases={3: 0, 4: 1} if bufs is not None else {},
         compiler_params=pltpu.CompilerParams(dimension_semantics=("arbitrary",), vmem_limit_bytes=ALL_VMEM),
         cost_estimate=pl.CostEstimate(flops=4 * size * hidden, bytes_accessed=16 * size * hidden, transcendentals=0),
-    )(first, *kept, *other, *(bufs or ()))
+    )(first, kept, other, *(bufs or ()))
+
+
+def join_place_body(count, layer, start, first_ref, *refs):
+    up_out, down_out, up_ref, down_ref, sem = refs[-5:]
+    first = first_ref[0] == 1
+    kept = jnp.concatenate([r[...] for r in refs[:count]])
+    other = jnp.concatenate([r[...] for r in refs[count : 2 * count]])
+    size = kept.shape[0]
+    down_ref[...] = jnp.where(first, other, kept)
+    down_copy = pltpu.make_async_copy(down_ref, down_out.at[layer, pl.ds(start, size), :], sem.at[0])
+    down_copy.start()
+    up_ref[...] = jnp.where(first, kept, other).T
+    up_copy = pltpu.make_async_copy(up_ref, up_out.at[layer, :, pl.ds(start, size)], sem.at[1])
+    up_copy.start()
+    down_copy.wait()
+    up_copy.wait()
+
+
+def join_place_call(first, pieces, layer, start, bufs):
+    hidden = pieces[0][0].shape[1]
+    size = sum(n for _, _, _, n in pieces)
+    piece_specs = [pl.BlockSpec((n, hidden), lambda i, first, block=low // n: (block, 0)) for _, _, low, n in pieces]
+    any_spec = pl.BlockSpec(memory_space=pl.ANY)
+    count = len(pieces)
+    return pl.pallas_call(
+        functools.partial(join_place_body, count, layer, start),
+        out_shape=[jax.ShapeDtypeStruct(b.shape, b.dtype) for b in bufs],
+        grid_spec=pltpu.PrefetchScalarGridSpec(
+            num_scalar_prefetch=1,
+            grid=(1,),
+            in_specs=piece_specs * 2 + [any_spec] * 2,
+            out_specs=[any_spec] * 2,
+            scratch_shapes=[pltpu.VMEM((hidden, size), F32), pltpu.VMEM((size, hidden), F32), pltpu.SemaphoreType.DMA((2,))],
+        ),
+        input_output_aliases={1 + 2 * count: 0, 2 + 2 * count: 1},
+        compiler_params=pltpu.CompilerParams(dimension_semantics=("arbitrary",), vmem_limit_bytes=ALL_VMEM),
+        cost_estimate=pl.CostEstimate(flops=4 * size * hidden, bytes_accessed=16 * size * hidden, transcendentals=0),
+    )(first, *[p[0] for p in pieces], *[p[1] for p in pieces], *bufs)
 
 
 def solution(mesh):
@@ -386,8 +417,10 @@
             held[1] = lax.dynamic_slice(held[0], (layer, 0, begin, start), (1, rows, seq, size))[0]
             return to_model(held[1], flip)
 
-        held[1] = jnp.where(first, w_up[1], w_down[1])
-        far_w = [None, to_model(held[1], 2)]
+        head = jnp.where(first, w_up[1, :FIRST], w_down[1, :FIRST])
+        w_pair = lax.optimization_barrier((w_up, w_down, head))
+        held[1] = jnp.where(first, w_pair[0][1, FIRST:], w_pair[1][1, FIRST:])
+        far_w = [None, jnp.concatenate([to_model(head, 2), to_model(held[1], 2)])]
         h_one = [h_from(1, 2), h_from(1, 3)]
         h_near = [None, h_from(1, 1)]
         w_pair = lax.optimization_barrier((w_up, w_down, held[1]))
@@ -402,7 +435,7 @@
         packed = []
         for flip in (2, 3):
             packed.append(pack_call(jnp.reshape(me ^ flip, (1,)).astype(jnp.int32), h_saved, 0, small_start, seq))
-        h_small = [[to_model(packed[0][j], 2), to_model(packed[1][j], 3)] for j in range(3)]
+        h_small = [[to_model(packed[0][j], 2), to_model(packed[1][j], 3)] for j in range(4)]
 
         up, down = [{0: w_up} for _ in range(layers)], [{0: w_down} for _ in range(layers)]
         near_up, near_down = to_model(w_up, 1), to_model(w_down, 1)
@@ -423,8 +456,9 @@
             return stay + to_data(away)
 
         def place(pieces, layer, start, bufs):
-            kept, other = zip(*pieces)
-            return place_call(first_flag, kept, other, layer, start, layers, width, bufs)
+            if len(pieces) > 1:
+                return join_place_call(first_flag, pieces, layer, start, bufs)
+            return place_call(first_flag, *pieces[0], layer, start, layers, width, bufs)
 
         carry, dw_0, dw_1 = call(1, grad_out, [h_saved, h_near[1]], (0, 1), None, False)
         near = partial_sum(dw_0, dw_1)
@@ -435,7 +469,7 @@
 
         carry, dw_0, dw_1 = call(0, grad_mid, [h_saved, h_near[0]], (0, 1), None, False)
         near = partial_sum(dw_0, dw_1)
-        bounds = [0, 384, 512, width - SMALL, width]
+        bounds = [0, 384, 448, 576, width - SMALL, width]
         near_part = lax.optimization_barrier(tuple(near[a:b] for a, b in zip(bounds, bounds[1:])))
         pieces = []
 
@@ -451,19 +485,23 @@
         carry, dw_2, dw_3 = wide_call(0, grad_mid, x_saved, h_zero[1], up_pair, down_pair, BLOCKS[0], carry)
         far = partial_sum(dw_2, dw_3)
         exchange(1, far[: bounds[2] - bounds[1]])
+        exchange(2, far[bounds[2] - bounds[1] : bounds[3] - bounds[1]])
         carry, grad_mid, x_saved = paired(carry), paired(grad_mid), paired(x_saved, 1)
         dw_2, dw_3, pre_1 = small_call(0, grad_mid, x_saved, h_small[0], down_pair, small_start, 0, None, None)
-        exchange(2, jnp.concatenate([far[bounds[2] - bounds[1] :], partial_sum(dw_2, dw_3)]))
-        dw_2, dw_3, grad_x = small_call(
-            0, grad_mid, x_saved, h_small[1], down_pair, small_start + SMALL, 0, None, (carry, pre_1, small_up))
-        dw_2, dw_3, pre_2 = small_call(
-            0, grad_mid, x_saved, h_small[2], down_pair, small_start + SMALL, EARLY, (dw_2, dw_3), None)
-        exchange(3, partial_sum(dw_2, dw_3))
-        for half in range(2):
-            grad_x = finish_call(carry, (pre_1, pre_2), small_up, half, grad_x)
-        for unit in range(2):
-            bufs = place([pieces[unit]], 0, bounds[unit], bufs)
-        bufs = place(pieces[2:], 0, bounds[2], bufs)
+        exchange(3, jnp.concatenate([far[bounds[3] - bounds[1] :], partial_sum(dw_2, dw_3)]))
+        last = small_start + SMALL
+        early, late = CHUNKS[0], CHUNKS[0] + CHUNKS[1]
+        dw_2, dw_3, grad_x = small_call(0, grad_mid, x_saved, h_small[1], down_pair, last, 0, None, (carry, pre_1, small_up))
+        dw_2, dw_3, pre_2 = small_call(0, grad_mid, x_saved, h_small[2], down_pair, last, early, (dw_2, dw_3), None)
+        grad_x = finish_call(carry, (pre_1, pre_2), small_up, early, 0, 1, grad_x)
+        dw_2, dw_3, pre_3 = small_call(0, grad_mid, x_saved, h_small[3], down_pair, last, late, (dw_2, dw_3), None)
+        exchange(4, partial_sum(dw_2, dw_3))
+        grad_x = finish_call(carry, (pre_1, pre_2), small_up, early, 1, 1, grad_x)
+        grad_x = finish_call(carry, (pre_1, pre_3), small_up, late, 0, 2, grad_x)
+        bufs = place([pieces[0]], 0, 0, bufs)
+        middle = [(*pieces[1], 0, 64), (*pieces[2], 0, 128), (*pieces[3], 0, 64)]
+        bufs = place(middle, 0, bounds[1], bufs)
+        bufs = place([(*pieces[3], 64, 64), (*pieces[4], 0, 64)], 0, small_start, bufs)
         grad_x = grad_x.reshape(grad_out.shape)
         return grad_x, bufs[0], bufs[1]
 

time: 1650 us -> 1670 us (1.012)
  waiting for transfers between devices: 897 us -> 914 us
    ppermute x14 -> x15, waiting for transfers between devices: 120 us -> 153 us  [to_data(): return lax.ppermute(value, 'data', [(0, 1), (1, 0)])]
    ppermute x34 -> x38, waiting for transfers between devices: 777 us -> 762 us  [to_model(): return lax.ppermute(value, 'model', [(i, i ^ flip) for i in range(n_model)])]
    pallas_call x3 -> x4, Pallas kernels: 43.9 us -> 44 us  [small_call(): pl.pallas_call(functools.partial(small_body, init is not None, finish is...]
  transfers between devices with their start and end apart: 48 -> 53, of which waited for: 12 -> 14; matrix products, arithmetic and copies ran while one was open for 4% -> 4% of each run, Pallas kernels for 37% -> 37%
where the time goes in v5:
time: 1670 us
  waiting for transfers between devices  914 us (55%)
  Pallas kernels  615 us (37%)
  local copies, waits for them, and re-layouts  66.3 us (4%)
  starting transfers between devices  42.8 us (3%)
  other arithmetic  27.8 us (2%)
    ppermute x38, waiting for transfers between devices, to_model(): return lax.ppermute(value, 'model', [(i, i ^ flip) for i in range(n_model)])  762 us
    pallas_call x4, Pallas kernels, block_call(): pl.pallas_call(functools.partial(block_body, carry is not None, final, ro...  439 us
    ppermute x15, waiting for transfers between devices, to_data(): return lax.ppermute(value, 'data', [(0, 1), (1, 0)])  153 us
    squeeze x8, local copies, waits for them, and re-layouts, h_from(): lax.dynamic_slice(held[0], (layer, 0, begin, start), (1, rows, seq, size))  60.6 us
    pallas_call x1, Pallas kernels, wide_call(): pl.pallas_call(functools.partial(wide_body, start), out_shape=[jax.ShapeD...  54.4 us
    pallas_call x4, Pallas kernels, small_call(): pl.pallas_call(functools.partial(small_body, init is not None, finish is...  44 us
  transfers between devices with their start and end apart: 53, of which 14 were waited for; matrix products, arithmetic and copies ran while one was open for 4% of the time, Pallas kernels for 37%

profile of v5, /device:TPU:0, one launch (start us, length us, event | category | flops | bytes accessed | tf_op | source)
XLA Modules:
  0.0 1667.6 jit_solution(17684079851451457295)
XLA Ops:
  1.7 1.5 select_bitcast_fusion.1
  3.3 10.6 dynamic-slice_bitcast_fusion.3
  13.9 10.6 dynamic-slice_bitcast_fusion.2
  24.5 7.2 dynamic-slice_bitcast_fusion.1
  32.5 2.6 collective-permute-start.1
  35.1 2.0 collective-permute-start.2
  37.3 545.1 %collective-permute-done.2 = bf16[192,768]{1,0:T(8,128)(2,1)S(1)} collective-permute-done((bf16[192,768]{1,0:T(8,128)(2,1)S(1)}, bf16[192,768]{1,0:T(8,128)(2,1)S(1)}, u32[]{:S(2)}, u32[]{:S(2)}) %collective-permute-start.2) | collective-permute-done | bytes 294944 | tf_op jit(solution)/shard_map/ppermute | solution.py:398
  582.4 2.1 collective-permute-start.3
  584.5 41.9 %collective-permute-done.3 = bf16[576,768]{1,0:T(8,128)(2,1)S(1)} collective-permute-done((bf16[576,768]{1,0:T(8,128)(2,1)S(1)}, bf16[576,768]{1,0:T(8,128)(2,1)S(1)}, u32[]{:S(2)}, u32[]{:S(2)}) %collective-permute-start.3) | collective-permute-done | bytes 884768 | tf_op jit(solution)/shard_map/ppermute | solution.py:398
  626.5 1.7 collective-permute-start.4
  628.5 26.8 %collective-permute-done.4 = bf16[768,768]{1,0:T(8,128)(2,1)S(1)} collective-permute-done((bf16[768,768]{1,0:T(8,128)(2,1)S(1)}, bf16[768,768]{1,0:T(8,128)(2,1)S(1)}, u32[]{:S(2)}, u32[]{:S(2)}) %collective-permute-start.4) | collective-permute-done | bytes 1179680 | tf_op jit(solution)/shard_map/ppermute | solution.py:401
  655.3 24.2 %collective-permute-done.13 = bf16[768,768]{1,0:T(8,128)(2,1)S(1)} collective-permute-done((bf16[768,768]{1,0:T(8,128)(2,1)S(1)}, bf16[768,768]{1,0:T(8,128)(2,1)S(1)}, u32[]{:S(2)}, u32[]{:S(2)}) %collective-permute-start.13) | collective-permute-done | bytes 1179680 | tf_op jit(solution)/shard_map/ppermute | solution.py:401
  680.6 10.6 dynamic-slice_bitcast_fusion
  691.2 6.2 dynamic-slice_bitcast_fusion.5
  697.4 6.3 dynamic-slice_bitcast_fusion.4
  703.7 3.0 broadcast_select_fusion.2
  706.7 1.6 broadcast_select_fusion
  709.4 119.7 %shard_map.76 = (f32[16,512,768]{2,1,0:T(8,128)}, f32[2,768,768]{2,1,0:T(8,128)}, f32[2,768,768]{2,1,0:T(8,128)}) custom-call(s32[1]{0:T(128)} %bitcast._, bf16[16,512,768]{2,1,0:T(8,128)(2,1)} %refs_0_.3, bf16[2,16,512,768]{3,2,1,0:T(8,128)(2,1)} %x_ref.1, bf16[2,16,2048,768]{3,2,1,0:T(8,128)(2,1)} %hi_ref.3, ...), custom_call_target="tpu_custom_call" | custom-call | flops 77309411328 | bytes 50331648 | tf_op jit(solution)/shard_map/pallas_call | solution.py:113
  831.3 121.2 %shard_map.77 = (bf16[16,512,768]{2,1,0:T(8,128)(2,1)}, f32[2,768,768]{2,1,0:T(8,128)}, f32[2,768,768]{2,1,0:T(8,128)}) custom-call(s32[1]{0:T(128)} %bitcast._, bf16[16,512,768]{2,1,0:T(8,128)(2,1)} %refs_0_.3, bf16[2,16,512,768]{3,2,1,0:T(8,128)(2,1)} %x_ref.1, bf16[16,512,768]{2,1,0:T(8,128)(2,1)} %collective-permute-done.refs_2_, ...), custom_call_target="tpu_custom_call" | custom-call | flops 77309411328 | bytes 50331648 | tf_op jit(solution)/shard_map/pallas_call | solution.py:113
  953.0 119.5 %shard_map.78 = (f32[16,512,768]{2,1,0:T(8,128)}, f32[2,768,768]{2,1,0:T(8,128)}, f32[2,768,768]{2,1,0:T(8,128)}) custom-call(s32[1]{0:T(128)} %bitcast._, bf16[16,512,768]{2,1,0:T(8,128)(2,1)} %get-tuple-element.83.refs_0_.grad_ref, bf16[2,16,512,768]{3,2,1,0:T(8,128)(2,1)} %x_ref.1, bf16[2,16,2048,768]{3,2,1,0:T(8,128)(2,1)} %hi_ref.3, ...), custom_call_target="tpu_custom_call" | custom-call | flops 77309411328 | bytes 50331648 | tf_op jit(solution)/shard_map/pallas_call | solution.py:113
  1073.0 27.5 %collective-permute-done.17.refs_3_ = bf16[16,512,384]{2,1,0:T(8,128)(2,1)} collective-permute-done((bf16[16,512,384]{2,1,0:T(8,128)(2,1)}, bf16[16,512,384]{2,1,0:T(8,128)(2,1)}, u32[]{:S(2)}, u32[]{:S(2)}) %collective-permute-start.17) | collective-permute-done | bytes 6291488 | tf_op jit(solution)/shard_map/ppermute | solution.py:398
  1100.6 78.2 %shard_map.79 = (f32[16,512,768]{2,1,0:T(8,128)}, f32[2,384,768]{2,1,0:T(8,128)}, f32[2,384,768]{2,1,0:T(8,128)}) custom-call(s32[1]{0:T(128)} %bitcast._, bf16[16,512,768]{2,1,0:T(8,128)(2,1)} %get-tuple-element.83.refs_0_.grad_ref, bf16[2,16,512,768]{3,2,1,0:T(8,128)(2,1)} %x_ref.1, bf16[16,512,384]{2,1,0:T(8,128)(2,1)} %collective-permute-done.16.refs_2_, ...), custom_call_target="tpu_custom_call" | custom-call | flops 38654705664 | bytes 50331648 | tf_op jit(solution)/shard_map/pallas_call | solution.py:113
  1179.7 4.6 dynamic-slice_bitcast_fusion.7
  1184.2 4.6 dynamic-slice_bitcast_fusion.6
  1190.4 7.0 shard_map.97
  1198.7 6.3 shard_map.81
  1205.0 1.5 collective-permute-start.25
  1206.5 6.3 shard_map.82
  1213.4 37.7 %collective-permute-done.50 = f32[768,768]{1,0:T(8,128)} collective-permute-done((f32[768,768]{1,0:T(8,128)}, f32[768,768]{1,0:T(8,128)}, u32[]{:S(2)}, u32[]{:S(2)}) %collective-permute-start.50) | collective-permute-done | bytes 2359328 | tf_op jit(solution)/shard_map/ppermute | solution.py:401
  1251.3 4.5 shard_map.95
  1255.8 7.0 shard_map.96
  1262.8 7.0 shard_map.91
  1269.9 4.1 add.67
  1274.0 112.0 %collective-permute-done.21.h_a = bf16[2,512,128]{2,1,0:T(8,128)(2,1)S(1)} collective-permute-done((bf16[2,512,128]{2,1,0:T(8,128)(2,1)S(1)}, bf16[2,512,128]{2,1,0:T(8,128)(2,1)S(1)}, u32[]{:S(2)}, u32[]{:S(2)}) %collective-permute-start.21) | collective-permute-done | bytes 262176 | tf_op jit(solution)/shard_map/ppermute | solution.py:398
  1387.2 4.1 collective-permute-done.22.h_b
  1394.6 1.5 collective-permute-start.51
  1396.1 54.4 %shard_map.80 = (f32[16,512,768]{2,1,0:T(8,128)}, f32[2,256,768]{2,1,0:T(8,128)}, f32[2,256,768]{2,1,0:T(8,128)}) custom-call(bf16[16,512,768]{2,1,0:T(8,128)(2,1)} %get-tuple-element.83.refs_0_.grad_ref, bf16[2,16,512,768]{3,2,1,0:T(8,128)(2,1)} %x_ref.1, bf16[16,512,256]{2,1,0:T(8,128)(2,1)} %collective-permute-done.10.h_a, ...), custom_call_target="tpu_custom_call" | custom-call | flops 25769803776 | bytes 75497472 | tf_op jit(solution)/shard_map/pallas_call | solution.py:191
  1451.1 19.9 %collective-permute-done.48 = f32[768,768]{1,0:T(8,128)} collective-permute-done((f32[768,768]{1,0:T(8,128)}, f32[768,768]{1,0:T(8,128)}, u32[]{:S(2)}, u32[]{:S(2)}) %collective-permute-start.48) | collective-permute-done | bytes 2359328 | tf_op jit(solution)/shard_map/ppermute | solution.py:401
  1471.0 2.0 shard_map.84.refs_2_.up_ref
  1473.0 3.0 add.64
  1477.2 4.2 add_add_fusion.kept_ref
  1481.4 25.8 %collective-permute-done.23.h_a = bf16[3,512,128]{2,1,0:T(8,128)(2,1)S(1)} collective-permute-done((bf16[3,512,128]{2,1,0:T(8,128)(2,1)S(1)}, bf16[3,512,128]{2,1,0:T(8,128)(2,1)S(1)}, u32[]{:S(2)}, u32[]{:S(2)}) %collective-permute-start.23) | collective-permute-done | bytes 393248 | tf_op jit(solution)/shard_map/ppermute | solution.py:398
  1507.3 1.3 collective-permute-start.45
  1509.1 16.8 %shard_map.83 = (f32[2,64,768]{2,1,0:T(8,128)}, f32[2,64,768]{2,1,0:T(8,128)}, bf16[2,8,512,128]{3,2,1,0:T(8,128)(2,1)}) custom-call(bf16[2,8,512,768]{3,2,1,0:T(8,128)(2,1)} %bitcast.38, bf16[2,2,8,512,768]{4,3,2,1,0:T(8,128)(2,1)} %bitcast.30, bf16[8,512,128]{2,1,0:T(8,128)(2,1)} %collective-permute-done.19.h_a, ...), custom_call_target="tpu_custom_call" | custom-call | flops 4831838208 | bytes 25165824 | tf_op jit(solution)/shard_map/pallas_call | solution.py:248
  1526.2 12.7 shard_map.85
  1538.9 2.9 shard_map.92
  1541.7 1.5 collective-permute-start.30
  1543.3 8.2 shard_map.86
  1551.5 6.3 shard_map.87
  1558.6 1.9 shard_map.93
  1561.2 2.7 add.56
  1565.4 2.5 add.65.kept_ref
  1570.0 1.9 shard_map.94
  1571.9 21.3 %collective-permute-done.32 = f32[64,768]{1,0:T(8,128)} collective-permute-done((f32[64,768]{1,0:T(8,128)}, f32[64,768]{1,0:T(8,128)}, u32[]{:S(2)}, u32[]{:S(2)}) %collective-permute-start.32) | collective-permute-done | bytes 196640 | tf_op jit(solution)/shard_map/ppermute | solution.py:401
  1594.3 1.5 add.57
  1599.2 22.8 %collective-permute-done.35 = f32[64,768]{1,0:T(8,128)S(1)} collective-permute-done((f32[64,768]{1,0:T(8,128)S(1)}, f32[64,768]{1,0:T(8,128)S(1)}, u32[]{:S(2)}, u32[]{:S(2)}) %collective-permute-start.35) | collective-permute-done | bytes 196640 | tf_op jit(solution)/shard_map/ppermute | solution.py:401
  1625.5 4.3 collective-permute-done.39
  1635.4 5.4 shard_map.88._
  1640.8 5.4 shard_map.89._
  1646.2 6.0 shard_map.90
  1652.1 5.9 shard_map.98
  1658.0 3.8 shard_map.99
  1661.8 2.7 shard_map.100
  1665.2 2.2 shard_map.101
  (149 shorter events, 38.8 us)
Async XLA Ops:
  24.5 12.7 copy-start.2
  31.6 677.2 %collective-permute-start.7 = (bf16[16,512,768]{2,1,0:T(8,128)(2,1)S(1)}, bf16[16,512,768]{2,1,0:T(8,128)(2,1)}, u32[]{:S(2)}, u32[]{:S(2)}) collective-permute-start(bf16[16,512,768]{2,1,0:T(8,128)(2,1)S(1)} %dynamic-slice_bitcast_fusion.1), channel_id=1, source_target_pairs={{0,1},{1,0},{2,3},{3,2},{4,5},{5,4},{6,7},{7,6}} | collective-permute-start | bytes 37748744 | tf_op jit(solution)/shard_map/ppermute | solution.py:398
  32.5 797.9 %collective-permute-start.1 = (bf16[16,512,768]{2,1,0:T(8,128)(2,1)}, bf16[16,512,768]{2,1,0:T(8,128)(2,1)}, u32[]{:S(2)}, u32[]{:S(2)}) collective-permute-start(bf16[16,512,768]{2,1,0:T(8,128)(2,1)} %dynamic-slice_bitcast_fusion.2), channel_id=1, source_target_pairs={{0,3},{1,2},{2,1},{3,0},{4,7},{5,6},{6,5},{7,4}} | collective-permute-start | bytes 37748744 | tf_op jit(solution)/shard_map/ppermute | solution.py:398
  35.1 796.2 %collective-permute-start = (bf16[16,512,768]{2,1,0:T(8,128)(2,1)}, bf16[16,512,768]{2,1,0:T(8,128)(2,1)}, u32[]{:S(2)}, u32[]{:S(2)}) collective-permute-start(bf16[16,512,768]{2,1,0:T(8,128)(2,1)} %dynamic-slice_bitcast_fusion.3), channel_id=1, source_target_pairs={{0,2},{1,3},{2,0},{3,1},{4,6},{5,7},{6,4},{7,5}} | collective-permute-start | bytes 37748744 | tf_op jit(solution)/shard_map/ppermute | solution.py:398
  35.1 547.3 %collective-permute-start.2 = (bf16[192,768]{1,0:T(8,128)(2,1)S(1)}, bf16[192,768]{1,0:T(8,128)(2,1)S(1)}, u32[]{:S(2)}, u32[]{:S(2)}) collective-permute-start(bf16[192,768]{1,0:T(8,128)(2,1)S(1)} %select_bitcast_fusion.2), channel_id=1, source_target_pairs={{0,2},{1,3},{2,0},{3,1},{4,6},{5,7},{6,4},{7,5}} | collective-permute-start | bytes 884744 | tf_op jit(solution)/shard_map/ppermute | solution.py:398
  37.3 590.9 %collective-permute-start.12 = (bf16[768,768]{1,0:T(8,128)(2,1)S(1)}, bf16[768,768]{1,0:T(8,128)(2,1)S(1)}, u32[]{:S(2)}, u32[]{:S(2)}) collective-permute-start(bf16[768,768]{1,0:T(8,128)(2,1)S(1)} %select_bitcast_fusion), channel_id=1, source_target_pairs={{0,2},{1,3},{2,0},{3,1},{4,6},{5,7},{6,4},{7,5}} | collective-permute-start | bytes 3538952 | tf_op jit(solution)/shard_map/ppermute | solution.py:398
  582.4 44.0 %collective-permute-start.3 = (bf16[576,768]{1,0:T(8,128)(2,1)S(1)}, bf16[576,768]{1,0:T(8,128)(2,1)S(1)}, u32[]{:S(2)}, u32[]{:S(2)}) collective-permute-start(bf16[576,768]{1,0:T(8,128)(2,1)S(1)} %select_bitcast_fusion.1), channel_id=1, source_target_pairs={{0,2},{1,3},{2,0},{3,1},{4,6},{5,7},{6,4},{7,5}} | collective-permute-start | bytes 2654216 | tf_op jit(solution)/shard_map/ppermute | solution.py:398
  626.5 28.9 %collective-permute-start.4 = (bf16[768,768]{1,0:T(8,128)(2,1)S(1)}, bf16[768,768]{1,0:T(8,128)(2,1)S(1)}, u32[]{:S(2)}, u32[]{:S(2)}) collective-permute-start(bf16[768,768]{1,0:T(8,128)(2,1)S(1)} %constant_dynamic-update-slice_fusion), channel_id=1, source_target_pairs={{0,4},{4,0},{1,5},{5,1},{2,6},{6,2},{3,7},{7,3}} | collective-permute-start | bytes 3538952 | tf_op jit(solution)/shard_map/ppermute | solution.py:401
  628.2 27.2 %copy-start.6 = (bf16[768,768]{1,0:T(8,128)(2,1)}, bf16[768,768]{1,0:T(8,128)(2,1)S(1)}, u32[]{:S(2)}) copy-start(bf16[768,768]{1,0:T(8,128)(2,1)S(1)} %collective-permute-done.12) | copy-start | bytes 3538948
  628.2 51.3 %collective-permute-start.13 = (bf16[768,768]{1,0:T(8,128)(2,1)S(1)}, bf16[768,768]{1,0:T(8,128)(2,1)S(1)}, u32[]{:S(2)}, u32[]{:S(2)}) collective-permute-start(bf16[768,768]{1,0:T(8,128)(2,1)S(1)} %collective-permute-done.12), channel_id=1, source_target_pairs={{0,4},{4,0},{1,5},{5,1},{2,6},{6,2},{3,7},{7,3}} | collective-permute-start | bytes 3538952 | tf_op jit(solution)/shard_map/ppermute | solution.py:401
  655.3 24.2 %copy-start.8 = (bf16[768,768]{1,0:T(8,128)(2,1)}, bf16[768,768]{1,0:T(8,128)(2,1)S(1)}, u32[]{:S(2)}) copy-start(bf16[768,768]{1,0:T(8,128)(2,1)S(1)} %collective-permute-done.4) | copy-start | bytes 3538948
  655.3 53.0 %collective-permute-start.8 = (bf16[2,768,768]{2,1,0:T(8,128)(2,1)S(1)}, bf16[2,768,768]{2,1,0:T(8,128)(2,1)}, u32[]{:S(2)}, u32[]{:S(2)}) collective-permute-start(bf16[2,768,768]{2,1,0:T(8,128)(2,1)S(1)} %copy-done.2), channel_id=1, source_target_pairs={{0,1},{1,0},{2,3},{3,2},{4,5},{5,4},{6,7},{7,6}} | collective-permute-start | bytes 7077896 | tf_op jit(solution)/shard_map/ppermute | solution.py:398
  680.5 28.3 %collective-permute-start.9 = (bf16[2,768,768]{2,1,0:T(8,128)(2,1)S(1)}, bf16[2,768,768]{2,1,0:T(8,128)(2,1)}, u32[]{:S(2)}, u32[]{:S(2)}) collective-permute-start(bf16[2,768,768]{2,1,0:T(8,128)(2,1)S(1)} %copy-done.1), channel_id=1, source_target_pairs={{0,1},{1,0},{2,3},{3,2},{4,5},{5,4},{6,7},{7,6}} | collective-permute-start | bytes 7077896 | tf_op jit(solution)/shard_map/ppermute | solution.py:398
  708.4 244.2 %collective-permute-start.18 = (bf16[16,512,768]{2,1,0:T(8,128)(2,1)}, bf16[16,512,768]{2,1,0:T(8,128)(2,1)}, u32[]{:S(2)}, u32[]{:S(2)}) collective-permute-start(bf16[16,512,768]{2,1,0:T(8,128)(2,1)} %dynamic-slice_bitcast_fusion), channel_id=1, source_target_pairs={{0,1},{1,0},{2,3},{3,2},{4,5},{5,4},{6,7},{7,6}} | collective-permute-start | bytes 37748744 | tf_op jit(solution)/shard_map/ppermute | solution.py:398
  708.9 120.2 %collective-permute-start.5 = (bf16[768,768]{1,0:T(8,128)(2,1)}, bf16[768,768]{1,0:T(8,128)(2,1)}, u32[]{:S(2)}, u32[]{:S(2)}) collective-permute-start(bf16[768,768]{1,0:T(8,128)(2,1)} %get-tuple-element.158.refs_4_), channel_id=1, source_target_pairs={{0,1},{1,0},{2,3},{3,2},{4,5},{5,4},{6,7},{7,6}} | collective-permute-start | bytes 3538952 | tf_op jit(solution)/shard_map/ppermute | solution.py:398
  708.9 121.4 %collective-permute-start.6 = (bf16[768,768]{1,0:T(8,128)(2,1)}, bf16[768,768]{1,0:T(8,128)(2,1)}, u32[]{:S(2)}, u32[]{:S(2)}) collective-permute-start(bf16[768,768]{1,0:T(8,128)(2,1)} %get-tuple-element.157.refs_6_), channel_id=1, source_target_pairs={{0,1},{1,0},{2,3},{3,2},{4,5},{5,4},{6,7},{7,6}} | collective-permute-start | bytes 3538952 | tf_op jit(solution)/shard_map/ppermute | solution.py:398
  829.1 271.4 %collective-permute-start.16 = (bf16[16,512,384]{2,1,0:T(8,128)(2,1)}, bf16[16,512,384]{2,1,0:T(8,128)(2,1)}, u32[]{:S(2)}, u32[]{:S(2)}) collective-permute-start(bf16[16,512,384]{2,1,0:T(8,128)(2,1)} %dynamic-slice_bitcast_fusion.5), channel_id=1, source_target_pairs={{0,2},{1,3},{2,0},{3,1},{4,6},{5,7},{6,4},{7,5}} | collective-permute-start | bytes 18874376 | tf_op jit(solution)/shard_map/ppermute | solution.py:398
  830.3 270.3 %collective-permute-start.17 = (bf16[16,512,384]{2,1,0:T(8,128)(2,1)}, bf16[16,512,384]{2,1,0:T(8,128)(2,1)}, u32[]{:S(2)}, u32[]{:S(2)}) collective-permute-start(bf16[16,512,384]{2,1,0:T(8,128)(2,1)} %dynamic-slice_bitcast_fusion.4), channel_id=1, source_target_pairs={{0,3},{1,2},{2,1},{3,0},{4,7},{5,6},{6,5},{7,4}} | collective-permute-start | bytes 18874376 | tf_op jit(solution)/shard_map/ppermute | solution.py:398
  830.4 242.1 %collective-permute-start.14 = (bf16[768,768]{1,0:T(8,128)(2,1)}, bf16[768,768]{1,0:T(8,128)(2,1)}, u32[]{:S(2)}, u32[]{:S(2)}) collective-permute-start(bf16[768,768]{1,0:T(8,128)(2,1)} %get-tuple-element.156.refs_4_.up_a), channel_id=1, source_target_pairs={{0,1},{1,0},{2,3},{3,2},{4,5},{5,4},{6,7},{7,6}} | collective-permute-start | bytes 3538952 | tf_op jit(solution)/shard_map/ppermute | solution.py:398
  831.3 241.4 %collective-permute-start.15 = (bf16[768,768]{1,0:T(8,128)(2,1)}, bf16[768,768]{1,0:T(8,128)(2,1)}, u32[]{:S(2)}, u32[]{:S(2)}) collective-permute-start(bf16[768,768]{1,0:T(8,128)(2,1)} %get-tuple-element.155.refs_6_.down_a), channel_id=1, source_target_pairs={{0,1},{1,0},{2,3},{3,2},{4,5},{5,4},{6,7},{7,6}} | collective-permute-start | bytes 3538952 | tf_op jit(solution)/shard_map/ppermute | solution.py:398
  952.5 237.1 %collective-permute-start.49 = (f32[2,768,768]{2,1,0:T(8,128)}, f32[2,768,768]{2,1,0:T(8,128)}, u32[]{:S(2)}, u32[]{:S(2)}) collective-permute-start(f32[2,768,768]{2,1,0:T(8,128)} %get-tuple-element.140), channel_id=1, source_target_pairs={{0,1},{1,0},{2,3},{3,2},{4,5},{5,4},{6,7},{7,6}} | collective-permute-start | bytes 14155784 | tf_op jit(solution)/shard_map/ppermute | solution.py:398
  1072.5 132.5 %collective-permute-start.47 = (f32[2,768,768]{2,1,0:T(8,128)}, f32[2,768,768]{2,1,0:T(8,128)}, u32[]{:S(2)}, u32[]{:S(2)}) collective-permute-start(f32[2,768,768]{2,1,0:T(8,128)} %get-tuple-element.136), channel_id=1, source_target_pairs={{0,1},{1,0},{2,3},{3,2},{4,5},{5,4},{6,7},{7,6}} | collective-permute-start | bytes 14155784 | tf_op jit(solution)/shard_map/ppermute | solution.py:398
  1072.7 140.1 %collective-permute-start.27 = (f32[2,768,768]{2,1,0:T(8,128)}, f32[2,768,768]{2,1,0:T(8,128)}, u32[]{:S(2)}, u32[]{:S(2)}) collective-permute-start(f32[2,768,768]{2,1,0:T(8,128)} %get-tuple-element.111), channel_id=1, source_target_pairs={{0,1},{1,0},{2,3},{3,2},{4,5},{5,4},{6,7},{7,6}} | collective-permute-start | bytes 14155784 | tf_op jit(solution)/shard_map/ppermute | solution.py:398
  1178.8 18.7 %collective-permute-start.43 = (f32[2,384,768]{2,1,0:T(8,128)}, f32[2,384,768]{2,1,0:T(8,128)}, u32[]{:S(2)}, u32[]{:S(2)}) collective-permute-start(f32[2,384,768]{2,1,0:T(8,128)} %get-tuple-element.132), channel_id=1, source_target_pairs={{0,1},{1,0},{2,3},{3,2},{4,5},{5,4},{6,7},{7,6}} | collective-permute-start | bytes 7077896 | tf_op jit(solution)/shard_map/ppermute | solution.py:398
  1188.8 204.6 %collective-permute-start.11 = (bf16[16,512,256]{2,1,0:T(8,128)(2,1)}, bf16[16,512,256]{2,1,0:T(8,128)(2,1)}, u32[]{:S(2)}, u32[]{:S(2)}) collective-permute-start(bf16[16,512,256]{2,1,0:T(8,128)(2,1)} %dynamic-slice_bitcast_fusion.6), channel_id=1, source_target_pairs={{0,3},{1,2},{2,1},{3,0},{4,7},{5,6},{6,5},{7,4}} | collective-permute-start | bytes 12582920 | tf_op jit(solution)/shard_map/ppermute | solution.py:398
  1189.6 205.0 %collective-permute-start.10 = (bf16[16,512,256]{2,1,0:T(8,128)(2,1)}, bf16[16,512,256]{2,1,0:T(8,128)(2,1)}, u32[]{:S(2)}, u32[]{:S(2)}) collective-permute-start(bf16[16,512,256]{2,1,0:T(8,128)(2,1)} %dynamic-slice_bitcast_fusion.7), channel_id=1, source_target_pairs={{0,2},{1,3},{2,0},{3,1},{4,6},{5,7},{6,4},{7,5}} | collective-permute-start | bytes 12582920 | tf_op jit(solution)/shard_map/ppermute | solution.py:398
  1197.5 53.7 %collective-permute-start.50 = (f32[768,768]{1,0:T(8,128)}, f32[768,768]{1,0:T(8,128)}, u32[]{:S(2)}, u32[]{:S(2)}) collective-permute-start(f32[768,768]{1,0:T(8,128)} %get-tuple-element.142), channel_id=1, source_target_pairs={{0,4},{4,0},{1,5},{5,1},{2,6},{6,2},{3,7},{7,3}} | collective-permute-start | bytes 7077896 | tf_op jit(solution)/shard_map/ppermute | solution.py:401
  1205.0 187.5 %collective-permute-start.25 = (bf16[3,512,128]{2,1,0:T(8,128)(2,1)}, bf16[3,512,128]{2,1,0:T(8,128)(2,1)S(1)}, u32[]{:S(2)}, u32[]{:S(2)}) collective-permute-start(bf16[3,512,128]{2,1,0:T(8,128)(2,1)} %get-tuple-element.101), channel_id=1, source_target_pairs={{0,2},{1,3},{2,0},{3,1},{4,6},{5,7},{6,4},{7,5}} | collective-permute-start | bytes 1179656 | tf_op jit(solution)/shard_map/ppermute | solution.py:398
  1212.9 173.1 %collective-permute-start.21 = (bf16[2,512,128]{2,1,0:T(8,128)(2,1)S(1)}, bf16[2,512,128]{2,1,0:T(8,128)(2,1)S(1)}, u32[]{:S(2)}, u32[]{:S(2)}) collective-permute-start(bf16[2,512,128]{2,1,0:T(8,128)(2,1)S(1)} %copy-done.22), channel_id=1, source_target_pairs={{0,2},{1,3},{2,0},{3,1},{4,6},{5,7},{6,4},{7,5}} | collective-permute-start | bytes 786440 | tf_op jit(solution)/shard_map/ppermute | solution.py:398
  1251.2 140.1 %collective-permute-start.22 = (bf16[2,512,128]{2,1,0:T(8,128)(2,1)}, bf16[2,512,128]{2,1,0:T(8,128)(2,1)}, u32[]{:S(2)}, u32[]{:S(2)}) collective-permute-start(bf16[2,512,128]{2,1,0:T(8,128)(2,1)} %get-tuple-element.98), channel_id=1, source_target_pairs={{0,3},{1,2},{2,1},{3,0},{4,7},{5,6},{6,5},{7,4}} | collective-permute-start | bytes 786440 | tf_op jit(solution)/shard_map/ppermute | solution.py:398
  1386.7 63.8 %collective-permute-start.26 = (bf16[3,512,128]{2,1,0:T(8,128)(2,1)}, bf16[3,512,128]{2,1,0:T(8,128)(2,1)S(1)}, u32[]{:S(2)}, u32[]{:S(2)}) collective-permute-start(bf16[3,512,128]{2,1,0:T(8,128)(2,1)} %get-tuple-element.102), channel_id=1, source_target_pairs={{0,3},{1,2},{2,1},{3,0},{4,7},{5,6},{6,5},{7,4}} | collective-permute-start | bytes 1179656 | tf_op jit(solution)/shard_map/ppermute | solution.py:398
  1391.3 59.3 %collective-permute-start.44 = (f32[384,768]{1,0:T(8,128)}, f32[384,768]{1,0:T(8,128)}, u32[]{:S(2)}, u32[]{:S(2)}) collective-permute-start(f32[384,768]{1,0:T(8,128)} %get-tuple-element.134), channel_id=1, source_target_pairs={{0,4},{4,0},{1,5},{5,1},{2,6},{6,2},{3,7},{7,3}} | collective-permute-start | bytes 3538952 | tf_op jit(solution)/shard_map/ppermute | solution.py:401
  1392.6 58.0 %copy-start.12 = (bf16[3,512,128]{2,1,0:T(8,128)(2,1)}, bf16[3,512,128]{2,1,0:T(8,128)(2,1)S(1)}, u32[]{:S(2)}) copy-start(bf16[3,512,128]{2,1,0:T(8,128)(2,1)S(1)} %collective-permute-done.25.h_a) | copy-start | bytes 1179652
  1392.6 78.4 %collective-permute-start.48 = (f32[768,768]{1,0:T(8,128)}, f32[768,768]{1,0:T(8,128)}, u32[]{:S(2)}, u32[]{:S(2)}) collective-permute-start(f32[768,768]{1,0:T(8,128)} %get-tuple-element.138), channel_id=1, source_target_pairs={{0,4},{4,0},{1,5},{5,1},{2,6},{6,2},{3,7},{7,3}} | collective-permute-start | bytes 7077896 | tf_op jit(solution)/shard_map/ppermute | solution.py:401
  1393.3 167.1 %collective-permute-start.28 = (f32[768,768]{1,0:T(8,128)}, f32[768,768]{1,0:T(8,128)}, u32[]{:S(2)}, u32[]{:S(2)}) collective-permute-start(f32[768,768]{1,0:T(8,128)} %get-tuple-element.113), channel_id=1, source_target_pairs={{0,4},{4,0},{1,5},{5,1},{2,6},{6,2},{3,7},{7,3}} | collective-permute-start | bytes 7077896 | tf_op jit(solution)/shard_map/ppermute | solution.py:401
  1394.6 81.4 %collective-permute-start.51 = (f32[768,768]{1,0:T(8,128)}, f32[768,768]{1,0:T(8,128)}, u32[]{:S(2)}, u32[]{:S(2)}) collective-permute-start(f32[768,768]{1,0:T(8,128)} %add.67), channel_id=1, source_target_pairs={{0,2},{1,3},{2,0},{3,1},{4,6},{5,7},{6,4},{7,5}} | collective-permute-start | bytes 7077896 | tf_op jit(solution)/shard_map/ppermute | solution.py:398
  1450.5 25.4 %copy-start.13 = (bf16[3,512,128]{2,1,0:T(8,128)(2,1)}, bf16[3,512,128]{2,1,0:T(8,128)(2,1)S(1)}, u32[]{:S(2)}) copy-start(bf16[3,512,128]{2,1,0:T(8,128)(2,1)S(1)} %collective-permute-done.26.h_b) | copy-start | bytes 1179652
  1450.5 75.4 %collective-permute-start.29 = (f32[2,256,768]{2,1,0:T(8,128)}, f32[2,256,768]{2,1,0:T(8,128)}, u32[]{:S(2)}, u32[]{:S(2)}) collective-permute-start(f32[2,256,768]{2,1,0:T(8,128)} %get-tuple-element.116), channel_id=1, source_target_pairs={{0,1},{1,0},{2,3},{3,2},{4,5},{5,4},{6,7},{7,6}} | collective-permute-start | bytes 4718600 | tf_op jit(solution)/shard_map/ppermute | solution.py:398
  1450.6 56.7 %collective-permute-start.19 = (bf16[8,512,128]{2,1,0:T(8,128)(2,1)}, bf16[8,512,128]{2,1,0:T(8,128)(2,1)}, u32[]{:S(2)}, u32[]{:S(2)}) collective-permute-start(bf16[8,512,128]{2,1,0:T(8,128)(2,1)} %get-tuple-element.94), channel_id=1, source_target_pairs={{0,2},{1,3},{2,0},{3,1},{4,6},{5,7},{6,4},{7,5}} | collective-permute-start | bytes 3145736 | tf_op jit(solution)/shard_map/ppermute | solution.py:398
  1471.0 37.6 %collective-permute-start.20 = (bf16[8,512,128]{2,1,0:T(8,128)(2,1)}, bf16[8,512,128]{2,1,0:T(8,128)(2,1)}, u32[]{:S(2)}, u32[]{:S(2)}) collective-permute-start(bf16[8,512,128]{2,1,0:T(8,128)(2,1)} %get-tuple-element.95), channel_id=1, source_target_pairs={{0,3},{1,2},{2,1},{3,0},{4,7},{5,6},{6,5},{7,4}} | collective-permute-start | bytes 3145736 | tf_op jit(solution)/shard_map/ppermute | solution.py:398
  1476.0 31.3 %collective-permute-start.23 = (bf16[3,512,128]{2,1,0:T(8,128)(2,1)S(1)}, bf16[3,512,128]{2,1,0:T(8,128)(2,1)S(1)}, u32[]{:S(2)}, u32[]{:S(2)}) collective-permute-start(bf16[3,512,128]{2,1,0:T(8,128)(2,1)S(1)} %copy-done.21), channel_id=1, source_target_pairs={{0,2},{1,3},{2,0},{3,1},{4,6},{5,7},{6,4},{7,5}} | collective-permute-start | bytes 1179656 | tf_op jit(solution)/shard_map/ppermute | solution.py:398
  1507.2 18.7 %copy-start.14 = (bf16[3,512,128]{2,1,0:T(8,128)(2,1)}, bf16[3,512,128]{2,1,0:T(8,128)(2,1)S(1)}, u32[]{:S(2)}) copy-start(bf16[3,512,128]{2,1,0:T(8,128)(2,1)S(1)} %collective-permute-done.23.h_a) | copy-start | bytes 1179652
  1507.3 34.5 %collective-permute-start.24 = (bf16[3,512,128]{2,1,0:T(8,128)(2,1)}, bf16[3,512,128]{2,1,0:T(8,128)(2,1)S(1)}, u32[]{:S(2)}, u32[]{:S(2)}) collective-permute-start(bf16[3,512,128]{2,1,0:T(8,128)(2,1)} %get-tuple-element.100), channel_id=1, source_target_pairs={{0,3},{1,2},{2,1},{3,0},{4,7},{5,6},{6,5},{7,4}} | collective-permute-start | bytes 1179656 | tf_op jit(solution)/shard_map/ppermute | solution.py:398
  1507.3 58.2 %collective-permute-start.45 = (f32[384,768]{1,0:T(8,128)}, f32[384,768]{1,0:T(8,128)}, u32[]{:S(2)}, u32[]{:S(2)}) collective-permute-start(f32[384,768]{1,0:T(8,128)} %add.64), channel_id=1, source_target_pairs={{0,2},{1,3},{2,0},{3,1},{4,6},{5,7},{6,4},{7,5}} | collective-permute-start | bytes 3538952 | tf_op jit(solution)/shard_map/ppermute | solution.py:398
  1508.6 126.0 %collective-permute-start.52 = (f32[768,768]{1,0:T(8,128)}, f32[768,768]{1,0:T(8,128)}, u32[]{:S(2)}, u32[]{:S(2)}) collective-permute-start(f32[768,768]{1,0:T(8,128)} %add_add_fusion.kept_ref), channel_id=1, source_target_pairs={{0,4},{4,0},{1,5},{5,1},{2,6},{6,2},{3,7},{7,3}} | collective-permute-start | bytes 7077896 | tf_op jit(solution)/shard_map/ppermute | solution.py:401
  1525.9 31.9 %collective-permute-start.31 = (f32[2,64,768]{2,1,0:T(8,128)}, f32[2,64,768]{2,1,0:T(8,128)S(1)}, u32[]{:S(2)}, u32[]{:S(2)}) collective-permute-start(f32[2,64,768]{2,1,0:T(8,128)} %get-tuple-element.120), channel_id=1, source_target_pairs={{0,1},{1,0},{2,3},{3,2},{4,5},{5,4},{6,7},{7,6}} | collective-permute-start | bytes 1179656 | tf_op jit(solution)/shard_map/ppermute | solution.py:398
  1541.7 52.5 %collective-permute-start.30 = (f32[256,768]{1,0:T(8,128)}, f32[256,768]{1,0:T(8,128)}, u32[]{:S(2)}, u32[]{:S(2)}) collective-permute-start(f32[256,768]{1,0:T(8,128)} %get-tuple-element.118), channel_id=1, source_target_pairs={{0,4},{4,0},{1,5},{5,1},{2,6},{6,2},{3,7},{7,3}} | collective-permute-start | bytes 2359304 | tf_op jit(solution)/shard_map/ppermute | solution.py:401
  1557.8 11.4 collective-permute-start.34
  1560.5 32.7 %collective-permute-start.32 = (f32[64,768]{1,0:T(8,128)}, f32[64,768]{1,0:T(8,128)}, u32[]{:S(2)}, u32[]{:S(2)}) collective-permute-start(f32[64,768]{1,0:T(8,128)} %get-tuple-element.122), channel_id=1, source_target_pairs={{0,4},{4,0},{1,5},{5,1},{2,6},{6,2},{3,7},{7,3}} | collective-permute-start | bytes 589832 | tf_op jit(solution)/shard_map/ppermute | solution.py:401
  1567.9 90.1 %collective-permute-start.46 = (f32[384,768]{1,0:T(8,128)}, f32[384,768]{1,0:T(8,128)}, u32[]{:S(2)}, u32[]{:S(2)}) collective-permute-start(f32[384,768]{1,0:T(8,128)} %add.65.kept_ref), channel_id=1, source_target_pairs={{0,4},{4,0},{1,5},{5,1},{2,6},{6,2},{3,7},{7,3}} | collective-permute-start | bytes 3538952 | tf_op jit(solution)/shard_map/ppermute | solution.py:401
  1594.3 29.0 %copy-start.19 = (f32[64,768]{1,0:T(8,128)S(1)}, f32[64,768]{1,0:T(8,128)}, u32[]{:S(2)}) copy-start(f32[64,768]{1,0:T(8,128)} %get-tuple-element.126) | copy-start | bytes 589828
  1595.8 29.7 %copy-start.5 = (f32[128,768]{1,0:T(8,128)S(1)}, f32[128,768]{1,0:T(8,128)}, u32[]{:S(2)}) copy-start(f32[128,768]{1,0:T(8,128)} %get-tuple-element.114) | copy-start | bytes 1179652
  1595.8 35.2 %copy-start.11 = (f32[64,768]{1,0:T(8,128)S(1)}, f32[64,768]{1,0:T(8,128)}, u32[]{:S(2)}) copy-start(f32[64,768]{1,0:T(8,128)} %get-tuple-element.128) | copy-start | bytes 589828
  1595.8 27.5 %collective-permute-start.40 = (f32[128,768]{1,0:T(8,128)S(1)}, f32[128,768]{1,0:T(8,128)S(1)}, u32[]{:S(2)}, u32[]{:S(2)}) collective-permute-start(f32[128,768]{1,0:T(8,128)S(1)} %slice.63), channel_id=1, source_target_pairs={{0,2},{1,3},{2,0},{3,1},{4,6},{5,7},{6,4},{7,5}} | collective-permute-start | bytes 1179656 | tf_op jit(solution)/shard_map/ppermute | solution.py:398
  1597.2 27.0 %collective-permute-start.33 = (f32[128,768]{1,0:T(8,128)S(1)}, f32[128,768]{1,0:T(8,128)S(1)}, u32[]{:S(2)}, u32[]{:S(2)}) collective-permute-start(f32[128,768]{1,0:T(8,128)S(1)} %pad_maximum_fusion), channel_id=1, source_target_pairs={{0,2},{1,3},{2,0},{3,1},{4,6},{5,7},{6,4},{7,5}} | collective-permute-start | bytes 1179656 | tf_op jit(solution)/shard_map/ppermute | solution.py:398
  1598.0 24.1 %collective-permute-start.35 = (f32[64,768]{1,0:T(8,128)S(1)}, f32[64,768]{1,0:T(8,128)S(1)}, u32[]{:S(2)}, u32[]{:S(2)}) collective-permute-start(f32[64,768]{1,0:T(8,128)S(1)} %copy-done.23), channel_id=1, source_target_pairs={{0,4},{4,0},{1,5},{5,1},{2,6},{6,2},{3,7},{7,3}} | collective-permute-start | bytes 589832 | tf_op jit(solution)/shard_map/ppermute | solution.py:401
  1622.0 7.8 collective-permute-start.39
  1623.3 9.3 collective-permute-start.36
  1624.2 16.6 copy-start.4
  1624.2 37.6 %collective-permute-start.42 = (f32[128,768]{1,0:T(8,128)S(1)}, f32[128,768]{1,0:T(8,128)}, u32[]{:S(2)}, u32[]{:S(2)}) collective-permute-start(f32[128,768]{1,0:T(8,128)S(1)} %add.63.refs_1_), channel_id=1, source_target_pairs={{0,4},{4,0},{1,5},{5,1},{2,6},{6,2},{3,7},{7,3}} | collective-permute-start | bytes 1179656 | tf_op jit(solution)/shard_map/ppermute | solution.py:401
  1625.5 15.2 copy-start
  1629.8 32.0 %collective-permute-start.37 = (f32[128,768]{1,0:T(8,128)S(1)}, f32[128,768]{1,0:T(8,128)}, u32[]{:S(2)}, u32[]{:S(2)}) collective-permute-start(f32[128,768]{1,0:T(8,128)S(1)} %add.59.refs_2_.refs_0_), channel_id=1, source_target_pairs={{0,4},{4,0},{1,5},{5,1},{2,6},{6,2},{3,7},{7,3}} | collective-permute-start | bytes 1179656 | tf_op jit(solution)/shard_map/ppermute | solution.py:401
  1632.6 29.2 %collective-permute-start.41 = (f32[64,768]{1,0:T(8,128)}, f32[64,768]{1,0:T(8,128)}, u32[]{:S(2)}, u32[]{:S(2)}) collective-permute-start(f32[64,768]{1,0:T(8,128)} %add.62.refs_0_), channel_id=1, source_target_pairs={{0,4},{4,0},{1,5},{5,1},{2,6},{6,2},{3,7},{7,3}} | collective-permute-start | bytes 589832 | tf_op jit(solution)/shard_map/ppermute | solution.py:401
  1634.6 29.9 %collective-permute-start.38 = (f32[64,768]{1,0:T(8,128)}, f32[64,768]{1,0:T(8,128)S(1)}, u32[]{:S(2)}, u32[]{:S(2)}) collective-permute-start(f32[64,768]{1,0:T(8,128)} %add.61.refs_1_), channel_id=1, source_target_pairs={{0,4},{4,0},{1,5},{5,1},{2,6},{6,2},{3,7},{7,3}} | collective-permute-start | bytes 589832 | tf_op jit(solution)/shard_map/ppermute | solution.py:401
  (13 other events, 41.4 us)

commit v6 on v5

--- a/solution.py
+++ b/solution.py
@@ -13,7 +13,7 @@
 BLOCKS = (384, 256)
 LANES = 128
 SMALL = 64
-CHUNKS = (3, 3, 2)
+CHUNKS = (4, 2, 2)
 FIRST = 192
 ALL_VMEM = 66_000_000
 
@@ -205,25 +205,26 @@
     refs = list(refs)
     carry_ref, early_ref, up_ref = (refs.pop(0) for _ in range(3)) if finish else (None,) * 3
     dw_pair, out_ref = refs[-3:-1], refs[-1]
+    seq, hidden = grad_ref.shape[2:]
 
     @pl.when(pl.program_id(0) == 0)
     def _():
         for i, dw in enumerate(dw_pair):
             dw[...] = refs[i][...] if has_init else jnp.zeros_like(dw)
 
-    h_pair = swap_lanes(h_a[0].astype(F32), h_b[0].astype(F32))
-    down = jnp.concatenate([down_a[...], down_b[...]])
-    for r, h in enumerate(h_pair):
-        grad, x = grad_ref[r, 0], x_ref[0, r, 0]
-        pre, act = unit_grads(grad, h, down)
-        for kind, part in enumerate((dot(pre, x, 0, 0), dot(act, grad, 0, 0))):
-            dw_pair[0][kind] += part[:SMALL]
-            dw_pair[1][kind] += part[SMALL:]
+    h = jnp.concatenate(swap_lanes(h_a[0].astype(F32), h_b[0].astype(F32)))
+    grad, x = grad_ref[...].reshape(2 * seq, hidden), x_ref[...].reshape(2 * seq, hidden)
+    pre, act = unit_grads(grad, h, jnp.concatenate([down_a[...], down_b[...]]))
+    for kind, part in enumerate((dot(pre, x, 0, 0), dot(act, grad, 0, 0))):
+        dw_pair[0][kind] += part[:SMALL]
+        dw_pair[1][kind] += part[SMALL:]
+    for r in range(2):
+        row = pre[r * seq : (r + 1) * seq]
         if finish:
-            total = carry_ref[r, 0] + dot(jnp.concatenate([early_ref[r, 0], pre], axis=1), up_ref[...], 1, 1)
+            total = carry_ref[r, 0] + dot(jnp.concatenate([early_ref[r, 0], row], axis=1), up_ref[...], 1, 1)
             out_ref[r, 0] = total.astype(BF16)
         else:
-            out_ref[r, 0] = pre
+            out_ref[r, 0] = row
 
 
 def paired(value, axis=0):
@@ -231,31 +232,35 @@
     return value.reshape(shape[:axis] + (2, shape[axis] // 2) + shape[axis + 1 :])
 
 
-def small_call(layer, grad, x_saved, h_pair, down_pair, start, first_pair, init, finish):
+def small_call(layer, grad, x_saved, h_pair, down_pair, start, first_pair, init=None, finish=None, pre=None, pre_pairs=None, pre_first=0):
     _, _, seq, hidden = grad.shape
     pairs = h_pair[0].shape[0]
     row_spec = pl.BlockSpec((2, 1, seq, hidden), lambda b: (0, b + first_pair, 0, 0))
-    pre_spec = pl.BlockSpec((2, 1, seq, LANES), lambda b: (0, b, 0, 0))
+    early_spec = pl.BlockSpec((2, 1, seq, LANES), lambda b: (0, b + first_pair, 0, 0))
+    pre_spec = pl.BlockSpec((2, 1, seq, LANES), lambda b: (0, b + pre_first, 0, 0))
     h_spec = pl.BlockSpec((1, seq, LANES), lambda b: (b, 0, 0))
     down_spec = pl.BlockSpec((SMALL, hidden), lambda b: (start // SMALL, 0))
     dw_shape = (2, SMALL, hidden)
     dw_spec = pl.BlockSpec(dw_shape, lambda b: (0, 0, 0))
     in_specs = [row_spec, pl.BlockSpec((1, 2, 1, seq, hidden), lambda b: (layer, 0, b + first_pair, 0, 0)), h_spec, h_spec, down_spec, down_spec]
     if finish:
-        in_specs += [row_spec, pre_spec, pl.BlockSpec(finish[2].shape, lambda b: (0, 0))]
+        in_specs += [row_spec, early_spec, pl.BlockSpec(finish[2].shape, lambda b: (0, 0))]
     if init:
         in_specs += [dw_spec] * 2
+    if pre is not None:
+        in_specs.append(pl.BlockSpec(memory_space=pl.ANY))
     return pl.pallas_call(
         functools.partial(small_body, init is not None, finish is not None),
         out_shape=[jax.ShapeDtypeStruct(dw_shape, F32)] * 2
-        + [jax.ShapeDtypeStruct(grad.shape if finish else (2, pairs, seq, LANES), BF16)],
+        + [jax.ShapeDtypeStruct(grad.shape if finish else (2, pre_pairs or pairs, seq, LANES), BF16)],
         grid=(pairs,),
         in_specs=in_specs,
         out_specs=[dw_spec, dw_spec, row_spec if finish else pre_spec],
+        input_output_aliases={} if pre is None else {len(in_specs) - 1: 2},
         compiler_params=pltpu.CompilerParams(dimension_semantics=("arbitrary",), vmem_limit_bytes=ALL_VMEM),
         cost_estimate=pl.CostEstimate(
             flops=24 * pairs * seq * hidden * SMALL, bytes_accessed=8 * pairs * seq * hidden, transcendentals=4 * pairs * seq * SMALL),
-    )(grad, x_saved, *h_pair, *down_pair, *(finish or ()), *(init or ()))
+    )(grad, x_saved, *h_pair, *down_pair, *(finish or ()), *(init or ()), *(() if pre is None else (pre,)))
 
 
 def join_body(up_a, up_b, out_ref):
@@ -464,7 +469,8 @@
         near = partial_sum(dw_0, dw_1)
         grad_mid, dw_2, dw_3 = call(1, grad_out, h_one, (2, 3), carry, True)
         far = partial_sum(dw_2, dw_3)
-        kept = near + to_model(far, 2)
+        near, part = lax.optimization_barrier(near), to_model(far, 2)
+        kept = near + part
         bufs = place([(kept, to_data(kept))], 1, 0, None)
 
         carry, dw_0, dw_1 = call(0, grad_mid, [h_saved, h_near[0]], (0, 1), None, False)
@@ -487,17 +493,19 @@
         exchange(1, far[: bounds[2] - bounds[1]])
         exchange(2, far[bounds[2] - bounds[1] : bounds[3] - bounds[1]])
         carry, grad_mid, x_saved = paired(carry), paired(grad_mid), paired(x_saved, 1)
-        dw_2, dw_3, pre_1 = small_call(0, grad_mid, x_saved, h_small[0], down_pair, small_start, 0, None, None)
+        dw_2, dw_3, pre_1 = small_call(0, grad_mid, x_saved, h_small[0], down_pair, small_start, 0)
         exchange(3, jnp.concatenate([far[bounds[3] - bounds[1] :], partial_sum(dw_2, dw_3)]))
         last = small_start + SMALL
-        early, late = CHUNKS[0], CHUNKS[0] + CHUNKS[1]
-        dw_2, dw_3, grad_x = small_call(0, grad_mid, x_saved, h_small[1], down_pair, last, 0, None, (carry, pre_1, small_up))
-        dw_2, dw_3, pre_2 = small_call(0, grad_mid, x_saved, h_small[2], down_pair, last, early, (dw_2, dw_3), None)
-        grad_x = finish_call(carry, (pre_1, pre_2), small_up, early, 0, 1, grad_x)
-        dw_2, dw_3, pre_3 = small_call(0, grad_mid, x_saved, h_small[3], down_pair, last, late, (dw_2, dw_3), None)
+        early, late = CHUNKS[0], CHUNKS[1] + CHUNKS[2]
+        dw_2, dw_3, grad_x = small_call(
+            0, grad_mid, x_saved, h_small[1], down_pair, last, 0, finish=(carry, pre_1, small_up))
+        dw_2, dw_3, pre_2 = small_call(
+            0, grad_mid, x_saved, h_small[2], down_pair, last, early, init=(dw_2, dw_3), pre_pairs=late)
+        dw_2, dw_3, pre_2 = small_call(
+            0, grad_mid, x_saved, h_small[3], down_pair, last, early + CHUNKS[1], init=(dw_2, dw_3),
+            pre=pre_2, pre_pairs=late, pre_first=CHUNKS[1])
         exchange(4, partial_sum(dw_2, dw_3))
-        grad_x = finish_call(carry, (pre_1, pre_2), small_up, early, 1, 1, grad_x)
-        grad_x = finish_call(carry, (pre_1, pre_3), small_up, late, 0, 2, grad_x)
+        grad_x = finish_call(carry, (pre_1, pre_2), small_up, early, 0, 2, grad_x)
         bufs = place([pieces[0]], 0, 0, bufs)
         middle = [(*pieces[1], 0, 64), (*pieces[2], 0, 128), (*pieces[3], 0, 64)]
         bufs = place(middle, 0, bounds[1], bufs)

time: 1670 us -> 1730 us (1.036)
  waiting for transfers between devices: 914 us -> 974 us
    ppermute x38, waiting for transfers between devices: 762 us -> 800 us  [to_model(): return lax.ppermute(value, 'model', [(i, i ^ flip) for i in range(n_model)])]
    ppermute x15, waiting for transfers between devices: 153 us -> 174 us  [to_data(): return lax.ppermute(value, 'data', [(0, 1), (1, 0)])]
  transfers between devices with their start and end apart: 53 -> 53, of which waited for: 14 -> 13; matrix products, arithmetic and copies ran while one was open for 4% -> 3% of each run, Pallas kernels for 37% -> 35%
where the time goes in v6:
time: 1730 us
  waiting for transfers between devices  974 us (56%)
  Pallas kernels  613 us (35%)
  local copies, waits for them, and re-layouts  65.9 us (4%)
  starting transfers between devices  44.1 us (3%)
  other arithmetic  28.9 us (2%)
    ppermute x38, waiting for transfers between devices, to_model(): return lax.ppermute(value, 'model', [(i, i ^ flip) for i in range(n_model)])  800 us
    pallas_call x4, Pallas kernels, block_call(): pl.pallas_call(functools.partial(block_body, carry is not None, final, ro...  438 us
    ppermute x15, waiting for transfers between devices, to_data(): return lax.ppermute(value, 'data', [(0, 1), (1, 0)])  174 us
    squeeze x8, local copies, waits for them, and re-layouts, h_from(): lax.dynamic_slice(held[0], (layer, 0, begin, start), (1, rows, seq, size))  60.8 us
    pallas_call x1, Pallas kernels, wide_call(): pl.pallas_call(functools.partial(wide_body, start), out_shape=[jax.ShapeD...  54.5 us
    pallas_call x4, Pallas kernels, small_call(): pl.pallas_call(functools.partial(small_body, init is not None, finish is...  47.5 us
  transfers between devices with their start and end apart: 53, of which 13 were waited for; matrix products, arithmetic and copies ran while one was open for 3% of the time, Pallas kernels for 35%

profile of v6, /device:TPU:0, one launch (start us, length us, event | category | flops | bytes accessed | tf_op | source)
XLA Modules:
  0.0 1726.5 jit_solution(11765732928663628045)
XLA Ops:
  3.3 10.6 dynamic-slice_bitcast_fusion.3
  13.9 10.6 dynamic-slice_bitcast_fusion.2
  24.5 7.2 dynamic-slice_bitcast_fusion.1
  32.5 2.6 collective-permute-start.1
  35.1 2.0 collective-permute-start.2
  37.3 545.1 %collective-permute-done.2 = bf16[192,768]{1,0:T(8,128)(2,1)S(1)} collective-permute-done((bf16[192,768]{1,0:T(8,128)(2,1)S(1)}, bf16[192,768]{1,0:T(8,128)(2,1)S(1)}, u32[]{:S(2)}, u32[]{:S(2)}) %collective-permute-start.2) | collective-permute-done | bytes 294944 | tf_op jit(solution)/shard_map/ppermute | solution.py:403
  582.4 2.1 collective-permute-start.3
  584.5 41.9 %collective-permute-done.3 = bf16[576,768]{1,0:T(8,128)(2,1)S(1)} collective-permute-done((bf16[576,768]{1,0:T(8,128)(2,1)S(1)}, bf16[576,768]{1,0:T(8,128)(2,1)S(1)}, u32[]{:S(2)}, u32[]{:S(2)}) %collective-permute-start.3) | collective-permute-done | bytes 884768 | tf_op jit(solution)/shard_map/ppermute | solution.py:403
  626.5 1.7 collective-permute-start.4
  628.6 26.8 %collective-permute-done.4 = bf16[768,768]{1,0:T(8,128)(2,1)S(1)} collective-permute-done((bf16[768,768]{1,0:T(8,128)(2,1)S(1)}, bf16[768,768]{1,0:T(8,128)(2,1)S(1)}, u32[]{:S(2)}, u32[]{:S(2)}) %collective-permute-start.4) | collective-permute-done | bytes 1179680 | tf_op jit(solution)/shard_map/ppermute | solution.py:406
  655.4 24.2 %collective-permute-done.13 = bf16[768,768]{1,0:T(8,128)(2,1)S(1)} collective-permute-done((bf16[768,768]{1,0:T(8,128)(2,1)S(1)}, bf16[768,768]{1,0:T(8,128)(2,1)S(1)}, u32[]{:S(2)}, u32[]{:S(2)}) %collective-permute-start.13) | collective-permute-done | bytes 1179680 | tf_op jit(solution)/shard_map/ppermute | solution.py:406
  680.6 10.7 dynamic-slice_bitcast_fusion
  691.2 6.3 dynamic-slice_bitcast_fusion.5
  697.5 6.3 dynamic-slice_bitcast_fusion.4
  703.8 3.0 broadcast_select_fusion.2
  706.8 1.6 broadcast_select_fusion
  709.5 119.7 %shard_map.76 = (f32[16,512,768]{2,1,0:T(8,128)}, f32[2,768,768]{2,1,0:T(8,128)}, f32[2,768,768]{2,1,0:T(8,128)}) custom-call(s32[1]{0:T(128)} %bitcast._, bf16[16,512,768]{2,1,0:T(8,128)(2,1)} %refs_0_.3, bf16[2,16,512,768]{3,2,1,0:T(8,128)(2,1)} %x_ref.1, bf16[2,16,2048,768]{3,2,1,0:T(8,128)(2,1)} %hi_ref.3, ...), custom_call_target="tpu_custom_call" | custom-call | flops 77309411328 | bytes 50331648 | tf_op jit(solution)/shard_map/pallas_call | solution.py:113
  831.4 121.2 %shard_map.77 = (bf16[16,512,768]{2,1,0:T(8,128)(2,1)}, f32[2,768,768]{2,1,0:T(8,128)}, f32[2,768,768]{2,1,0:T(8,128)}) custom-call(s32[1]{0:T(128)} %bitcast._, bf16[16,512,768]{2,1,0:T(8,128)(2,1)} %refs_0_.3, bf16[2,16,512,768]{3,2,1,0:T(8,128)(2,1)} %x_ref.1, bf16[16,512,768]{2,1,0:T(8,128)(2,1)} %collective-permute-done.refs_2_, ...), custom_call_target="tpu_custom_call" | custom-call | flops 77309411328 | bytes 50331648 | tf_op jit(solution)/shard_map/pallas_call | solution.py:113
  953.1 119.4 %shard_map.78 = (f32[16,512,768]{2,1,0:T(8,128)}, f32[2,768,768]{2,1,0:T(8,128)}, f32[2,768,768]{2,1,0:T(8,128)}) custom-call(s32[1]{0:T(128)} %bitcast._, bf16[16,512,768]{2,1,0:T(8,128)(2,1)} %get-tuple-element.83.refs_0_.grad_ref, bf16[2,16,512,768]{3,2,1,0:T(8,128)(2,1)} %x_ref.1, bf16[2,16,2048,768]{3,2,1,0:T(8,128)(2,1)} %hi_ref.3, ...), custom_call_target="tpu_custom_call" | custom-call | flops 77309411328 | bytes 50331648 | tf_op jit(solution)/shard_map/pallas_call | solution.py:113
  1072.8 27.9 %collective-permute-done.17.refs_3_ = bf16[16,512,384]{2,1,0:T(8,128)(2,1)} collective-permute-done((bf16[16,512,384]{2,1,0:T(8,128)(2,1)}, bf16[16,512,384]{2,1,0:T(8,128)(2,1)}, u32[]{:S(2)}, u32[]{:S(2)}) %collective-permute-start.17) | collective-permute-done | bytes 6291488 | tf_op jit(solution)/shard_map/ppermute | solution.py:403
  1100.7 78.2 %shard_map.79 = (f32[16,512,768]{2,1,0:T(8,128)}, f32[2,384,768]{2,1,0:T(8,128)}, f32[2,384,768]{2,1,0:T(8,128)}) custom-call(s32[1]{0:T(128)} %bitcast._, bf16[16,512,768]{2,1,0:T(8,128)(2,1)} %get-tuple-element.83.refs_0_.grad_ref, bf16[2,16,512,768]{3,2,1,0:T(8,128)(2,1)} %x_ref.1, bf16[16,512,384]{2,1,0:T(8,128)(2,1)} %collective-permute-done.16.refs_2_, ...), custom_call_target="tpu_custom_call" | custom-call | flops 38654705664 | bytes 50331648 | tf_op jit(solution)/shard_map/pallas_call | solution.py:113
  1179.7 6.3 shard_map.81
  1187.3 4.6 dynamic-slice_bitcast_fusion.7
  1191.8 4.6 dynamic-slice_bitcast_fusion.6
  1197.9 6.3 shard_map.82
  1205.0 7.1 shard_map.95
  1212.1 172.9 %collective-permute-done.24.h_b = bf16[2,512,128]{2,1,0:T(8,128)(2,1)S(1)} collective-permute-done((bf16[2,512,128]{2,1,0:T(8,128)(2,1)}, bf16[2,512,128]{2,1,0:T(8,128)(2,1)S(1)}, u32[]{:S(2)}, u32[]{:S(2)}) %collective-permute-start.24) | collective-permute-done | bytes 262176 | tf_op jit(solution)/shard_map/ppermute | solution.py:403
  1385.0 1.5 collective-permute-start.50
  1387.1 51.5 %collective-permute-done.50 = f32[768,768]{1,0:T(8,128)} collective-permute-done((f32[768,768]{1,0:T(8,128)}, f32[768,768]{1,0:T(8,128)}, u32[]{:S(2)}, u32[]{:S(2)}) %collective-permute-start.50) | collective-permute-done | bytes 2359328 | tf_op jit(solution)/shard_map/ppermute | solution.py:406
  1438.6 4.5 shard_map.93
  1443.0 7.0 shard_map.94
  1450.1 4.1 add.67
  1455.0 1.5 collective-permute-start.44
  1458.2 54.5 %shard_map.80 = (f32[16,512,768]{2,1,0:T(8,128)}, f32[2,256,768]{2,1,0:T(8,128)}, f32[2,256,768]{2,1,0:T(8,128)}) custom-call(bf16[16,512,768]{2,1,0:T(8,128)(2,1)} %get-tuple-element.83.refs_0_.grad_ref, bf16[2,16,512,768]{3,2,1,0:T(8,128)(2,1)} %x_ref.1, bf16[16,512,256]{2,1,0:T(8,128)(2,1)} %collective-permute-done.10.h_a, ...), custom_call_target="tpu_custom_call" | custom-call | flops 25769803776 | bytes 75497472 | tf_op jit(solution)/shard_map/pallas_call | solution.py:191
  1512.8 7.1 shard_map.89
  1519.8 1.5 collective-permute-start.28
  1522.0 12.7 collective-permute-done.48
  1536.2 1.9 shard_map.84.refs_2_.up_ref
  1538.2 2.9 add.64
  1541.1 2.0 add.66
  1543.1 3.3 add.68.kept_ref
  1546.4 7.0 collective-permute-done.20.h_b
  1554.7 1.5 collective-permute-start.52
  1556.2 18.3 %shard_map.83 = (f32[2,64,768]{2,1,0:T(8,128)}, f32[2,64,768]{2,1,0:T(8,128)}, bf16[2,8,512,128]{3,2,1,0:T(8,128)(2,1)}) custom-call(bf16[2,8,512,768]{3,2,1,0:T(8,128)(2,1)} %bitcast.34, bf16[2,2,8,512,768]{4,3,2,1,0:T(8,128)(2,1)} %bitcast.30, bf16[8,512,128]{2,1,0:T(8,128)(2,1)} %collective-permute-done.19.h_a, ...), custom_call_target="tpu_custom_call" | custom-call | flops 4831838208 | bytes 25165824 | tf_op jit(solution)/shard_map/pallas_call | solution.py:252
  1574.6 2.9 shard_map.90
  1578.2 15.1 shard_map.85
  1593.4 7.0 shard_map.86
  1600.4 7.0 shard_map.87
  1608.2 1.9 shard_map.91
  1611.4 2.7 add.56
  1615.6 2.5 add.65.kept_ref
  1618.8 1.9 shard_map.92
  1620.7 36.0 %collective-permute-done.32 = f32[64,768]{1,0:T(8,128)S(1)} collective-permute-done((f32[64,768]{1,0:T(8,128)}, f32[64,768]{1,0:T(8,128)S(1)}, u32[]{:S(2)}, u32[]{:S(2)}) %collective-permute-start.32) | collective-permute-done | bytes 196640 | tf_op jit(solution)/shard_map/ppermute | solution.py:406
  1662.2 1.5 collective-permute-start.35
  1663.7 22.6 %collective-permute-done.35 = f32[64,768]{1,0:T(8,128)S(1)} collective-permute-done((f32[64,768]{1,0:T(8,128)S(1)}, f32[64,768]{1,0:T(8,128)S(1)}, u32[]{:S(2)}, u32[]{:S(2)}) %collective-permute-start.35) | collective-permute-done | bytes 196640 | tf_op jit(solution)/shard_map/ppermute | solution.py:406
  1688.4 1.6 collective-permute-start.42
  1690.0 4.0 collective-permute-done.39
  1694.0 1.5 collective-permute-start.37
  1697.4 1.5 collective-permute-start.41
  1700.2 10.9 shard_map.88
  1711.1 5.9 shard_map.96
  1717.0 3.8 shard_map.97
  1720.8 2.7 shard_map.98
  1724.2 2.2 shard_map.99
  (144 shorter events, 36.5 us)
Async XLA Ops:
  31.7 677.3 %collective-permute-start.7 = (bf16[16,512,768]{2,1,0:T(8,128)(2,1)S(1)}, bf16[16,512,768]{2,1,0:T(8,128)(2,1)}, u32[]{:S(2)}, u32[]{:S(2)}) collective-permute-start(bf16[16,512,768]{2,1,0:T(8,128)(2,1)S(1)} %dynamic-slice_bitcast_fusion.1), channel_id=1, source_target_pairs={{0,1},{1,0},{2,3},{3,2},{4,5},{5,4},{6,7},{7,6}} | collective-permute-start | bytes 37748744 | tf_op jit(solution)/shard_map/ppermute | solution.py:403
  32.5 798.0 %collective-permute-start.1 = (bf16[16,512,768]{2,1,0:T(8,128)(2,1)}, bf16[16,512,768]{2,1,0:T(8,128)(2,1)}, u32[]{:S(2)}, u32[]{:S(2)}) collective-permute-start(bf16[16,512,768]{2,1,0:T(8,128)(2,1)} %dynamic-slice_bitcast_fusion.2), channel_id=1, source_target_pairs={{0,3},{1,2},{2,1},{3,0},{4,7},{5,6},{6,5},{7,4}} | collective-permute-start | bytes 37748744 | tf_op jit(solution)/shard_map/ppermute | solution.py:403
  35.1 796.2 %collective-permute-start = (bf16[16,512,768]{2,1,0:T(8,128)(2,1)}, bf16[16,512,768]{2,1,0:T(8,128)(2,1)}, u32[]{:S(2)}, u32[]{:S(2)}) collective-permute-start(bf16[16,512,768]{2,1,0:T(8,128)(2,1)} %dynamic-slice_bitcast_fusion.3), channel_id=1, source_target_pairs={{0,2},{1,3},{2,0},{3,1},{4,6},{5,7},{6,4},{7,5}} | collective-permute-start | bytes 37748744 | tf_op jit(solution)/shard_map/ppermute | solution.py:403
  35.1 547.3 %collective-permute-start.2 = (bf16[192,768]{1,0:T(8,128)(2,1)S(1)}, bf16[192,768]{1,0:T(8,128)(2,1)S(1)}, u32[]{:S(2)}, u32[]{:S(2)}) collective-permute-start(bf16[192,768]{1,0:T(8,128)(2,1)S(1)} %select_bitcast_fusion.2), channel_id=1, source_target_pairs={{0,2},{1,3},{2,0},{3,1},{4,6},{5,7},{6,4},{7,5}} | collective-permute-start | bytes 884744 | tf_op jit(solution)/shard_map/ppermute | solution.py:403
  37.3 590.9 %collective-permute-start.12 = (bf16[768,768]{1,0:T(8,128)(2,1)S(1)}, bf16[768,768]{1,0:T(8,128)(2,1)S(1)}, u32[]{:S(2)}, u32[]{:S(2)}) collective-permute-start(bf16[768,768]{1,0:T(8,128)(2,1)S(1)} %select_bitcast_fusion), channel_id=1, source_target_pairs={{0,2},{1,3},{2,0},{3,1},{4,6},{5,7},{6,4},{7,5}} | collective-permute-start | bytes 3538952 | tf_op jit(solution)/shard_map/ppermute | solution.py:403
  582.4 44.0 %collective-permute-start.3 = (bf16[576,768]{1,0:T(8,128)(2,1)S(1)}, bf16[576,768]{1,0:T(8,128)(2,1)S(1)}, u32[]{:S(2)}, u32[]{:S(2)}) collective-permute-start(bf16[576,768]{1,0:T(8,128)(2,1)S(1)} %select_bitcast_fusion.1), channel_id=1, source_target_pairs={{0,2},{1,3},{2,0},{3,1},{4,6},{5,7},{6,4},{7,5}} | collective-permute-start | bytes 2654216 | tf_op jit(solution)/shard_map/ppermute | solution.py:403
  626.5 28.9 %collective-permute-start.4 = (bf16[768,768]{1,0:T(8,128)(2,1)S(1)}, bf16[768,768]{1,0:T(8,128)(2,1)S(1)}, u32[]{:S(2)}, u32[]{:S(2)}) collective-permute-start(bf16[768,768]{1,0:T(8,128)(2,1)S(1)} %constant_dynamic-update-slice_fusion), channel_id=1, source_target_pairs={{0,4},{4,0},{1,5},{5,1},{2,6},{6,2},{3,7},{7,3}} | collective-permute-start | bytes 3538952 | tf_op jit(solution)/shard_map/ppermute | solution.py:406
  628.2 27.2 %copy-start.6 = (bf16[768,768]{1,0:T(8,128)(2,1)}, bf16[768,768]{1,0:T(8,128)(2,1)S(1)}, u32[]{:S(2)}) copy-start(bf16[768,768]{1,0:T(8,128)(2,1)S(1)} %collective-permute-done.12) | copy-start | bytes 3538948
  628.2 51.3 %collective-permute-start.13 = (bf16[768,768]{1,0:T(8,128)(2,1)S(1)}, bf16[768,768]{1,0:T(8,128)(2,1)S(1)}, u32[]{:S(2)}, u32[]{:S(2)}) collective-permute-start(bf16[768,768]{1,0:T(8,128)(2,1)S(1)} %collective-permute-done.12), channel_id=1, source_target_pairs={{0,4},{4,0},{1,5},{5,1},{2,6},{6,2},{3,7},{7,3}} | collective-permute-start | bytes 3538952 | tf_op jit(solution)/shard_map/ppermute | solution.py:406
  655.4 24.2 %copy-start.8 = (bf16[768,768]{1,0:T(8,128)(2,1)}, bf16[768,768]{1,0:T(8,128)(2,1)S(1)}, u32[]{:S(2)}) copy-start(bf16[768,768]{1,0:T(8,128)(2,1)S(1)} %collective-permute-done.4) | copy-start | bytes 3538948
  655.4 53.1 %collective-permute-start.8 = (bf16[2,768,768]{2,1,0:T(8,128)(2,1)S(1)}, bf16[2,768,768]{2,1,0:T(8,128)(2,1)}, u32[]{:S(2)}, u32[]{:S(2)}) collective-permute-start(bf16[2,768,768]{2,1,0:T(8,128)(2,1)S(1)} %copy-done.3), channel_id=1, source_target_pairs={{0,1},{1,0},{2,3},{3,2},{4,5},{5,4},{6,7},{7,6}} | collective-permute-start | bytes 7077896 | tf_op jit(solution)/shard_map/ppermute | solution.py:403
  680.6 28.4 %collective-permute-start.9 = (bf16[2,768,768]{2,1,0:T(8,128)(2,1)S(1)}, bf16[2,768,768]{2,1,0:T(8,128)(2,1)}, u32[]{:S(2)}, u32[]{:S(2)}) collective-permute-start(bf16[2,768,768]{2,1,0:T(8,128)(2,1)S(1)} %copy-done.2), channel_id=1, source_target_pairs={{0,1},{1,0},{2,3},{3,2},{4,5},{5,4},{6,7},{7,6}} | collective-permute-start | bytes 7077896 | tf_op jit(solution)/shard_map/ppermute | solution.py:403
  708.4 244.2 %collective-permute-start.18 = (bf16[16,512,768]{2,1,0:T(8,128)(2,1)}, bf16[16,512,768]{2,1,0:T(8,128)(2,1)}, u32[]{:S(2)}, u32[]{:S(2)}) collective-permute-start(bf16[16,512,768]{2,1,0:T(8,128)(2,1)} %dynamic-slice_bitcast_fusion), channel_id=1, source_target_pairs={{0,1},{1,0},{2,3},{3,2},{4,5},{5,4},{6,7},{7,6}} | collective-permute-start | bytes 37748744 | tf_op jit(solution)/shard_map/ppermute | solution.py:403
  708.9 120.2 %collective-permute-start.5 = (bf16[768,768]{1,0:T(8,128)(2,1)}, bf16[768,768]{1,0:T(8,128)(2,1)}, u32[]{:S(2)}, u32[]{:S(2)}) collective-permute-start(bf16[768,768]{1,0:T(8,128)(2,1)} %get-tuple-element.158.refs_4_), channel_id=1, source_target_pairs={{0,1},{1,0},{2,3},{3,2},{4,5},{5,4},{6,7},{7,6}} | collective-permute-start | bytes 3538952 | tf_op jit(solution)/shard_map/ppermute | solution.py:403
  709.0 121.4 %collective-permute-start.6 = (bf16[768,768]{1,0:T(8,128)(2,1)}, bf16[768,768]{1,0:T(8,128)(2,1)}, u32[]{:S(2)}, u32[]{:S(2)}) collective-permute-start(bf16[768,768]{1,0:T(8,128)(2,1)} %get-tuple-element.157.refs_6_), channel_id=1, source_target_pairs={{0,1},{1,0},{2,3},{3,2},{4,5},{5,4},{6,7},{7,6}} | collective-permute-start | bytes 3538952 | tf_op jit(solution)/shard_map/ppermute | solution.py:403
  829.2 271.5 %collective-permute-start.16 = (bf16[16,512,384]{2,1,0:T(8,128)(2,1)}, bf16[16,512,384]{2,1,0:T(8,128)(2,1)}, u32[]{:S(2)}, u32[]{:S(2)}) collective-permute-start(bf16[16,512,384]{2,1,0:T(8,128)(2,1)} %dynamic-slice_bitcast_fusion.5), channel_id=1, source_target_pairs={{0,2},{1,3},{2,0},{3,1},{4,6},{5,7},{6,4},{7,5}} | collective-permute-start | bytes 18874376 | tf_op jit(solution)/shard_map/ppermute | solution.py:403
  830.4 270.3 %collective-permute-start.17 = (bf16[16,512,384]{2,1,0:T(8,128)(2,1)}, bf16[16,512,384]{2,1,0:T(8,128)(2,1)}, u32[]{:S(2)}, u32[]{:S(2)}) collective-permute-start(bf16[16,512,384]{2,1,0:T(8,128)(2,1)} %dynamic-slice_bitcast_fusion.4), channel_id=1, source_target_pairs={{0,3},{1,2},{2,1},{3,0},{4,7},{5,6},{6,5},{7,4}} | collective-permute-start | bytes 18874376 | tf_op jit(solution)/shard_map/ppermute | solution.py:403
  830.5 242.0 %collective-permute-start.14 = (bf16[768,768]{1,0:T(8,128)(2,1)}, bf16[768,768]{1,0:T(8,128)(2,1)}, u32[]{:S(2)}, u32[]{:S(2)}) collective-permute-start(bf16[768,768]{1,0:T(8,128)(2,1)} %get-tuple-element.156.refs_4_.up_a), channel_id=1, source_target_pairs={{0,1},{1,0},{2,3},{3,2},{4,5},{5,4},{6,7},{7,6}} | collective-permute-start | bytes 3538952 | tf_op jit(solution)/shard_map/ppermute | solution.py:403
  831.4 241.4 %collective-permute-start.15 = (bf16[768,768]{1,0:T(8,128)(2,1)}, bf16[768,768]{1,0:T(8,128)(2,1)}, u32[]{:S(2)}, u32[]{:S(2)}) collective-permute-start(bf16[768,768]{1,0:T(8,128)(2,1)} %get-tuple-element.155.refs_6_.down_a), channel_id=1, source_target_pairs={{0,1},{1,0},{2,3},{3,2},{4,5},{5,4},{6,7},{7,6}} | collective-permute-start | bytes 3538952 | tf_op jit(solution)/shard_map/ppermute | solution.py:403
  952.6 251.6 %collective-permute-start.49 = (f32[2,768,768]{2,1,0:T(8,128)}, f32[2,768,768]{2,1,0:T(8,128)}, u32[]{:S(2)}, u32[]{:S(2)}) collective-permute-start(f32[2,768,768]{2,1,0:T(8,128)} %get-tuple-element.140), channel_id=1, source_target_pairs={{0,1},{1,0},{2,3},{3,2},{4,5},{5,4},{6,7},{7,6}} | collective-permute-start | bytes 14155784 | tf_op jit(solution)/shard_map/ppermute | solution.py:403
  1072.5 314.0 %collective-permute-start.47 = (f32[2,768,768]{2,1,0:T(8,128)}, f32[2,768,768]{2,1,0:T(8,128)}, u32[]{:S(2)}, u32[]{:S(2)}) collective-permute-start(f32[2,768,768]{2,1,0:T(8,128)} %get-tuple-element.136), channel_id=1, source_target_pairs={{0,1},{1,0},{2,3},{3,2},{4,5},{5,4},{6,7},{7,6}} | collective-permute-start | bytes 14155784 | tf_op jit(solution)/shard_map/ppermute | solution.py:403
  1178.8 207.7 %collective-permute-start.43 = (f32[2,384,768]{2,1,0:T(8,128)}, f32[2,384,768]{2,1,0:T(8,128)}, u32[]{:S(2)}, u32[]{:S(2)}) collective-permute-start(f32[2,384,768]{2,1,0:T(8,128)} %get-tuple-element.132), channel_id=1, source_target_pairs={{0,1},{1,0},{2,3},{3,2},{4,5},{5,4},{6,7},{7,6}} | collective-permute-start | bytes 7077896 | tf_op jit(solution)/shard_map/ppermute | solution.py:403
  1186.1 10.6 collective-permute-start.23
  1196.4 260.1 %collective-permute-start.11 = (bf16[16,512,256]{2,1,0:T(8,128)(2,1)}, bf16[16,512,256]{2,1,0:T(8,128)(2,1)}, u32[]{:S(2)}, u32[]{:S(2)}) collective-permute-start(bf16[16,512,256]{2,1,0:T(8,128)(2,1)} %dynamic-slice_bitcast_fusion.6), channel_id=1, source_target_pairs={{0,3},{1,2},{2,1},{3,0},{4,7},{5,6},{6,5},{7,4}} | collective-permute-start | bytes 12582920 | tf_op jit(solution)/shard_map/ppermute | solution.py:403
  1196.6 260.4 %collective-permute-start.10 = (bf16[16,512,256]{2,1,0:T(8,128)(2,1)}, bf16[16,512,256]{2,1,0:T(8,128)(2,1)}, u32[]{:S(2)}, u32[]{:S(2)}) collective-permute-start(bf16[16,512,256]{2,1,0:T(8,128)(2,1)} %dynamic-slice_bitcast_fusion.7), channel_id=1, source_target_pairs={{0,2},{1,3},{2,0},{3,1},{4,6},{5,7},{6,4},{7,5}} | collective-permute-start | bytes 12582920 | tf_op jit(solution)/shard_map/ppermute | solution.py:403
  1204.2 180.8 %collective-permute-start.24 = (bf16[2,512,128]{2,1,0:T(8,128)(2,1)}, bf16[2,512,128]{2,1,0:T(8,128)(2,1)S(1)}, u32[]{:S(2)}, u32[]{:S(2)}) collective-permute-start(bf16[2,512,128]{2,1,0:T(8,128)(2,1)} %get-tuple-element.100), channel_id=1, source_target_pairs={{0,3},{1,2},{2,1},{3,0},{4,7},{5,6},{6,5},{7,4}} | collective-permute-start | bytes 786440 | tf_op jit(solution)/shard_map/ppermute | solution.py:403
  1385.0 58.0 %copy-start.14 = (bf16[2,512,128]{2,1,0:T(8,128)(2,1)}, bf16[2,512,128]{2,1,0:T(8,128)(2,1)S(1)}, u32[]{:S(2)}) copy-start(bf16[2,512,128]{2,1,0:T(8,128)(2,1)S(1)} %collective-permute-done.24.h_b) | copy-start | bytes 786436
  1385.0 53.6 %collective-permute-start.50 = (f32[768,768]{1,0:T(8,128)}, f32[768,768]{1,0:T(8,128)}, u32[]{:S(2)}, u32[]{:S(2)}) collective-permute-start(f32[768,768]{1,0:T(8,128)} %get-tuple-element.142), channel_id=1, source_target_pairs={{0,4},{4,0},{1,5},{5,1},{2,6},{6,2},{3,7},{7,3}} | collective-permute-start | bytes 7077896 | tf_op jit(solution)/shard_map/ppermute | solution.py:406
  1386.5 126.2 %collective-permute-start.27 = (f32[2,768,768]{2,1,0:T(8,128)}, f32[2,768,768]{2,1,0:T(8,128)}, u32[]{:S(2)}, u32[]{:S(2)}) collective-permute-start(f32[2,768,768]{2,1,0:T(8,128)} %get-tuple-element.111), channel_id=1, source_target_pairs={{0,1},{1,0},{2,3},{3,2},{4,5},{5,4},{6,7},{7,6}} | collective-permute-start | bytes 14155784 | tf_op jit(solution)/shard_map/ppermute | solution.py:403
  1386.5 67.6 %collective-permute-start.21 = (bf16[2,512,128]{2,1,0:T(8,128)(2,1)}, bf16[2,512,128]{2,1,0:T(8,128)(2,1)S(1)}, u32[]{:S(2)}, u32[]{:S(2)}) collective-permute-start(bf16[2,512,128]{2,1,0:T(8,128)(2,1)} %get-tuple-element.97), channel_id=1, source_target_pairs={{0,2},{1,3},{2,0},{3,1},{4,6},{5,7},{6,4},{7,5}} | collective-permute-start | bytes 786440 | tf_op jit(solution)/shard_map/ppermute | solution.py:403
  1438.5 16.5 collective-permute-start.22
  1454.2 58.5 %copy-start.15 = (bf16[2,512,128]{2,1,0:T(8,128)(2,1)}, bf16[2,512,128]{2,1,0:T(8,128)(2,1)S(1)}, u32[]{:S(2)}) copy-start(bf16[2,512,128]{2,1,0:T(8,128)(2,1)S(1)} %collective-permute-done.21.h_a) | copy-start | bytes 786436
  1454.2 65.6 %collective-permute-start.19 = (bf16[8,512,128]{2,1,0:T(8,128)(2,1)}, bf16[8,512,128]{2,1,0:T(8,128)(2,1)}, u32[]{:S(2)}, u32[]{:S(2)}) collective-permute-start(bf16[8,512,128]{2,1,0:T(8,128)(2,1)} %get-tuple-element.94), channel_id=1, source_target_pairs={{0,2},{1,3},{2,0},{3,1},{4,6},{5,7},{6,4},{7,5}} | collective-permute-start | bytes 3145736 | tf_op jit(solution)/shard_map/ppermute | solution.py:403
  1455.0 57.7 %copy-start.16 = (bf16[2,512,128]{2,1,0:T(8,128)(2,1)}, bf16[2,512,128]{2,1,0:T(8,128)(2,1)S(1)}, u32[]{:S(2)}) copy-start(bf16[2,512,128]{2,1,0:T(8,128)(2,1)S(1)} %collective-permute-done.22.h_b) | copy-start | bytes 786436
  1455.0 66.3 %collective-permute-start.44 = (f32[384,768]{1,0:T(8,128)}, f32[384,768]{1,0:T(8,128)}, u32[]{:S(2)}, u32[]{:S(2)}) collective-permute-start(f32[384,768]{1,0:T(8,128)} %get-tuple-element.134), channel_id=1, source_target_pairs={{0,4},{4,0},{1,5},{5,1},{2,6},{6,2},{3,7},{7,3}} | collective-permute-start | bytes 3538952 | tf_op jit(solution)/shard_map/ppermute | solution.py:406
  1456.6 78.1 %collective-permute-start.48 = (f32[768,768]{1,0:T(8,128)}, f32[768,768]{1,0:T(8,128)}, u32[]{:S(2)}, u32[]{:S(2)}) collective-permute-start(f32[768,768]{1,0:T(8,128)} %get-tuple-element.138), channel_id=1, source_target_pairs={{0,4},{4,0},{1,5},{5,1},{2,6},{6,2},{3,7},{7,3}} | collective-permute-start | bytes 7077896 | tf_op jit(solution)/shard_map/ppermute | solution.py:406
  1457.1 78.9 %collective-permute-start.51 = (f32[768,768]{1,0:T(8,128)}, f32[768,768]{1,0:T(8,128)}, u32[]{:S(2)}, u32[]{:S(2)}) collective-permute-start(f32[768,768]{1,0:T(8,128)} %add.67), channel_id=1, source_target_pairs={{0,2},{1,3},{2,0},{3,1},{4,6},{5,7},{6,4},{7,5}} | collective-permute-start | bytes 7077896 | tf_op jit(solution)/shard_map/ppermute | solution.py:403
  1512.7 42.0 %collective-permute-start.29 = (f32[2,256,768]{2,1,0:T(8,128)}, f32[2,256,768]{2,1,0:T(8,128)}, u32[]{:S(2)}, u32[]{:S(2)}) collective-permute-start(f32[2,256,768]{2,1,0:T(8,128)} %get-tuple-element.116), channel_id=1, source_target_pairs={{0,1},{1,0},{2,3},{3,2},{4,5},{5,4},{6,7},{7,6}} | collective-permute-start | bytes 4718600 | tf_op jit(solution)/shard_map/ppermute | solution.py:403
  1519.8 90.2 %collective-permute-start.28 = (f32[768,768]{1,0:T(8,128)}, f32[768,768]{1,0:T(8,128)}, u32[]{:S(2)}, u32[]{:S(2)}) collective-permute-start(f32[768,768]{1,0:T(8,128)} %get-tuple-element.113), channel_id=1, source_target_pairs={{0,4},{4,0},{1,5},{5,1},{2,6},{6,2},{3,7},{7,3}} | collective-permute-start | bytes 7077896 | tf_op jit(solution)/shard_map/ppermute | solution.py:406
  1521.4 32.1 %collective-permute-start.20 = (bf16[8,512,128]{2,1,0:T(8,128)(2,1)}, bf16[8,512,128]{2,1,0:T(8,128)(2,1)}, u32[]{:S(2)}, u32[]{:S(2)}) collective-permute-start(bf16[8,512,128]{2,1,0:T(8,128)(2,1)} %get-tuple-element.95), channel_id=1, source_target_pairs={{0,3},{1,2},{2,1},{3,0},{4,7},{5,6},{6,5},{7,4}} | collective-permute-start | bytes 3145736 | tf_op jit(solution)/shard_map/ppermute | solution.py:403
  1534.7 42.7 %collective-permute-start.25 = (bf16[4,512,128]{2,1,0:T(8,128)(2,1)}, bf16[4,512,128]{2,1,0:T(8,128)(2,1)S(1)}, u32[]{:S(2)}, u32[]{:S(2)}) collective-permute-start(bf16[4,512,128]{2,1,0:T(8,128)(2,1)} %get-tuple-element.101), channel_id=1, source_target_pairs={{0,2},{1,3},{2,0},{3,1},{4,6},{5,7},{6,4},{7,5}} | collective-permute-start | bytes 1572872 | tf_op jit(solution)/shard_map/ppermute | solution.py:403
  1535.9 41.5 %collective-permute-start.26 = (bf16[4,512,128]{2,1,0:T(8,128)(2,1)}, bf16[4,512,128]{2,1,0:T(8,128)(2,1)}, u32[]{:S(2)}, u32[]{:S(2)}) collective-permute-start(bf16[4,512,128]{2,1,0:T(8,128)(2,1)} %get-tuple-element.102), channel_id=1, source_target_pairs={{0,3},{1,2},{2,1},{3,0},{4,7},{5,6},{6,5},{7,4}} | collective-permute-start | bytes 1572872 | tf_op jit(solution)/shard_map/ppermute | solution.py:403
  1553.4 62.2 %collective-permute-start.45 = (f32[384,768]{1,0:T(8,128)}, f32[384,768]{1,0:T(8,128)}, u32[]{:S(2)}, u32[]{:S(2)}) collective-permute-start(f32[384,768]{1,0:T(8,128)} %add.64), channel_id=1, source_target_pairs={{0,2},{1,3},{2,0},{3,1},{4,6},{5,7},{6,4},{7,5}} | collective-permute-start | bytes 3538952 | tf_op jit(solution)/shard_map/ppermute | solution.py:403
  1554.7 145.0 %collective-permute-start.52 = (f32[768,768]{1,0:T(8,128)}, f32[768,768]{1,0:T(8,128)}, u32[]{:S(2)}, u32[]{:S(2)}) collective-permute-start(f32[768,768]{1,0:T(8,128)} %add.68.kept_ref), channel_id=1, source_target_pairs={{0,4},{4,0},{1,5},{5,1},{2,6},{6,2},{3,7},{7,3}} | collective-permute-start | bytes 7077896 | tf_op jit(solution)/shard_map/ppermute | solution.py:406
  1577.4 30.0 %collective-permute-start.31 = (f32[2,64,768]{2,1,0:T(8,128)}, f32[2,64,768]{2,1,0:T(8,128)S(1)}, u32[]{:S(2)}, u32[]{:S(2)}) collective-permute-start(f32[2,64,768]{2,1,0:T(8,128)} %get-tuple-element.120), channel_id=1, source_target_pairs={{0,1},{1,0},{2,3},{3,2},{4,5},{5,4},{6,7},{7,6}} | collective-permute-start | bytes 1179656 | tf_op jit(solution)/shard_map/ppermute | solution.py:403
  1577.5 81.0 %collective-permute-start.30 = (f32[256,768]{1,0:T(8,128)}, f32[256,768]{1,0:T(8,128)}, u32[]{:S(2)}, u32[]{:S(2)}) collective-permute-start(f32[256,768]{1,0:T(8,128)} %get-tuple-element.118), channel_id=1, source_target_pairs={{0,4},{4,0},{1,5},{5,1},{2,6},{6,2},{3,7},{7,3}} | collective-permute-start | bytes 2359304 | tf_op jit(solution)/shard_map/ppermute | solution.py:406
  1607.4 11.4 collective-permute-start.34
  1610.1 46.7 %collective-permute-start.32 = (f32[64,768]{1,0:T(8,128)}, f32[64,768]{1,0:T(8,128)S(1)}, u32[]{:S(2)}, u32[]{:S(2)}) collective-permute-start(f32[64,768]{1,0:T(8,128)} %get-tuple-element.122), channel_id=1, source_target_pairs={{0,4},{4,0},{1,5},{5,1},{2,6},{6,2},{3,7},{7,3}} | collective-permute-start | bytes 589832 | tf_op jit(solution)/shard_map/ppermute | solution.py:406
  1615.6 41.8 %copy-start.17 = (f32[64,768]{1,0:T(8,128)S(1)}, f32[64,768]{1,0:T(8,128)}, u32[]{:S(2)}) copy-start(f32[64,768]{1,0:T(8,128)} %get-tuple-element.121) | copy-start | bytes 589828
  1618.1 98.9 %collective-permute-start.46 = (f32[384,768]{1,0:T(8,128)}, f32[384,768]{1,0:T(8,128)}, u32[]{:S(2)}, u32[]{:S(2)}) collective-permute-start(f32[384,768]{1,0:T(8,128)} %add.65.kept_ref), channel_id=1, source_target_pairs={{0,4},{4,0},{1,5},{5,1},{2,6},{6,2},{3,7},{7,3}} | collective-permute-start | bytes 3538952 | tf_op jit(solution)/shard_map/ppermute | solution.py:406
  1658.4 28.7 %copy-start.18 = (f32[64,768]{1,0:T(8,128)S(1)}, f32[64,768]{1,0:T(8,128)}, u32[]{:S(2)}) copy-start(f32[64,768]{1,0:T(8,128)} %get-tuple-element.126) | copy-start | bytes 589828
  1660.0 30.0 %copy-start.5 = (f32[128,768]{1,0:T(8,128)S(1)}, f32[128,768]{1,0:T(8,128)}, u32[]{:S(2)}) copy-start(f32[128,768]{1,0:T(8,128)} %get-tuple-element.114) | copy-start | bytes 1179652
  1660.0 35.6 %copy-start.11 = (f32[64,768]{1,0:T(8,128)S(1)}, f32[64,768]{1,0:T(8,128)}, u32[]{:S(2)}) copy-start(f32[64,768]{1,0:T(8,128)} %get-tuple-element.128) | copy-start | bytes 589828
  1660.0 27.2 %collective-permute-start.40 = (f32[128,768]{1,0:T(8,128)S(1)}, f32[128,768]{1,0:T(8,128)S(1)}, u32[]{:S(2)}, u32[]{:S(2)}) collective-permute-start(f32[128,768]{1,0:T(8,128)S(1)} %slice.63), channel_id=1, source_target_pairs={{0,2},{1,3},{2,0},{3,1},{4,6},{5,7},{6,4},{7,5}} | collective-permute-start | bytes 1179656 | tf_op jit(solution)/shard_map/ppermute | solution.py:403
  1661.3 27.1 %collective-permute-start.33 = (f32[128,768]{1,0:T(8,128)S(1)}, f32[128,768]{1,0:T(8,128)S(1)}, u32[]{:S(2)}, u32[]{:S(2)}) collective-permute-start(f32[128,768]{1,0:T(8,128)S(1)} %pad_maximum_fusion), channel_id=1, source_target_pairs={{0,2},{1,3},{2,0},{3,1},{4,6},{5,7},{6,4},{7,5}} | collective-permute-start | bytes 1179656 | tf_op jit(solution)/shard_map/ppermute | solution.py:403
  1662.2 24.1 %collective-permute-start.35 = (f32[64,768]{1,0:T(8,128)S(1)}, f32[64,768]{1,0:T(8,128)S(1)}, u32[]{:S(2)}, u32[]{:S(2)}) collective-permute-start(f32[64,768]{1,0:T(8,128)S(1)} %copy-done.21), channel_id=1, source_target_pairs={{0,4},{4,0},{1,5},{5,1},{2,6},{6,2},{3,7},{7,3}} | collective-permute-start | bytes 589832 | tf_op jit(solution)/shard_map/ppermute | solution.py:406
  1686.3 7.8 collective-permute-start.39
  1687.2 10.2 collective-permute-start.36
  1688.4 22.7 %copy-start.4 = (f32[128,768]{1,0:T(8,128)}, f32[128,768]{1,0:T(8,128)S(1)}, u32[]{:S(2)}) copy-start(f32[128,768]{1,0:T(8,128)S(1)} %add.63.refs_1_) | copy-start | bytes 1179652
  1688.4 32.4 %collective-permute-start.42 = (f32[128,768]{1,0:T(8,128)S(1)}, f32[128,768]{1,0:T(8,128)}, u32[]{:S(2)}, u32[]{:S(2)}) collective-permute-start(f32[128,768]{1,0:T(8,128)S(1)} %add.63.refs_1_), channel_id=1, source_target_pairs={{0,4},{4,0},{1,5},{5,1},{2,6},{6,2},{3,7},{7,3}} | collective-permute-start | bytes 1179656 | tf_op jit(solution)/shard_map/ppermute | solution.py:406
  1690.0 21.1 %copy-start = (f32[128,768]{1,0:T(8,128)}, f32[128,768]{1,0:T(8,128)S(1)}, u32[]{:S(2)}) copy-start(f32[128,768]{1,0:T(8,128)S(1)} %add.59.refs_2_.refs_0_) | copy-start | bytes 1179652
  1694.0 26.8 %collective-permute-start.37 = (f32[128,768]{1,0:T(8,128)S(1)}, f32[128,768]{1,0:T(8,128)}, u32[]{:S(2)}, u32[]{:S(2)}) collective-permute-start(f32[128,768]{1,0:T(8,128)S(1)} %add.59.refs_2_.refs_0_), channel_id=1, source_target_pairs={{0,4},{4,0},{1,5},{5,1},{2,6},{6,2},{3,7},{7,3}} | collective-permute-start | bytes 1179656 | tf_op jit(solution)/shard_map/ppermute | solution.py:406
  1697.4 23.4 %collective-permute-start.41 = (f32[64,768]{1,0:T(8,128)}, f32[64,768]{1,0:T(8,128)}, u32[]{:S(2)}, u32[]{:S(2)}) collective-permute-start(f32[64,768]{1,0:T(8,128)} %add.62.refs_0_), channel_id=1, source_target_pairs={{0,4},{4,0},{1,5},{5,1},{2,6},{6,2},{3,7},{7,3}} | collective-permute-start | bytes 589832 | tf_op jit(solution)/shard_map/ppermute | solution.py:406
  1699.7 23.8 %collective-permute-start.38 = (f32[64,768]{1,0:T(8,128)}, f32[64,768]{1,0:T(8,128)S(1)}, u32[]{:S(2)}, u32[]{:S(2)}) collective-permute-start(f32[64,768]{1,0:T(8,128)} %add.61.refs_1_), channel_id=1, source_target_pairs={{0,4},{4,0},{1,5},{5,1},{2,6},{6,2},{3,7},{7,3}} | collective-permute-start | bytes 589832 | tf_op jit(solution)/shard_map/ppermute | solution.py:406
  (11 other events, 42.0 us)

commit v7 on v5

--- a/solution.py
+++ b/solution.py
@@ -13,7 +13,7 @@
 BLOCKS = (384, 256)
 LANES = 128
 SMALL = 64
-CHUNKS = (3, 3, 2)
+CHUNKS = (5, 3)
 FIRST = 192
 ALL_VMEM = 66_000_000
 
@@ -231,10 +231,11 @@
     return value.reshape(shape[:axis] + (2, shape[axis] // 2) + shape[axis + 1 :])
 
 
-def small_call(layer, grad, x_saved, h_pair, down_pair, start, first_pair, init, finish):
+def small_call(layer, grad, x_saved, h_pair, down_pair, start, first_pair, init=None, finish=None):
     _, _, seq, hidden = grad.shape
     pairs = h_pair[0].shape[0]
     row_spec = pl.BlockSpec((2, 1, seq, hidden), lambda b: (0, b + first_pair, 0, 0))
+    early_spec = pl.BlockSpec((2, 1, seq, LANES), lambda b: (0, b + first_pair, 0, 0))
     pre_spec = pl.BlockSpec((2, 1, seq, LANES), lambda b: (0, b, 0, 0))
     h_spec = pl.BlockSpec((1, seq, LANES), lambda b: (b, 0, 0))
     down_spec = pl.BlockSpec((SMALL, hidden), lambda b: (start // SMALL, 0))
@@ -242,7 +243,7 @@
     dw_spec = pl.BlockSpec(dw_shape, lambda b: (0, 0, 0))
     in_specs = [row_spec, pl.BlockSpec((1, 2, 1, seq, hidden), lambda b: (layer, 0, b + first_pair, 0, 0)), h_spec, h_spec, down_spec, down_spec]
     if finish:
-        in_specs += [row_spec, pre_spec, pl.BlockSpec(finish[2].shape, lambda b: (0, 0))]
+        in_specs += [row_spec, early_spec, pl.BlockSpec(finish[2].shape, lambda b: (0, 0))]
     if init:
         in_specs += [dw_spec] * 2
     return pl.pallas_call(
@@ -435,7 +436,7 @@
         packed = []
         for flip in (2, 3):
             packed.append(pack_call(jnp.reshape(me ^ flip, (1,)).astype(jnp.int32), h_saved, 0, small_start, seq))
-        h_small = [[to_model(packed[0][j], 2), to_model(packed[1][j], 3)] for j in range(4)]
+        h_small = [[to_model(packed[0][j], 2), to_model(packed[1][j], 3)] for j in range(3)]
 
         up, down = [{0: w_up} for _ in range(layers)], [{0: w_down} for _ in range(layers)]
         near_up, near_down = to_model(w_up, 1), to_model(w_down, 1)
@@ -453,7 +454,8 @@
         def partial_sum(keep, give):
             theirs = to_model(give, 1)
             stay, away = pair_call(first_flag, keep, theirs)
-            return stay + to_data(away)
+            theirs = to_data(away)
+            return stay + theirs
 
         def place(pieces, layer, start, bufs):
             if len(pieces) > 1:
@@ -464,7 +466,8 @@
         near = partial_sum(dw_0, dw_1)
         grad_mid, dw_2, dw_3 = call(1, grad_out, h_one, (2, 3), carry, True)
         far = partial_sum(dw_2, dw_3)
-        kept = near + to_model(far, 2)
+        near, part = lax.optimization_barrier(near), to_model(far, 2)
+        kept = near + part
         bufs = place([(kept, to_data(kept))], 1, 0, None)
 
         carry, dw_0, dw_1 = call(0, grad_mid, [h_saved, h_near[0]], (0, 1), None, False)
@@ -487,17 +490,16 @@
         exchange(1, far[: bounds[2] - bounds[1]])
         exchange(2, far[bounds[2] - bounds[1] : bounds[3] - bounds[1]])
         carry, grad_mid, x_saved = paired(carry), paired(grad_mid), paired(x_saved, 1)
-        dw_2, dw_3, pre_1 = small_call(0, grad_mid, x_saved, h_small[0], down_pair, small_start, 0, None, None)
+        dw_2, dw_3, pre_1 = small_call(0, grad_mid, x_saved, h_small[0], down_pair, small_start, 0)
         exchange(3, jnp.concatenate([far[bounds[3] - bounds[1] :], partial_sum(dw_2, dw_3)]))
         last = small_start + SMALL
-        early, late = CHUNKS[0], CHUNKS[0] + CHUNKS[1]
-        dw_2, dw_3, grad_x = small_call(0, grad_mid, x_saved, h_small[1], down_pair, last, 0, None, (carry, pre_1, small_up))
-        dw_2, dw_3, pre_2 = small_call(0, grad_mid, x_saved, h_small[2], down_pair, last, early, (dw_2, dw_3), None)
-        grad_x = finish_call(carry, (pre_1, pre_2), small_up, early, 0, 1, grad_x)
-        dw_2, dw_3, pre_3 = small_call(0, grad_mid, x_saved, h_small[3], down_pair, last, late, (dw_2, dw_3), None)
+        early = CHUNKS[0]
+        dw_2, dw_3, grad_x = small_call(
+            0, grad_mid, x_saved, h_small[1], down_pair, last, 0, finish=(carry, pre_1, small_up))
+        dw_2, dw_3, pre_2 = small_call(
+            0, grad_mid, x_saved, h_small[2], down_pair, last, early, init=(dw_2, dw_3))
         exchange(4, partial_sum(dw_2, dw_3))
-        grad_x = finish_call(carry, (pre_1, pre_2), small_up, early, 1, 1, grad_x)
-        grad_x = finish_call(carry, (pre_1, pre_3), small_up, late, 0, 2, grad_x)
+        grad_x = finish_call(carry, (pre_1, pre_2), small_up, early, 0, 2, grad_x)
         bufs = place([pieces[0]], 0, 0, bufs)
         middle = [(*pieces[1], 0, 64), (*pieces[2], 0, 128), (*pieces[3], 0, 64)]
         bufs = place(middle, 0, bounds[1], bufs)

time: 1670 us -> 1660 us (level)
    ppermute x38 -> x36, waiting for transfers between devices: 762 us -> 750 us  [to_model(): return lax.ppermute(value, 'model', [(i, i ^ flip) for i in range(n_model)])]
    pallas_call x4 -> x3, Pallas kernels: 44 us -> 43.8 us  [small_call(): pl.pallas_call(functools.partial(small_body, init is not None, finish is...]
  transfers between devices with their start and end apart: 53 -> 51, of which waited for: 14 -> 15; matrix products, arithmetic and copies ran while one was open for 4% -> 4% of each run, Pallas kernels for 37% -> 37%
where the time goes in v7:
time: 1660 us
  waiting for transfers between devices  911 us (55%)
  Pallas kernels  607 us (37%)
  local copies, waits for them, and re-layouts  64.9 us (4%)
  starting transfers between devices  42.9 us (3%)
  other arithmetic  29.1 us (2%)
    ppermute x36, waiting for transfers between devices, to_model(): return lax.ppermute(value, 'model', [(i, i ^ flip) for i in range(n_model)])  750 us
    pallas_call x4, Pallas kernels, block_call(): pl.pallas_call(functools.partial(block_body, carry is not None, final, ro...  439 us
    ppermute x15, waiting for transfers between devices, to_data(): return lax.ppermute(value, 'data', [(0, 1), (1, 0)])  161 us
    squeeze x8, local copies, waits for them, and re-layouts, h_from(): lax.dynamic_slice(held[0], (layer, 0, begin, start), (1, rows, seq, size))  60.8 us
    pallas_call x1, Pallas kernels, wide_call(): pl.pallas_call(functools.partial(wide_body, start), out_shape=[jax.ShapeD...  54.5 us
    pallas_call x3, Pallas kernels, small_call(): pl.pallas_call(functools.partial(small_body, init is not None, finish is...  43.8 us
  transfers between devices with their start and end apart: 51, of which 15 were waited for; matrix products, arithmetic and copies ran while one was open for 4% of the time, Pallas kernels for 37%

profile of v7, /device:TPU:0, one launch (start us, length us, event | category | flops | bytes accessed | tf_op | source)
XLA Modules:
  0.0 1656.1 jit_solution(9546574784786304153)
XLA Ops:
  1.7 1.5 select_bitcast_fusion.1
  3.3 10.6 dynamic-slice_bitcast_fusion.3
  13.9 10.6 dynamic-slice_bitcast_fusion.2
  24.5 7.2 dynamic-slice_bitcast_fusion.1
  32.5 2.6 collective-permute-start.1
  35.1 2.0 collective-permute-start.2
  37.3 545.1 %collective-permute-done.2 = bf16[192,768]{1,0:T(8,128)(2,1)S(1)} collective-permute-done((bf16[192,768]{1,0:T(8,128)(2,1)S(1)}, bf16[192,768]{1,0:T(8,128)(2,1)S(1)}, u32[]{:S(2)}, u32[]{:S(2)}) %collective-permute-start.2) | collective-permute-done | bytes 294944 | tf_op jit(solution)/shard_map/ppermute | solution.py:399
  582.4 2.1 collective-permute-start.3
  584.5 41.9 %collective-permute-done.3 = bf16[576,768]{1,0:T(8,128)(2,1)S(1)} collective-permute-done((bf16[576,768]{1,0:T(8,128)(2,1)S(1)}, bf16[576,768]{1,0:T(8,128)(2,1)S(1)}, u32[]{:S(2)}, u32[]{:S(2)}) %collective-permute-start.3) | collective-permute-done | bytes 884768 | tf_op jit(solution)/shard_map/ppermute | solution.py:399
  626.5 1.7 collective-permute-start.4
  628.6 26.8 %collective-permute-done.4 = bf16[768,768]{1,0:T(8,128)(2,1)S(1)} collective-permute-done((bf16[768,768]{1,0:T(8,128)(2,1)S(1)}, bf16[768,768]{1,0:T(8,128)(2,1)S(1)}, u32[]{:S(2)}, u32[]{:S(2)}) %collective-permute-start.4) | collective-permute-done | bytes 1179680 | tf_op jit(solution)/shard_map/ppermute | solution.py:402
  655.4 24.2 %collective-permute-done.13 = bf16[768,768]{1,0:T(8,128)(2,1)S(1)} collective-permute-done((bf16[768,768]{1,0:T(8,128)(2,1)S(1)}, bf16[768,768]{1,0:T(8,128)(2,1)S(1)}, u32[]{:S(2)}, u32[]{:S(2)}) %collective-permute-start.13) | collective-permute-done | bytes 1179680 | tf_op jit(solution)/shard_map/ppermute | solution.py:402
  680.6 10.6 dynamic-slice_bitcast_fusion
  691.2 6.2 dynamic-slice_bitcast_fusion.5
  697.5 6.3 dynamic-slice_bitcast_fusion.4
  703.8 3.0 broadcast_select_fusion.2
  706.8 1.6 broadcast_select_fusion
  709.4 119.7 %shard_map.76 = (f32[16,512,768]{2,1,0:T(8,128)}, f32[2,768,768]{2,1,0:T(8,128)}, f32[2,768,768]{2,1,0:T(8,128)}) custom-call(s32[1]{0:T(128)} %bitcast._, bf16[16,512,768]{2,1,0:T(8,128)(2,1)} %refs_0_.3, bf16[2,16,512,768]{3,2,1,0:T(8,128)(2,1)} %x_ref.1, bf16[2,16,2048,768]{3,2,1,0:T(8,128)(2,1)} %hi_ref.3, ...), custom_call_target="tpu_custom_call" | custom-call | flops 77309411328 | bytes 50331648 | tf_op jit(solution)/shard_map/pallas_call | solution.py:113
  831.3 121.2 %shard_map.77 = (bf16[16,512,768]{2,1,0:T(8,128)(2,1)}, f32[2,768,768]{2,1,0:T(8,128)}, f32[2,768,768]{2,1,0:T(8,128)}) custom-call(s32[1]{0:T(128)} %bitcast._, bf16[16,512,768]{2,1,0:T(8,128)(2,1)} %refs_0_.3, bf16[2,16,512,768]{3,2,1,0:T(8,128)(2,1)} %x_ref.1, bf16[16,512,768]{2,1,0:T(8,128)(2,1)} %collective-permute-done.refs_2_, ...), custom_call_target="tpu_custom_call" | custom-call | flops 77309411328 | bytes 50331648 | tf_op jit(solution)/shard_map/pallas_call | solution.py:113
  953.0 119.5 %shard_map.78 = (f32[16,512,768]{2,1,0:T(8,128)}, f32[2,768,768]{2,1,0:T(8,128)}, f32[2,768,768]{2,1,0:T(8,128)}) custom-call(s32[1]{0:T(128)} %bitcast._, bf16[16,512,768]{2,1,0:T(8,128)(2,1)} %get-tuple-element.78.refs_0_.grad_ref, bf16[2,16,512,768]{3,2,1,0:T(8,128)(2,1)} %x_ref.1, bf16[2,16,2048,768]{3,2,1,0:T(8,128)(2,1)} %hi_ref.3, ...), custom_call_target="tpu_custom_call" | custom-call | flops 77309411328 | bytes 50331648 | tf_op jit(solution)/shard_map/pallas_call | solution.py:113
  1072.7 27.9 %collective-permute-done.17.refs_3_ = bf16[16,512,384]{2,1,0:T(8,128)(2,1)} collective-permute-done((bf16[16,512,384]{2,1,0:T(8,128)(2,1)}, bf16[16,512,384]{2,1,0:T(8,128)(2,1)}, u32[]{:S(2)}, u32[]{:S(2)}) %collective-permute-start.17) | collective-permute-done | bytes 6291488 | tf_op jit(solution)/shard_map/ppermute | solution.py:399
  1100.7 78.2 %shard_map.79 = (f32[16,512,768]{2,1,0:T(8,128)}, f32[2,384,768]{2,1,0:T(8,128)}, f32[2,384,768]{2,1,0:T(8,128)}) custom-call(s32[1]{0:T(128)} %bitcast._, bf16[16,512,768]{2,1,0:T(8,128)(2,1)} %get-tuple-element.78.refs_0_.grad_ref, bf16[2,16,512,768]{3,2,1,0:T(8,128)(2,1)} %x_ref.1, bf16[16,512,384]{2,1,0:T(8,128)(2,1)} %collective-permute-done.16.refs_2_, ...), custom_call_target="tpu_custom_call" | custom-call | flops 38654705664 | bytes 50331648 | tf_op jit(solution)/shard_map/pallas_call | solution.py:113
  1179.8 4.6 dynamic-slice_bitcast_fusion.7
  1184.3 4.6 dynamic-slice_bitcast_fusion.6
  1190.6 7.1 shard_map.94
  1199.0 6.3 shard_map.81
  1205.2 6.3 shard_map.82
  1211.5 1.5 collective-permute-start.21
  1213.0 38.4 %collective-permute-done.48 = f32[768,768]{1,0:T(8,128)} collective-permute-done((f32[768,768]{1,0:T(8,128)}, f32[768,768]{1,0:T(8,128)}, u32[]{:S(2)}, u32[]{:S(2)}) %collective-permute-start.48) | collective-permute-done | bytes 2359328 | tf_op jit(solution)/shard_map/ppermute | solution.py:402
  1251.6 4.5 shard_map.92
  1256.0 7.0 shard_map.93
  1263.1 4.2 add.67
  1267.3 113.2 %collective-permute-done.21.h_a = bf16[3,512,128]{2,1,0:T(8,128)(2,1)S(1)} collective-permute-done((bf16[3,512,128]{2,1,0:T(8,128)(2,1)}, bf16[3,512,128]{2,1,0:T(8,128)(2,1)S(1)}, u32[]{:S(2)}, u32[]{:S(2)}) %collective-permute-start.21) | collective-permute-done | bytes 393248 | tf_op jit(solution)/shard_map/ppermute | solution.py:399
  1381.8 6.8 collective-permute-done.22.h_b
  1391.8 54.5 %shard_map.80 = (f32[16,512,768]{2,1,0:T(8,128)}, f32[2,256,768]{2,1,0:T(8,128)}, f32[2,256,768]{2,1,0:T(8,128)}) custom-call(bf16[16,512,768]{2,1,0:T(8,128)(2,1)} %get-tuple-element.78.refs_0_.grad_ref, bf16[2,16,512,768]{3,2,1,0:T(8,128)(2,1)} %x_ref.1, bf16[16,512,256]{2,1,0:T(8,128)(2,1)} %collective-permute-done.10.h_a, ...), custom_call_target="tpu_custom_call" | custom-call | flops 25769803776 | bytes 75497472 | tf_op jit(solution)/shard_map/pallas_call | solution.py:191
  1446.4 7.1 shard_map.88
  1453.5 1.5 collective-permute-start.26
  1455.3 13.0 collective-permute-done.46
  1469.5 2.0 shard_map.84.refs_2_.up_ref
  1471.5 3.0 add.64
  1474.5 2.0 add.66
  1476.5 3.4 add.68.kept_ref
  1479.8 4.3 collective-permute-done.20.h_b
  1485.4 1.5 collective-permute-start.50
  1486.9 16.8 %shard_map.83 = (f32[2,64,768]{2,1,0:T(8,128)}, f32[2,64,768]{2,1,0:T(8,128)}, bf16[2,8,512,128]{3,2,1,0:T(8,128)(2,1)}) custom-call(bf16[2,8,512,768]{3,2,1,0:T(8,128)(2,1)} %bitcast.33, bf16[2,2,8,512,768]{4,3,2,1,0:T(8,128)(2,1)} %bitcast.30, bf16[8,512,128]{2,1,0:T(8,128)(2,1)} %collective-permute-done.19.h_a, ...), custom_call_target="tpu_custom_call" | custom-call | flops 4831838208 | bytes 25165824 | tf_op jit(solution)/shard_map/pallas_call | solution.py:249
  1503.7 2.9 shard_map.89
  1506.6 5.6 collective-permute-done.24.h_b
  1513.5 18.8 %shard_map.85 = (f32[2,64,768]{2,1,0:T(8,128)}, f32[2,64,768]{2,1,0:T(8,128)}, bf16[2,8,512,768]{3,2,1,0:T(8,128)(2,1)}) custom-call(bf16[2,8,512,768]{3,2,1,0:T(8,128)(2,1)} %bitcast.34, bf16[2,2,8,512,768]{4,3,2,1,0:T(8,128)(2,1)} %bitcast.31, bf16[5,512,128]{2,1,0:T(8,128)(2,1)} %copy-done.12, bf16[5,512,128]{2,1,0:T(8,128)(2,1)} %collective-permute-done.24.h_b, ...), custom_call_target="tpu_custom_call" | custom-call | flops 3019898880 | bytes 15728640 | tf_op jit(solution)/shard_map/pallas_call | solution.py:249
  1532.3 8.3 shard_map.86
  1540.8 1.9 shard_map.90
  1543.5 2.7 add.56
  1547.8 2.5 add.65.kept_ref
  1552.2 1.9 shard_map.91
  1554.1 36.4 %collective-permute-done.30 = f32[64,768]{1,0:T(8,128)} collective-permute-done((f32[64,768]{1,0:T(8,128)}, f32[64,768]{1,0:T(8,128)}, u32[]{:S(2)}, u32[]{:S(2)}) %collective-permute-start.30) | collective-permute-done | bytes 196640 | tf_op jit(solution)/shard_map/ppermute | solution.py:402
  1591.6 1.5 add.57
  1593.1 1.3 collective-permute-start.38
  1596.5 22.6 %collective-permute-done.33 = f32[64,768]{1,0:T(8,128)S(1)} collective-permute-done((f32[64,768]{1,0:T(8,128)S(1)}, f32[64,768]{1,0:T(8,128)S(1)}, u32[]{:S(2)}, u32[]{:S(2)}) %collective-permute-start.33) | collective-permute-done | bytes 196640 | tf_op jit(solution)/shard_map/ppermute | solution.py:402
  1621.3 1.3 collective-permute-start.40
  1622.6 4.3 collective-permute-done.37
  1632.3 8.4 shard_map.87
  1640.7 5.9 shard_map.95
  1646.6 3.8 shard_map.96
  1650.4 2.7 shard_map.97
  1653.8 2.2 shard_map.98
  (133 shorter events, 36.2 us)
Async XLA Ops:
  24.5 12.7 copy-start.2
  24.5 12.7 copy-start.3
  31.7 677.3 %collective-permute-start.7 = (bf16[16,512,768]{2,1,0:T(8,128)(2,1)S(1)}, bf16[16,512,768]{2,1,0:T(8,128)(2,1)}, u32[]{:S(2)}, u32[]{:S(2)}) collective-permute-start(bf16[16,512,768]{2,1,0:T(8,128)(2,1)S(1)} %dynamic-slice_bitcast_fusion.1), channel_id=1, source_target_pairs={{0,1},{1,0},{2,3},{3,2},{4,5},{5,4},{6,7},{7,6}} | collective-permute-start | bytes 37748744 | tf_op jit(solution)/shard_map/ppermute | solution.py:399
  32.5 797.9 %collective-permute-start.1 = (bf16[16,512,768]{2,1,0:T(8,128)(2,1)}, bf16[16,512,768]{2,1,0:T(8,128)(2,1)}, u32[]{:S(2)}, u32[]{:S(2)}) collective-permute-start(bf16[16,512,768]{2,1,0:T(8,128)(2,1)} %dynamic-slice_bitcast_fusion.2), channel_id=1, source_target_pairs={{0,3},{1,2},{2,1},{3,0},{4,7},{5,6},{6,5},{7,4}} | collective-permute-start | bytes 37748744 | tf_op jit(solution)/shard_map/ppermute | solution.py:399
  35.1 796.2 %collective-permute-start = (bf16[16,512,768]{2,1,0:T(8,128)(2,1)}, bf16[16,512,768]{2,1,0:T(8,128)(2,1)}, u32[]{:S(2)}, u32[]{:S(2)}) collective-permute-start(bf16[16,512,768]{2,1,0:T(8,128)(2,1)} %dynamic-slice_bitcast_fusion.3), channel_id=1, source_target_pairs={{0,2},{1,3},{2,0},{3,1},{4,6},{5,7},{6,4},{7,5}} | collective-permute-start | bytes 37748744 | tf_op jit(solution)/shard_map/ppermute | solution.py:399
  35.1 547.3 %collective-permute-start.2 = (bf16[192,768]{1,0:T(8,128)(2,1)S(1)}, bf16[192,768]{1,0:T(8,128)(2,1)S(1)}, u32[]{:S(2)}, u32[]{:S(2)}) collective-permute-start(bf16[192,768]{1,0:T(8,128)(2,1)S(1)} %select_bitcast_fusion.2), channel_id=1, source_target_pairs={{0,2},{1,3},{2,0},{3,1},{4,6},{5,7},{6,4},{7,5}} | collective-permute-start | bytes 884744 | tf_op jit(solution)/shard_map/ppermute | solution.py:399
  37.3 590.9 %collective-permute-start.12 = (bf16[768,768]{1,0:T(8,128)(2,1)S(1)}, bf16[768,768]{1,0:T(8,128)(2,1)S(1)}, u32[]{:S(2)}, u32[]{:S(2)}) collective-permute-start(bf16[768,768]{1,0:T(8,128)(2,1)S(1)} %select_bitcast_fusion), channel_id=1, source_target_pairs={{0,2},{1,3},{2,0},{3,1},{4,6},{5,7},{6,4},{7,5}} | collective-permute-start | bytes 3538952 | tf_op jit(solution)/shard_map/ppermute | solution.py:399
  582.4 44.0 %collective-permute-start.3 = (bf16[576,768]{1,0:T(8,128)(2,1)S(1)}, bf16[576,768]{1,0:T(8,128)(2,1)S(1)}, u32[]{:S(2)}, u32[]{:S(2)}) collective-permute-start(bf16[576,768]{1,0:T(8,128)(2,1)S(1)} %select_bitcast_fusion.1), channel_id=1, source_target_pairs={{0,2},{1,3},{2,0},{3,1},{4,6},{5,7},{6,4},{7,5}} | collective-permute-start | bytes 2654216 | tf_op jit(solution)/shard_map/ppermute | solution.py:399
  626.5 28.9 %collective-permute-start.4 = (bf16[768,768]{1,0:T(8,128)(2,1)S(1)}, bf16[768,768]{1,0:T(8,128)(2,1)S(1)}, u32[]{:S(2)}, u32[]{:S(2)}) collective-permute-start(bf16[768,768]{1,0:T(8,128)(2,1)S(1)} %constant_dynamic-update-slice_fusion), channel_id=1, source_target_pairs={{0,4},{4,0},{1,5},{5,1},{2,6},{6,2},{3,7},{7,3}} | collective-permute-start | bytes 3538952 | tf_op jit(solution)/shard_map/ppermute | solution.py:402
  628.2 27.2 %copy-start.6 = (bf16[768,768]{1,0:T(8,128)(2,1)}, bf16[768,768]{1,0:T(8,128)(2,1)S(1)}, u32[]{:S(2)}) copy-start(bf16[768,768]{1,0:T(8,128)(2,1)S(1)} %collective-permute-done.12) | copy-start | bytes 3538948
  628.2 51.3 %collective-permute-start.13 = (bf16[768,768]{1,0:T(8,128)(2,1)S(1)}, bf16[768,768]{1,0:T(8,128)(2,1)S(1)}, u32[]{:S(2)}, u32[]{:S(2)}) collective-permute-start(bf16[768,768]{1,0:T(8,128)(2,1)S(1)} %collective-permute-done.12), channel_id=1, source_target_pairs={{0,4},{4,0},{1,5},{5,1},{2,6},{6,2},{3,7},{7,3}} | collective-permute-start | bytes 3538952 | tf_op jit(solution)/shard_map/ppermute | solution.py:402
  655.4 24.2 %copy-start.8 = (bf16[768,768]{1,0:T(8,128)(2,1)}, bf16[768,768]{1,0:T(8,128)(2,1)S(1)}, u32[]{:S(2)}) copy-start(bf16[768,768]{1,0:T(8,128)(2,1)S(1)} %collective-permute-done.4) | copy-start | bytes 3538948
  655.4 53.0 %collective-permute-start.8 = (bf16[2,768,768]{2,1,0:T(8,128)(2,1)S(1)}, bf16[2,768,768]{2,1,0:T(8,128)(2,1)}, u32[]{:S(2)}, u32[]{:S(2)}) collective-permute-start(bf16[2,768,768]{2,1,0:T(8,128)(2,1)S(1)} %copy-done.3), channel_id=1, source_target_pairs={{0,1},{1,0},{2,3},{3,2},{4,5},{5,4},{6,7},{7,6}} | collective-permute-start | bytes 7077896 | tf_op jit(solution)/shard_map/ppermute | solution.py:399
  680.6 28.3 %collective-permute-start.9 = (bf16[2,768,768]{2,1,0:T(8,128)(2,1)S(1)}, bf16[2,768,768]{2,1,0:T(8,128)(2,1)}, u32[]{:S(2)}, u32[]{:S(2)}) collective-permute-start(bf16[2,768,768]{2,1,0:T(8,128)(2,1)S(1)} %copy-done.2), channel_id=1, source_target_pairs={{0,1},{1,0},{2,3},{3,2},{4,5},{5,4},{6,7},{7,6}} | collective-permute-start | bytes 7077896 | tf_op jit(solution)/shard_map/ppermute | solution.py:399
  708.4 244.1 %collective-permute-start.18 = (bf16[16,512,768]{2,1,0:T(8,128)(2,1)}, bf16[16,512,768]{2,1,0:T(8,128)(2,1)}, u32[]{:S(2)}, u32[]{:S(2)}) collective-permute-start(bf16[16,512,768]{2,1,0:T(8,128)(2,1)} %dynamic-slice_bitcast_fusion), channel_id=1, source_target_pairs={{0,1},{1,0},{2,3},{3,2},{4,5},{5,4},{6,7},{7,6}} | collective-permute-start | bytes 37748744 | tf_op jit(solution)/shard_map/ppermute | solution.py:399
  708.9 120.2 %collective-permute-start.5 = (bf16[768,768]{1,0:T(8,128)(2,1)}, bf16[768,768]{1,0:T(8,128)(2,1)}, u32[]{:S(2)}, u32[]{:S(2)}) collective-permute-start(bf16[768,768]{1,0:T(8,128)(2,1)} %get-tuple-element.148.refs_4_), channel_id=1, source_target_pairs={{0,1},{1,0},{2,3},{3,2},{4,5},{5,4},{6,7},{7,6}} | collective-permute-start | bytes 3538952 | tf_op jit(solution)/shard_map/ppermute | solution.py:399
  708.9 121.4 %collective-permute-start.6 = (bf16[768,768]{1,0:T(8,128)(2,1)}, bf16[768,768]{1,0:T(8,128)(2,1)}, u32[]{:S(2)}, u32[]{:S(2)}) collective-permute-start(bf16[768,768]{1,0:T(8,128)(2,1)} %get-tuple-element.147.refs_6_), channel_id=1, source_target_pairs={{0,1},{1,0},{2,3},{3,2},{4,5},{5,4},{6,7},{7,6}} | collective-permute-start | bytes 3538952 | tf_op jit(solution)/shard_map/ppermute | solution.py:399
  829.1 271.5 %collective-permute-start.16 = (bf16[16,512,384]{2,1,0:T(8,128)(2,1)}, bf16[16,512,384]{2,1,0:T(8,128)(2,1)}, u32[]{:S(2)}, u32[]{:S(2)}) collective-permute-start(bf16[16,512,384]{2,1,0:T(8,128)(2,1)} %dynamic-slice_bitcast_fusion.5), channel_id=1, source_target_pairs={{0,2},{1,3},{2,0},{3,1},{4,6},{5,7},{6,4},{7,5}} | collective-permute-start | bytes 18874376 | tf_op jit(solution)/shard_map/ppermute | solution.py:399
  830.3 270.3 %collective-permute-start.17 = (bf16[16,512,384]{2,1,0:T(8,128)(2,1)}, bf16[16,512,384]{2,1,0:T(8,128)(2,1)}, u32[]{:S(2)}, u32[]{:S(2)}) collective-permute-start(bf16[16,512,384]{2,1,0:T(8,128)(2,1)} %dynamic-slice_bitcast_fusion.4), channel_id=1, source_target_pairs={{0,3},{1,2},{2,1},{3,0},{4,7},{5,6},{6,5},{7,4}} | collective-permute-start | bytes 18874376 | tf_op jit(solution)/shard_map/ppermute | solution.py:399
  830.5 242.0 %collective-permute-start.14 = (bf16[768,768]{1,0:T(8,128)(2,1)}, bf16[768,768]{1,0:T(8,128)(2,1)}, u32[]{:S(2)}, u32[]{:S(2)}) collective-permute-start(bf16[768,768]{1,0:T(8,128)(2,1)} %get-tuple-element.146.refs_4_.up_a), channel_id=1, source_target_pairs={{0,1},{1,0},{2,3},{3,2},{4,5},{5,4},{6,7},{7,6}} | collective-permute-start | bytes 3538952 | tf_op jit(solution)/shard_map/ppermute | solution.py:399
  831.3 241.4 %collective-permute-start.15 = (bf16[768,768]{1,0:T(8,128)(2,1)}, bf16[768,768]{1,0:T(8,128)(2,1)}, u32[]{:S(2)}, u32[]{:S(2)}) collective-permute-start(bf16[768,768]{1,0:T(8,128)(2,1)} %get-tuple-element.145.refs_6_.down_a), channel_id=1, source_target_pairs={{0,1},{1,0},{2,3},{3,2},{4,5},{5,4},{6,7},{7,6}} | collective-permute-start | bytes 3538952 | tf_op jit(solution)/shard_map/ppermute | solution.py:399
  952.5 238.1 %collective-permute-start.47 = (f32[2,768,768]{2,1,0:T(8,128)}, f32[2,768,768]{2,1,0:T(8,128)}, u32[]{:S(2)}, u32[]{:S(2)}) collective-permute-start(f32[2,768,768]{2,1,0:T(8,128)} %get-tuple-element.130), channel_id=1, source_target_pairs={{0,1},{1,0},{2,3},{3,2},{4,5},{5,4},{6,7},{7,6}} | collective-permute-start | bytes 14155784 | tf_op jit(solution)/shard_map/ppermute | solution.py:399
  1072.5 139.0 %collective-permute-start.45 = (f32[2,768,768]{2,1,0:T(8,128)}, f32[2,768,768]{2,1,0:T(8,128)}, u32[]{:S(2)}, u32[]{:S(2)}) collective-permute-start(f32[2,768,768]{2,1,0:T(8,128)} %get-tuple-element.126), channel_id=1, source_target_pairs={{0,1},{1,0},{2,3},{3,2},{4,5},{5,4},{6,7},{7,6}} | collective-permute-start | bytes 14155784 | tf_op jit(solution)/shard_map/ppermute | solution.py:399
  1178.9 20.1 %collective-permute-start.41 = (f32[2,384,768]{2,1,0:T(8,128)}, f32[2,384,768]{2,1,0:T(8,128)}, u32[]{:S(2)}, u32[]{:S(2)}) collective-permute-start(f32[2,384,768]{2,1,0:T(8,128)} %get-tuple-element.122), channel_id=1, source_target_pairs={{0,1},{1,0},{2,3},{3,2},{4,5},{5,4},{6,7},{7,6}} | collective-permute-start | bytes 7077896 | tf_op jit(solution)/shard_map/ppermute | solution.py:399
  1189.0 200.9 %collective-permute-start.11 = (bf16[16,512,256]{2,1,0:T(8,128)(2,1)}, bf16[16,512,256]{2,1,0:T(8,128)(2,1)}, u32[]{:S(2)}, u32[]{:S(2)}) collective-permute-start(bf16[16,512,256]{2,1,0:T(8,128)(2,1)} %dynamic-slice_bitcast_fusion.6), channel_id=1, source_target_pairs={{0,3},{1,2},{2,1},{3,0},{4,7},{5,6},{6,5},{7,4}} | collective-permute-start | bytes 12582920 | tf_op jit(solution)/shard_map/ppermute | solution.py:399
  1189.8 200.8 %collective-permute-start.10 = (bf16[16,512,256]{2,1,0:T(8,128)(2,1)}, bf16[16,512,256]{2,1,0:T(8,128)(2,1)}, u32[]{:S(2)}, u32[]{:S(2)}) collective-permute-start(bf16[16,512,256]{2,1,0:T(8,128)(2,1)} %dynamic-slice_bitcast_fusion.7), channel_id=1, source_target_pairs={{0,2},{1,3},{2,0},{3,1},{4,6},{5,7},{6,4},{7,5}} | collective-permute-start | bytes 12582920 | tf_op jit(solution)/shard_map/ppermute | solution.py:399
  1197.7 53.7 %collective-permute-start.48 = (f32[768,768]{1,0:T(8,128)}, f32[768,768]{1,0:T(8,128)}, u32[]{:S(2)}, u32[]{:S(2)}) collective-permute-start(f32[768,768]{1,0:T(8,128)} %get-tuple-element.132), channel_id=1, source_target_pairs={{0,4},{4,0},{1,5},{5,1},{2,6},{6,2},{3,7},{7,3}} | collective-permute-start | bytes 7077896 | tf_op jit(solution)/shard_map/ppermute | solution.py:402
  1199.0 247.4 %collective-permute-start.25 = (f32[2,768,768]{2,1,0:T(8,128)}, f32[2,768,768]{2,1,0:T(8,128)}, u32[]{:S(2)}, u32[]{:S(2)}) collective-permute-start(f32[2,768,768]{2,1,0:T(8,128)} %get-tuple-element.101), channel_id=1, source_target_pairs={{0,1},{1,0},{2,3},{3,2},{4,5},{5,4},{6,7},{7,6}} | collective-permute-start | bytes 14155784 | tf_op jit(solution)/shard_map/ppermute | solution.py:399
  1211.5 169.0 %collective-permute-start.21 = (bf16[3,512,128]{2,1,0:T(8,128)(2,1)}, bf16[3,512,128]{2,1,0:T(8,128)(2,1)S(1)}, u32[]{:S(2)}, u32[]{:S(2)}) collective-permute-start(bf16[3,512,128]{2,1,0:T(8,128)(2,1)} %get-tuple-element.92), channel_id=1, source_target_pairs={{0,2},{1,3},{2,0},{3,1},{4,6},{5,7},{6,4},{7,5}} | collective-permute-start | bytes 1179656 | tf_op jit(solution)/shard_map/ppermute | solution.py:399
  1251.4 137.2 %collective-permute-start.22 = (bf16[3,512,128]{2,1,0:T(8,128)(2,1)}, bf16[3,512,128]{2,1,0:T(8,128)(2,1)S(1)}, u32[]{:S(2)}, u32[]{:S(2)}) collective-permute-start(bf16[3,512,128]{2,1,0:T(8,128)(2,1)} %get-tuple-element.93), channel_id=1, source_target_pairs={{0,3},{1,2},{2,1},{3,0},{4,7},{5,6},{6,5},{7,4}} | collective-permute-start | bytes 1179656 | tf_op jit(solution)/shard_map/ppermute | solution.py:399
  1380.6 65.8 %copy-start.13 = (bf16[3,512,128]{2,1,0:T(8,128)(2,1)}, bf16[3,512,128]{2,1,0:T(8,128)(2,1)S(1)}, u32[]{:S(2)}) copy-start(bf16[3,512,128]{2,1,0:T(8,128)(2,1)S(1)} %collective-permute-done.21.h_a) | copy-start | bytes 1179652
  1380.6 72.9 %collective-permute-start.19 = (bf16[8,512,128]{2,1,0:T(8,128)(2,1)}, bf16[8,512,128]{2,1,0:T(8,128)(2,1)}, u32[]{:S(2)}, u32[]{:S(2)}) collective-permute-start(bf16[8,512,128]{2,1,0:T(8,128)(2,1)} %get-tuple-element.89), channel_id=1, source_target_pairs={{0,2},{1,3},{2,0},{3,1},{4,6},{5,7},{6,4},{7,5}} | collective-permute-start | bytes 3145736 | tf_op jit(solution)/shard_map/ppermute | solution.py:399
  1388.6 57.8 %copy-start.14 = (bf16[3,512,128]{2,1,0:T(8,128)(2,1)}, bf16[3,512,128]{2,1,0:T(8,128)(2,1)S(1)}, u32[]{:S(2)}) copy-start(bf16[3,512,128]{2,1,0:T(8,128)(2,1)S(1)} %collective-permute-done.22.h_b) | copy-start | bytes 1179652
  1388.6 66.4 %collective-permute-start.42 = (f32[384,768]{1,0:T(8,128)}, f32[384,768]{1,0:T(8,128)}, u32[]{:S(2)}, u32[]{:S(2)}) collective-permute-start(f32[384,768]{1,0:T(8,128)} %get-tuple-element.124), channel_id=1, source_target_pairs={{0,4},{4,0},{1,5},{5,1},{2,6},{6,2},{3,7},{7,3}} | collective-permute-start | bytes 3538952 | tf_op jit(solution)/shard_map/ppermute | solution.py:402
  1389.8 78.5 %collective-permute-start.46 = (f32[768,768]{1,0:T(8,128)}, f32[768,768]{1,0:T(8,128)}, u32[]{:S(2)}, u32[]{:S(2)}) collective-permute-start(f32[768,768]{1,0:T(8,128)} %get-tuple-element.128), channel_id=1, source_target_pairs={{0,4},{4,0},{1,5},{5,1},{2,6},{6,2},{3,7},{7,3}} | collective-permute-start | bytes 7077896 | tf_op jit(solution)/shard_map/ppermute | solution.py:402
  1390.6 78.9 %collective-permute-start.49 = (f32[768,768]{1,0:T(8,128)}, f32[768,768]{1,0:T(8,128)}, u32[]{:S(2)}, u32[]{:S(2)}) collective-permute-start(f32[768,768]{1,0:T(8,128)} %add.67), channel_id=1, source_target_pairs={{0,2},{1,3},{2,0},{3,1},{4,6},{5,7},{6,4},{7,5}} | collective-permute-start | bytes 7077896 | tf_op jit(solution)/shard_map/ppermute | solution.py:399
  1446.4 39.1 %collective-permute-start.27 = (f32[2,256,768]{2,1,0:T(8,128)}, f32[2,256,768]{2,1,0:T(8,128)}, u32[]{:S(2)}, u32[]{:S(2)}) collective-permute-start(f32[2,256,768]{2,1,0:T(8,128)} %get-tuple-element.106), channel_id=1, source_target_pairs={{0,1},{1,0},{2,3},{3,2},{4,5},{5,4},{6,7},{7,6}} | collective-permute-start | bytes 4718600 | tf_op jit(solution)/shard_map/ppermute | solution.py:399
  1453.5 89.3 %collective-permute-start.26 = (f32[768,768]{1,0:T(8,128)}, f32[768,768]{1,0:T(8,128)}, u32[]{:S(2)}, u32[]{:S(2)}) collective-permute-start(f32[768,768]{1,0:T(8,128)} %get-tuple-element.103), channel_id=1, source_target_pairs={{0,4},{4,0},{1,5},{5,1},{2,6},{6,2},{3,7},{7,3}} | collective-permute-start | bytes 7077896 | tf_op jit(solution)/shard_map/ppermute | solution.py:402
  1455.0 29.2 %collective-permute-start.20 = (bf16[8,512,128]{2,1,0:T(8,128)(2,1)}, bf16[8,512,128]{2,1,0:T(8,128)(2,1)}, u32[]{:S(2)}, u32[]{:S(2)}) collective-permute-start(bf16[8,512,128]{2,1,0:T(8,128)(2,1)} %get-tuple-element.90), channel_id=1, source_target_pairs={{0,3},{1,2},{2,1},{3,0},{4,7},{5,6},{6,5},{7,4}} | collective-permute-start | bytes 3145736 | tf_op jit(solution)/shard_map/ppermute | solution.py:399
  1468.3 38.3 %collective-permute-start.23 = (bf16[5,512,128]{2,1,0:T(8,128)(2,1)}, bf16[5,512,128]{2,1,0:T(8,128)(2,1)S(1)}, u32[]{:S(2)}, u32[]{:S(2)}) collective-permute-start(bf16[5,512,128]{2,1,0:T(8,128)(2,1)} %get-tuple-element.94), channel_id=1, source_target_pairs={{0,2},{1,3},{2,0},{3,1},{4,6},{5,7},{6,4},{7,5}} | collective-permute-start | bytes 1966088 | tf_op jit(solution)/shard_map/ppermute | solution.py:399
  1469.5 42.7 %collective-permute-start.24 = (bf16[5,512,128]{2,1,0:T(8,128)(2,1)}, bf16[5,512,128]{2,1,0:T(8,128)(2,1)}, u32[]{:S(2)}, u32[]{:S(2)}) collective-permute-start(bf16[5,512,128]{2,1,0:T(8,128)(2,1)} %get-tuple-element.95), channel_id=1, source_target_pairs={{0,3},{1,2},{2,1},{3,0},{4,7},{5,6},{6,5},{7,4}} | collective-permute-start | bytes 1966088 | tf_op jit(solution)/shard_map/ppermute | solution.py:399
  1484.2 63.6 %collective-permute-start.43 = (f32[384,768]{1,0:T(8,128)}, f32[384,768]{1,0:T(8,128)}, u32[]{:S(2)}, u32[]{:S(2)}) collective-permute-start(f32[384,768]{1,0:T(8,128)} %add.64), channel_id=1, source_target_pairs={{0,2},{1,3},{2,0},{3,1},{4,6},{5,7},{6,4},{7,5}} | collective-permute-start | bytes 3538952 | tf_op jit(solution)/shard_map/ppermute | solution.py:399
  1485.4 146.1 %collective-permute-start.50 = (f32[768,768]{1,0:T(8,128)}, f32[768,768]{1,0:T(8,128)}, u32[]{:S(2)}, u32[]{:S(2)}) collective-permute-start(f32[768,768]{1,0:T(8,128)} %add.68.kept_ref), channel_id=1, source_target_pairs={{0,4},{4,0},{1,5},{5,1},{2,6},{6,2},{3,7},{7,3}} | collective-permute-start | bytes 7077896 | tf_op jit(solution)/shard_map/ppermute | solution.py:402
  1506.6 6.9 copy-start.12
  1506.6 33.9 %collective-permute-start.29 = (f32[2,64,768]{2,1,0:T(8,128)}, f32[2,64,768]{2,1,0:T(8,128)}, u32[]{:S(2)}, u32[]{:S(2)}) collective-permute-start(f32[2,64,768]{2,1,0:T(8,128)} %get-tuple-element.110), channel_id=1, source_target_pairs={{0,1},{1,0},{2,3},{3,2},{4,5},{5,4},{6,7},{7,6}} | collective-permute-start | bytes 1179656 | tf_op jit(solution)/shard_map/ppermute | solution.py:399
  1512.3 79.3 %collective-permute-start.28 = (f32[256,768]{1,0:T(8,128)}, f32[256,768]{1,0:T(8,128)}, u32[]{:S(2)}, u32[]{:S(2)}) collective-permute-start(f32[256,768]{1,0:T(8,128)} %get-tuple-element.108), channel_id=1, source_target_pairs={{0,4},{4,0},{1,5},{5,1},{2,6},{6,2},{3,7},{7,3}} | collective-permute-start | bytes 2359304 | tf_op jit(solution)/shard_map/ppermute | solution.py:402
  1540.6 10.9 collective-permute-start.32
  1542.7 47.7 %collective-permute-start.30 = (f32[64,768]{1,0:T(8,128)}, f32[64,768]{1,0:T(8,128)}, u32[]{:S(2)}, u32[]{:S(2)}) collective-permute-start(f32[64,768]{1,0:T(8,128)} %get-tuple-element.112), channel_id=1, source_target_pairs={{0,4},{4,0},{1,5},{5,1},{2,6},{6,2},{3,7},{7,3}} | collective-permute-start | bytes 589832 | tf_op jit(solution)/shard_map/ppermute | solution.py:402
  1550.2 96.4 %collective-permute-start.44 = (f32[384,768]{1,0:T(8,128)}, f32[384,768]{1,0:T(8,128)}, u32[]{:S(2)}, u32[]{:S(2)}) collective-permute-start(f32[384,768]{1,0:T(8,128)} %add.65.kept_ref), channel_id=1, source_target_pairs={{0,4},{4,0},{1,5},{5,1},{2,6},{6,2},{3,7},{7,3}} | collective-permute-start | bytes 3538952 | tf_op jit(solution)/shard_map/ppermute | solution.py:402
  1591.5 3.7 copy-start.18
  1591.5 28.8 %copy-start.16 = (f32[64,768]{1,0:T(8,128)S(1)}, f32[64,768]{1,0:T(8,128)}, u32[]{:S(2)}) copy-start(f32[64,768]{1,0:T(8,128)} %get-tuple-element.116) | copy-start | bytes 589828
  1593.1 29.5 %copy-start.5 = (f32[128,768]{1,0:T(8,128)S(1)}, f32[128,768]{1,0:T(8,128)}, u32[]{:S(2)}) copy-start(f32[128,768]{1,0:T(8,128)} %get-tuple-element.104) | copy-start | bytes 1179652
  1593.1 35.0 %copy-start.11 = (f32[64,768]{1,0:T(8,128)S(1)}, f32[64,768]{1,0:T(8,128)}, u32[]{:S(2)}) copy-start(f32[64,768]{1,0:T(8,128)} %get-tuple-element.118) | copy-start | bytes 589828
  1593.1 27.3 %collective-permute-start.38 = (f32[128,768]{1,0:T(8,128)S(1)}, f32[128,768]{1,0:T(8,128)S(1)}, u32[]{:S(2)}, u32[]{:S(2)}) collective-permute-start(f32[128,768]{1,0:T(8,128)S(1)} %slice.63), channel_id=1, source_target_pairs={{0,2},{1,3},{2,0},{3,1},{4,6},{5,7},{6,4},{7,5}} | collective-permute-start | bytes 1179656 | tf_op jit(solution)/shard_map/ppermute | solution.py:399
  1594.4 26.8 %collective-permute-start.31 = (f32[128,768]{1,0:T(8,128)S(1)}, f32[128,768]{1,0:T(8,128)S(1)}, u32[]{:S(2)}, u32[]{:S(2)}) collective-permute-start(f32[128,768]{1,0:T(8,128)S(1)} %pad_maximum_fusion), channel_id=1, source_target_pairs={{0,2},{1,3},{2,0},{3,1},{4,6},{5,7},{6,4},{7,5}} | collective-permute-start | bytes 1179656 | tf_op jit(solution)/shard_map/ppermute | solution.py:399
  1595.3 23.9 %collective-permute-start.33 = (f32[64,768]{1,0:T(8,128)S(1)}, f32[64,768]{1,0:T(8,128)S(1)}, u32[]{:S(2)}, u32[]{:S(2)}) collective-permute-start(f32[64,768]{1,0:T(8,128)S(1)} %copy-done.18), channel_id=1, source_target_pairs={{0,4},{4,0},{1,5},{5,1},{2,6},{6,2},{3,7},{7,3}} | collective-permute-start | bytes 589832 | tf_op jit(solution)/shard_map/ppermute | solution.py:402
  1619.1 7.8 collective-permute-start.37
  1620.4 9.1 collective-permute-start.34
  1621.3 19.4 %copy-start.4 = (f32[128,768]{1,0:T(8,128)}, f32[128,768]{1,0:T(8,128)S(1)}, u32[]{:S(2)}) copy-start(f32[128,768]{1,0:T(8,128)S(1)} %add.63.refs_1_) | copy-start | bytes 1179652
  1621.3 29.1 %collective-permute-start.40 = (f32[128,768]{1,0:T(8,128)S(1)}, f32[128,768]{1,0:T(8,128)}, u32[]{:S(2)}, u32[]{:S(2)}) collective-permute-start(f32[128,768]{1,0:T(8,128)S(1)} %add.63.refs_1_), channel_id=1, source_target_pairs={{0,4},{4,0},{1,5},{5,1},{2,6},{6,2},{3,7},{7,3}} | collective-permute-start | bytes 1179656 | tf_op jit(solution)/shard_map/ppermute | solution.py:402
  1622.6 18.1 %copy-start = (f32[128,768]{1,0:T(8,128)}, f32[128,768]{1,0:T(8,128)S(1)}, u32[]{:S(2)}) copy-start(f32[128,768]{1,0:T(8,128)S(1)} %add.59.refs_2_.refs_0_) | copy-start | bytes 1179652
  1626.9 23.5 %collective-permute-start.35 = (f32[128,768]{1,0:T(8,128)S(1)}, f32[128,768]{1,0:T(8,128)}, u32[]{:S(2)}, u32[]{:S(2)}) collective-permute-start(f32[128,768]{1,0:T(8,128)S(1)} %add.59.refs_2_.refs_0_), channel_id=1, source_target_pairs={{0,4},{4,0},{1,5},{5,1},{2,6},{6,2},{3,7},{7,3}} | collective-permute-start | bytes 1179656 | tf_op jit(solution)/shard_map/ppermute | solution.py:402
  1629.5 20.9 %collective-permute-start.39 = (f32[64,768]{1,0:T(8,128)}, f32[64,768]{1,0:T(8,128)}, u32[]{:S(2)}, u32[]{:S(2)}) collective-permute-start(f32[64,768]{1,0:T(8,128)} %add.62.refs_0_), channel_id=1, source_target_pairs={{0,4},{4,0},{1,5},{5,1},{2,6},{6,2},{3,7},{7,3}} | collective-permute-start | bytes 589832 | tf_op jit(solution)/shard_map/ppermute | solution.py:402
  1631.5 21.6 %collective-permute-start.36 = (f32[64,768]{1,0:T(8,128)}, f32[64,768]{1,0:T(8,128)S(1)}, u32[]{:S(2)}, u32[]{:S(2)}) collective-permute-start(f32[64,768]{1,0:T(8,128)} %add.61.refs_1_), channel_id=1, source_target_pairs={{0,4},{4,0},{1,5},{5,1},{2,6},{6,2},{3,7},{7,3}} | collective-permute-start | bytes 589832 | tf_op jit(solution)/shard_map/ppermute | solution.py:402
  (6 other events, 11.5 us)

commit v8 on v7

--- a/solution.py
+++ b/solution.py
@@ -13,7 +13,7 @@
 BLOCKS = (384, 256)
 LANES = 128
 SMALL = 64
-CHUNKS = (5, 3)
+CHUNKS = (3, 3, 2)
 FIRST = 192
 ALL_VMEM = 66_000_000
 
@@ -354,12 +354,24 @@
     )(first, kept, other, *(bufs or ()))
 
 
-def join_place_body(count, layer, start, first_ref, *refs):
-    up_out, down_out, up_ref, down_ref, sem = refs[-5:]
+def join_place_body(spans, layer, start, first_ref, *refs):
+    count = len(spans)
+    size = sum(n for _, n in spans)
+    mine_ref, theirs_ref = refs[2 * count : 2 * count + 2]
+    up_out, down_out, near_ref, far_ref, up_ref, down_ref, sem = refs[-7:]
+    loads = [(ref.at[pl.ds(start, size)], near_ref.at[k]) for k, ref in enumerate((mine_ref, theirs_ref))]
+    for k in range(2):
+        place = 0
+        for (low, n), ref in zip(spans, refs[k * count : (k + 1) * count]):
+            loads.append((ref.at[pl.ds(low, n)], far_ref.at[k, pl.ds(place, n)]))
+            place += n
+    copies = [pltpu.make_async_copy(src, dst, sem.at[i]) for i, (src, dst) in enumerate(loads)]
+    for copy in copies:
+        copy.start()
+    for copy in copies:
+        copy.wait()
     first = first_ref[0] == 1
-    kept = jnp.concatenate([r[...] for r in refs[:count]])
-    other = jnp.concatenate([r[...] for r in refs[count : 2 * count]])
-    size = kept.shape[0]
+    kept, other = near_ref[0] + far_ref[0], near_ref[1] + far_ref[1]
     down_ref[...] = jnp.where(first, other, kept)
     down_copy = pltpu.make_async_copy(down_ref, down_out.at[layer, pl.ds(start, size), :], sem.at[0])
     down_copy.start()
@@ -370,26 +382,27 @@
     up_copy.wait()
 
 
-def join_place_call(first, pieces, layer, start, bufs):
-    hidden = pieces[0][0].shape[1]
-    size = sum(n for _, _, _, n in pieces)
-    piece_specs = [pl.BlockSpec((n, hidden), lambda i, first, block=low // n: (block, 0)) for _, _, low, n in pieces]
+def join_place_call(first, pieces, near_pair, layer, start, bufs):
+    hidden = near_pair[0].shape[1]
+    spans = [(low, n) for _, _, low, n in pieces]
+    size = sum(n for _, n in spans)
     any_spec = pl.BlockSpec(memory_space=pl.ANY)
-    count = len(pieces)
-    return pl.pallas_call(
-        functools.partial(join_place_body, count, layer, start),
+    count = 2 * len(pieces) + 2
+    return pl.pallas_call(
+        functools.partial(join_place_body, spans, layer, start),
         out_shape=[jax.ShapeDtypeStruct(b.shape, b.dtype) for b in bufs],
         grid_spec=pltpu.PrefetchScalarGridSpec(
             num_scalar_prefetch=1,
             grid=(1,),
-            in_specs=piece_specs * 2 + [any_spec] * 2,
+            in_specs=[any_spec] * (count + 2),
             out_specs=[any_spec] * 2,
-            scratch_shapes=[pltpu.VMEM((hidden, size), F32), pltpu.VMEM((size, hidden), F32), pltpu.SemaphoreType.DMA((2,))],
+            scratch_shapes=[pltpu.VMEM((2, size, hidden), F32)] * 2
+            + [pltpu.VMEM((hidden, size), F32), pltpu.VMEM((size, hidden), F32), pltpu.SemaphoreType.DMA((count,))],
         ),
-        input_output_aliases={1 + 2 * count: 0, 2 + 2 * count: 1},
-        compiler_params=pltpu.CompilerParams(dimension_semantics=("arbitrary",), vmem_limit_bytes=ALL_VMEM),
-        cost_estimate=pl.CostEstimate(flops=4 * size * hidden, bytes_accessed=16 * size * hidden, transcendentals=0),
-    )(first, *[p[0] for p in pieces], *[p[1] for p in pieces], *bufs)
+        input_output_aliases={1 + count: 0, 2 + count: 1},
+        compiler_params=pltpu.CompilerParams(dimension_semantics=("arbitrary",), vmem_limit_bytes=ALL_VMEM),
+        cost_estimate=pl.CostEstimate(flops=4 * size * hidden, bytes_accessed=24 * size * hidden, transcendentals=0),
+    )(first, *[p[0] for p in pieces], *[p[1] for p in pieces], *near_pair, *bufs)
 
 
 def solution(mesh):
@@ -436,7 +449,7 @@
         packed = []
         for flip in (2, 3):
             packed.append(pack_call(jnp.reshape(me ^ flip, (1,)).astype(jnp.int32), h_saved, 0, small_start, seq))
-        h_small = [[to_model(packed[0][j], 2), to_model(packed[1][j], 3)] for j in range(3)]
+        h_small = [[to_model(packed[0][j], 2), to_model(packed[1][j], 3)] for j in range(4)]
 
         up, down = [{0: w_up} for _ in range(layers)], [{0: w_down} for _ in range(layers)]
         near_up, near_down = to_model(w_up, 1), to_model(w_down, 1)
@@ -457,9 +470,9 @@
             theirs = to_data(away)
             return stay + theirs
 
-        def place(pieces, layer, start, bufs):
-            if len(pieces) > 1:
-                return join_place_call(first_flag, pieces, layer, start, bufs)
+        def place(pieces, layer, start, bufs, near_pair=None):
+            if near_pair is not None:
+                return join_place_call(first_flag, pieces, near_pair, layer, start, bufs)
             return place_call(first_flag, *pieces[0], layer, start, layers, width, bufs)
 
         carry, dw_0, dw_1 = call(1, grad_out, [h_saved, h_near[1]], (0, 1), None, False)
@@ -473,37 +486,39 @@
         carry, dw_0, dw_1 = call(0, grad_mid, [h_saved, h_near[0]], (0, 1), None, False)
         near = partial_sum(dw_0, dw_1)
         bounds = [0, 384, 448, 576, width - SMALL, width]
-        near_part = lax.optimization_barrier(tuple(near[a:b] for a, b in zip(bounds, bounds[1:])))
+        near_pair = (near, to_data(near))
         pieces = []
 
-        def exchange(unit, far):
+        def exchange(far):
             part = to_model(far, 2)
-            kept = near_part[unit] + part
-            pieces.append((kept, to_data(kept)))
+            pieces.append((part, to_data(part)))
 
         down_pair, up_pair = [down[0][f] for f in (2, 3)], [up[0][f] for f in (2, 3)]
         small_up = join_call(up_pair, small_start)
         carry, dw_2, dw_3 = call(0, grad_mid, h_zero[0], (2, 3), carry, False, 0, BLOCKS[0])
-        exchange(0, partial_sum(dw_2, dw_3))
+        exchange(partial_sum(dw_2, dw_3))
         carry, dw_2, dw_3 = wide_call(0, grad_mid, x_saved, h_zero[1], up_pair, down_pair, BLOCKS[0], carry)
         far = partial_sum(dw_2, dw_3)
-        exchange(1, far[: bounds[2] - bounds[1]])
-        exchange(2, far[bounds[2] - bounds[1] : bounds[3] - bounds[1]])
+        exchange(far[: bounds[2] - bounds[1]])
+        exchange(far[bounds[2] - bounds[1] : bounds[3] - bounds[1]])
         carry, grad_mid, x_saved = paired(carry), paired(grad_mid), paired(x_saved, 1)
         dw_2, dw_3, pre_1 = small_call(0, grad_mid, x_saved, h_small[0], down_pair, small_start, 0)
-        exchange(3, jnp.concatenate([far[bounds[3] - bounds[1] :], partial_sum(dw_2, dw_3)]))
+        exchange(jnp.concatenate([far[bounds[3] - bounds[1] :], partial_sum(dw_2, dw_3)]))
         last = small_start + SMALL
-        early = CHUNKS[0]
+        early, late = CHUNKS[0], CHUNKS[0] + CHUNKS[1]
         dw_2, dw_3, grad_x = small_call(
             0, grad_mid, x_saved, h_small[1], down_pair, last, 0, finish=(carry, pre_1, small_up))
         dw_2, dw_3, pre_2 = small_call(
             0, grad_mid, x_saved, h_small[2], down_pair, last, early, init=(dw_2, dw_3))
-        exchange(4, partial_sum(dw_2, dw_3))
+        dw_2, dw_3, pre_3 = small_call(
+            0, grad_mid, x_saved, h_small[3], down_pair, last, late, init=(dw_2, dw_3))
+        exchange(partial_sum(dw_2, dw_3))
         grad_x = finish_call(carry, (pre_1, pre_2), small_up, early, 0, 2, grad_x)
-        bufs = place([pieces[0]], 0, 0, bufs)
+        grad_x = finish_call(carry, (pre_1, pre_3), small_up, late, 0, 2, grad_x)
+        bufs = place([(*pieces[0], 0, bounds[1])], 0, 0, bufs, near_pair)
         middle = [(*pieces[1], 0, 64), (*pieces[2], 0, 128), (*pieces[3], 0, 64)]
-        bufs = place(middle, 0, bounds[1], bufs)
-        bufs = place([(*pieces[3], 64, 64), (*pieces[4], 0, 64)], 0, small_start, bufs)
+        bufs = place(middle, 0, bounds[1], bufs, near_pair)
+        bufs = place([(*pieces[3], 64, 64), (*pieces[4], 0, 64)], 0, small_start, bufs, near_pair)
         grad_x = grad_x.reshape(grad_out.shape)
         return grad_x, bufs[0], bufs[1]
 

time: 1660 us -> 1750 us (1.054)
  waiting for transfers between devices: 911 us -> 1000 us
    ppermute x15 -> x16, waiting for transfers between devices: 161 us -> 240 us  [to_data(): return lax.ppermute(value, 'data', [(0, 1), (1, 0)])]
    ppermute x36 -> x38, waiting for transfers between devices: 750 us -> 760 us  [to_model(): return lax.ppermute(value, 'model', [(i, i ^ flip) for i in range(n_model)])]
    pallas_call x3 -> x4, Pallas kernels: 43.8 us -> 44 us  [small_call(): pl.pallas_call(functools.partial(small_body, init is not None, finish is...]
  transfers between devices with their start and end apart: 51 -> 54, of which waited for: 15 -> 14; matrix products, arithmetic and copies ran while one was open for 4% -> 3% of each run, Pallas kernels for 37% -> 35%
where the time goes in v8:
time: 1750 us
  waiting for transfers between devices  1000 us (57%)
  Pallas kernels  614 us (35%)
  local copies, waits for them, and re-layouts  62.8 us (4%)
  starting transfers between devices  46.6 us (3%)
  other arithmetic  26.1 us (1%)
    ppermute x38, waiting for transfers between devices, to_model(): return lax.ppermute(value, 'model', [(i, i ^ flip) for i in range(n_model)])  760 us
    pallas_call x4, Pallas kernels, block_call(): pl.pallas_call(functools.partial(block_body, carry is not None, final, ro...  439 us
    ppermute x16, waiting for transfers between devices, to_data(): return lax.ppermute(value, 'data', [(0, 1), (1, 0)])  240 us
    squeeze x8, local copies, waits for them, and re-layouts, h_from(): lax.dynamic_slice(held[0], (layer, 0, begin, start), (1, rows, seq, size))  60.7 us
    pallas_call x1, Pallas kernels, wide_call(): pl.pallas_call(functools.partial(wide_body, start), out_shape=[jax.ShapeD...  54.5 us
    pallas_call x4, Pallas kernels, small_call(): pl.pallas_call(functools.partial(small_body, init is not None, finish is...  44 us
  transfers between devices with their start and end apart: 54, of which 14 were waited for; matrix products, arithmetic and copies ran while one was open for 3% of the time, Pallas kernels for 35%

profile of v8, /device:TPU:0, one launch (start us, length us, event | category | flops | bytes accessed | tf_op | source)
XLA Modules:
  0.0 1750.3 jit_solution(5405185428570155278)
XLA Ops:
  1.7 1.5 select_bitcast_fusion.1
  3.3 10.6 dynamic-slice_bitcast_fusion.3
  13.9 10.6 dynamic-slice_bitcast_fusion.2
  24.5 7.2 dynamic-slice_bitcast_fusion.1
  32.5 2.6 collective-permute-start.1
  35.1 2.0 collective-permute-start.2
  37.3 545.1 %collective-permute-done.2 = bf16[192,768]{1,0:T(8,128)(2,1)S(1)} collective-permute-done((bf16[192,768]{1,0:T(8,128)(2,1)S(1)}, bf16[192,768]{1,0:T(8,128)(2,1)S(1)}, u32[]{:S(2)}, u32[]{:S(2)}) %collective-permute-start.2) | collective-permute-done | bytes 294944 | tf_op jit(solution)/shard_map/ppermute | solution.py:412
  582.4 2.1 collective-permute-start.3
  584.5 41.9 %collective-permute-done.3 = bf16[576,768]{1,0:T(8,128)(2,1)S(1)} collective-permute-done((bf16[576,768]{1,0:T(8,128)(2,1)S(1)}, bf16[576,768]{1,0:T(8,128)(2,1)S(1)}, u32[]{:S(2)}, u32[]{:S(2)}) %collective-permute-start.3) | collective-permute-done | bytes 884768 | tf_op jit(solution)/shard_map/ppermute | solution.py:412
  626.5 1.7 collective-permute-start.4
  628.6 26.8 %collective-permute-done.4 = bf16[768,768]{1,0:T(8,128)(2,1)S(1)} collective-permute-done((bf16[768,768]{1,0:T(8,128)(2,1)S(1)}, bf16[768,768]{1,0:T(8,128)(2,1)S(1)}, u32[]{:S(2)}, u32[]{:S(2)}) %collective-permute-start.4) | collective-permute-done | bytes 1179680 | tf_op jit(solution)/shard_map/ppermute | solution.py:415
  655.4 24.2 %collective-permute-done.13 = bf16[768,768]{1,0:T(8,128)(2,1)S(1)} collective-permute-done((bf16[768,768]{1,0:T(8,128)(2,1)S(1)}, bf16[768,768]{1,0:T(8,128)(2,1)S(1)}, u32[]{:S(2)}, u32[]{:S(2)}) %collective-permute-start.13) | collective-permute-done | bytes 1179680 | tf_op jit(solution)/shard_map/ppermute | solution.py:415
  680.6 10.6 dynamic-slice_bitcast_fusion
  691.2 6.2 dynamic-slice_bitcast_fusion.5
  697.5 6.3 dynamic-slice_bitcast_fusion.4
  703.8 3.0 broadcast_select_fusion.2
  706.8 1.6 broadcast_select_fusion
  709.4 119.7 %shard_map.76 = (f32[16,512,768]{2,1,0:T(8,128)}, f32[2,768,768]{2,1,0:T(8,128)}, f32[2,768,768]{2,1,0:T(8,128)}) custom-call(s32[1]{0:T(128)} %bitcast._, bf16[16,512,768]{2,1,0:T(8,128)(2,1)} %refs_0_.3, bf16[2,16,512,768]{3,2,1,0:T(8,128)(2,1)} %x_ref.1, bf16[2,16,2048,768]{3,2,1,0:T(8,128)(2,1)} %hi_ref.3, ...), custom_call_target="tpu_custom_call" | custom-call | flops 77309411328 | bytes 50331648 | tf_op jit(solution)/shard_map/pallas_call | solution.py:113
  831.3 121.2 %shard_map.77 = (bf16[16,512,768]{2,1,0:T(8,128)(2,1)}, f32[2,768,768]{2,1,0:T(8,128)}, f32[2,768,768]{2,1,0:T(8,128)}) custom-call(s32[1]{0:T(128)} %bitcast._, bf16[16,512,768]{2,1,0:T(8,128)(2,1)} %refs_0_.3, bf16[2,16,512,768]{3,2,1,0:T(8,128)(2,1)} %x_ref.1, bf16[16,512,768]{2,1,0:T(8,128)(2,1)} %collective-permute-done.refs_2_, ...), custom_call_target="tpu_custom_call" | custom-call | flops 77309411328 | bytes 50331648 | tf_op jit(solution)/shard_map/pallas_call | solution.py:113
  953.0 119.5 %shard_map.78 = (f32[16,512,768]{2,1,0:T(8,128)}, f32[2,768,768]{2,1,0:T(8,128)}, f32[2,768,768]{2,1,0:T(8,128)}) custom-call(s32[1]{0:T(128)} %bitcast._, bf16[16,512,768]{2,1,0:T(8,128)(2,1)} %get-tuple-element.78.refs_0_.grad_ref, bf16[2,16,512,768]{3,2,1,0:T(8,128)(2,1)} %x_ref.1, bf16[2,16,2048,768]{3,2,1,0:T(8,128)(2,1)} %hi_ref.3, ...), custom_call_target="tpu_custom_call" | custom-call | flops 77309411328 | bytes 50331648 | tf_op jit(solution)/shard_map/pallas_call | solution.py:113
  1073.1 27.6 %collective-permute-done.17.refs_3_ = bf16[16,512,384]{2,1,0:T(8,128)(2,1)} collective-permute-done((bf16[16,512,384]{2,1,0:T(8,128)(2,1)}, bf16[16,512,384]{2,1,0:T(8,128)(2,1)}, u32[]{:S(2)}, u32[]{:S(2)}) %collective-permute-start.17) | collective-permute-done | bytes 6291488 | tf_op jit(solution)/shard_map/ppermute | solution.py:412
  1100.7 78.2 %shard_map.79 = (f32[16,512,768]{2,1,0:T(8,128)}, f32[2,384,768]{2,1,0:T(8,128)}, f32[2,384,768]{2,1,0:T(8,128)}) custom-call(s32[1]{0:T(128)} %bitcast._, bf16[16,512,768]{2,1,0:T(8,128)(2,1)} %get-tuple-element.78.refs_0_.grad_ref, bf16[2,16,512,768]{3,2,1,0:T(8,128)(2,1)} %x_ref.1, bf16[16,512,384]{2,1,0:T(8,128)(2,1)} %collective-permute-done.16.refs_2_, ...), custom_call_target="tpu_custom_call" | custom-call | flops 38654705664 | bytes 50331648 | tf_op jit(solution)/shard_map/pallas_call | solution.py:113
  1179.8 4.6 dynamic-slice_bitcast_fusion.7
  1184.3 4.5 dynamic-slice_bitcast_fusion.6
  1190.5 7.1 shard_map.96
  1198.9 6.3 shard_map.81
  1205.1 1.5 collective-permute-start.19
  1207.2 44.1 %collective-permute-done.51 = f32[768,768]{1,0:T(8,128)} collective-permute-done((f32[768,768]{1,0:T(8,128)}, f32[768,768]{1,0:T(8,128)}, u32[]{:S(2)}, u32[]{:S(2)}) %collective-permute-start.51) | collective-permute-done | bytes 2359328 | tf_op jit(solution)/shard_map/ppermute | solution.py:415
  1252.5 6.3 shard_map.82
  1258.8 4.6 shard_map.94
  1263.4 7.1 shard_map.95
  1270.4 7.0 shard_map.93
  1277.5 4.1 add.47
  1281.5 126.8 %collective-permute-done.21.h_a = bf16[2,512,128]{2,1,0:T(8,128)(2,1)S(1)} collective-permute-done((bf16[2,512,128]{2,1,0:T(8,128)(2,1)}, bf16[2,512,128]{2,1,0:T(8,128)(2,1)S(1)}, u32[]{:S(2)}, u32[]{:S(2)}) %collective-permute-start.21) | collective-permute-done | bytes 262176 | tf_op jit(solution)/shard_map/ppermute | solution.py:412
  1409.1 1.5 collective-permute-start.45
  1411.1 1.5 collective-permute-start.38
  1413.2 54.5 %shard_map.80 = (f32[16,512,768]{2,1,0:T(8,128)}, f32[2,256,768]{2,1,0:T(8,128)}, f32[2,256,768]{2,1,0:T(8,128)}) custom-call(bf16[16,512,768]{2,1,0:T(8,128)(2,1)} %get-tuple-element.78.refs_0_.grad_ref, bf16[2,16,512,768]{3,2,1,0:T(8,128)(2,1)} %x_ref.1, bf16[16,512,256]{2,1,0:T(8,128)(2,1)} %collective-permute-done.10.h_a, ...), custom_call_target="tpu_custom_call" | custom-call | flops 25769803776 | bytes 75497472 | tf_op jit(solution)/shard_map/pallas_call | solution.py:191
  1467.7 2.0 shard_map.84.refs_2_.up_ref
  1469.7 1.6 collective-permute-start.26
  1471.3 17.5 %collective-permute-done.49 = f32[768,768]{1,0:T(8,128)} collective-permute-done((f32[768,768]{1,0:T(8,128)}, f32[768,768]{1,0:T(8,128)}, u32[]{:S(2)}, u32[]{:S(2)}) %collective-permute-start.49) | collective-permute-done | bytes 2359328 | tf_op jit(solution)/shard_map/ppermute | solution.py:415
  1489.6 16.8 shard_map.83
  1506.5 2.9 add.45
  1509.4 2.0 add.46
  1511.4 3.4 add.48.kept_ref
  1514.8 1.7 collective-permute-start.22
  1517.7 21.3 %collective-permute-done.38 = f32[768,768]{1,0:T(8,128)} collective-permute-done((f32[768,768]{1,0:T(8,128)}, f32[768,768]{1,0:T(8,128)}, u32[]{:S(2)}, u32[]{:S(2)}) %collective-permute-start.38) | collective-permute-done | bytes 2359328 | tf_op jit(solution)/shard_map/ppermute | solution.py:415
  1540.5 12.6 shard_map.85
  1553.2 4.1 add.44.refs_2_.refs_6_.refs_4_
  1558.0 8.2 shard_map.86
  1566.2 6.3 shard_map.87
  1572.6 2.8 shard_map.90
  1576.9 1.9 shard_map.92
  1580.9 1.9 shard_map.91
  1582.8 82.2 %collective-permute-done.33 = f32[64,768]{1,0:T(8,128)S(1)} collective-permute-done((f32[64,768]{1,0:T(8,128)}, f32[64,768]{1,0:T(8,128)S(1)}, u32[]{:S(2)}, u32[]{:S(2)}) %collective-permute-start.33) | collective-permute-done | bytes 196640 | tf_op jit(solution)/shard_map/ppermute | solution.py:415
  1669.3 23.9 %collective-permute-done.30 = f32[64,768]{1,0:T(8,128)S(1)} collective-permute-done((f32[64,768]{1,0:T(8,128)}, f32[64,768]{1,0:T(8,128)S(1)}, u32[]{:S(2)}, u32[]{:S(2)}) %collective-permute-start.30) | collective-permute-done | bytes 196640 | tf_op jit(solution)/shard_map/ppermute | solution.py:415
  1695.4 5.7 collective-permute-done.40.refs_0_
  1701.9 7.5 collective-permute-done.31.refs_2_.refs_0_
  1711.0 5.0 collective-permute-done.41.refs_1_
  1719.4 8.4 shard_map.88._
  1727.9 6.0 shard_map.89
  1733.9 5.9 shard_map.97
  1739.8 4.1 shard_map.98
  1744.6 3.2 shard_map.99
  1747.8 2.3 shard_map.100
  (129 shorter events, 36.1 us)
Async XLA Ops:
  24.5 12.7 copy-start.2
  31.7 677.3 %collective-permute-start.7 = (bf16[16,512,768]{2,1,0:T(8,128)(2,1)S(1)}, bf16[16,512,768]{2,1,0:T(8,128)(2,1)}, u32[]{:S(2)}, u32[]{:S(2)}) collective-permute-start(bf16[16,512,768]{2,1,0:T(8,128)(2,1)S(1)} %dynamic-slice_bitcast_fusion.1), channel_id=1, source_target_pairs={{0,1},{1,0},{2,3},{3,2},{4,5},{5,4},{6,7},{7,6}} | collective-permute-start | bytes 37748744 | tf_op jit(solution)/shard_map/ppermute | solution.py:412
  32.5 797.9 %collective-permute-start.1 = (bf16[16,512,768]{2,1,0:T(8,128)(2,1)}, bf16[16,512,768]{2,1,0:T(8,128)(2,1)}, u32[]{:S(2)}, u32[]{:S(2)}) collective-permute-start(bf16[16,512,768]{2,1,0:T(8,128)(2,1)} %dynamic-slice_bitcast_fusion.2), channel_id=1, source_target_pairs={{0,3},{1,2},{2,1},{3,0},{4,7},{5,6},{6,5},{7,4}} | collective-permute-start | bytes 37748744 | tf_op jit(solution)/shard_map/ppermute | solution.py:412
  35.1 796.2 %collective-permute-start = (bf16[16,512,768]{2,1,0:T(8,128)(2,1)}, bf16[16,512,768]{2,1,0:T(8,128)(2,1)}, u32[]{:S(2)}, u32[]{:S(2)}) collective-permute-start(bf16[16,512,768]{2,1,0:T(8,128)(2,1)} %dynamic-slice_bitcast_fusion.3), channel_id=1, source_target_pairs={{0,2},{1,3},{2,0},{3,1},{4,6},{5,7},{6,4},{7,5}} | collective-permute-start | bytes 37748744 | tf_op jit(solution)/shard_map/ppermute | solution.py:412
  35.1 547.3 %collective-permute-start.2 = (bf16[192,768]{1,0:T(8,128)(2,1)S(1)}, bf16[192,768]{1,0:T(8,128)(2,1)S(1)}, u32[]{:S(2)}, u32[]{:S(2)}) collective-permute-start(bf16[192,768]{1,0:T(8,128)(2,1)S(1)} %select_bitcast_fusion.2), channel_id=1, source_target_pairs={{0,2},{1,3},{2,0},{3,1},{4,6},{5,7},{6,4},{7,5}} | collective-permute-start | bytes 884744 | tf_op jit(solution)/shard_map/ppermute | solution.py:412
  37.3 590.9 %collective-permute-start.12 = (bf16[768,768]{1,0:T(8,128)(2,1)S(1)}, bf16[768,768]{1,0:T(8,128)(2,1)S(1)}, u32[]{:S(2)}, u32[]{:S(2)}) collective-permute-start(bf16[768,768]{1,0:T(8,128)(2,1)S(1)} %select_bitcast_fusion), channel_id=1, source_target_pairs={{0,2},{1,3},{2,0},{3,1},{4,6},{5,7},{6,4},{7,5}} | collective-permute-start | bytes 3538952 | tf_op jit(solution)/shard_map/ppermute | solution.py:412
  582.4 44.0 %collective-permute-start.3 = (bf16[576,768]{1,0:T(8,128)(2,1)S(1)}, bf16[576,768]{1,0:T(8,128)(2,1)S(1)}, u32[]{:S(2)}, u32[]{:S(2)}) collective-permute-start(bf16[576,768]{1,0:T(8,128)(2,1)S(1)} %select_bitcast_fusion.1), channel_id=1, source_target_pairs={{0,2},{1,3},{2,0},{3,1},{4,6},{5,7},{6,4},{7,5}} | collective-permute-start | bytes 2654216 | tf_op jit(solution)/shard_map/ppermute | solution.py:412
  626.5 28.9 %collective-permute-start.4 = (bf16[768,768]{1,0:T(8,128)(2,1)S(1)}, bf16[768,768]{1,0:T(8,128)(2,1)S(1)}, u32[]{:S(2)}, u32[]{:S(2)}) collective-permute-start(bf16[768,768]{1,0:T(8,128)(2,1)S(1)} %constant_dynamic-update-slice_fusion), channel_id=1, source_target_pairs={{0,4},{4,0},{1,5},{5,1},{2,6},{6,2},{3,7},{7,3}} | collective-permute-start | bytes 3538952 | tf_op jit(solution)/shard_map/ppermute | solution.py:415
  628.2 27.2 %copy-start.5 = (bf16[768,768]{1,0:T(8,128)(2,1)}, bf16[768,768]{1,0:T(8,128)(2,1)S(1)}, u32[]{:S(2)}) copy-start(bf16[768,768]{1,0:T(8,128)(2,1)S(1)} %collective-permute-done.12) | copy-start | bytes 3538948
  628.2 51.3 %collective-permute-start.13 = (bf16[768,768]{1,0:T(8,128)(2,1)S(1)}, bf16[768,768]{1,0:T(8,128)(2,1)S(1)}, u32[]{:S(2)}, u32[]{:S(2)}) collective-permute-start(bf16[768,768]{1,0:T(8,128)(2,1)S(1)} %collective-permute-done.12), channel_id=1, source_target_pairs={{0,4},{4,0},{1,5},{5,1},{2,6},{6,2},{3,7},{7,3}} | collective-permute-start | bytes 3538952 | tf_op jit(solution)/shard_map/ppermute | solution.py:415
  655.4 24.2 %copy-start.7 = (bf16[768,768]{1,0:T(8,128)(2,1)}, bf16[768,768]{1,0:T(8,128)(2,1)S(1)}, u32[]{:S(2)}) copy-start(bf16[768,768]{1,0:T(8,128)(2,1)S(1)} %collective-permute-done.4) | copy-start | bytes 3538948
  655.4 53.0 %collective-permute-start.8 = (bf16[2,768,768]{2,1,0:T(8,128)(2,1)S(1)}, bf16[2,768,768]{2,1,0:T(8,128)(2,1)}, u32[]{:S(2)}, u32[]{:S(2)}) collective-permute-start(bf16[2,768,768]{2,1,0:T(8,128)(2,1)S(1)} %copy-done.2), channel_id=1, source_target_pairs={{0,1},{1,0},{2,3},{3,2},{4,5},{5,4},{6,7},{7,6}} | collective-permute-start | bytes 7077896 | tf_op jit(solution)/shard_map/ppermute | solution.py:412
  680.6 28.3 %collective-permute-start.9 = (bf16[2,768,768]{2,1,0:T(8,128)(2,1)S(1)}, bf16[2,768,768]{2,1,0:T(8,128)(2,1)}, u32[]{:S(2)}, u32[]{:S(2)}) collective-permute-start(bf16[2,768,768]{2,1,0:T(8,128)(2,1)S(1)} %copy-done.1), channel_id=1, source_target_pairs={{0,1},{1,0},{2,3},{3,2},{4,5},{5,4},{6,7},{7,6}} | collective-permute-start | bytes 7077896 | tf_op jit(solution)/shard_map/ppermute | solution.py:412
  708.4 244.1 %collective-permute-start.18 = (bf16[16,512,768]{2,1,0:T(8,128)(2,1)}, bf16[16,512,768]{2,1,0:T(8,128)(2,1)}, u32[]{:S(2)}, u32[]{:S(2)}) collective-permute-start(bf16[16,512,768]{2,1,0:T(8,128)(2,1)} %dynamic-slice_bitcast_fusion), channel_id=1, source_target_pairs={{0,1},{1,0},{2,3},{3,2},{4,5},{5,4},{6,7},{7,6}} | collective-permute-start | bytes 37748744 | tf_op jit(solution)/shard_map/ppermute | solution.py:412
  708.9 120.2 %collective-permute-start.5 = (bf16[768,768]{1,0:T(8,128)(2,1)}, bf16[768,768]{1,0:T(8,128)(2,1)}, u32[]{:S(2)}, u32[]{:S(2)}) collective-permute-start(bf16[768,768]{1,0:T(8,128)(2,1)} %get-tuple-element.144.refs_4_), channel_id=1, source_target_pairs={{0,1},{1,0},{2,3},{3,2},{4,5},{5,4},{6,7},{7,6}} | collective-permute-start | bytes 3538952 | tf_op jit(solution)/shard_map/ppermute | solution.py:412
  708.9 121.4 %collective-permute-start.6 = (bf16[768,768]{1,0:T(8,128)(2,1)}, bf16[768,768]{1,0:T(8,128)(2,1)}, u32[]{:S(2)}, u32[]{:S(2)}) collective-permute-start(bf16[768,768]{1,0:T(8,128)(2,1)} %get-tuple-element.143.refs_6_), channel_id=1, source_target_pairs={{0,1},{1,0},{2,3},{3,2},{4,5},{5,4},{6,7},{7,6}} | collective-permute-start | bytes 3538952 | tf_op jit(solution)/shard_map/ppermute | solution.py:412
  829.1 271.5 %collective-permute-start.16 = (bf16[16,512,384]{2,1,0:T(8,128)(2,1)}, bf16[16,512,384]{2,1,0:T(8,128)(2,1)}, u32[]{:S(2)}, u32[]{:S(2)}) collective-permute-start(bf16[16,512,384]{2,1,0:T(8,128)(2,1)} %dynamic-slice_bitcast_fusion.5), channel_id=1, source_target_pairs={{0,2},{1,3},{2,0},{3,1},{4,6},{5,7},{6,4},{7,5}} | collective-permute-start | bytes 18874376 | tf_op jit(solution)/shard_map/ppermute | solution.py:412
  830.3 270.3 %collective-permute-start.17 = (bf16[16,512,384]{2,1,0:T(8,128)(2,1)}, bf16[16,512,384]{2,1,0:T(8,128)(2,1)}, u32[]{:S(2)}, u32[]{:S(2)}) collective-permute-start(bf16[16,512,384]{2,1,0:T(8,128)(2,1)} %dynamic-slice_bitcast_fusion.4), channel_id=1, source_target_pairs={{0,3},{1,2},{2,1},{3,0},{4,7},{5,6},{6,5},{7,4}} | collective-permute-start | bytes 18874376 | tf_op jit(solution)/shard_map/ppermute | solution.py:412
  830.5 242.0 %collective-permute-start.14 = (bf16[768,768]{1,0:T(8,128)(2,1)}, bf16[768,768]{1,0:T(8,128)(2,1)}, u32[]{:S(2)}, u32[]{:S(2)}) collective-permute-start(bf16[768,768]{1,0:T(8,128)(2,1)} %get-tuple-element.142.refs_4_.up_a), channel_id=1, source_target_pairs={{0,1},{1,0},{2,3},{3,2},{4,5},{5,4},{6,7},{7,6}} | collective-permute-start | bytes 3538952 | tf_op jit(solution)/shard_map/ppermute | solution.py:412
  831.3 241.5 %collective-permute-start.15 = (bf16[768,768]{1,0:T(8,128)(2,1)}, bf16[768,768]{1,0:T(8,128)(2,1)}, u32[]{:S(2)}, u32[]{:S(2)}) collective-permute-start(bf16[768,768]{1,0:T(8,128)(2,1)} %get-tuple-element.141.refs_6_.down_a), channel_id=1, source_target_pairs={{0,1},{1,0},{2,3},{3,2},{4,5},{5,4},{6,7},{7,6}} | collective-permute-start | bytes 3538952 | tf_op jit(solution)/shard_map/ppermute | solution.py:412
  952.5 237.2 %collective-permute-start.50 = (f32[2,768,768]{2,1,0:T(8,128)}, f32[2,768,768]{2,1,0:T(8,128)}, u32[]{:S(2)}, u32[]{:S(2)}) collective-permute-start(f32[2,768,768]{2,1,0:T(8,128)} %get-tuple-element.130), channel_id=1, source_target_pairs={{0,1},{1,0},{2,3},{3,2},{4,5},{5,4},{6,7},{7,6}} | collective-permute-start | bytes 14155784 | tf_op jit(solution)/shard_map/ppermute | solution.py:412
  1072.5 132.6 %collective-permute-start.48 = (f32[2,768,768]{2,1,0:T(8,128)}, f32[2,768,768]{2,1,0:T(8,128)}, u32[]{:S(2)}, u32[]{:S(2)}) collective-permute-start(f32[2,768,768]{2,1,0:T(8,128)} %get-tuple-element.126), channel_id=1, source_target_pairs={{0,1},{1,0},{2,3},{3,2},{4,5},{5,4},{6,7},{7,6}} | collective-permute-start | bytes 14155784 | tf_op jit(solution)/shard_map/ppermute | solution.py:412
  1072.8 133.8 %collective-permute-start.37 = (f32[2,768,768]{2,1,0:T(8,128)}, f32[2,768,768]{2,1,0:T(8,128)}, u32[]{:S(2)}, u32[]{:S(2)}) collective-permute-start(f32[2,768,768]{2,1,0:T(8,128)} %get-tuple-element.118), channel_id=1, source_target_pairs={{0,1},{1,0},{2,3},{3,2},{4,5},{5,4},{6,7},{7,6}} | collective-permute-start | bytes 14155784 | tf_op jit(solution)/shard_map/ppermute | solution.py:412
  1178.9 18.7 %collective-permute-start.44 = (f32[2,384,768]{2,1,0:T(8,128)}, f32[2,384,768]{2,1,0:T(8,128)}, u32[]{:S(2)}, u32[]{:S(2)}) collective-permute-start(f32[2,384,768]{2,1,0:T(8,128)} %get-tuple-element.122), channel_id=1, source_target_pairs={{0,1},{1,0},{2,3},{3,2},{4,5},{5,4},{6,7},{7,6}} | collective-permute-start | bytes 7077896 | tf_op jit(solution)/shard_map/ppermute | solution.py:412
  1188.9 222.3 %collective-permute-start.11 = (bf16[16,512,256]{2,1,0:T(8,128)(2,1)}, bf16[16,512,256]{2,1,0:T(8,128)(2,1)}, u32[]{:S(2)}, u32[]{:S(2)}) collective-permute-start(bf16[16,512,256]{2,1,0:T(8,128)(2,1)} %dynamic-slice_bitcast_fusion.6), channel_id=1, source_target_pairs={{0,3},{1,2},{2,1},{3,0},{4,7},{5,6},{6,5},{7,4}} | collective-permute-start | bytes 12582920 | tf_op jit(solution)/shard_map/ppermute | solution.py:412
  1189.7 222.9 %collective-permute-start.10 = (bf16[16,512,256]{2,1,0:T(8,128)(2,1)}, bf16[16,512,256]{2,1,0:T(8,128)(2,1)}, u32[]{:S(2)}, u32[]{:S(2)}) collective-permute-start(bf16[16,512,256]{2,1,0:T(8,128)(2,1)} %dynamic-slice_bitcast_fusion.7), channel_id=1, source_target_pairs={{0,2},{1,3},{2,0},{3,1},{4,6},{5,7},{6,4},{7,5}} | collective-permute-start | bytes 12582920 | tf_op jit(solution)/shard_map/ppermute | solution.py:412
  1197.6 53.7 %collective-permute-start.51 = (f32[768,768]{1,0:T(8,128)}, f32[768,768]{1,0:T(8,128)}, u32[]{:S(2)}, u32[]{:S(2)}) collective-permute-start(f32[768,768]{1,0:T(8,128)} %get-tuple-element.132), channel_id=1, source_target_pairs={{0,4},{4,0},{1,5},{5,1},{2,6},{6,2},{3,7},{7,3}} | collective-permute-start | bytes 7077896 | tf_op jit(solution)/shard_map/ppermute | solution.py:415
  1205.1 205.5 %collective-permute-start.19 = (bf16[8,512,128]{2,1,0:T(8,128)(2,1)}, bf16[8,512,128]{2,1,0:T(8,128)(2,1)}, u32[]{:S(2)}, u32[]{:S(2)}) collective-permute-start(bf16[8,512,128]{2,1,0:T(8,128)(2,1)} %get-tuple-element.89), channel_id=1, source_target_pairs={{0,2},{1,3},{2,0},{3,1},{4,6},{5,7},{6,4},{7,5}} | collective-permute-start | bytes 3145736 | tf_op jit(solution)/shard_map/ppermute | solution.py:412
  1206.6 202.5 %collective-permute-start.25 = (bf16[3,512,128]{2,1,0:T(8,128)(2,1)}, bf16[3,512,128]{2,1,0:T(8,128)(2,1)S(1)}, u32[]{:S(2)}, u32[]{:S(2)}) collective-permute-start(bf16[3,512,128]{2,1,0:T(8,128)(2,1)} %get-tuple-element.96), channel_id=1, source_target_pairs={{0,2},{1,3},{2,0},{3,1},{4,6},{5,7},{6,4},{7,5}} | collective-permute-start | bytes 1179656 | tf_op jit(solution)/shard_map/ppermute | solution.py:412
  1251.3 157.1 %collective-permute-start.21 = (bf16[2,512,128]{2,1,0:T(8,128)(2,1)}, bf16[2,512,128]{2,1,0:T(8,128)(2,1)S(1)}, u32[]{:S(2)}, u32[]{:S(2)}) collective-permute-start(bf16[2,512,128]{2,1,0:T(8,128)(2,1)} %get-tuple-element.92), channel_id=1, source_target_pairs={{0,2},{1,3},{2,0},{3,1},{4,6},{5,7},{6,4},{7,5}} | collective-permute-start | bytes 786440 | tf_op jit(solution)/shard_map/ppermute | solution.py:412
  1408.4 59.3 %copy-start.14 = (bf16[2,512,128]{2,1,0:T(8,128)(2,1)}, bf16[2,512,128]{2,1,0:T(8,128)(2,1)S(1)}, u32[]{:S(2)}) copy-start(bf16[2,512,128]{2,1,0:T(8,128)(2,1)S(1)} %collective-permute-done.21.h_a) | copy-start | bytes 786436
  1408.4 59.3 %collective-permute-start.20 = (bf16[8,512,128]{2,1,0:T(8,128)(2,1)}, bf16[8,512,128]{2,1,0:T(8,128)(2,1)}, u32[]{:S(2)}, u32[]{:S(2)}) collective-permute-start(bf16[8,512,128]{2,1,0:T(8,128)(2,1)} %get-tuple-element.90), channel_id=1, source_target_pairs={{0,3},{1,2},{2,1},{3,0},{4,7},{5,6},{6,5},{7,4}} | collective-permute-start | bytes 3145736 | tf_op jit(solution)/shard_map/ppermute | solution.py:412
  1409.1 58.6 %copy-start.11 = (bf16[3,512,128]{2,1,0:T(8,128)(2,1)}, bf16[3,512,128]{2,1,0:T(8,128)(2,1)S(1)}, u32[]{:S(2)}) copy-start(bf16[3,512,128]{2,1,0:T(8,128)(2,1)S(1)} %collective-permute-done.25.h_a) | copy-start | bytes 1179652
  1409.1 60.6 %collective-permute-start.45 = (f32[384,768]{1,0:T(8,128)}, f32[384,768]{1,0:T(8,128)}, u32[]{:S(2)}, u32[]{:S(2)}) collective-permute-start(f32[384,768]{1,0:T(8,128)} %get-tuple-element.124), channel_id=1, source_target_pairs={{0,4},{4,0},{1,5},{5,1},{2,6},{6,2},{3,7},{7,3}} | collective-permute-start | bytes 3538952 | tf_op jit(solution)/shard_map/ppermute | solution.py:415
  1410.6 78.2 %collective-permute-start.49 = (f32[768,768]{1,0:T(8,128)}, f32[768,768]{1,0:T(8,128)}, u32[]{:S(2)}, u32[]{:S(2)}) collective-permute-start(f32[768,768]{1,0:T(8,128)} %get-tuple-element.128), channel_id=1, source_target_pairs={{0,4},{4,0},{1,5},{5,1},{2,6},{6,2},{3,7},{7,3}} | collective-permute-start | bytes 7077896 | tf_op jit(solution)/shard_map/ppermute | solution.py:415
  1411.1 127.9 %collective-permute-start.38 = (f32[768,768]{1,0:T(8,128)}, f32[768,768]{1,0:T(8,128)}, u32[]{:S(2)}, u32[]{:S(2)}) collective-permute-start(f32[768,768]{1,0:T(8,128)} %get-tuple-element.120), channel_id=1, source_target_pairs={{0,4},{4,0},{1,5},{5,1},{2,6},{6,2},{3,7},{7,3}} | collective-permute-start | bytes 7077896 | tf_op jit(solution)/shard_map/ppermute | solution.py:415
  1412.6 77.0 %collective-permute-start.52 = (f32[768,768]{1,0:T(8,128)}, f32[768,768]{1,0:T(8,128)}, u32[]{:S(2)}, u32[]{:S(2)}) collective-permute-start(f32[768,768]{1,0:T(8,128)} %add.47), channel_id=1, source_target_pairs={{0,2},{1,3},{2,0},{3,1},{4,6},{5,7},{6,4},{7,5}} | collective-permute-start | bytes 7077896 | tf_op jit(solution)/shard_map/ppermute | solution.py:412
  1467.7 104.9 %collective-permute-start.27 = (f32[2,256,768]{2,1,0:T(8,128)}, f32[2,256,768]{2,1,0:T(8,128)}, u32[]{:S(2)}, u32[]{:S(2)}) collective-permute-start(f32[2,256,768]{2,1,0:T(8,128)} %get-tuple-element.106), channel_id=1, source_target_pairs={{0,1},{1,0},{2,3},{3,2},{4,5},{5,4},{6,7},{7,6}} | collective-permute-start | bytes 4718600 | tf_op jit(solution)/shard_map/ppermute | solution.py:412
  1469.7 45.1 %collective-permute-start.26 = (bf16[3,512,128]{2,1,0:T(8,128)(2,1)}, bf16[3,512,128]{2,1,0:T(8,128)(2,1)}, u32[]{:S(2)}, u32[]{:S(2)}) collective-permute-start(bf16[3,512,128]{2,1,0:T(8,128)(2,1)} %get-tuple-element.97), channel_id=1, source_target_pairs={{0,3},{1,2},{2,1},{3,0},{4,7},{5,6},{6,5},{7,4}} | collective-permute-start | bytes 1179656 | tf_op jit(solution)/shard_map/ppermute | solution.py:412
  1488.8 27.7 %collective-permute-start.23 = (bf16[3,512,128]{2,1,0:T(8,128)(2,1)}, bf16[3,512,128]{2,1,0:T(8,128)(2,1)S(1)}, u32[]{:S(2)}, u32[]{:S(2)}) collective-permute-start(bf16[3,512,128]{2,1,0:T(8,128)(2,1)} %get-tuple-element.94), channel_id=1, source_target_pairs={{0,2},{1,3},{2,0},{3,1},{4,6},{5,7},{6,4},{7,5}} | collective-permute-start | bytes 1179656 | tf_op jit(solution)/shard_map/ppermute | solution.py:412
  1489.6 67.7 %collective-permute-start.24 = (bf16[3,512,128]{2,1,0:T(8,128)(2,1)}, bf16[3,512,128]{2,1,0:T(8,128)(2,1)S(1)}, u32[]{:S(2)}, u32[]{:S(2)}) collective-permute-start(bf16[3,512,128]{2,1,0:T(8,128)(2,1)} %get-tuple-element.95), channel_id=1, source_target_pairs={{0,3},{1,2},{2,1},{3,0},{4,7},{5,6},{6,5},{7,4}} | collective-permute-start | bytes 1179656 | tf_op jit(solution)/shard_map/ppermute | solution.py:412
  1514.8 51.5 %collective-permute-start.22 = (bf16[2,512,128]{2,1,0:T(8,128)(2,1)}, bf16[2,512,128]{2,1,0:T(8,128)(2,1)}, u32[]{:S(2)}, u32[]{:S(2)}) collective-permute-start(bf16[2,512,128]{2,1,0:T(8,128)(2,1)} %get-tuple-element.93), channel_id=1, source_target_pairs={{0,3},{1,2},{2,1},{3,0},{4,7},{5,6},{6,5},{7,4}} | collective-permute-start | bytes 786440 | tf_op jit(solution)/shard_map/ppermute | solution.py:412
  1516.5 36.7 %copy-start.12 = (bf16[3,512,128]{2,1,0:T(8,128)(2,1)}, bf16[3,512,128]{2,1,0:T(8,128)(2,1)S(1)}, u32[]{:S(2)}) copy-start(bf16[3,512,128]{2,1,0:T(8,128)(2,1)S(1)} %collective-permute-done.23.h_a) | copy-start | bytes 1179652
  1516.5 63.1 %collective-permute-start.46 = (f32[384,768]{1,0:T(8,128)}, f32[384,768]{1,0:T(8,128)}, u32[]{:S(2)}, u32[]{:S(2)}) collective-permute-start(f32[384,768]{1,0:T(8,128)} %add.45), channel_id=1, source_target_pairs={{0,2},{1,3},{2,0},{3,1},{4,6},{5,7},{6,4},{7,5}} | collective-permute-start | bytes 3538952 | tf_op jit(solution)/shard_map/ppermute | solution.py:412
  1539.0 178.9 %collective-permute-start.53 = (f32[768,768]{1,0:T(8,128)}, f32[768,768]{1,0:T(8,128)}, u32[]{:S(2)}, u32[]{:S(2)}) collective-permute-start(f32[768,768]{1,0:T(8,128)} %add.48.kept_ref), channel_id=1, source_target_pairs={{0,4},{4,0},{1,5},{5,1},{2,6},{6,2},{3,7},{7,3}} | collective-permute-start | bytes 7077896 | tf_op jit(solution)/shard_map/ppermute | solution.py:415
  1557.3 182.5 %collective-permute-start.39 = (f32[768,768]{1,0:T(8,128)}, f32[768,768]{1,0:T(8,128)}, u32[]{:S(2)}, u32[]{:S(2)}) collective-permute-start(f32[768,768]{1,0:T(8,128)} %add.44.refs_2_.refs_6_.refs_4_), channel_id=1, source_target_pairs={{0,4},{4,0},{1,5},{5,1},{2,6},{6,2},{3,7},{7,3}} | collective-permute-start | bytes 7077896 | tf_op jit(solution)/shard_map/ppermute | solution.py:415
  1572.6 4.2 collective-permute-start.32
  1575.4 92.6 %copy-start.10 = (f32[256,768]{1,0:T(8,128)S(1)}, f32[256,768]{1,0:T(8,128)}, u32[]{:S(2)}) copy-start(f32[256,768]{1,0:T(8,128)} %get-tuple-element.107) | copy-start | bytes 2359300
  1575.4 92.0 %collective-permute-start.28 = (f32[256,768]{1,0:T(8,128)}, f32[256,768]{1,0:T(8,128)}, u32[]{:S(2)}, u32[]{:S(2)}) collective-permute-start(f32[256,768]{1,0:T(8,128)} %get-tuple-element.108), channel_id=1, source_target_pairs={{0,4},{4,0},{1,5},{5,1},{2,6},{6,2},{3,7},{7,3}} | collective-permute-start | bytes 2359304 | tf_op jit(solution)/shard_map/ppermute | solution.py:415
  1576.7 2.1 collective-permute-start.29
  1578.9 86.1 %collective-permute-start.33 = (f32[64,768]{1,0:T(8,128)}, f32[64,768]{1,0:T(8,128)S(1)}, u32[]{:S(2)}, u32[]{:S(2)}) collective-permute-start(f32[64,768]{1,0:T(8,128)} %get-tuple-element.116), channel_id=1, source_target_pairs={{0,4},{4,0},{1,5},{5,1},{2,6},{6,2},{3,7},{7,3}} | collective-permute-start | bytes 589832 | tf_op jit(solution)/shard_map/ppermute | solution.py:415
  1579.6 137.8 %collective-permute-start.47 = (f32[384,768]{1,0:T(8,128)}, f32[384,768]{1,0:T(8,128)}, u32[]{:S(2)}, u32[]{:S(2)}) collective-permute-start(f32[384,768]{1,0:T(8,128)} %collective-permute-done.46.refs_0_), channel_id=1, source_target_pairs={{0,4},{4,0},{1,5},{5,1},{2,6},{6,2},{3,7},{7,3}} | collective-permute-start | bytes 3538952 | tf_op jit(solution)/shard_map/ppermute | solution.py:415
  1582.8 111.2 %copy-start.16 = (f32[64,768]{1,0:T(8,128)S(1)}, f32[64,768]{1,0:T(8,128)}, u32[]{:S(2)}) copy-start(f32[64,768]{1,0:T(8,128)} %get-tuple-element.111) | copy-start | bytes 589828
  1665.0 28.3 %collective-permute-start.30 = (f32[64,768]{1,0:T(8,128)}, f32[64,768]{1,0:T(8,128)S(1)}, u32[]{:S(2)}, u32[]{:S(2)}) collective-permute-start(f32[64,768]{1,0:T(8,128)} %get-tuple-element.112), channel_id=1, source_target_pairs={{0,4},{4,0},{1,5},{5,1},{2,6},{6,2},{3,7},{7,3}} | collective-permute-start | bytes 589832 | tf_op jit(solution)/shard_map/ppermute | solution.py:415
  1667.4 26.7 %collective-permute-start.34 = (f32[64,768]{1,0:T(8,128)S(1)}, f32[64,768]{1,0:T(8,128)S(1)}, u32[]{:S(2)}, u32[]{:S(2)}) collective-permute-start(f32[64,768]{1,0:T(8,128)S(1)} %add.43), channel_id=1, source_target_pairs={{0,2},{1,3},{2,0},{3,1},{4,6},{5,7},{6,4},{7,5}} | collective-permute-start | bytes 589832 | tf_op jit(solution)/shard_map/ppermute | solution.py:412
  1693.2 7.9 collective-permute-start.40
  1694.2 33.7 %copy-start.15 = (f32[64,768]{1,0:T(8,128)}, f32[64,768]{1,0:T(8,128)S(1)}, u32[]{:S(2)}) copy-start(f32[64,768]{1,0:T(8,128)S(1)} %collective-permute-done.34.refs_1_) | copy-start | bytes 589828
  1694.2 15.3 collective-permute-start.31
  1701.1 14.8 collective-permute-start.41
  1709.4 18.4 %copy-start.3 = (f32[128,768]{1,0:T(8,128)}, f32[128,768]{1,0:T(8,128)S(1)}, u32[]{:S(2)}) copy-start(f32[128,768]{1,0:T(8,128)S(1)} %collective-permute-done.31.refs_2_.refs_0_) | copy-start | bytes 1179652
  1709.5 34.4 %collective-permute-start.35 = (f32[128,768]{1,0:T(8,128)S(1)}, f32[128,768]{1,0:T(8,128)S(1)}, u32[]{:S(2)}, u32[]{:S(2)}) collective-permute-start(f32[128,768]{1,0:T(8,128)S(1)} %collective-permute-done.31.refs_2_.refs_0_), channel_id=1, source_target_pairs={{0,4},{4,0},{1,5},{5,1},{2,6},{6,2},{3,7},{7,3}} | collective-permute-start | bytes 1179656 | tf_op jit(solution)/shard_map/ppermute | solution.py:415
  1715.9 27.9 %collective-permute-start.43 = (f32[128,768]{1,0:T(8,128)}, f32[128,768]{1,0:T(8,128)}, u32[]{:S(2)}, u32[]{:S(2)}) collective-permute-start(f32[128,768]{1,0:T(8,128)} %collective-permute-done.41.refs_1_), channel_id=1, source_target_pairs={{0,4},{4,0},{1,5},{5,1},{2,6},{6,2},{3,7},{7,3}} | collective-permute-start | bytes 1179656 | tf_op jit(solution)/shard_map/ppermute | solution.py:415
  1717.4 26.4 %collective-permute-start.42 = (f32[64,768]{1,0:T(8,128)}, f32[64,768]{1,0:T(8,128)}, u32[]{:S(2)}, u32[]{:S(2)}) collective-permute-start(f32[64,768]{1,0:T(8,128)} %collective-permute-done.40.refs_0_), channel_id=1, source_target_pairs={{0,4},{4,0},{1,5},{5,1},{2,6},{6,2},{3,7},{7,3}} | collective-permute-start | bytes 589832 | tf_op jit(solution)/shard_map/ppermute | solution.py:415
  1717.9 29.8 %collective-permute-start.36 = (f32[64,768]{1,0:T(8,128)S(1)}, f32[64,768]{1,0:T(8,128)}, u32[]{:S(2)}, u32[]{:S(2)}) collective-permute-start(f32[64,768]{1,0:T(8,128)S(1)} %collective-permute-done.34.refs_1_), channel_id=1, source_target_pairs={{0,4},{4,0},{1,5},{5,1},{2,6},{6,2},{3,7},{7,3}} | collective-permute-start | bytes 589832 | tf_op jit(solution)/shard_map/ppermute | solution.py:415
  (7 other events, 24.2 us)

commit v9 on v8

--- a/solution.py
+++ b/solution.py
@@ -231,12 +231,12 @@
     return value.reshape(shape[:axis] + (2, shape[axis] // 2) + shape[axis + 1 :])
 
 
-def small_call(layer, grad, x_saved, h_pair, down_pair, start, first_pair, init=None, finish=None):
+def small_call(layer, grad, x_saved, h_pair, down_pair, start, first_pair, init=None, finish=None, pre=None, pre_pairs=None, pre_first=0):
     _, _, seq, hidden = grad.shape
     pairs = h_pair[0].shape[0]
     row_spec = pl.BlockSpec((2, 1, seq, hidden), lambda b: (0, b + first_pair, 0, 0))
     early_spec = pl.BlockSpec((2, 1, seq, LANES), lambda b: (0, b + first_pair, 0, 0))
-    pre_spec = pl.BlockSpec((2, 1, seq, LANES), lambda b: (0, b, 0, 0))
+    pre_spec = pl.BlockSpec((2, 1, seq, LANES), lambda b: (0, b + pre_first, 0, 0))
     h_spec = pl.BlockSpec((1, seq, LANES), lambda b: (b, 0, 0))
     down_spec = pl.BlockSpec((SMALL, hidden), lambda b: (start // SMALL, 0))
     dw_shape = (2, SMALL, hidden)
@@ -246,17 +246,20 @@
         in_specs += [row_spec, early_spec, pl.BlockSpec(finish[2].shape, lambda b: (0, 0))]
     if init:
         in_specs += [dw_spec] * 2
+    if pre is not None:
+        in_specs.append(pl.BlockSpec(memory_space=pl.ANY))
     return pl.pallas_call(
         functools.partial(small_body, init is not None, finish is not None),
         out_shape=[jax.ShapeDtypeStruct(dw_shape, F32)] * 2
-        + [jax.ShapeDtypeStruct(grad.shape if finish else (2, pairs, seq, LANES), BF16)],
+        + [jax.ShapeDtypeStruct(grad.shape if finish else (2, pre_pairs or pairs, seq, LANES), BF16)],
         grid=(pairs,),
         in_specs=in_specs,
         out_specs=[dw_spec, dw_spec, row_spec if finish else pre_spec],
+        input_output_aliases={} if pre is None else {len(in_specs) - 1: 2},
         compiler_params=pltpu.CompilerParams(dimension_semantics=("arbitrary",), vmem_limit_bytes=ALL_VMEM),
         cost_estimate=pl.CostEstimate(
             flops=24 * pairs * seq * hidden * SMALL, bytes_accessed=8 * pairs * seq * hidden, transcendentals=4 * pairs * seq * SMALL),
-    )(grad, x_saved, *h_pair, *down_pair, *(finish or ()), *(init or ()))
+    )(grad, x_saved, *h_pair, *down_pair, *(finish or ()), *(init or ()), *(() if pre is None else (pre,)))
 
 
 def join_body(up_a, up_b, out_ref):
@@ -509,12 +512,12 @@
         dw_2, dw_3, grad_x = small_call(
             0, grad_mid, x_saved, h_small[1], down_pair, last, 0, finish=(carry, pre_1, small_up))
         dw_2, dw_3, pre_2 = small_call(
-            0, grad_mid, x_saved, h_small[2], down_pair, last, early, init=(dw_2, dw_3))
-        dw_2, dw_3, pre_3 = small_call(
-            0, grad_mid, x_saved, h_small[3], down_pair, last, late, init=(dw_2, dw_3))
+            0, grad_mid, x_saved, h_small[2], down_pair, last, early, init=(dw_2, dw_3), pre_pairs=rows // 2 - early)
+        dw_2, dw_3, pre_2 = small_call(
+            0, grad_mid, x_saved, h_small[3], down_pair, last, late, init=(dw_2, dw_3),
+            pre=pre_2, pre_pairs=rows // 2 - early, pre_first=late - early)
         exchange(partial_sum(dw_2, dw_3))
         grad_x = finish_call(carry, (pre_1, pre_2), small_up, early, 0, 2, grad_x)
-        grad_x = finish_call(carry, (pre_1, pre_3), small_up, late, 0, 2, grad_x)
         bufs = place([(*pieces[0], 0, bounds[1])], 0, 0, bufs, near_pair)
         middle = [(*pieces[1], 0, 64), (*pieces[2], 0, 128), (*pieces[3], 0, 64)]
         bufs = place(middle, 0, bounds[1], bufs, near_pair)

time: 1750 us -> 1750 us (level)
  no operation moved by 1% of the time
where the time goes in v9:
time: 1750 us
  waiting for transfers between devices  1000 us (57%)
  Pallas kernels  613 us (35%)
  local copies, waits for them, and re-layouts  62.8 us (4%)
  starting transfers between devices  46.6 us (3%)
  other arithmetic  26.1 us (1%)
    ppermute x38, waiting for transfers between devices, to_model(): return lax.ppermute(value, 'model', [(i, i ^ flip) for i in range(n_model)])  760 us
    pallas_call x4, Pallas kernels, block_call(): pl.pallas_call(functools.partial(block_body, carry is not None, final, ro...  439 us
    ppermute x16, waiting for transfers between devices, to_data(): return lax.ppermute(value, 'data', [(0, 1), (1, 0)])  240 us
    squeeze x8, local copies, waits for them, and re-layouts, h_from(): lax.dynamic_slice(held[0], (layer, 0, begin, start), (1, rows, seq, size))  60.7 us
    pallas_call x1, Pallas kernels, wide_call(): pl.pallas_call(functools.partial(wide_body, start), out_shape=[jax.ShapeD...  54.5 us
    pallas_call x4, Pallas kernels, small_call(): pl.pallas_call(functools.partial(small_body, init is not None, finish is...  44 us
  transfers between devices with their start and end apart: 54, of which 14 were waited for; matrix products, arithmetic and copies ran while one was open for 3% of the time, Pallas kernels for 35%

profile of v9, /device:TPU:0, one launch (start us, length us, event | category | flops | bytes accessed | tf_op | source)
XLA Modules:
  0.0 1749.3 jit_solution(56833685183385041)
XLA Ops:
  1.7 1.5 select_bitcast_fusion.1
  3.3 10.6 dynamic-slice_bitcast_fusion.3
  13.9 10.6 dynamic-slice_bitcast_fusion.2
  24.5 7.2 dynamic-slice_bitcast_fusion.1
  32.5 2.6 collective-permute-start.1
  35.1 2.0 collective-permute-start.2
  37.3 545.1 %collective-permute-done.2 = bf16[192,768]{1,0:T(8,128)(2,1)S(1)} collective-permute-done((bf16[192,768]{1,0:T(8,128)(2,1)S(1)}, bf16[192,768]{1,0:T(8,128)(2,1)S(1)}, u32[]{:S(2)}, u32[]{:S(2)}) %collective-permute-start.2) | collective-permute-done | bytes 294944 | tf_op jit(solution)/shard_map/ppermute | solution.py:415
  582.4 2.1 collective-permute-start.3
  584.5 41.9 %collective-permute-done.3 = bf16[576,768]{1,0:T(8,128)(2,1)S(1)} collective-permute-done((bf16[576,768]{1,0:T(8,128)(2,1)S(1)}, bf16[576,768]{1,0:T(8,128)(2,1)S(1)}, u32[]{:S(2)}, u32[]{:S(2)}) %collective-permute-start.3) | collective-permute-done | bytes 884768 | tf_op jit(solution)/shard_map/ppermute | solution.py:415
  626.5 1.7 collective-permute-start.4
  628.6 26.8 %collective-permute-done.4 = bf16[768,768]{1,0:T(8,128)(2,1)S(1)} collective-permute-done((bf16[768,768]{1,0:T(8,128)(2,1)S(1)}, bf16[768,768]{1,0:T(8,128)(2,1)S(1)}, u32[]{:S(2)}, u32[]{:S(2)}) %collective-permute-start.4) | collective-permute-done | bytes 1179680 | tf_op jit(solution)/shard_map/ppermute | solution.py:418
  655.4 24.2 %collective-permute-done.13 = bf16[768,768]{1,0:T(8,128)(2,1)S(1)} collective-permute-done((bf16[768,768]{1,0:T(8,128)(2,1)S(1)}, bf16[768,768]{1,0:T(8,128)(2,1)S(1)}, u32[]{:S(2)}, u32[]{:S(2)}) %collective-permute-start.13) | collective-permute-done | bytes 1179680 | tf_op jit(solution)/shard_map/ppermute | solution.py:418
  680.6 10.6 dynamic-slice_bitcast_fusion
  691.2 6.2 dynamic-slice_bitcast_fusion.5
  697.5 6.3 dynamic-slice_bitcast_fusion.4
  703.8 3.0 broadcast_select_fusion.2
  706.8 1.6 broadcast_select_fusion
  709.4 119.7 %shard_map.76 = (f32[16,512,768]{2,1,0:T(8,128)}, f32[2,768,768]{2,1,0:T(8,128)}, f32[2,768,768]{2,1,0:T(8,128)}) custom-call(s32[1]{0:T(128)} %bitcast._, bf16[16,512,768]{2,1,0:T(8,128)(2,1)} %refs_0_.3, bf16[2,16,512,768]{3,2,1,0:T(8,128)(2,1)} %x_ref.1, bf16[2,16,2048,768]{3,2,1,0:T(8,128)(2,1)} %hi_ref.3, ...), custom_call_target="tpu_custom_call" | custom-call | flops 77309411328 | bytes 50331648 | tf_op jit(solution)/shard_map/pallas_call | solution.py:113
  831.3 121.2 %shard_map.77 = (bf16[16,512,768]{2,1,0:T(8,128)(2,1)}, f32[2,768,768]{2,1,0:T(8,128)}, f32[2,768,768]{2,1,0:T(8,128)}) custom-call(s32[1]{0:T(128)} %bitcast._, bf16[16,512,768]{2,1,0:T(8,128)(2,1)} %refs_0_.3, bf16[2,16,512,768]{3,2,1,0:T(8,128)(2,1)} %x_ref.1, bf16[16,512,768]{2,1,0:T(8,128)(2,1)} %collective-permute-done.refs_2_, ...), custom_call_target="tpu_custom_call" | custom-call | flops 77309411328 | bytes 50331648 | tf_op jit(solution)/shard_map/pallas_call | solution.py:113
  953.0 119.5 %shard_map.78 = (f32[16,512,768]{2,1,0:T(8,128)}, f32[2,768,768]{2,1,0:T(8,128)}, f32[2,768,768]{2,1,0:T(8,128)}) custom-call(s32[1]{0:T(128)} %bitcast._, bf16[16,512,768]{2,1,0:T(8,128)(2,1)} %get-tuple-element.78.refs_0_.grad_ref, bf16[2,16,512,768]{3,2,1,0:T(8,128)(2,1)} %x_ref.1, bf16[2,16,2048,768]{3,2,1,0:T(8,128)(2,1)} %hi_ref.3, ...), custom_call_target="tpu_custom_call" | custom-call | flops 77309411328 | bytes 50331648 | tf_op jit(solution)/shard_map/pallas_call | solution.py:113
  1073.1 27.6 %collective-permute-done.17.refs_3_ = bf16[16,512,384]{2,1,0:T(8,128)(2,1)} collective-permute-done((bf16[16,512,384]{2,1,0:T(8,128)(2,1)}, bf16[16,512,384]{2,1,0:T(8,128)(2,1)}, u32[]{:S(2)}, u32[]{:S(2)}) %collective-permute-start.17) | collective-permute-done | bytes 6291488 | tf_op jit(solution)/shard_map/ppermute | solution.py:415
  1100.7 78.2 %shard_map.79 = (f32[16,512,768]{2,1,0:T(8,128)}, f32[2,384,768]{2,1,0:T(8,128)}, f32[2,384,768]{2,1,0:T(8,128)}) custom-call(s32[1]{0:T(128)} %bitcast._, bf16[16,512,768]{2,1,0:T(8,128)(2,1)} %get-tuple-element.78.refs_0_.grad_ref, bf16[2,16,512,768]{3,2,1,0:T(8,128)(2,1)} %x_ref.1, bf16[16,512,384]{2,1,0:T(8,128)(2,1)} %collective-permute-done.16.refs_2_, ...), custom_call_target="tpu_custom_call" | custom-call | flops 38654705664 | bytes 50331648 | tf_op jit(solution)/shard_map/pallas_call | solution.py:113
  1179.8 4.6 dynamic-slice_bitcast_fusion.7
  1184.3 4.5 dynamic-slice_bitcast_fusion.6
  1190.5 7.1 shard_map.95
  1198.9 6.3 shard_map.81
  1205.1 1.5 collective-permute-start.19
  1207.2 44.1 %collective-permute-done.51 = f32[768,768]{1,0:T(8,128)} collective-permute-done((f32[768,768]{1,0:T(8,128)}, f32[768,768]{1,0:T(8,128)}, u32[]{:S(2)}, u32[]{:S(2)}) %collective-permute-start.51) | collective-permute-done | bytes 2359328 | tf_op jit(solution)/shard_map/ppermute | solution.py:418
  1252.5 6.3 shard_map.82
  1258.8 4.6 shard_map.93
  1263.4 7.1 shard_map.94
  1270.4 7.0 shard_map.92
  1277.5 4.1 add.47
  1281.5 126.8 %collective-permute-done.21.h_a = bf16[2,512,128]{2,1,0:T(8,128)(2,1)S(1)} collective-permute-done((bf16[2,512,128]{2,1,0:T(8,128)(2,1)}, bf16[2,512,128]{2,1,0:T(8,128)(2,1)S(1)}, u32[]{:S(2)}, u32[]{:S(2)}) %collective-permute-start.21) | collective-permute-done | bytes 262176 | tf_op jit(solution)/shard_map/ppermute | solution.py:415
  1409.1 1.5 collective-permute-start.45
  1411.1 1.5 collective-permute-start.38
  1413.2 54.5 %shard_map.80 = (f32[16,512,768]{2,1,0:T(8,128)}, f32[2,256,768]{2,1,0:T(8,128)}, f32[2,256,768]{2,1,0:T(8,128)}) custom-call(bf16[16,512,768]{2,1,0:T(8,128)(2,1)} %get-tuple-element.78.refs_0_.grad_ref, bf16[2,16,512,768]{3,2,1,0:T(8,128)(2,1)} %x_ref.1, bf16[16,512,256]{2,1,0:T(8,128)(2,1)} %collective-permute-done.10.h_a, ...), custom_call_target="tpu_custom_call" | custom-call | flops 25769803776 | bytes 75497472 | tf_op jit(solution)/shard_map/pallas_call | solution.py:191
  1467.7 2.0 shard_map.84.refs_2_.up_ref
  1469.7 1.6 collective-permute-start.26
  1471.3 17.5 %collective-permute-done.49 = f32[768,768]{1,0:T(8,128)} collective-permute-done((f32[768,768]{1,0:T(8,128)}, f32[768,768]{1,0:T(8,128)}, u32[]{:S(2)}, u32[]{:S(2)}) %collective-permute-start.49) | collective-permute-done | bytes 2359328 | tf_op jit(solution)/shard_map/ppermute | solution.py:418
  1489.6 16.8 shard_map.83
  1506.5 2.9 add.45
  1509.4 2.0 add.46
  1511.4 3.4 add.48.kept_ref
  1514.8 1.7 collective-permute-start.22
  1517.7 21.3 %collective-permute-done.38 = f32[768,768]{1,0:T(8,128)} collective-permute-done((f32[768,768]{1,0:T(8,128)}, f32[768,768]{1,0:T(8,128)}, u32[]{:S(2)}, u32[]{:S(2)}) %collective-permute-start.38) | collective-permute-done | bytes 2359328 | tf_op jit(solution)/shard_map/ppermute | solution.py:418
  1540.5 12.6 shard_map.85
  1553.2 4.1 add.44.refs_2_.refs_6_.refs_4_
  1558.0 8.2 shard_map.86
  1566.2 6.3 shard_map.87
  1572.6 2.8 shard_map.89
  1576.9 1.9 shard_map.91
  1580.9 1.9 shard_map.90
  1582.8 82.2 %collective-permute-done.33 = f32[64,768]{1,0:T(8,128)S(1)} collective-permute-done((f32[64,768]{1,0:T(8,128)}, f32[64,768]{1,0:T(8,128)S(1)}, u32[]{:S(2)}, u32[]{:S(2)}) %collective-permute-start.33) | collective-permute-done | bytes 196640 | tf_op jit(solution)/shard_map/ppermute | solution.py:418
  1669.3 23.9 %collective-permute-done.30 = f32[64,768]{1,0:T(8,128)S(1)} collective-permute-done((f32[64,768]{1,0:T(8,128)}, f32[64,768]{1,0:T(8,128)S(1)}, u32[]{:S(2)}, u32[]{:S(2)}) %collective-permute-start.30) | collective-permute-done | bytes 196640 | tf_op jit(solution)/shard_map/ppermute | solution.py:418
  1695.4 5.7 collective-permute-done.40.refs_0_
  1701.9 7.5 collective-permute-done.31.refs_2_.refs_0_
  1711.0 5.0 collective-permute-done.41.refs_1_
  1717.9 1.5 collective-permute-start.36
  1719.4 13.4 shard_map.88
  1732.9 5.9 shard_map.96
  1738.8 4.1 shard_map.97
  1743.6 3.2 shard_map.98
  1746.8 2.3 shard_map.99
  (128 shorter events, 34.6 us)
Async XLA Ops:
  24.5 12.7 copy-start.2
  31.7 677.3 %collective-permute-start.7 = (bf16[16,512,768]{2,1,0:T(8,128)(2,1)S(1)}, bf16[16,512,768]{2,1,0:T(8,128)(2,1)}, u32[]{:S(2)}, u32[]{:S(2)}) collective-permute-start(bf16[16,512,768]{2,1,0:T(8,128)(2,1)S(1)} %dynamic-slice_bitcast_fusion.1), channel_id=1, source_target_pairs={{0,1},{1,0},{2,3},{3,2},{4,5},{5,4},{6,7},{7,6}} | collective-permute-start | bytes 37748744 | tf_op jit(solution)/shard_map/ppermute | solution.py:415
  32.5 797.9 %collective-permute-start.1 = (bf16[16,512,768]{2,1,0:T(8,128)(2,1)}, bf16[16,512,768]{2,1,0:T(8,128)(2,1)}, u32[]{:S(2)}, u32[]{:S(2)}) collective-permute-start(bf16[16,512,768]{2,1,0:T(8,128)(2,1)} %dynamic-slice_bitcast_fusion.2), channel_id=1, source_target_pairs={{0,3},{1,2},{2,1},{3,0},{4,7},{5,6},{6,5},{7,4}} | collective-permute-start | bytes 37748744 | tf_op jit(solution)/shard_map/ppermute | solution.py:415
  35.1 796.2 %collective-permute-start = (bf16[16,512,768]{2,1,0:T(8,128)(2,1)}, bf16[16,512,768]{2,1,0:T(8,128)(2,1)}, u32[]{:S(2)}, u32[]{:S(2)}) collective-permute-start(bf16[16,512,768]{2,1,0:T(8,128)(2,1)} %dynamic-slice_bitcast_fusion.3), channel_id=1, source_target_pairs={{0,2},{1,3},{2,0},{3,1},{4,6},{5,7},{6,4},{7,5}} | collective-permute-start | bytes 37748744 | tf_op jit(solution)/shard_map/ppermute | solution.py:415
  35.1 547.3 %collective-permute-start.2 = (bf16[192,768]{1,0:T(8,128)(2,1)S(1)}, bf16[192,768]{1,0:T(8,128)(2,1)S(1)}, u32[]{:S(2)}, u32[]{:S(2)}) collective-permute-start(bf16[192,768]{1,0:T(8,128)(2,1)S(1)} %select_bitcast_fusion.2), channel_id=1, source_target_pairs={{0,2},{1,3},{2,0},{3,1},{4,6},{5,7},{6,4},{7,5}} | collective-permute-start | bytes 884744 | tf_op jit(solution)/shard_map/ppermute | solution.py:415
  37.3 590.9 %collective-permute-start.12 = (bf16[768,768]{1,0:T(8,128)(2,1)S(1)}, bf16[768,768]{1,0:T(8,128)(2,1)S(1)}, u32[]{:S(2)}, u32[]{:S(2)}) collective-permute-start(bf16[768,768]{1,0:T(8,128)(2,1)S(1)} %select_bitcast_fusion), channel_id=1, source_target_pairs={{0,2},{1,3},{2,0},{3,1},{4,6},{5,7},{6,4},{7,5}} | collective-permute-start | bytes 3538952 | tf_op jit(solution)/shard_map/ppermute | solution.py:415
  582.4 44.0 %collective-permute-start.3 = (bf16[576,768]{1,0:T(8,128)(2,1)S(1)}, bf16[576,768]{1,0:T(8,128)(2,1)S(1)}, u32[]{:S(2)}, u32[]{:S(2)}) collective-permute-start(bf16[576,768]{1,0:T(8,128)(2,1)S(1)} %select_bitcast_fusion.1), channel_id=1, source_target_pairs={{0,2},{1,3},{2,0},{3,1},{4,6},{5,7},{6,4},{7,5}} | collective-permute-start | bytes 2654216 | tf_op jit(solution)/shard_map/ppermute | solution.py:415
  626.5 28.9 %collective-permute-start.4 = (bf16[768,768]{1,0:T(8,128)(2,1)S(1)}, bf16[768,768]{1,0:T(8,128)(2,1)S(1)}, u32[]{:S(2)}, u32[]{:S(2)}) collective-permute-start(bf16[768,768]{1,0:T(8,128)(2,1)S(1)} %constant_dynamic-update-slice_fusion), channel_id=1, source_target_pairs={{0,4},{4,0},{1,5},{5,1},{2,6},{6,2},{3,7},{7,3}} | collective-permute-start | bytes 3538952 | tf_op jit(solution)/shard_map/ppermute | solution.py:418
  628.2 27.2 %copy-start.5 = (bf16[768,768]{1,0:T(8,128)(2,1)}, bf16[768,768]{1,0:T(8,128)(2,1)S(1)}, u32[]{:S(2)}) copy-start(bf16[768,768]{1,0:T(8,128)(2,1)S(1)} %collective-permute-done.12) | copy-start | bytes 3538948
  628.2 51.3 %collective-permute-start.13 = (bf16[768,768]{1,0:T(8,128)(2,1)S(1)}, bf16[768,768]{1,0:T(8,128)(2,1)S(1)}, u32[]{:S(2)}, u32[]{:S(2)}) collective-permute-start(bf16[768,768]{1,0:T(8,128)(2,1)S(1)} %collective-permute-done.12), channel_id=1, source_target_pairs={{0,4},{4,0},{1,5},{5,1},{2,6},{6,2},{3,7},{7,3}} | collective-permute-start | bytes 3538952 | tf_op jit(solution)/shard_map/ppermute | solution.py:418
  655.4 24.2 %copy-start.7 = (bf16[768,768]{1,0:T(8,128)(2,1)}, bf16[768,768]{1,0:T(8,128)(2,1)S(1)}, u32[]{:S(2)}) copy-start(bf16[768,768]{1,0:T(8,128)(2,1)S(1)} %collective-permute-done.4) | copy-start | bytes 3538948
  655.4 53.0 %collective-permute-start.8 = (bf16[2,768,768]{2,1,0:T(8,128)(2,1)S(1)}, bf16[2,768,768]{2,1,0:T(8,128)(2,1)}, u32[]{:S(2)}, u32[]{:S(2)}) collective-permute-start(bf16[2,768,768]{2,1,0:T(8,128)(2,1)S(1)} %copy-done.2), channel_id=1, source_target_pairs={{0,1},{1,0},{2,3},{3,2},{4,5},{5,4},{6,7},{7,6}} | collective-permute-start | bytes 7077896 | tf_op jit(solution)/shard_map/ppermute | solution.py:415
  680.6 28.3 %collective-permute-start.9 = (bf16[2,768,768]{2,1,0:T(8,128)(2,1)S(1)}, bf16[2,768,768]{2,1,0:T(8,128)(2,1)}, u32[]{:S(2)}, u32[]{:S(2)}) collective-permute-start(bf16[2,768,768]{2,1,0:T(8,128)(2,1)S(1)} %copy-done.1), channel_id=1, source_target_pairs={{0,1},{1,0},{2,3},{3,2},{4,5},{5,4},{6,7},{7,6}} | collective-permute-start | bytes 7077896 | tf_op jit(solution)/shard_map/ppermute | solution.py:415
  708.4 244.1 %collective-permute-start.18 = (bf16[16,512,768]{2,1,0:T(8,128)(2,1)}, bf16[16,512,768]{2,1,0:T(8,128)(2,1)}, u32[]{:S(2)}, u32[]{:S(2)}) collective-permute-start(bf16[16,512,768]{2,1,0:T(8,128)(2,1)} %dynamic-slice_bitcast_fusion), channel_id=1, source_target_pairs={{0,1},{1,0},{2,3},{3,2},{4,5},{5,4},{6,7},{7,6}} | collective-permute-start | bytes 37748744 | tf_op jit(solution)/shard_map/ppermute | solution.py:415
  708.9 120.2 %collective-permute-start.5 = (bf16[768,768]{1,0:T(8,128)(2,1)}, bf16[768,768]{1,0:T(8,128)(2,1)}, u32[]{:S(2)}, u32[]{:S(2)}) collective-permute-start(bf16[768,768]{1,0:T(8,128)(2,1)} %get-tuple-element.144.refs_4_), channel_id=1, source_target_pairs={{0,1},{1,0},{2,3},{3,2},{4,5},{5,4},{6,7},{7,6}} | collective-permute-start | bytes 3538952 | tf_op jit(solution)/shard_map/ppermute | solution.py:415
  708.9 121.4 %collective-permute-start.6 = (bf16[768,768]{1,0:T(8,128)(2,1)}, bf16[768,768]{1,0:T(8,128)(2,1)}, u32[]{:S(2)}, u32[]{:S(2)}) collective-permute-start(bf16[768,768]{1,0:T(8,128)(2,1)} %get-tuple-element.143.refs_6_), channel_id=1, source_target_pairs={{0,1},{1,0},{2,3},{3,2},{4,5},{5,4},{6,7},{7,6}} | collective-permute-start | bytes 3538952 | tf_op jit(solution)/shard_map/ppermute | solution.py:415
  829.1 271.5 %collective-permute-start.16 = (bf16[16,512,384]{2,1,0:T(8,128)(2,1)}, bf16[16,512,384]{2,1,0:T(8,128)(2,1)}, u32[]{:S(2)}, u32[]{:S(2)}) collective-permute-start(bf16[16,512,384]{2,1,0:T(8,128)(2,1)} %dynamic-slice_bitcast_fusion.5), channel_id=1, source_target_pairs={{0,2},{1,3},{2,0},{3,1},{4,6},{5,7},{6,4},{7,5}} | collective-permute-start | bytes 18874376 | tf_op jit(solution)/shard_map/ppermute | solution.py:415
  830.3 270.3 %collective-permute-start.17 = (bf16[16,512,384]{2,1,0:T(8,128)(2,1)}, bf16[16,512,384]{2,1,0:T(8,128)(2,1)}, u32[]{:S(2)}, u32[]{:S(2)}) collective-permute-start(bf16[16,512,384]{2,1,0:T(8,128)(2,1)} %dynamic-slice_bitcast_fusion.4), channel_id=1, source_target_pairs={{0,3},{1,2},{2,1},{3,0},{4,7},{5,6},{6,5},{7,4}} | collective-permute-start | bytes 18874376 | tf_op jit(solution)/shard_map/ppermute | solution.py:415
  830.5 242.0 %collective-permute-start.14 = (bf16[768,768]{1,0:T(8,128)(2,1)}, bf16[768,768]{1,0:T(8,128)(2,1)}, u32[]{:S(2)}, u32[]{:S(2)}) collective-permute-start(bf16[768,768]{1,0:T(8,128)(2,1)} %get-tuple-element.142.refs_4_.up_a), channel_id=1, source_target_pairs={{0,1},{1,0},{2,3},{3,2},{4,5},{5,4},{6,7},{7,6}} | collective-permute-start | bytes 3538952 | tf_op jit(solution)/shard_map/ppermute | solution.py:415
  831.3 241.5 %collective-permute-start.15 = (bf16[768,768]{1,0:T(8,128)(2,1)}, bf16[768,768]{1,0:T(8,128)(2,1)}, u32[]{:S(2)}, u32[]{:S(2)}) collective-permute-start(bf16[768,768]{1,0:T(8,128)(2,1)} %get-tuple-element.141.refs_6_.down_a), channel_id=1, source_target_pairs={{0,1},{1,0},{2,3},{3,2},{4,5},{5,4},{6,7},{7,6}} | collective-permute-start | bytes 3538952 | tf_op jit(solution)/shard_map/ppermute | solution.py:415
  952.5 237.2 %collective-permute-start.50 = (f32[2,768,768]{2,1,0:T(8,128)}, f32[2,768,768]{2,1,0:T(8,128)}, u32[]{:S(2)}, u32[]{:S(2)}) collective-permute-start(f32[2,768,768]{2,1,0:T(8,128)} %get-tuple-element.130), channel_id=1, source_target_pairs={{0,1},{1,0},{2,3},{3,2},{4,5},{5,4},{6,7},{7,6}} | collective-permute-start | bytes 14155784 | tf_op jit(solution)/shard_map/ppermute | solution.py:415
  1072.5 132.6 %collective-permute-start.48 = (f32[2,768,768]{2,1,0:T(8,128)}, f32[2,768,768]{2,1,0:T(8,128)}, u32[]{:S(2)}, u32[]{:S(2)}) collective-permute-start(f32[2,768,768]{2,1,0:T(8,128)} %get-tuple-element.126), channel_id=1, source_target_pairs={{0,1},{1,0},{2,3},{3,2},{4,5},{5,4},{6,7},{7,6}} | collective-permute-start | bytes 14155784 | tf_op jit(solution)/shard_map/ppermute | solution.py:415
  1072.8 133.8 %collective-permute-start.37 = (f32[2,768,768]{2,1,0:T(8,128)}, f32[2,768,768]{2,1,0:T(8,128)}, u32[]{:S(2)}, u32[]{:S(2)}) collective-permute-start(f32[2,768,768]{2,1,0:T(8,128)} %get-tuple-element.118), channel_id=1, source_target_pairs={{0,1},{1,0},{2,3},{3,2},{4,5},{5,4},{6,7},{7,6}} | collective-permute-start | bytes 14155784 | tf_op jit(solution)/shard_map/ppermute | solution.py:415
  1178.9 18.7 %collective-permute-start.44 = (f32[2,384,768]{2,1,0:T(8,128)}, f32[2,384,768]{2,1,0:T(8,128)}, u32[]{:S(2)}, u32[]{:S(2)}) collective-permute-start(f32[2,384,768]{2,1,0:T(8,128)} %get-tuple-element.122), channel_id=1, source_target_pairs={{0,1},{1,0},{2,3},{3,2},{4,5},{5,4},{6,7},{7,6}} | collective-permute-start | bytes 7077896 | tf_op jit(solution)/shard_map/ppermute | solution.py:415
  1188.9 222.3 %collective-permute-start.11 = (bf16[16,512,256]{2,1,0:T(8,128)(2,1)}, bf16[16,512,256]{2,1,0:T(8,128)(2,1)}, u32[]{:S(2)}, u32[]{:S(2)}) collective-permute-start(bf16[16,512,256]{2,1,0:T(8,128)(2,1)} %dynamic-slice_bitcast_fusion.6), channel_id=1, source_target_pairs={{0,3},{1,2},{2,1},{3,0},{4,7},{5,6},{6,5},{7,4}} | collective-permute-start | bytes 12582920 | tf_op jit(solution)/shard_map/ppermute | solution.py:415
  1189.7 222.9 %collective-permute-start.10 = (bf16[16,512,256]{2,1,0:T(8,128)(2,1)}, bf16[16,512,256]{2,1,0:T(8,128)(2,1)}, u32[]{:S(2)}, u32[]{:S(2)}) collective-permute-start(bf16[16,512,256]{2,1,0:T(8,128)(2,1)} %dynamic-slice_bitcast_fusion.7), channel_id=1, source_target_pairs={{0,2},{1,3},{2,0},{3,1},{4,6},{5,7},{6,4},{7,5}} | collective-permute-start | bytes 12582920 | tf_op jit(solution)/shard_map/ppermute | solution.py:415
  1197.6 53.7 %collective-permute-start.51 = (f32[768,768]{1,0:T(8,128)}, f32[768,768]{1,0:T(8,128)}, u32[]{:S(2)}, u32[]{:S(2)}) collective-permute-start(f32[768,768]{1,0:T(8,128)} %get-tuple-element.132), channel_id=1, source_target_pairs={{0,4},{4,0},{1,5},{5,1},{2,6},{6,2},{3,7},{7,3}} | collective-permute-start | bytes 7077896 | tf_op jit(solution)/shard_map/ppermute | solution.py:418
  1205.1 205.5 %collective-permute-start.19 = (bf16[8,512,128]{2,1,0:T(8,128)(2,1)}, bf16[8,512,128]{2,1,0:T(8,128)(2,1)}, u32[]{:S(2)}, u32[]{:S(2)}) collective-permute-start(bf16[8,512,128]{2,1,0:T(8,128)(2,1)} %get-tuple-element.89), channel_id=1, source_target_pairs={{0,2},{1,3},{2,0},{3,1},{4,6},{5,7},{6,4},{7,5}} | collective-permute-start | bytes 3145736 | tf_op jit(solution)/shard_map/ppermute | solution.py:415
  1206.6 202.5 %collective-permute-start.25 = (bf16[3,512,128]{2,1,0:T(8,128)(2,1)}, bf16[3,512,128]{2,1,0:T(8,128)(2,1)S(1)}, u32[]{:S(2)}, u32[]{:S(2)}) collective-permute-start(bf16[3,512,128]{2,1,0:T(8,128)(2,1)} %get-tuple-element.96), channel_id=1, source_target_pairs={{0,2},{1,3},{2,0},{3,1},{4,6},{5,7},{6,4},{7,5}} | collective-permute-start | bytes 1179656 | tf_op jit(solution)/shard_map/ppermute | solution.py:415
  1251.3 157.1 %collective-permute-start.21 = (bf16[2,512,128]{2,1,0:T(8,128)(2,1)}, bf16[2,512,128]{2,1,0:T(8,128)(2,1)S(1)}, u32[]{:S(2)}, u32[]{:S(2)}) collective-permute-start(bf16[2,512,128]{2,1,0:T(8,128)(2,1)} %get-tuple-element.92), channel_id=1, source_target_pairs={{0,2},{1,3},{2,0},{3,1},{4,6},{5,7},{6,4},{7,5}} | collective-permute-start | bytes 786440 | tf_op jit(solution)/shard_map/ppermute | solution.py:415
  1408.4 59.3 %copy-start.14 = (bf16[2,512,128]{2,1,0:T(8,128)(2,1)}, bf16[2,512,128]{2,1,0:T(8,128)(2,1)S(1)}, u32[]{:S(2)}) copy-start(bf16[2,512,128]{2,1,0:T(8,128)(2,1)S(1)} %collective-permute-done.21.h_a) | copy-start | bytes 786436
  1408.4 59.3 %collective-permute-start.20 = (bf16[8,512,128]{2,1,0:T(8,128)(2,1)}, bf16[8,512,128]{2,1,0:T(8,128)(2,1)}, u32[]{:S(2)}, u32[]{:S(2)}) collective-permute-start(bf16[8,512,128]{2,1,0:T(8,128)(2,1)} %get-tuple-element.90), channel_id=1, source_target_pairs={{0,3},{1,2},{2,1},{3,0},{4,7},{5,6},{6,5},{7,4}} | collective-permute-start | bytes 3145736 | tf_op jit(solution)/shard_map/ppermute | solution.py:415
  1409.1 58.6 %copy-start.11 = (bf16[3,512,128]{2,1,0:T(8,128)(2,1)}, bf16[3,512,128]{2,1,0:T(8,128)(2,1)S(1)}, u32[]{:S(2)}) copy-start(bf16[3,512,128]{2,1,0:T(8,128)(2,1)S(1)} %collective-permute-done.25.h_a) | copy-start | bytes 1179652
  1409.1 60.6 %collective-permute-start.45 = (f32[384,768]{1,0:T(8,128)}, f32[384,768]{1,0:T(8,128)}, u32[]{:S(2)}, u32[]{:S(2)}) collective-permute-start(f32[384,768]{1,0:T(8,128)} %get-tuple-element.124), channel_id=1, source_target_pairs={{0,4},{4,0},{1,5},{5,1},{2,6},{6,2},{3,7},{7,3}} | collective-permute-start | bytes 3538952 | tf_op jit(solution)/shard_map/ppermute | solution.py:418
  1410.6 78.2 %collective-permute-start.49 = (f32[768,768]{1,0:T(8,128)}, f32[768,768]{1,0:T(8,128)}, u32[]{:S(2)}, u32[]{:S(2)}) collective-permute-start(f32[768,768]{1,0:T(8,128)} %get-tuple-element.128), channel_id=1, source_target_pairs={{0,4},{4,0},{1,5},{5,1},{2,6},{6,2},{3,7},{7,3}} | collective-permute-start | bytes 7077896 | tf_op jit(solution)/shard_map/ppermute | solution.py:418
  1411.1 127.9 %collective-permute-start.38 = (f32[768,768]{1,0:T(8,128)}, f32[768,768]{1,0:T(8,128)}, u32[]{:S(2)}, u32[]{:S(2)}) collective-permute-start(f32[768,768]{1,0:T(8,128)} %get-tuple-element.120), channel_id=1, source_target_pairs={{0,4},{4,0},{1,5},{5,1},{2,6},{6,2},{3,7},{7,3}} | collective-permute-start | bytes 7077896 | tf_op jit(solution)/shard_map/ppermute | solution.py:418
  1412.6 77.0 %collective-permute-start.52 = (f32[768,768]{1,0:T(8,128)}, f32[768,768]{1,0:T(8,128)}, u32[]{:S(2)}, u32[]{:S(2)}) collective-permute-start(f32[768,768]{1,0:T(8,128)} %add.47), channel_id=1, source_target_pairs={{0,2},{1,3},{2,0},{3,1},{4,6},{5,7},{6,4},{7,5}} | collective-permute-start | bytes 7077896 | tf_op jit(solution)/shard_map/ppermute | solution.py:415
  1467.7 104.9 %collective-permute-start.27 = (f32[2,256,768]{2,1,0:T(8,128)}, f32[2,256,768]{2,1,0:T(8,128)}, u32[]{:S(2)}, u32[]{:S(2)}) collective-permute-start(f32[2,256,768]{2,1,0:T(8,128)} %get-tuple-element.106), channel_id=1, source_target_pairs={{0,1},{1,0},{2,3},{3,2},{4,5},{5,4},{6,7},{7,6}} | collective-permute-start | bytes 4718600 | tf_op jit(solution)/shard_map/ppermute | solution.py:415
  1469.7 45.1 %collective-permute-start.26 = (bf16[3,512,128]{2,1,0:T(8,128)(2,1)}, bf16[3,512,128]{2,1,0:T(8,128)(2,1)}, u32[]{:S(2)}, u32[]{:S(2)}) collective-permute-start(bf16[3,512,128]{2,1,0:T(8,128)(2,1)} %get-tuple-element.97), channel_id=1, source_target_pairs={{0,3},{1,2},{2,1},{3,0},{4,7},{5,6},{6,5},{7,4}} | collective-permute-start | bytes 1179656 | tf_op jit(solution)/shard_map/ppermute | solution.py:415
  1488.8 27.7 %collective-permute-start.23 = (bf16[3,512,128]{2,1,0:T(8,128)(2,1)}, bf16[3,512,128]{2,1,0:T(8,128)(2,1)S(1)}, u32[]{:S(2)}, u32[]{:S(2)}) collective-permute-start(bf16[3,512,128]{2,1,0:T(8,128)(2,1)} %get-tuple-element.94), channel_id=1, source_target_pairs={{0,2},{1,3},{2,0},{3,1},{4,6},{5,7},{6,4},{7,5}} | collective-permute-start | bytes 1179656 | tf_op jit(solution)/shard_map/ppermute | solution.py:415
  1489.6 67.7 %collective-permute-start.24 = (bf16[3,512,128]{2,1,0:T(8,128)(2,1)}, bf16[3,512,128]{2,1,0:T(8,128)(2,1)S(1)}, u32[]{:S(2)}, u32[]{:S(2)}) collective-permute-start(bf16[3,512,128]{2,1,0:T(8,128)(2,1)} %get-tuple-element.95), channel_id=1, source_target_pairs={{0,3},{1,2},{2,1},{3,0},{4,7},{5,6},{6,5},{7,4}} | collective-permute-start | bytes 1179656 | tf_op jit(solution)/shard_map/ppermute | solution.py:415
  1514.8 51.5 %collective-permute-start.22 = (bf16[2,512,128]{2,1,0:T(8,128)(2,1)}, bf16[2,512,128]{2,1,0:T(8,128)(2,1)}, u32[]{:S(2)}, u32[]{:S(2)}) collective-permute-start(bf16[2,512,128]{2,1,0:T(8,128)(2,1)} %get-tuple-element.93), channel_id=1, source_target_pairs={{0,3},{1,2},{2,1},{3,0},{4,7},{5,6},{6,5},{7,4}} | collective-permute-start | bytes 786440 | tf_op jit(solution)/shard_map/ppermute | solution.py:415
  1516.5 36.7 %copy-start.12 = (bf16[3,512,128]{2,1,0:T(8,128)(2,1)}, bf16[3,512,128]{2,1,0:T(8,128)(2,1)S(1)}, u32[]{:S(2)}) copy-start(bf16[3,512,128]{2,1,0:T(8,128)(2,1)S(1)} %collective-permute-done.23.h_a) | copy-start | bytes 1179652
  1516.5 63.0 %collective-permute-start.46 = (f32[384,768]{1,0:T(8,128)}, f32[384,768]{1,0:T(8,128)}, u32[]{:S(2)}, u32[]{:S(2)}) collective-permute-start(f32[384,768]{1,0:T(8,128)} %add.45), channel_id=1, source_target_pairs={{0,2},{1,3},{2,0},{3,1},{4,6},{5,7},{6,4},{7,5}} | collective-permute-start | bytes 3538952 | tf_op jit(solution)/shard_map/ppermute | solution.py:415
  1539.0 178.9 %collective-permute-start.53 = (f32[768,768]{1,0:T(8,128)}, f32[768,768]{1,0:T(8,128)}, u32[]{:S(2)}, u32[]{:S(2)}) collective-permute-start(f32[768,768]{1,0:T(8,128)} %add.48.kept_ref), channel_id=1, source_target_pairs={{0,4},{4,0},{1,5},{5,1},{2,6},{6,2},{3,7},{7,3}} | collective-permute-start | bytes 7077896 | tf_op jit(solution)/shard_map/ppermute | solution.py:418
  1557.3 181.5 %collective-permute-start.39 = (f32[768,768]{1,0:T(8,128)}, f32[768,768]{1,0:T(8,128)}, u32[]{:S(2)}, u32[]{:S(2)}) collective-permute-start(f32[768,768]{1,0:T(8,128)} %add.44.refs_2_.refs_6_.refs_4_), channel_id=1, source_target_pairs={{0,4},{4,0},{1,5},{5,1},{2,6},{6,2},{3,7},{7,3}} | collective-permute-start | bytes 7077896 | tf_op jit(solution)/shard_map/ppermute | solution.py:418
  1572.5 4.2 collective-permute-start.32
  1575.4 92.6 %copy-start.10 = (f32[256,768]{1,0:T(8,128)S(1)}, f32[256,768]{1,0:T(8,128)}, u32[]{:S(2)}) copy-start(f32[256,768]{1,0:T(8,128)} %get-tuple-element.107) | copy-start | bytes 2359300
  1575.4 92.0 %collective-permute-start.28 = (f32[256,768]{1,0:T(8,128)}, f32[256,768]{1,0:T(8,128)}, u32[]{:S(2)}, u32[]{:S(2)}) collective-permute-start(f32[256,768]{1,0:T(8,128)} %get-tuple-element.108), channel_id=1, source_target_pairs={{0,4},{4,0},{1,5},{5,1},{2,6},{6,2},{3,7},{7,3}} | collective-permute-start | bytes 2359304 | tf_op jit(solution)/shard_map/ppermute | solution.py:418
  1576.7 2.1 collective-permute-start.29
  1578.8 86.2 %collective-permute-start.33 = (f32[64,768]{1,0:T(8,128)}, f32[64,768]{1,0:T(8,128)S(1)}, u32[]{:S(2)}, u32[]{:S(2)}) collective-permute-start(f32[64,768]{1,0:T(8,128)} %get-tuple-element.116), channel_id=1, source_target_pairs={{0,4},{4,0},{1,5},{5,1},{2,6},{6,2},{3,7},{7,3}} | collective-permute-start | bytes 589832 | tf_op jit(solution)/shard_map/ppermute | solution.py:418
  1579.5 137.9 %collective-permute-start.47 = (f32[384,768]{1,0:T(8,128)}, f32[384,768]{1,0:T(8,128)}, u32[]{:S(2)}, u32[]{:S(2)}) collective-permute-start(f32[384,768]{1,0:T(8,128)} %collective-permute-done.46.refs_0_), channel_id=1, source_target_pairs={{0,4},{4,0},{1,5},{5,1},{2,6},{6,2},{3,7},{7,3}} | collective-permute-start | bytes 3538952 | tf_op jit(solution)/shard_map/ppermute | solution.py:418
  1582.8 111.3 %copy-start.16 = (f32[64,768]{1,0:T(8,128)S(1)}, f32[64,768]{1,0:T(8,128)}, u32[]{:S(2)}) copy-start(f32[64,768]{1,0:T(8,128)} %get-tuple-element.111) | copy-start | bytes 589828
  1665.0 28.3 %collective-permute-start.30 = (f32[64,768]{1,0:T(8,128)}, f32[64,768]{1,0:T(8,128)S(1)}, u32[]{:S(2)}, u32[]{:S(2)}) collective-permute-start(f32[64,768]{1,0:T(8,128)} %get-tuple-element.112), channel_id=1, source_target_pairs={{0,4},{4,0},{1,5},{5,1},{2,6},{6,2},{3,7},{7,3}} | collective-permute-start | bytes 589832 | tf_op jit(solution)/shard_map/ppermute | solution.py:418
  1667.4 26.7 %collective-permute-start.34 = (f32[64,768]{1,0:T(8,128)S(1)}, f32[64,768]{1,0:T(8,128)S(1)}, u32[]{:S(2)}, u32[]{:S(2)}) collective-permute-start(f32[64,768]{1,0:T(8,128)S(1)} %add.43), channel_id=1, source_target_pairs={{0,2},{1,3},{2,0},{3,1},{4,6},{5,7},{6,4},{7,5}} | collective-permute-start | bytes 589832 | tf_op jit(solution)/shard_map/ppermute | solution.py:415
  1693.2 7.9 collective-permute-start.40
  1694.2 38.7 %copy-start.15 = (f32[64,768]{1,0:T(8,128)}, f32[64,768]{1,0:T(8,128)S(1)}, u32[]{:S(2)}) copy-start(f32[64,768]{1,0:T(8,128)S(1)} %collective-permute-done.34.refs_1_) | copy-start | bytes 589828
  1694.2 15.3 collective-permute-start.31
  1701.1 14.8 collective-permute-start.41
  1709.4 23.4 %copy-start.3 = (f32[128,768]{1,0:T(8,128)}, f32[128,768]{1,0:T(8,128)S(1)}, u32[]{:S(2)}) copy-start(f32[128,768]{1,0:T(8,128)S(1)} %collective-permute-done.31.refs_2_.refs_0_) | copy-start | bytes 1179652
  1709.5 33.4 %collective-permute-start.35 = (f32[128,768]{1,0:T(8,128)S(1)}, f32[128,768]{1,0:T(8,128)S(1)}, u32[]{:S(2)}, u32[]{:S(2)}) collective-permute-start(f32[128,768]{1,0:T(8,128)S(1)} %collective-permute-done.31.refs_2_.refs_0_), channel_id=1, source_target_pairs={{0,4},{4,0},{1,5},{5,1},{2,6},{6,2},{3,7},{7,3}} | collective-permute-start | bytes 1179656 | tf_op jit(solution)/shard_map/ppermute | solution.py:418
  1715.9 27.0 %collective-permute-start.43 = (f32[128,768]{1,0:T(8,128)}, f32[128,768]{1,0:T(8,128)}, u32[]{:S(2)}, u32[]{:S(2)}) collective-permute-start(f32[128,768]{1,0:T(8,128)} %collective-permute-done.41.refs_1_), channel_id=1, source_target_pairs={{0,4},{4,0},{1,5},{5,1},{2,6},{6,2},{3,7},{7,3}} | collective-permute-start | bytes 1179656 | tf_op jit(solution)/shard_map/ppermute | solution.py:418
  1717.4 25.4 %collective-permute-start.42 = (f32[64,768]{1,0:T(8,128)}, f32[64,768]{1,0:T(8,128)}, u32[]{:S(2)}, u32[]{:S(2)}) collective-permute-start(f32[64,768]{1,0:T(8,128)} %collective-permute-done.40.refs_0_), channel_id=1, source_target_pairs={{0,4},{4,0},{1,5},{5,1},{2,6},{6,2},{3,7},{7,3}} | collective-permute-start | bytes 589832 | tf_op jit(solution)/shard_map/ppermute | solution.py:418
  1717.9 28.9 %collective-permute-start.36 = (f32[64,768]{1,0:T(8,128)S(1)}, f32[64,768]{1,0:T(8,128)}, u32[]{:S(2)}, u32[]{:S(2)}) collective-permute-start(f32[64,768]{1,0:T(8,128)S(1)} %collective-permute-done.34.refs_1_), channel_id=1, source_target_pairs={{0,4},{4,0},{1,5},{5,1},{2,6},{6,2},{3,7},{7,3}} | collective-permute-start | bytes 589832 | tf_op jit(solution)/shard_map/ppermute | solution.py:418
  (7 other events, 24.2 us)

commit v10 on v9

--- a/solution.py
+++ b/solution.py
@@ -16,6 +16,7 @@
 CHUNKS = (3, 3, 2)
 FIRST = 192
 ALL_VMEM = 66_000_000
+TAIL_VMEM = 24 * 2**20
 
 
 def gelu_parts(pre_act):
@@ -231,7 +232,7 @@
     return value.reshape(shape[:axis] + (2, shape[axis] // 2) + shape[axis + 1 :])
 
 
-def small_call(layer, grad, x_saved, h_pair, down_pair, start, first_pair, init=None, finish=None, pre=None, pre_pairs=None, pre_first=0):
+def small_call(layer, grad, x_saved, h_pair, down_pair, start, first_pair, init=None, finish=None, pre=None, pre_pairs=None, pre_first=0, vmem=TAIL_VMEM):
     _, _, seq, hidden = grad.shape
     pairs = h_pair[0].shape[0]
     row_spec = pl.BlockSpec((2, 1, seq, hidden), lambda b: (0, b + first_pair, 0, 0))
@@ -256,7 +257,7 @@
         in_specs=in_specs,
         out_specs=[dw_spec, dw_spec, row_spec if finish else pre_spec],
         input_output_aliases={} if pre is None else {len(in_specs) - 1: 2},
-        compiler_params=pltpu.CompilerParams(dimension_semantics=("arbitrary",), vmem_limit_bytes=ALL_VMEM),
+        compiler_params=pltpu.CompilerParams(dimension_semantics=("arbitrary",), vmem_limit_bytes=vmem),
         cost_estimate=pl.CostEstimate(
             flops=24 * pairs * seq * hidden * SMALL, bytes_accessed=8 * pairs * seq * hidden, transcendentals=4 * pairs * seq * SMALL),
     )(grad, x_saved, *h_pair, *down_pair, *(finish or ()), *(init or ()), *(() if pre is None else (pre,)))
@@ -276,7 +277,7 @@
         grid=(1,),
         in_specs=[up_spec, up_spec],
         out_specs=pl.BlockSpec((hidden, 2 * LANES), lambda i: (0, 0)),
-        compiler_params=pltpu.CompilerParams(dimension_semantics=("arbitrary",), vmem_limit_bytes=ALL_VMEM),
+        compiler_params=pltpu.CompilerParams(dimension_semantics=("arbitrary",), vmem_limit_bytes=TAIL_VMEM),
         cost_estimate=pl.CostEstimate(flops=hidden * LANES, bytes_accessed=8 * hidden * LANES, transcendentals=0),
     )(*up_pair)
 
@@ -286,20 +287,19 @@
     out_ref[0, 0] = total.astype(BF16)
 
 
-def finish_call(carry, pre_pair, ups, first_pair, first_half, halves, out):
+def finish_call(carry, pre_pair, ups, first_pair, pairs, late_first, out):
     _, _, seq, hidden = carry.shape
-    count = pre_pair[1].shape[1]
-    row_spec = pl.BlockSpec((1, 1, seq, hidden), lambda r, b: (r + first_half, b + first_pair, 0, 0))
-    pre_specs = [pl.BlockSpec((1, 1, seq, LANES), lambda r, b, first=first: (r + first_half, b + first, 0, 0)) for first in (first_pair, 0)]
-    rows = halves * count
+    row_spec = pl.BlockSpec((1, 1, seq, hidden), lambda r, b: (r, b + first_pair, 0, 0))
+    pre_specs = [pl.BlockSpec((1, 1, seq, LANES), lambda r, b, first=first: (r, b + first, 0, 0)) for first in (first_pair, first_pair - late_first)]
+    rows = 2 * pairs
     return pl.pallas_call(
         finish_body,
         out_shape=jax.ShapeDtypeStruct(carry.shape, BF16),
-        grid=(halves, count),
+        grid=(2, pairs),
         in_specs=[row_spec, *pre_specs, pl.BlockSpec(ups.shape, lambda r, b: (0, 0)), pl.BlockSpec(memory_space=pl.ANY)],
         out_specs=row_spec,
         input_output_aliases={4: 0},
-        compiler_params=pltpu.CompilerParams(dimension_semantics=("arbitrary", "arbitrary"), vmem_limit_bytes=ALL_VMEM),
+        compiler_params=pltpu.CompilerParams(dimension_semantics=("arbitrary", "arbitrary"), vmem_limit_bytes=44 * 2**20),
         cost_estimate=pl.CostEstimate(flops=4 * rows * seq * hidden * LANES, bytes_accessed=7 * rows * seq * hidden, transcendentals=0),
     )(carry, *pre_pair, ups, out)
 
@@ -321,7 +321,7 @@
         out_shape=[jax.ShapeDtypeStruct((size, hidden), F32)] * 2,
         grid_spec=pltpu.PrefetchScalarGridSpec(
             num_scalar_prefetch=1, grid=(size // step,), in_specs=[both_spec] * 2, out_specs=[one_spec] * 2),
-        compiler_params=pltpu.CompilerParams(dimension_semantics=("arbitrary",), vmem_limit_bytes=ALL_VMEM),
+        compiler_params=pltpu.CompilerParams(dimension_semantics=("arbitrary",), vmem_limit_bytes=TAIL_VMEM),
         cost_estimate=pl.CostEstimate(flops=4 * mine.size, bytes_accessed=12 * mine.size, transcendentals=0),
     )(first, mine, theirs)
 
@@ -352,29 +352,18 @@
             ],
         ),
         input_output_aliases={3: 0, 4: 1} if bufs is not None else {},
-        compiler_params=pltpu.CompilerParams(dimension_semantics=("arbitrary",), vmem_limit_bytes=ALL_VMEM),
+        compiler_params=pltpu.CompilerParams(dimension_semantics=("arbitrary",), vmem_limit_bytes=TAIL_VMEM),
         cost_estimate=pl.CostEstimate(flops=4 * size * hidden, bytes_accessed=16 * size * hidden, transcendentals=0),
     )(first, kept, other, *(bufs or ()))
 
 
-def join_place_body(spans, layer, start, first_ref, *refs):
-    count = len(spans)
-    size = sum(n for _, n in spans)
-    mine_ref, theirs_ref = refs[2 * count : 2 * count + 2]
-    up_out, down_out, near_ref, far_ref, up_ref, down_ref, sem = refs[-7:]
-    loads = [(ref.at[pl.ds(start, size)], near_ref.at[k]) for k, ref in enumerate((mine_ref, theirs_ref))]
-    for k in range(2):
-        place = 0
-        for (low, n), ref in zip(spans, refs[k * count : (k + 1) * count]):
-            loads.append((ref.at[pl.ds(low, n)], far_ref.at[k, pl.ds(place, n)]))
-            place += n
-    copies = [pltpu.make_async_copy(src, dst, sem.at[i]) for i, (src, dst) in enumerate(loads)]
-    for copy in copies:
-        copy.start()
-    for copy in copies:
-        copy.wait()
+def join_place_body(blocks, pieces, layer, start, first_ref, *refs):
+    refs = list(refs)
+    mine, theirs, kept_far, other_far = (jnp.concatenate([refs.pop(0)[...] for _ in range(n)]) for n in (blocks, blocks, pieces, pieces))
+    up_out, down_out, up_ref, down_ref, sem = refs[-5:]
+    size = mine.shape[0]
     first = first_ref[0] == 1
-    kept, other = near_ref[0] + far_ref[0], near_ref[1] + far_ref[1]
+    kept, other = mine + kept_far, theirs + other_far
     down_ref[...] = jnp.where(first, other, kept)
     down_copy = pltpu.make_async_copy(down_ref, down_out.at[layer, pl.ds(start, size), :], sem.at[0])
     down_copy.start()
@@ -387,25 +376,27 @@
 
 def join_place_call(first, pieces, near_pair, layer, start, bufs):
     hidden = near_pair[0].shape[1]
-    spans = [(low, n) for _, _, low, n in pieces]
-    size = sum(n for _, n in spans)
+    size = sum(n for _, _, _, n in pieces)
+    block = size if start % size == 0 else LANES
+    near_specs = [pl.BlockSpec((block, hidden), lambda i, first, at=at: (at, 0)) for at in range(start // block, (start + size) // block)]
+    piece_specs = [pl.BlockSpec((n, hidden), lambda i, first, at=low // n: (at, 0)) for _, _, low, n in pieces]
     any_spec = pl.BlockSpec(memory_space=pl.ANY)
-    count = 2 * len(pieces) + 2
-    return pl.pallas_call(
-        functools.partial(join_place_body, spans, layer, start),
+    blocks, count = len(near_specs), len(pieces)
+    operands = [near_pair[0]] * blocks + [near_pair[1]] * blocks + [p[0] for p in pieces] + [p[1] for p in pieces]
+    return pl.pallas_call(
+        functools.partial(join_place_body, blocks, count, layer, start),
         out_shape=[jax.ShapeDtypeStruct(b.shape, b.dtype) for b in bufs],
         grid_spec=pltpu.PrefetchScalarGridSpec(
             num_scalar_prefetch=1,
             grid=(1,),
-            in_specs=[any_spec] * (count + 2),
+            in_specs=near_specs * 2 + piece_specs * 2 + [any_spec] * 2,
             out_specs=[any_spec] * 2,
-            scratch_shapes=[pltpu.VMEM((2, size, hidden), F32)] * 2
-            + [pltpu.VMEM((hidden, size), F32), pltpu.VMEM((size, hidden), F32), pltpu.SemaphoreType.DMA((count,))],
+            scratch_shapes=[pltpu.VMEM((hidden, size), F32), pltpu.VMEM((size, hidden), F32), pltpu.SemaphoreType.DMA((2,))],
         ),
-        input_output_aliases={1 + count: 0, 2 + count: 1},
-        compiler_params=pltpu.CompilerParams(dimension_semantics=("arbitrary",), vmem_limit_bytes=ALL_VMEM),
+        input_output_aliases={1 + len(operands): 0, 2 + len(operands): 1},
+        compiler_params=pltpu.CompilerParams(dimension_semantics=("arbitrary",), vmem_limit_bytes=TAIL_VMEM),
         cost_estimate=pl.CostEstimate(flops=4 * size * hidden, bytes_accessed=24 * size * hidden, transcendentals=0),
-    )(first, *[p[0] for p in pieces], *[p[1] for p in pieces], *near_pair, *bufs)
+    )(first, *operands, *bufs)
 
 
 def solution(mesh):
@@ -512,12 +503,13 @@
         dw_2, dw_3, grad_x = small_call(
             0, grad_mid, x_saved, h_small[1], down_pair, last, 0, finish=(carry, pre_1, small_up))
         dw_2, dw_3, pre_2 = small_call(
-            0, grad_mid, x_saved, h_small[2], down_pair, last, early, init=(dw_2, dw_3), pre_pairs=rows // 2 - early)
+            0, grad_mid, x_saved, h_small[2], down_pair, last, early, init=(dw_2, dw_3), vmem=TAIL_VMEM, pre_pairs=rows // 2 - early)
         dw_2, dw_3, pre_2 = small_call(
-            0, grad_mid, x_saved, h_small[3], down_pair, last, late, init=(dw_2, dw_3),
+            0, grad_mid[:, late:], x_saved[:1, :, late:], h_small[3], down_pair, last, 0, init=(dw_2, dw_3), vmem=TAIL_VMEM,
             pre=pre_2, pre_pairs=rows // 2 - early, pre_first=late - early)
         exchange(partial_sum(dw_2, dw_3))
-        grad_x = finish_call(carry, (pre_1, pre_2), small_up, early, 0, 2, grad_x)
+        for first_pair, pairs in ((early, 2), (early + 2, rows // 2 - early - 2)):
+            grad_x = finish_call(carry, (pre_1, pre_2), small_up, first_pair, pairs, early, grad_x)
         bufs = place([(*pieces[0], 0, bounds[1])], 0, 0, bufs, near_pair)
         middle = [(*pieces[1], 0, 64), (*pieces[2], 0, 128), (*pieces[3], 0, 64)]
         bufs = place(middle, 0, bounds[1], bufs, near_pair)

time: 1750 us -> 1740 us (level)
  Pallas kernels: 613 us -> 583 us
  local copies, waits for them, and re-layouts: 62.8 us -> 86.5 us
    unnamed x35 -> x59, local copies, waits for them, and re-layouts: 2.03 us -> 21.3 us
  transfers between devices with their start and end apart: 54 -> 54, of which waited for: 14 -> 15; matrix products, arithmetic and copies ran while one was open for 3% -> 3% of each run, Pallas kernels for 35% -> 33%
where the time goes in v10:
time: 1740 us
  waiting for transfers between devices  1000 us (57%)
  Pallas kernels  583 us (34%)
  local copies, waits for them, and re-layouts  86.5 us (5%)
  starting transfers between devices  47 us (3%)
  other arithmetic  20.2 us (1%)
    ppermute x38, waiting for transfers between devices, to_model(): return lax.ppermute(value, 'model', [(i, i ^ flip) for i in range(n_model)])  752 us
    pallas_call x4, Pallas kernels, block_call(): pl.pallas_call(functools.partial(block_body, carry is not None, final, ro...  438 us
    ppermute x16, waiting for transfers between devices, to_data(): return lax.ppermute(value, 'data', [(0, 1), (1, 0)])  250 us
    squeeze x8, local copies, waits for them, and re-layouts, h_from(): lax.dynamic_slice(held[0], (layer, 0, begin, start), (1, rows, seq, size))  60.8 us
    pallas_call x1, Pallas kernels, wide_call(): pl.pallas_call(functools.partial(wide_body, start), out_shape=[jax.ShapeD...  54.3 us
    pallas_call x4, Pallas kernels, small_call(): pl.pallas_call(functools.partial(small_body, init is not None, finish is...  36 us
  transfers between devices with their start and end apart: 54, of which 15 were waited for; matrix products, arithmetic and copies ran while one was open for 3% of the time, Pallas kernels for 33%

profile of v10, /device:TPU:0, one launch (start us, length us, event | category | flops | bytes accessed | tf_op | source)
XLA Modules:
  0.0 1740.1 jit_solution(14780891547374036321)
XLA Ops:
  1.7 1.5 select_bitcast_fusion.1
  3.3 10.6 dynamic-slice_bitcast_fusion.3
  13.9 10.6 dynamic-slice_bitcast_fusion.2
  24.5 7.2 dynamic-slice_bitcast_fusion.1
  32.5 2.6 collective-permute-start.1
  35.1 2.0 collective-permute-start.2
  37.3 545.1 %collective-permute-done.2 = bf16[192,768]{1,0:T(8,128)(2,1)S(1)} collective-permute-done((bf16[192,768]{1,0:T(8,128)(2,1)S(1)}, bf16[192,768]{1,0:T(8,128)(2,1)S(1)}, u32[]{:S(2)}, u32[]{:S(2)}) %collective-permute-start.2) | collective-permute-done | bytes 294944 | tf_op jit(solution)/shard_map/ppermute | solution.py:406
  582.4 2.1 collective-permute-start.3
  584.5 41.9 %collective-permute-done.3 = bf16[576,768]{1,0:T(8,128)(2,1)S(1)} collective-permute-done((bf16[576,768]{1,0:T(8,128)(2,1)S(1)}, bf16[576,768]{1,0:T(8,128)(2,1)S(1)}, u32[]{:S(2)}, u32[]{:S(2)}) %collective-permute-start.3) | collective-permute-done | bytes 884768 | tf_op jit(solution)/shard_map/ppermute | solution.py:406
  626.5 1.7 collective-permute-start.4
  628.5 26.8 %collective-permute-done.4 = bf16[768,768]{1,0:T(8,128)(2,1)S(1)} collective-permute-done((bf16[768,768]{1,0:T(8,128)(2,1)S(1)}, bf16[768,768]{1,0:T(8,128)(2,1)S(1)}, u32[]{:S(2)}, u32[]{:S(2)}) %collective-permute-start.4) | collective-permute-done | bytes 1179680 | tf_op jit(solution)/shard_map/ppermute | solution.py:409
  655.4 24.2 %collective-permute-done.13 = bf16[768,768]{1,0:T(8,128)(2,1)S(1)} collective-permute-done((bf16[768,768]{1,0:T(8,128)(2,1)S(1)}, bf16[768,768]{1,0:T(8,128)(2,1)S(1)}, u32[]{:S(2)}, u32[]{:S(2)}) %collective-permute-start.13) | collective-permute-done | bytes 1179680 | tf_op jit(solution)/shard_map/ppermute | solution.py:409
  680.6 10.6 dynamic-slice_bitcast_fusion
  691.2 6.3 dynamic-slice_bitcast_fusion.5
  697.5 6.3 dynamic-slice_bitcast_fusion.4
  703.8 3.0 broadcast_select_fusion.2
  706.7 1.6 broadcast_select_fusion
  709.3 119.7 %shard_map.76 = (f32[16,512,768]{2,1,0:T(8,128)}, f32[2,768,768]{2,1,0:T(8,128)}, f32[2,768,768]{2,1,0:T(8,128)}) custom-call(s32[1]{0:T(128)} %bitcast._, bf16[16,512,768]{2,1,0:T(8,128)(2,1)} %refs_0_.3, bf16[2,16,512,768]{3,2,1,0:T(8,128)(2,1)} %x_ref.1, bf16[2,16,2048,768]{3,2,1,0:T(8,128)(2,1)} %hi_ref.3, ...), custom_call_target="tpu_custom_call" | custom-call | flops 77309411328 | bytes 50331648 | tf_op jit(solution)/shard_map/pallas_call | solution.py:114
  831.2 121.2 %shard_map.77 = (bf16[16,512,768]{2,1,0:T(8,128)(2,1)}, f32[2,768,768]{2,1,0:T(8,128)}, f32[2,768,768]{2,1,0:T(8,128)}) custom-call(s32[1]{0:T(128)} %bitcast._, bf16[16,512,768]{2,1,0:T(8,128)(2,1)} %refs_0_.3, bf16[2,16,512,768]{3,2,1,0:T(8,128)(2,1)} %x_ref.1, bf16[16,512,768]{2,1,0:T(8,128)(2,1)} %collective-permute-done.refs_2_, ...), custom_call_target="tpu_custom_call" | custom-call | flops 77309411328 | bytes 50331648 | tf_op jit(solution)/shard_map/pallas_call | solution.py:114
  952.9 119.3 %shard_map.78 = (f32[16,512,768]{2,1,0:T(8,128)}, f32[2,768,768]{2,1,0:T(8,128)}, f32[2,768,768]{2,1,0:T(8,128)}) custom-call(s32[1]{0:T(128)} %bitcast._, bf16[16,512,768]{2,1,0:T(8,128)(2,1)} %get-tuple-element.78.refs_0_.grad_ref, bf16[2,16,512,768]{3,2,1,0:T(8,128)(2,1)} %x_ref.1, bf16[2,16,2048,768]{3,2,1,0:T(8,128)(2,1)} %hi_ref.3, ...), custom_call_target="tpu_custom_call" | custom-call | flops 77309411328 | bytes 50331648 | tf_op jit(solution)/shard_map/pallas_call | solution.py:114
  1072.7 27.8 %collective-permute-done.17.refs_3_ = bf16[16,512,384]{2,1,0:T(8,128)(2,1)} collective-permute-done((bf16[16,512,384]{2,1,0:T(8,128)(2,1)}, bf16[16,512,384]{2,1,0:T(8,128)(2,1)}, u32[]{:S(2)}, u32[]{:S(2)}) %collective-permute-start.17) | collective-permute-done | bytes 6291488 | tf_op jit(solution)/shard_map/ppermute | solution.py:406
  1100.5 78.3 %shard_map.79 = (f32[16,512,768]{2,1,0:T(8,128)}, f32[2,384,768]{2,1,0:T(8,128)}, f32[2,384,768]{2,1,0:T(8,128)}) custom-call(s32[1]{0:T(128)} %bitcast._, bf16[16,512,768]{2,1,0:T(8,128)(2,1)} %get-tuple-element.78.refs_0_.grad_ref, bf16[2,16,512,768]{3,2,1,0:T(8,128)(2,1)} %x_ref.1, bf16[16,512,384]{2,1,0:T(8,128)(2,1)} %collective-permute-done.16.refs_2_, ...), custom_call_target="tpu_custom_call" | custom-call | flops 38654705664 | bytes 50331648 | tf_op jit(solution)/shard_map/pallas_call | solution.py:114
  1179.7 4.6 dynamic-slice_bitcast_fusion.7
  1184.3 4.6 dynamic-slice_bitcast_fusion.6
  1190.5 2.3 copy-done.4
  1192.8 5.6 shard_map.96
  1202.6 6.3 shard_map.81
  1210.9 44.1 %collective-permute-done.51 = f32[768,768]{1,0:T(8,128)} collective-permute-done((f32[768,768]{1,0:T(8,128)}, f32[768,768]{1,0:T(8,128)}, u32[]{:S(2)}, u32[]{:S(2)}) %collective-permute-start.51) | collective-permute-done | bytes 2359328 | tf_op jit(solution)/shard_map/ppermute | solution.py:409
  1256.2 6.3 shard_map.82
  1262.6 1.7 copy-done.12
  1264.2 1.7 copy-done.14
  1265.9 1.9 shard_map.94
  1268.8 2.3 copy-done.2
  1271.2 5.6 shard_map.95
  1278.2 2.3 copy-done.3
  1280.6 5.8 shard_map.90
  1286.4 4.2 add.47
  1290.6 117.8 %collective-permute-done.21.h_a = bf16[2,512,128]{2,1,0:T(8,128)(2,1)S(1)} collective-permute-done((bf16[2,512,128]{2,1,0:T(8,128)(2,1)}, bf16[2,512,128]{2,1,0:T(8,128)(2,1)S(1)}, u32[]{:S(2)}, u32[]{:S(2)}) %collective-permute-start.21) | collective-permute-done | bytes 262176 | tf_op jit(solution)/shard_map/ppermute | solution.py:406
  1413.2 54.3 %shard_map.80 = (f32[16,512,768]{2,1,0:T(8,128)}, f32[2,256,768]{2,1,0:T(8,128)}, f32[2,256,768]{2,1,0:T(8,128)}) custom-call(bf16[16,512,768]{2,1,0:T(8,128)(2,1)} %get-tuple-element.78.refs_0_.grad_ref, bf16[2,16,512,768]{3,2,1,0:T(8,128)(2,1)} %x_ref.1, bf16[16,512,256]{2,1,0:T(8,128)(2,1)} %collective-permute-done.10.h_a, ...), custom_call_target="tpu_custom_call" | custom-call | flops 25769803776 | bytes 75497472 | tf_op jit(solution)/shard_map/pallas_call | solution.py:192
  1467.5 2.2 slice.45.x_ref
  1471.1 1.6 collective-permute-start.26
  1472.7 16.1 collective-permute-done.49
  1489.6 4.6 copy-done
  1494.2 14.6 shard_map.83
  1508.8 2.6 add.45
  1511.4 2.0 add.46
  1513.4 2.0 add.48.kept_ref
  1515.4 1.8 collective-permute-start.22
  1518.4 20.6 %collective-permute-done.28 = f32[768,768]{1,0:T(8,128)} collective-permute-done((f32[768,768]{1,0:T(8,128)}, f32[768,768]{1,0:T(8,128)}, u32[]{:S(2)}, u32[]{:S(2)}) %collective-permute-start.28) | collective-permute-done | bytes 2359328 | tf_op jit(solution)/shard_map/ppermute | solution.py:409
  1540.5 10.8 shard_map.85
  1551.3 2.0 add.41.refs_0_.refs_1_
  1553.8 6.3 shard_map.86
  1560.1 2.1 slice.44.grad_ref
  1562.2 4.4 shard_map.87
  1567.1 1.5 collective-permute-start.31
  1572.5 92.3 %collective-permute-done.36 = f32[64,768]{1,0:T(8,128)S(1)} collective-permute-done((f32[64,768]{1,0:T(8,128)S(1)}, f32[64,768]{1,0:T(8,128)S(1)}, u32[]{:S(2)}, u32[]{:S(2)}) %collective-permute-start.36) | collective-permute-done | bytes 196640 | tf_op jit(solution)/shard_map/ppermute | solution.py:409
  1667.0 26.0 %collective-permute-done.33 = f32[64,768]{1,0:T(8,128)S(1)} collective-permute-done((f32[64,768]{1,0:T(8,128)S(1)}, f32[64,768]{1,0:T(8,128)S(1)}, u32[]{:S(2)}, u32[]{:S(2)}) %collective-permute-start.33) | collective-permute-done | bytes 196640 | tf_op jit(solution)/shard_map/ppermute | solution.py:409
  1695.2 5.6 collective-permute-done.40.refs_4_
  1701.6 7.6 collective-permute-done.34.refs_6_.refs_2_
  1710.7 4.8 collective-permute-done.41.refs_5_
  1719.1 5.6 shard_map.88._
  1724.8 8.0 shard_map.89
  1732.8 3.0 shard_map.97
  1735.8 1.7 shard_map.98
  (155 shorter events, 47.3 us)
Async XLA Ops:
  24.5 12.7 copy-start.18
  24.5 12.7 copy-start.19
  31.7 677.2 %collective-permute-start.7 = (bf16[16,512,768]{2,1,0:T(8,128)(2,1)S(1)}, bf16[16,512,768]{2,1,0:T(8,128)(2,1)}, u32[]{:S(2)}, u32[]{:S(2)}) collective-permute-start(bf16[16,512,768]{2,1,0:T(8,128)(2,1)S(1)} %dynamic-slice_bitcast_fusion.1), channel_id=1, source_target_pairs={{0,1},{1,0},{2,3},{3,2},{4,5},{5,4},{6,7},{7,6}} | collective-permute-start | bytes 37748744 | tf_op jit(solution)/shard_map/ppermute | solution.py:406
  32.5 797.8 %collective-permute-start.1 = (bf16[16,512,768]{2,1,0:T(8,128)(2,1)}, bf16[16,512,768]{2,1,0:T(8,128)(2,1)}, u32[]{:S(2)}, u32[]{:S(2)}) collective-permute-start(bf16[16,512,768]{2,1,0:T(8,128)(2,1)} %dynamic-slice_bitcast_fusion.2), channel_id=1, source_target_pairs={{0,3},{1,2},{2,1},{3,0},{4,7},{5,6},{6,5},{7,4}} | collective-permute-start | bytes 37748744 | tf_op jit(solution)/shard_map/ppermute | solution.py:406
  35.1 796.1 %collective-permute-start = (bf16[16,512,768]{2,1,0:T(8,128)(2,1)}, bf16[16,512,768]{2,1,0:T(8,128)(2,1)}, u32[]{:S(2)}, u32[]{:S(2)}) collective-permute-start(bf16[16,512,768]{2,1,0:T(8,128)(2,1)} %dynamic-slice_bitcast_fusion.3), channel_id=1, source_target_pairs={{0,2},{1,3},{2,0},{3,1},{4,6},{5,7},{6,4},{7,5}} | collective-permute-start | bytes 37748744 | tf_op jit(solution)/shard_map/ppermute | solution.py:406
  35.1 547.3 %collective-permute-start.2 = (bf16[192,768]{1,0:T(8,128)(2,1)S(1)}, bf16[192,768]{1,0:T(8,128)(2,1)S(1)}, u32[]{:S(2)}, u32[]{:S(2)}) collective-permute-start(bf16[192,768]{1,0:T(8,128)(2,1)S(1)} %select_bitcast_fusion.2), channel_id=1, source_target_pairs={{0,2},{1,3},{2,0},{3,1},{4,6},{5,7},{6,4},{7,5}} | collective-permute-start | bytes 884744 | tf_op jit(solution)/shard_map/ppermute | solution.py:406
  37.3 590.9 %collective-permute-start.12 = (bf16[768,768]{1,0:T(8,128)(2,1)S(1)}, bf16[768,768]{1,0:T(8,128)(2,1)S(1)}, u32[]{:S(2)}, u32[]{:S(2)}) collective-permute-start(bf16[768,768]{1,0:T(8,128)(2,1)S(1)} %select_bitcast_fusion), channel_id=1, source_target_pairs={{0,2},{1,3},{2,0},{3,1},{4,6},{5,7},{6,4},{7,5}} | collective-permute-start | bytes 3538952 | tf_op jit(solution)/shard_map/ppermute | solution.py:406
  582.4 44.0 %collective-permute-start.3 = (bf16[576,768]{1,0:T(8,128)(2,1)S(1)}, bf16[576,768]{1,0:T(8,128)(2,1)S(1)}, u32[]{:S(2)}, u32[]{:S(2)}) collective-permute-start(bf16[576,768]{1,0:T(8,128)(2,1)S(1)} %select_bitcast_fusion.1), channel_id=1, source_target_pairs={{0,2},{1,3},{2,0},{3,1},{4,6},{5,7},{6,4},{7,5}} | collective-permute-start | bytes 2654216 | tf_op jit(solution)/shard_map/ppermute | solution.py:406
  626.5 28.9 %collective-permute-start.4 = (bf16[768,768]{1,0:T(8,128)(2,1)S(1)}, bf16[768,768]{1,0:T(8,128)(2,1)S(1)}, u32[]{:S(2)}, u32[]{:S(2)}) collective-permute-start(bf16[768,768]{1,0:T(8,128)(2,1)S(1)} %constant_dynamic-update-slice_fusion), channel_id=1, source_target_pairs={{0,4},{4,0},{1,5},{5,1},{2,6},{6,2},{3,7},{7,3}} | collective-permute-start | bytes 3538952 | tf_op jit(solution)/shard_map/ppermute | solution.py:409
  628.2 27.2 %copy-start.20 = (bf16[768,768]{1,0:T(8,128)(2,1)}, bf16[768,768]{1,0:T(8,128)(2,1)S(1)}, u32[]{:S(2)}) copy-start(bf16[768,768]{1,0:T(8,128)(2,1)S(1)} %collective-permute-done.12) | copy-start | bytes 3538948
  628.2 51.3 %collective-permute-start.13 = (bf16[768,768]{1,0:T(8,128)(2,1)S(1)}, bf16[768,768]{1,0:T(8,128)(2,1)S(1)}, u32[]{:S(2)}, u32[]{:S(2)}) collective-permute-start(bf16[768,768]{1,0:T(8,128)(2,1)S(1)} %collective-permute-done.12), channel_id=1, source_target_pairs={{0,4},{4,0},{1,5},{5,1},{2,6},{6,2},{3,7},{7,3}} | collective-permute-start | bytes 3538952 | tf_op jit(solution)/shard_map/ppermute | solution.py:409
  655.3 24.2 %copy-start.22 = (bf16[768,768]{1,0:T(8,128)(2,1)}, bf16[768,768]{1,0:T(8,128)(2,1)S(1)}, u32[]{:S(2)}) copy-start(bf16[768,768]{1,0:T(8,128)(2,1)S(1)} %collective-permute-done.4) | copy-start | bytes 3538948
  655.3 53.0 %collective-permute-start.8 = (bf16[2,768,768]{2,1,0:T(8,128)(2,1)S(1)}, bf16[2,768,768]{2,1,0:T(8,128)(2,1)}, u32[]{:S(2)}, u32[]{:S(2)}) collective-permute-start(bf16[2,768,768]{2,1,0:T(8,128)(2,1)S(1)} %copy-done.19), channel_id=1, source_target_pairs={{0,1},{1,0},{2,3},{3,2},{4,5},{5,4},{6,7},{7,6}} | collective-permute-start | bytes 7077896 | tf_op jit(solution)/shard_map/ppermute | solution.py:406
  680.6 28.3 %collective-permute-start.9 = (bf16[2,768,768]{2,1,0:T(8,128)(2,1)S(1)}, bf16[2,768,768]{2,1,0:T(8,128)(2,1)}, u32[]{:S(2)}, u32[]{:S(2)}) collective-permute-start(bf16[2,768,768]{2,1,0:T(8,128)(2,1)S(1)} %copy-done.18), channel_id=1, source_target_pairs={{0,1},{1,0},{2,3},{3,2},{4,5},{5,4},{6,7},{7,6}} | collective-permute-start | bytes 7077896 | tf_op jit(solution)/shard_map/ppermute | solution.py:406
  708.3 244.1 %collective-permute-start.18 = (bf16[16,512,768]{2,1,0:T(8,128)(2,1)}, bf16[16,512,768]{2,1,0:T(8,128)(2,1)}, u32[]{:S(2)}, u32[]{:S(2)}) collective-permute-start(bf16[16,512,768]{2,1,0:T(8,128)(2,1)} %dynamic-slice_bitcast_fusion), channel_id=1, source_target_pairs={{0,1},{1,0},{2,3},{3,2},{4,5},{5,4},{6,7},{7,6}} | collective-permute-start | bytes 37748744 | tf_op jit(solution)/shard_map/ppermute | solution.py:406
  708.8 120.2 %collective-permute-start.5 = (bf16[768,768]{1,0:T(8,128)(2,1)}, bf16[768,768]{1,0:T(8,128)(2,1)}, u32[]{:S(2)}, u32[]{:S(2)}) collective-permute-start(bf16[768,768]{1,0:T(8,128)(2,1)} %get-tuple-element.144.refs_4_), channel_id=1, source_target_pairs={{0,1},{1,0},{2,3},{3,2},{4,5},{5,4},{6,7},{7,6}} | collective-permute-start | bytes 3538952 | tf_op jit(solution)/shard_map/ppermute | solution.py:406
  708.8 121.4 %collective-permute-start.6 = (bf16[768,768]{1,0:T(8,128)(2,1)}, bf16[768,768]{1,0:T(8,128)(2,1)}, u32[]{:S(2)}, u32[]{:S(2)}) collective-permute-start(bf16[768,768]{1,0:T(8,128)(2,1)} %get-tuple-element.143.refs_6_), channel_id=1, source_target_pairs={{0,1},{1,0},{2,3},{3,2},{4,5},{5,4},{6,7},{7,6}} | collective-permute-start | bytes 3538952 | tf_op jit(solution)/shard_map/ppermute | solution.py:406
  829.0 271.5 %collective-permute-start.16 = (bf16[16,512,384]{2,1,0:T(8,128)(2,1)}, bf16[16,512,384]{2,1,0:T(8,128)(2,1)}, u32[]{:S(2)}, u32[]{:S(2)}) collective-permute-start(bf16[16,512,384]{2,1,0:T(8,128)(2,1)} %dynamic-slice_bitcast_fusion.5), channel_id=1, source_target_pairs={{0,2},{1,3},{2,0},{3,1},{4,6},{5,7},{6,4},{7,5}} | collective-permute-start | bytes 18874376 | tf_op jit(solution)/shard_map/ppermute | solution.py:406
  830.2 270.3 %collective-permute-start.17 = (bf16[16,512,384]{2,1,0:T(8,128)(2,1)}, bf16[16,512,384]{2,1,0:T(8,128)(2,1)}, u32[]{:S(2)}, u32[]{:S(2)}) collective-permute-start(bf16[16,512,384]{2,1,0:T(8,128)(2,1)} %dynamic-slice_bitcast_fusion.4), channel_id=1, source_target_pairs={{0,3},{1,2},{2,1},{3,0},{4,7},{5,6},{6,5},{7,4}} | collective-permute-start | bytes 18874376 | tf_op jit(solution)/shard_map/ppermute | solution.py:406
  830.4 241.8 %collective-permute-start.14 = (bf16[768,768]{1,0:T(8,128)(2,1)}, bf16[768,768]{1,0:T(8,128)(2,1)}, u32[]{:S(2)}, u32[]{:S(2)}) collective-permute-start(bf16[768,768]{1,0:T(8,128)(2,1)} %get-tuple-element.142.refs_4_.up_a), channel_id=1, source_target_pairs={{0,1},{1,0},{2,3},{3,2},{4,5},{5,4},{6,7},{7,6}} | collective-permute-start | bytes 3538952 | tf_op jit(solution)/shard_map/ppermute | solution.py:406
  831.2 241.3 %collective-permute-start.15 = (bf16[768,768]{1,0:T(8,128)(2,1)}, bf16[768,768]{1,0:T(8,128)(2,1)}, u32[]{:S(2)}, u32[]{:S(2)}) collective-permute-start(bf16[768,768]{1,0:T(8,128)(2,1)} %get-tuple-element.141.refs_6_.down_a), channel_id=1, source_target_pairs={{0,1},{1,0},{2,3},{3,2},{4,5},{5,4},{6,7},{7,6}} | collective-permute-start | bytes 3538952 | tf_op jit(solution)/shard_map/ppermute | solution.py:406
  952.4 237.3 %collective-permute-start.50 = (f32[2,768,768]{2,1,0:T(8,128)}, f32[2,768,768]{2,1,0:T(8,128)}, u32[]{:S(2)}, u32[]{:S(2)}) collective-permute-start(f32[2,768,768]{2,1,0:T(8,128)} %get-tuple-element.130), channel_id=1, source_target_pairs={{0,1},{1,0},{2,3},{3,2},{4,5},{5,4},{6,7},{7,6}} | collective-permute-start | bytes 14155784 | tf_op jit(solution)/shard_map/ppermute | solution.py:406
  1072.2 136.6 %collective-permute-start.48 = (f32[2,768,768]{2,1,0:T(8,128)}, f32[2,768,768]{2,1,0:T(8,128)}, u32[]{:S(2)}, u32[]{:S(2)}) collective-permute-start(f32[2,768,768]{2,1,0:T(8,128)} %get-tuple-element.126), channel_id=1, source_target_pairs={{0,1},{1,0},{2,3},{3,2},{4,5},{5,4},{6,7},{7,6}} | collective-permute-start | bytes 14155784 | tf_op jit(solution)/shard_map/ppermute | solution.py:406
  1072.5 137.9 %collective-permute-start.27 = (f32[2,768,768]{2,1,0:T(8,128)}, f32[2,768,768]{2,1,0:T(8,128)}, u32[]{:S(2)}, u32[]{:S(2)}) collective-permute-start(f32[2,768,768]{2,1,0:T(8,128)} %get-tuple-element.106), channel_id=1, source_target_pairs={{0,1},{1,0},{2,3},{3,2},{4,5},{5,4},{6,7},{7,6}} | collective-permute-start | bytes 14155784 | tf_op jit(solution)/shard_map/ppermute | solution.py:406
  1178.8 21.1 %collective-permute-start.44 = (f32[2,384,768]{2,1,0:T(8,128)}, f32[2,384,768]{2,1,0:T(8,128)S(1)}, u32[]{:S(2)}, u32[]{:S(2)}) collective-permute-start(f32[2,384,768]{2,1,0:T(8,128)} %get-tuple-element.122), channel_id=1, source_target_pairs={{0,1},{1,0},{2,3},{3,2},{4,5},{5,4},{6,7},{7,6}} | collective-permute-start | bytes 7077896 | tf_op jit(solution)/shard_map/ppermute | solution.py:406
  1188.9 222.3 %collective-permute-start.11 = (bf16[16,512,256]{2,1,0:T(8,128)(2,1)}, bf16[16,512,256]{2,1,0:T(8,128)(2,1)}, u32[]{:S(2)}, u32[]{:S(2)}) collective-permute-start(bf16[16,512,256]{2,1,0:T(8,128)(2,1)} %dynamic-slice_bitcast_fusion.6), channel_id=1, source_target_pairs={{0,3},{1,2},{2,1},{3,0},{4,7},{5,6},{6,5},{7,4}} | collective-permute-start | bytes 12582920 | tf_op jit(solution)/shard_map/ppermute | solution.py:406
  1189.7 222.9 %collective-permute-start.10 = (bf16[16,512,256]{2,1,0:T(8,128)(2,1)}, bf16[16,512,256]{2,1,0:T(8,128)(2,1)}, u32[]{:S(2)}, u32[]{:S(2)}) collective-permute-start(bf16[16,512,256]{2,1,0:T(8,128)(2,1)} %dynamic-slice_bitcast_fusion.7), channel_id=1, source_target_pairs={{0,2},{1,3},{2,0},{3,1},{4,6},{5,7},{6,4},{7,5}} | collective-permute-start | bytes 12582920 | tf_op jit(solution)/shard_map/ppermute | solution.py:406
  1201.3 53.7 %collective-permute-start.51 = (f32[768,768]{1,0:T(8,128)}, f32[768,768]{1,0:T(8,128)}, u32[]{:S(2)}, u32[]{:S(2)}) collective-permute-start(f32[768,768]{1,0:T(8,128)} %get-tuple-element.132), channel_id=1, source_target_pairs={{0,4},{4,0},{1,5},{5,1},{2,6},{6,2},{3,7},{7,3}} | collective-permute-start | bytes 7077896 | tf_op jit(solution)/shard_map/ppermute | solution.py:409
  1208.9 201.8 %collective-permute-start.19 = (bf16[8,512,128]{2,1,0:T(8,128)(2,1)}, bf16[8,512,128]{2,1,0:T(8,128)(2,1)}, u32[]{:S(2)}, u32[]{:S(2)}) collective-permute-start(bf16[8,512,128]{2,1,0:T(8,128)(2,1)} %get-tuple-element.89), channel_id=1, source_target_pairs={{0,2},{1,3},{2,0},{3,1},{4,6},{5,7},{6,4},{7,5}} | collective-permute-start | bytes 3145736 | tf_op jit(solution)/shard_map/ppermute | solution.py:406
  1210.4 198.7 %collective-permute-start.25 = (bf16[3,512,128]{2,1,0:T(8,128)(2,1)}, bf16[3,512,128]{2,1,0:T(8,128)(2,1)S(1)}, u32[]{:S(2)}, u32[]{:S(2)}) collective-permute-start(bf16[3,512,128]{2,1,0:T(8,128)(2,1)} %get-tuple-element.96), channel_id=1, source_target_pairs={{0,2},{1,3},{2,0},{3,1},{4,6},{5,7},{6,4},{7,5}} | collective-permute-start | bytes 1179656 | tf_op jit(solution)/shard_map/ppermute | solution.py:406
  1255.0 153.3 %collective-permute-start.21 = (bf16[2,512,128]{2,1,0:T(8,128)(2,1)}, bf16[2,512,128]{2,1,0:T(8,128)(2,1)S(1)}, u32[]{:S(2)}, u32[]{:S(2)}) collective-permute-start(bf16[2,512,128]{2,1,0:T(8,128)(2,1)} %get-tuple-element.92), channel_id=1, source_target_pairs={{0,2},{1,3},{2,0},{3,1},{4,6},{5,7},{6,4},{7,5}} | collective-permute-start | bytes 786440 | tf_op jit(solution)/shard_map/ppermute | solution.py:406
  1280.6 5.8 copy-start.11
  1408.3 59.2 %collective-permute-start.20 = (bf16[8,512,128]{2,1,0:T(8,128)(2,1)}, bf16[8,512,128]{2,1,0:T(8,128)(2,1)}, u32[]{:S(2)}, u32[]{:S(2)}) collective-permute-start(bf16[8,512,128]{2,1,0:T(8,128)(2,1)} %get-tuple-element.90), channel_id=1, source_target_pairs={{0,3},{1,2},{2,1},{3,0},{4,7},{5,6},{6,5},{7,4}} | collective-permute-start | bytes 3145736 | tf_op jit(solution)/shard_map/ppermute | solution.py:406
  1409.1 62.0 %collective-permute-start.45 = (f32[384,768]{1,0:T(8,128)}, f32[384,768]{1,0:T(8,128)}, u32[]{:S(2)}, u32[]{:S(2)}) collective-permute-start(f32[384,768]{1,0:T(8,128)} %get-tuple-element.124), channel_id=1, source_target_pairs={{0,4},{4,0},{1,5},{5,1},{2,6},{6,2},{3,7},{7,3}} | collective-permute-start | bytes 3538952 | tf_op jit(solution)/shard_map/ppermute | solution.py:409
  1410.6 78.2 %collective-permute-start.49 = (f32[768,768]{1,0:T(8,128)}, f32[768,768]{1,0:T(8,128)}, u32[]{:S(2)}, u32[]{:S(2)}) collective-permute-start(f32[768,768]{1,0:T(8,128)} %get-tuple-element.128), channel_id=1, source_target_pairs={{0,4},{4,0},{1,5},{5,1},{2,6},{6,2},{3,7},{7,3}} | collective-permute-start | bytes 7077896 | tf_op jit(solution)/shard_map/ppermute | solution.py:409
  1411.1 127.9 %collective-permute-start.28 = (f32[768,768]{1,0:T(8,128)}, f32[768,768]{1,0:T(8,128)}, u32[]{:S(2)}, u32[]{:S(2)}) collective-permute-start(f32[768,768]{1,0:T(8,128)} %get-tuple-element.108), channel_id=1, source_target_pairs={{0,4},{4,0},{1,5},{5,1},{2,6},{6,2},{3,7},{7,3}} | collective-permute-start | bytes 7077896 | tf_op jit(solution)/shard_map/ppermute | solution.py:409
  1412.6 76.9 %collective-permute-start.52 = (f32[768,768]{1,0:T(8,128)}, f32[768,768]{1,0:T(8,128)}, u32[]{:S(2)}, u32[]{:S(2)}) collective-permute-start(f32[768,768]{1,0:T(8,128)} %add.47), channel_id=1, source_target_pairs={{0,2},{1,3},{2,0},{3,1},{4,6},{5,7},{6,4},{7,5}} | collective-permute-start | bytes 7077896 | tf_op jit(solution)/shard_map/ppermute | solution.py:406
  1467.5 99.1 %collective-permute-start.30 = (f32[2,256,768]{2,1,0:T(8,128)}, f32[2,256,768]{2,1,0:T(8,128)S(1)}, u32[]{:S(2)}, u32[]{:S(2)}) collective-permute-start(f32[2,256,768]{2,1,0:T(8,128)} %get-tuple-element.110), channel_id=1, source_target_pairs={{0,1},{1,0},{2,3},{3,2},{4,5},{5,4},{6,7},{7,6}} | collective-permute-start | bytes 4718600 | tf_op jit(solution)/shard_map/ppermute | solution.py:406
  1469.8 19.0 %copy-start.25 = (bf16[3,512,128]{2,1,0:T(8,128)(2,1)S(1)}, bf16[3,512,128]{2,1,0:T(8,128)(2,1)}, u32[]{:S(2)}) copy-start(bf16[3,512,128]{2,1,0:T(8,128)(2,1)} %get-tuple-element.94) | copy-start | bytes 1179652
  1469.8 19.8 %copy-start.26 = (bf16[3,512,128]{2,1,0:T(8,128)(2,1)S(1)}, bf16[3,512,128]{2,1,0:T(8,128)(2,1)}, u32[]{:S(2)}) copy-start(bf16[3,512,128]{2,1,0:T(8,128)(2,1)} %get-tuple-element.95) | copy-start | bytes 1179652
  1469.8 19.8 %copy-start.1 = (bf16[768,768]{1,0:T(8,128)(2,1)S(1)}, bf16[768,768]{1,0:T(8,128)(2,1)}, u32[]{:S(2)}) copy-start(bf16[768,768]{1,0:T(8,128)(2,1)} %get-tuple-element.141.refs_6_.down_a) | copy-start | bytes 3538948
  1471.1 44.3 %collective-permute-start.26 = (bf16[3,512,128]{2,1,0:T(8,128)(2,1)S(1)}, bf16[3,512,128]{2,1,0:T(8,128)(2,1)S(1)}, u32[]{:S(2)}, u32[]{:S(2)}) collective-permute-start(bf16[3,512,128]{2,1,0:T(8,128)(2,1)S(1)} %copy-done.27), channel_id=1, source_target_pairs={{0,3},{1,2},{2,1},{3,0},{4,7},{5,6},{6,5},{7,4}} | collective-permute-start | bytes 1179656 | tf_op jit(solution)/shard_map/ppermute | solution.py:406
  1488.8 28.4 %collective-permute-start.23 = (bf16[3,512,128]{2,1,0:T(8,128)(2,1)S(1)}, bf16[3,512,128]{2,1,0:T(8,128)(2,1)S(1)}, u32[]{:S(2)}, u32[]{:S(2)}) collective-permute-start(bf16[3,512,128]{2,1,0:T(8,128)(2,1)S(1)} %copy-done.25), channel_id=1, source_target_pairs={{0,2},{1,3},{2,0},{3,1},{4,6},{5,7},{6,4},{7,5}} | collective-permute-start | bytes 1179656 | tf_op jit(solution)/shard_map/ppermute | solution.py:406
  1489.6 63.7 %collective-permute-start.24 = (bf16[3,512,128]{2,1,0:T(8,128)(2,1)S(1)}, bf16[3,512,128]{2,1,0:T(8,128)(2,1)S(1)}, u32[]{:S(2)}, u32[]{:S(2)}) collective-permute-start(bf16[3,512,128]{2,1,0:T(8,128)(2,1)S(1)} %copy-done.26), channel_id=1, source_target_pairs={{0,3},{1,2},{2,1},{3,0},{4,7},{5,6},{6,5},{7,4}} | collective-permute-start | bytes 1179656 | tf_op jit(solution)/shard_map/ppermute | solution.py:406
  1494.2 14.6 copy-start.17
  1515.4 46.8 %collective-permute-start.22 = (bf16[2,512,128]{2,1,0:T(8,128)(2,1)S(1)}, bf16[2,512,128]{2,1,0:T(8,128)(2,1)S(1)}, u32[]{:S(2)}, u32[]{:S(2)}) collective-permute-start(bf16[2,512,128]{2,1,0:T(8,128)(2,1)S(1)} %copy-done.28), channel_id=1, source_target_pairs={{0,3},{1,2},{2,1},{3,0},{4,7},{5,6},{6,5},{7,4}} | collective-permute-start | bytes 786440 | tf_op jit(solution)/shard_map/ppermute | solution.py:406
  1517.2 54.4 %collective-permute-start.46 = (f32[384,768]{1,0:T(8,128)}, f32[384,768]{1,0:T(8,128)S(1)}, u32[]{:S(2)}, u32[]{:S(2)}) collective-permute-start(f32[384,768]{1,0:T(8,128)} %add.45), channel_id=1, source_target_pairs={{0,2},{1,3},{2,0},{3,1},{4,6},{5,7},{6,4},{7,5}} | collective-permute-start | bytes 3538952 | tf_op jit(solution)/shard_map/ppermute | solution.py:406
  1539.0 178.6 %collective-permute-start.53 = (f32[768,768]{1,0:T(8,128)S(1)}, f32[768,768]{1,0:T(8,128)S(1)}, u32[]{:S(2)}, u32[]{:S(2)}) collective-permute-start(f32[768,768]{1,0:T(8,128)S(1)} %add.48.kept_ref), channel_id=1, source_target_pairs={{0,4},{4,0},{1,5},{5,1},{2,6},{6,2},{3,7},{7,3}} | collective-permute-start | bytes 7077896 | tf_op jit(solution)/shard_map/ppermute | solution.py:409
  1540.5 10.8 copy-start.7
  1553.3 182.5 %collective-permute-start.29 = (f32[768,768]{1,0:T(8,128)S(1)}, f32[768,768]{1,0:T(8,128)S(1)}, u32[]{:S(2)}, u32[]{:S(2)}) collective-permute-start(f32[768,768]{1,0:T(8,128)S(1)} %add.41.refs_0_.refs_1_), channel_id=1, source_target_pairs={{0,4},{4,0},{1,5},{5,1},{2,6},{6,2},{3,7},{7,3}} | collective-permute-start | bytes 7077896 | tf_op jit(solution)/shard_map/ppermute | solution.py:409
  1566.6 2.1 collective-permute-start.35
  1567.1 99.2 %collective-permute-start.31 = (f32[256,768]{1,0:T(8,128)S(1)}, f32[256,768]{1,0:T(8,128)S(1)}, u32[]{:S(2)}, u32[]{:S(2)}) collective-permute-start(f32[256,768]{1,0:T(8,128)S(1)} %get-tuple-element.112), channel_id=1, source_target_pairs={{0,4},{4,0},{1,5},{5,1},{2,6},{6,2},{3,7},{7,3}} | collective-permute-start | bytes 2359304 | tf_op jit(solution)/shard_map/ppermute | solution.py:409
  1568.7 1.7 collective-permute-start.32
  1570.4 94.4 %collective-permute-start.36 = (f32[64,768]{1,0:T(8,128)S(1)}, f32[64,768]{1,0:T(8,128)S(1)}, u32[]{:S(2)}, u32[]{:S(2)}) collective-permute-start(f32[64,768]{1,0:T(8,128)S(1)} %get-tuple-element.120), channel_id=1, source_target_pairs={{0,4},{4,0},{1,5},{5,1},{2,6},{6,2},{3,7},{7,3}} | collective-permute-start | bytes 589832 | tf_op jit(solution)/shard_map/ppermute | solution.py:409
  1571.6 145.5 %collective-permute-start.47 = (f32[384,768]{1,0:T(8,128)S(1)}, f32[384,768]{1,0:T(8,128)S(1)}, u32[]{:S(2)}, u32[]{:S(2)}) collective-permute-start(f32[384,768]{1,0:T(8,128)S(1)} %collective-permute-done.46.refs_2_), channel_id=1, source_target_pairs={{0,4},{4,0},{1,5},{5,1},{2,6},{6,2},{3,7},{7,3}} | collective-permute-start | bytes 3538952 | tf_op jit(solution)/shard_map/ppermute | solution.py:409
  1664.7 28.3 %collective-permute-start.33 = (f32[64,768]{1,0:T(8,128)S(1)}, f32[64,768]{1,0:T(8,128)S(1)}, u32[]{:S(2)}, u32[]{:S(2)}) collective-permute-start(f32[64,768]{1,0:T(8,128)S(1)} %get-tuple-element.116), channel_id=1, source_target_pairs={{0,4},{4,0},{1,5},{5,1},{2,6},{6,2},{3,7},{7,3}} | collective-permute-start | bytes 589832 | tf_op jit(solution)/shard_map/ppermute | solution.py:409
  1666.3 27.6 %collective-permute-start.37 = (f32[64,768]{1,0:T(8,128)S(1)}, f32[64,768]{1,0:T(8,128)S(1)}, u32[]{:S(2)}, u32[]{:S(2)}) collective-permute-start(f32[64,768]{1,0:T(8,128)S(1)} %add.44), channel_id=1, source_target_pairs={{0,2},{1,3},{2,0},{3,1},{4,6},{5,7},{6,4},{7,5}} | collective-permute-start | bytes 589832 | tf_op jit(solution)/shard_map/ppermute | solution.py:406
  1693.0 7.8 collective-permute-start.40
  1693.9 15.3 collective-permute-start.34
  1700.8 14.8 collective-permute-start.41
  1709.2 28.3 %collective-permute-start.38 = (f32[128,768]{1,0:T(8,128)S(1)}, f32[128,768]{1,0:T(8,128)S(1)}, u32[]{:S(2)}, u32[]{:S(2)}) collective-permute-start(f32[128,768]{1,0:T(8,128)S(1)} %collective-permute-done.34.refs_6_.refs_2_), channel_id=1, source_target_pairs={{0,4},{4,0},{1,5},{5,1},{2,6},{6,2},{3,7},{7,3}} | collective-permute-start | bytes 1179656 | tf_op jit(solution)/shard_map/ppermute | solution.py:409
  1715.6 22.0 %collective-permute-start.43 = (f32[128,768]{1,0:T(8,128)S(1)}, f32[128,768]{1,0:T(8,128)S(1)}, u32[]{:S(2)}, u32[]{:S(2)}) collective-permute-start(f32[128,768]{1,0:T(8,128)S(1)} %collective-permute-done.41.refs_5_), channel_id=1, source_target_pairs={{0,4},{4,0},{1,5},{5,1},{2,6},{6,2},{3,7},{7,3}} | collective-permute-start | bytes 1179656 | tf_op jit(solution)/shard_map/ppermute | solution.py:409
  1717.1 20.4 %collective-permute-start.42 = (f32[64,768]{1,0:T(8,128)S(1)}, f32[64,768]{1,0:T(8,128)S(1)}, u32[]{:S(2)}, u32[]{:S(2)}) collective-permute-start(f32[64,768]{1,0:T(8,128)S(1)} %collective-permute-done.40.refs_4_), channel_id=1, source_target_pairs={{0,4},{4,0},{1,5},{5,1},{2,6},{6,2},{3,7},{7,3}} | collective-permute-start | bytes 589832 | tf_op jit(solution)/shard_map/ppermute | solution.py:409
  1717.6 21.3 %collective-permute-start.39 = (f32[64,768]{1,0:T(8,128)S(1)}, f32[64,768]{1,0:T(8,128)S(1)}, u32[]{:S(2)}, u32[]{:S(2)}) collective-permute-start(f32[64,768]{1,0:T(8,128)S(1)} %collective-permute-done.37.refs_3_), channel_id=1, source_target_pairs={{0,4},{4,0},{1,5},{5,1},{2,6},{6,2},{3,7},{7,3}} | collective-permute-start | bytes 589832 | tf_op jit(solution)/shard_map/ppermute | solution.py:409
  (19 other events, 44.1 us)
